TPU v7x, 32 devices: a whole 2x2x4 slice. The times are simulated.
32 devices in a mesh: band: 8 (over z, y), dir: 4 (over x, core).
Axes of the slice: x: 2, y: 2, z: 4, core: 2. Of those that a mesh axis runs over, the one named last changes fastest.
Arguments:
- visibilities: float32 [8, 2, 2, 2, 16, 512], P('band'), may hold values from -6 to 6
- coherencies: float32 [8, 16, 2, 2, 2, 16, 512], P('band', 'dir'), may hold values from -1.2 to 1.2
- jones_start: float32 [8, 16, 2, 2, 2, 1024], P('band', 'dir'), may hold values from -3.6 to 3.6
- dual_start: float32 [8, 16, 2, 2, 2, 1024], P('band', 'dir'), may hold values from -6 to 6
- consensus_start: float32 [8, 16, 2, 2, 2, 1024], P(None, 'dir'), may hold values from -1.8 to 1.8
- freq_basis: float32 [8, 8], P('band'), may hold values from -1 to 1
- baseline_station_pairs: int32 [2, 512], replicated, may hold values from 0 to 1023
Outputs:
- jones_final: float32 [8, 16, 2, 2, 2, 1024], P('band', 'dir')
- dual_final: float32 [8, 16, 2, 2, 2, 1024], P('band', 'dir')
- consensus_coeffs: float32 [8, 16, 2, 2, 2, 1024], P(None, 'dir')
All inputs are finite; a program needn't handle non-finite values.
Results may differ from a plain program's by a relative error of at most 0.0003.
Values sent between devices are 32-bit elements; how exact they have to be, the bound alone decides.
No kernel may reach another device: no remote copies, remote signals or barrier semaphores. Data moves between devices by JAX's collectives and lax.ppermute only.
A program may use at most 128 MiB of HBM per device.

v0:
```python
import jax
import jax.numpy as jnp
from jax import lax
from jax.sharding import PartitionSpec as P

ITERS = 3


RHO = 5.0
RIDGE = 0.25


def small_mul(left, right):
    return left[:, 0:1] * right[0:1] + left[:, 1:2] * right[1:2]


def complex_mul(left, right):
    real_part = small_mul(left[0], right[0]) - small_mul(left[1], right[1])
    imag_part = small_mul(left[0], right[1]) + small_mul(left[1], right[0])
    return jnp.stack([real_part, imag_part])


def hermitian(value):
    return jnp.stack([jnp.swapaxes(value[0], 0, 1), -jnp.swapaxes(value[1], 0, 1)])


def solve_right(numer, matrix):
    adjugate = jnp.stack(
        [
            jnp.stack([matrix[:, 1, 1], -matrix[:, 0, 1]], axis=1),
            jnp.stack([-matrix[:, 1, 0], matrix[:, 0, 0]], axis=1),
        ],
        axis=1,
    )
    det_real = (
        matrix[0, 0, 0] * matrix[0, 1, 1]
        - matrix[1, 0, 0] * matrix[1, 1, 1]
        - (matrix[0, 0, 1] * matrix[0, 1, 0] - matrix[1, 0, 1] * matrix[1, 1, 0])
    )
    det_imag = (
        matrix[0, 0, 0] * matrix[1, 1, 1]
        + matrix[1, 0, 0] * matrix[0, 1, 1]
        - (matrix[0, 0, 1] * matrix[1, 1, 0] + matrix[1, 0, 1] * matrix[0, 1, 0])
    )
    product = complex_mul(numer, adjugate)
    divisor = det_real * det_real + det_imag * det_imag
    real_part = (product[0] * det_real + product[1] * det_imag) / divisor
    imag_part = (product[1] * det_real - product[0] * det_imag) / divisor
    return jnp.stack([real_part, imag_part])


def predict(jones_k, coher_k, first, second):
    jones_first = jnp.take(jones_k, first, axis=-1)[..., None, :]
    jones_second = jnp.take(jones_k, second, axis=-1)[..., None, :]
    return complex_mul(complex_mul(jones_first, coher_k), hermitian(jones_second))


def baseline_terms(target, jones_k, coher_k, first, second):
    jones_first = jnp.take(jones_k, first, axis=-1)[..., None, :]
    jones_second = jnp.take(jones_k, second, axis=-1)[..., None, :]
    along_term = complex_mul(coher_k, hermitian(jones_second))
    back_term = hermitian(complex_mul(jones_first, coher_k))
    flipped = hermitian(target)
    right_first = jnp.sum(complex_mul(target, hermitian(along_term)), axis=-2)
    normal_first = jnp.sum(complex_mul(along_term, hermitian(along_term)), axis=-2)
    right_second = jnp.sum(complex_mul(flipped, hermitian(back_term)), axis=-2)
    normal_second = jnp.sum(complex_mul(back_term, hermitian(back_term)), axis=-2)
    first_part = jnp.concatenate([right_first.reshape(8, -1), normal_first.reshape(8, -1)], axis=0)
    second_part = jnp.concatenate(
        [right_second.reshape(8, -1), normal_second.reshape(8, -1)], axis=0
    )
    return jnp.concatenate([first_part, second_part], axis=1)


def update_one(right_sum, normal_sum, consensus, dual):
    identity = jnp.stack([jnp.eye(2, dtype=jnp.float32), jnp.zeros((2, 2), jnp.float32)])[..., None]
    matrix = normal_sum + RHO * identity
    return solve_right(right_sum + RHO * consensus - dual, matrix)


def apply_inverse(scale_factor, sums):
    flat = sums.reshape(sums.shape[0], -1)
    return jax.scipy.linalg.cho_solve((scale_factor, True), flat).reshape(sums.shape)


def local(
    visibilities,
    coherencies,
    jones_start,
    dual_start,
    consensus_start,
    freq_basis,
    baseline_station_pairs,
):
    coefficient_row = freq_basis[0]
    terms = coefficient_row.shape[0]
    outer = coefficient_row[:, None] * coefficient_row[None, :]
    gram = lax.psum(outer, "band") + RIDGE * lax.axis_size("band") * jnp.eye(
        terms, dtype=jnp.float32
    )
    scale_factor = jnp.linalg.cholesky(gram)
    first = baseline_station_pairs[0]
    second = baseline_station_pairs[1]
    stations = jones_start.shape[-1]
    station_ids = jnp.arange(stations, dtype=jnp.int32)
    onehots = (jnp.concatenate([first, second])[:, None] == station_ids[None, :]).astype(
        jnp.float32
    )
    vis_band = visibilities[0]
    coher_band = coherencies[0]
    jones = jones_start[0]
    dual = dual_start[0]
    dirs = jones.shape[0]
    coeffs = consensus_start
    consensus = jnp.tensordot(coefficient_row, coeffs, axes=(0, 0), precision=lax.Precision.HIGHEST)
    for turn_index in range(ITERS):
        model_terms = jax.vmap(predict, (0, 0, None, None))(jones, coher_band, first, second)
        model_total = lax.psum(jnp.sum(model_terms, axis=0), "dir")
        residual = vis_band - model_total
        normal_terms = jax.vmap(baseline_terms, (0, 0, 0, None, None))(
            residual[None] + model_terms, jones, coher_band, first, second
        )
        stacked = normal_terms.reshape(dirs * 16, -1)
        segment = jnp.dot(stacked, onehots, precision=lax.Precision.HIGHEST)
        segment = segment.reshape((dirs, 2, 2, 2, 2, stations))
        jones = jax.vmap(update_one)(segment[:, 0], segment[:, 1], consensus, dual)
        local_terms = coefficient_row.reshape((terms, 1, 1, 1, 1, 1)) * (jones + dual / RHO)[None]
        coeff_sums = lax.psum(local_terms, "band")
        coeffs = apply_inverse(scale_factor, coeff_sums)
        consensus = jnp.tensordot(
            coefficient_row, coeffs, axes=(0, 0), precision=lax.Precision.HIGHEST
        )
        dual = dual + RHO * (jones - consensus)
    return (jones[None], dual[None], coeffs)


def solution(mesh):
    in_specs = (
        P("band", None, None, None, None, None),
        P("band", "dir", None, None, None, None, None),
        P("band", "dir", None, None, None, None),
        P("band", "dir", None, None, None, None),
        P(None, "dir", None, None, None, None),
        P("band", None),
        P(),
    )
    out_specs = (
        P("band", "dir", None, None, None, None),
        P("band", "dir", None, None, None, None),
        P(None, "dir", None, None, None, None),
    )
    return jax.shard_map(local, mesh=mesh, in_specs=in_specs, out_specs=out_specs, check_vma=False)
```

profile of v0, /device:TPU:0, one launch (start us, length us, event | category | flops | bytes accessed | tf_op | source)
XLA Modules:
  0.0 537.7 jit_solution(1846712404722757130)
XLA Ops:
  8.1 2.3 slice_bitcast_fusion.13
  10.4 4.4 copy.255
  14.8 7.1 %gather_fusion = f32[512,4,2,2,2]{1,4,3,2,0:T(2,128)} fusion(f32[4,2,2,2,1024]{0,3,4,2,1:T(2,128)} %bitcast.712, s32[1024]{0:T(1024)S(1)} %pad_clamp_fusion.1), kind=kCustom, calls=%fused_computation.clone | custom fusion | bytes 133120 | tf_op jit(solution)/shard_map/vmap(jit(_take))/gather | solution.py:53
  22.0 3.1 select_bitcast_fusion.5
  28.2 7.2 %gather_fusion.1 = f32[512,4,2,2,2]{1,4,3,2,0:T(2,128)} fusion(f32[4,2,2,2,1024]{0,3,4,2,1:T(2,128)} %bitcast.713, s32[1024]{0:T(1024)S(1)} %pad_clamp_fusion), kind=kCustom, calls=%fused_computation.1.clone | custom fusion | bytes 133120 | tf_op jit(solution)/shard_map/vmap(jit(_take))/gather | solution.py:54
  35.4 3.4 select_bitcast_fusion.4
  39.6 2.6 fusion.90
  62.6 2.1 fusion.13
  64.8 23.1 %psum.51 = f32[8,8]{0,1:T(8,128)S(1)} all-reduce(f32[8,8]{0,1:T(8,128)S(1)} %broadcast_multiply_fusion.3), channel_id=1, replica_groups=mesh['band'=8,'dir'=4] {'band'}, use_global_device_ids=true, to_apply=%region_12.14 | all-reduce | flops 64 | bytes 512 | tf_op jit(solution)/shard_map/psum | solution.py:98
  101.2 4.6 copy.288
  105.8 7.1 %gather_fusion.2 = f32[512,4,2,2,2]{1,4,3,2,0:T(2,128)} fusion(f32[4,2,2,2,1024]{0,3,4,2,1:T(2,128)} %copy.288, s32[1024]{0:T(1024)S(1)} %pad_clamp_fusion.1), kind=kCustom, calls=%fused_computation.2.clone | custom fusion | bytes 133120 | tf_op jit(solution)/shard_map/vmap(jit(_take))/gather | solution.py:53
  112.9 7.1 %gather_fusion.3 = f32[512,4,2,2,2]{1,4,3,2,0:T(2,128)} fusion(f32[4,2,2,2,1024]{0,3,4,2,1:T(2,128)} %copy.288, s32[1024]{0:T(1024)S(1)} %copy-done.112), kind=kCustom, calls=%fused_computation.3.clone | custom fusion | bytes 133120 | tf_op jit(solution)/shard_map/vmap(jit(_take))/gather | solution.py:54
  120.1 3.0 select_bitcast_fusion.3
  140.5 2.0 select_bitcast_fusion.2
  148.4 2.5 fusion.86
  153.6 2.1 add_subtract_fusion.15
  159.1 2.0 slice_bitcast_fusion.49
  168.2 1.9 slice_bitcast_fusion.63
  170.6 18.1 %all-reduce.10.cloned.1.call-done = f32[2,2,2,16,512]{4,3,2,1,0:T(8,128)} async-done(((f32[2,2,2,16,512]{4,3,2,1,0:T(8,128)}), f32[2,2,2,16,512]{4,3,2,1,0:T(8,128)}) %all-reduce.10.cloned.1.call-update) | async-done | bytes 262160 | tf_op jit(solution)/shard_map/psum | solution.py:118
  196.1 2.4 fusion.3
  198.6 72.6 %all-reduce.12.cloned.1.call-done = f32[8,32768]{1,0:T(8,128)} async-done(((f32[8,32768]{1,0:T(8,128)}), f32[8,32768]{1,0:T(8,128)}) %all-reduce.12.cloned.1.call-update) | async-done | bytes 1048592 | tf_op jit(solution)/shard_map/psum | solution.py:128
  271.2 2.3 fusion.68
  276.8 4.6 copy.327
  281.4 7.1 %gather_fusion.4 = f32[512,4,2,2,2]{1,4,3,2,0:T(2,128)} fusion(f32[4,2,2,2,1024]{0,3,4,2,1:T(2,128)} %copy.327, s32[1024]{0:T(1024)S(1)} %pad_clamp_fusion.1), kind=kCustom, calls=%fused_computation.4.clone | custom fusion | bytes 133120 | tf_op jit(solution)/shard_map/vmap(jit(_take))/gather | solution.py:53
  288.5 7.1 %gather_fusion.5 = f32[512,4,2,2,2]{1,4,3,2,0:T(2,128)} fusion(f32[4,2,2,2,1024]{0,3,4,2,1:T(2,128)} %copy.327, s32[1024]{0:T(1024)S(1)} %copy-done.113), kind=kCustom, calls=%fused_computation.5.clone | custom fusion | bytes 133120 | tf_op jit(solution)/shard_map/vmap(jit(_take))/gather | solution.py:54
  295.7 3.0 select_bitcast_fusion.1
  312.9 2.0 select_bitcast_fusion
  333.0 22.8 %all-reduce.14.cloned.1.call-done = f32[2,2,2,16,512]{4,3,2,1,0:T(8,128)} async-done(((f32[2,2,2,16,512]{4,3,2,1,0:T(8,128)}), f32[2,2,2,16,512]{4,3,2,1,0:T(8,128)}) %all-reduce.14.cloned.1.call-update) | async-done | bytes 262160 | tf_op jit(solution)/shard_map/psum | solution.py:118
  363.7 74.3 %all-reduce.16.cloned.1.call-done = f32[8,32768]{1,0:T(8,128)} async-done(((f32[8,32768]{1,0:T(8,128)}), f32[8,32768]{1,0:T(8,128)}) %all-reduce.16.cloned.1.call-update) | async-done | bytes 1048592 | tf_op jit(solution)/shard_map/psum | solution.py:128
  438.0 2.3 fusion.64
  446.3 77.2 %all-reduce.18.cloned.1.call-done = f32[8,32768]{1,0:T(8,128)} async-done(((f32[8,32768]{1,0:T(8,128)}), f32[8,32768]{1,0:T(8,128)}) %all-reduce.18.cloned.1.call-update) | async-done | bytes 1048592 | tf_op jit(solution)/shard_map/psum | solution.py:128
  523.5 2.3 fusion.60
  (500 shorter events, 135.3 us)
Async XLA Ops:
  7.2 55.4 %copy-start = (f32[8,4,2,2,2,1024]{5,4,3,2,1,0:T(2,128)S(1)}, f32[8,4,2,2,2,1024]{5,4,3,2,1,0:T(2,128)}, u32[]{:S(2)}) copy-start(f32[8,4,2,2,2,1024]{5,4,3,2,1,0:T(2,128)} %param.15) | copy-start | bytes 3145732
  7.2 84.3 %all-reduce.8.cloned.1.call-start = ((), (), s32[]{:S(2)}) async-start(), calls=%async_computation | async-start | bytes 524288 | tf_op jit(solution)/shard_map/psum | solution.py:118
  8.1 13.9 %copy-start.117 = (pred[512]{0:T(512)(128)(4,1)}, pred[512]{0:T(512)(128)(4,1)S(1)}, u32[]{:S(2)}) copy-start(pred[512]{0:T(512)(128)(4,1)S(1)} %compare_and_fusion) | copy-start | bytes 1540
  8.1 27.3 %copy-start.114 = (pred[512]{0:T(512)(128)(4,1)}, pred[512]{0:T(512)(128)(4,1)S(1)}, u32[]{:S(2)}) copy-start(pred[512]{0:T(512)(128)(4,1)S(1)} %compare_and_fusion.1) | copy-start | bytes 1540
  28.2 10.5 %copy-start.111 = (s32[1024]{0:T(1024)}, s32[1024]{0:T(1024)S(1)}, u32[]{:S(2)}) copy-start(s32[1024]{0:T(1024)S(1)} %pad_clamp_fusion) | copy-start | bytes 12292
  48.1 140.6 %all-reduce.10.cloned.1.call-start = ((), (), s32[]{:S(2)}) async-start(), calls=%async_computation.1 | async-start | bytes 524288 | tf_op jit(solution)/shard_map/psum | solution.py:118
  60.0 31.6 %copy-start.12 = (f32[1,2,2,2,16,512]{5,4,3,2,1,0:T(8,128)S(1)}, f32[1,2,2,2,16,512]{5,4,3,2,1,0:T(8,128)}, u32[]{:S(2)}) copy-start(f32[1,2,2,2,16,512]{5,4,3,2,1,0:T(8,128)} %param.11) | copy-start | bytes 786436
  101.1 4.7 copy-start.89
  101.2 4.7 copy-start.92
  101.2 11.7 %copy-start.112 = (s32[1024]{0:T(1024)S(1)}, s32[1024]{0:T(1024)}, u32[]{:S(2)}) copy-start(s32[1024]{0:T(1024)} %copy-done.111) | copy-start | bytes 12292
  101.2 18.9 %copy-start.118 = (pred[512]{0:T(512)(128)(4,1)S(1)}, pred[512]{0:T(512)(128)(4,1)}, u32[]{:S(2)}) copy-start(pred[512]{0:T(512)(128)(4,1)} %copy-done.117) | copy-start | bytes 1540
  153.5 4.2 copy-start.79
  153.5 4.2 copy-start.80
  158.1 5.8 %copy-start.4 = (f32[1,4,2,2,16,512]{5,4,3,2,1,0:T(8,128)}, f32[1,4,2,2,16,512]{5,4,3,2,1,0:T(8,128)S(1)}, u32[]{:S(2)}) copy-start(f32[1,4,2,2,16,512]{5,4,3,2,1,0:T(8,128)S(1)} %get-tuple-element.80) | copy-start | bytes 1572868
  158.1 5.8 %copy-start.5 = (f32[1,4,2,2,16,512]{5,4,3,2,1,0:T(8,128)}, f32[1,4,2,2,16,512]{5,4,3,2,1,0:T(8,128)S(1)}, u32[]{:S(2)}) copy-start(f32[1,4,2,2,16,512]{5,4,3,2,1,0:T(8,128)S(1)} %get-tuple-element.81) | copy-start | bytes 1572868
  159.0 112.1 %all-reduce.12.cloned.1.call-start = ((), (), s32[]{:S(2)}) async-start(), calls=%async_computation.2 | async-start | bytes 2097152 | tf_op jit(solution)/shard_map/psum | solution.py:128
  159.1 4.8 copy-start.21
  159.1 5.6 %copy-start.19 = (f32[4,2,2,16,512]{4,3,1,0,2:T(8,128)S(1)}, f32[4,2,2,16,512]{4,3,1,0,2:T(8,128)}, u32[]{:S(2)}) copy-start(f32[4,2,2,16,512]{4,3,1,0,2:T(8,128)} %get-tuple-element.79) | copy-start | bytes 1572868
  161.1 4.5 copy-start.95
  170.1 185.6 %all-reduce.14.cloned.1.call-start = ((), (), s32[]{:S(2)}) async-start(), calls=%async_computation.3 | async-start | bytes 524288 | tf_op jit(solution)/shard_map/psum | solution.py:118
  276.7 4.7 copy-start.83
  276.7 4.7 copy-start.86
  276.8 11.7 %copy-start.113 = (s32[1024]{0:T(1024)S(1)}, s32[1024]{0:T(1024)}, u32[]{:S(2)}) copy-start(s32[1024]{0:T(1024)} %copy-done.111) | copy-start | bytes 12292
  276.8 18.9 %copy-start.119 = (pred[512]{0:T(512)(128)(4,1)S(1)}, pred[512]{0:T(512)(128)(4,1)}, u32[]{:S(2)}) copy-start(pred[512]{0:T(512)(128)(4,1)} %copy-done.117) | copy-start | bytes 1540
  322.9 4.5 copy-start.20
  323.7 114.3 %all-reduce.16.cloned.1.call-start = ((), (), s32[]{:S(2)}) async-start(), calls=%async_computation.4 | async-start | bytes 2097152 | tf_op jit(solution)/shard_map/psum | solution.py:128
  323.7 4.5 copy-start.18
  324.6 4.5 copy-start.26
  324.6 4.5 copy-start.84
  324.6 4.5 copy-start.87
  332.7 190.8 %all-reduce.18.cloned.1.call-start = ((), (), s32[]{:S(2)}) async-start(), calls=%async_computation.5 | async-start | bytes 2097152 | tf_op jit(solution)/shard_map/psum | solution.py:128
  525.7 4.7 copy-start.1
  (97 other events, 188.2 us)
Sparse Core Ops, SparseCore 0:
  48.3 34.9 all-reduce.7
  159.1 29.5 all-reduce.9
  192.8 78.3 all-reduce.11
  323.8 31.8 all-reduce.13
  359.7 78.3 all-reduce.15
  445.6 77.8 all-reduce.17
where the time goes:
time: 548 us; the launch traced here: 538 us
  waiting for transfers between devices  265 us (48%)
  local copies, waits for them, and re-layouts  155 us (28%)
  other arithmetic  56.7 us (10%)
  blocking collectives  23.1 us (4%)
  matrix products  20.7 us (4%)
  between operations  16.6 us (3%)
    psum x3, waiting for transfers between devices, local(): coeff_sums = lax.psum(local_terms, 'band')  224 us
    mul x92, local copies, waits for them, and re-layouts, small_mul(): return left[:, 0:1] * right[0:1] + left[:, 1:2] * right[1:2]  57.9 us
    psum x3, waiting for transfers between devices, local(): model_total = lax.psum(jnp.sum(model_terms, axis=0), 'dir')  40.9 us
    psum x1, blocking collectives, local(): lax.psum(outer, 'band')  23.1 us
    gather x3, local copies, waits for them, and re-layouts, predict(): jones_second = jnp.take(jones_k, second, axis=-1)[..., None, :]  21.4 us
    gather x3, local copies, waits for them, and re-layouts, predict(): jones_first = jnp.take(jones_k, first, axis=-1)[..., None, :]  21.3 us
    slice x10, local copies, waits for them, and re-layouts, small_mul(): return left[:, 0:1] * right[0:1] + left[:, 1:2] * right[1:2]  16.4 us
    unnamed x250, local copies, waits for them, and re-layouts  15.9 us
  transfers between devices with their start and end apart: 6, of which 5 were waited for; matrix products, arithmetic and copies ran while one was open for 10% of the time, Pallas kernels for 0%

commit v1 on v0

v1 whole, which is shorter than its diff:
```python
import functools

import jax
import jax.numpy as jnp
from jax import lax
from jax.experimental import pallas as pl
from jax.experimental.pallas import tpu as pltpu
from jax.sharding import PartitionSpec as P

ITERS = 3
RHO = 5.0
RIDGE = 0.25
LANES = 128
SUBLANES = 8

VMEM = pl.BlockSpec(memory_space=pltpu.VMEM)
SMEM = pl.BlockSpec(memory_space=pltpu.SMEM)
PARAMS = pltpu.CompilerParams(vmem_limit_bytes=48 * 1024 * 1024)

INDEX = ((0, 0), (0, 1), (1, 0), (1, 1))


def comp(part, i, j):
    return part * 4 + i * 2 + j


def cadd(a, b):
    return (a[0] + b[0], a[1] + b[1])


def cmul(a, b):
    return (a[0] * b[0] - a[1] * b[1], a[0] * b[1] + a[1] * b[0])


def cmul_conj(a, b):
    return (a[0] * b[0] + a[1] * b[1], a[1] * b[0] - a[0] * b[1])


def mat_mul(a, b):
    return {(i, j): cadd(cmul(a[i, 0], b[0, j]), cmul(a[i, 1], b[1, j])) for i, j in INDEX}


def mat_mul_h(a, b):
    return {(i, j): cadd(cmul_conj(a[i, 0], b[j, 0]), cmul_conj(a[i, 1], b[j, 1])) for i, j in INDEX}


def mat_h_mul(a, b):
    return {(i, j): cadd(cmul_conj(b[0, j], a[0, i]), cmul_conj(b[1, j], a[1, i])) for i, j in INDEX}


def sq(a):
    return a[0] * a[0] + a[1] * a[1]


def split_dot(left, right, dims):
    high = left.astype(jnp.bfloat16)
    low = (left - high.astype(jnp.float32)).astype(jnp.bfloat16)
    both = jnp.concatenate([high, low], axis=0)
    out = lax.dot_general(both, right, (dims, ((), ())), preferred_element_type=jnp.float32)
    return out[: left.shape[0]] + out[left.shape[0] :]


def onehot_kernel(pairs_ref, out_ref):
    stations = out_ref.shape[0]
    baselines = pairs_ref.shape[1]
    for half in range(2):
        ids = pairs_ref[half : half + 1, :]
        for base in range(0, stations, LANES):
            station = lax.broadcasted_iota(jnp.int32, (LANES, baselines), 0) + base
            hit = jnp.where(station == ids, 1.0, 0.0).astype(jnp.bfloat16)
            out_ref[base : base + LANES, half * baselines : (half + 1) * baselines] = hit


def read_rows(ref, dirs, k, base, width):
    def one(part, i, j):
        row = comp(part, i, j) * dirs + k
        return jnp.broadcast_to(ref[row : row + 1, base : base + width], (SUBLANES, width))

    return {(i, j): (one(0, i, j), one(1, i, j)) for i, j in INDEX}


def model_kernel(parity_ref, jones_ref, onehot_ref, coher_ref, gathered_ref, mine_ref, other_ref):
    dirs = coher_ref.shape[0]
    times, baselines = coher_ref.shape[-2:]
    gathered_ref[...] = split_dot(jones_ref[...], onehot_ref[...], ((1,), (0,)))
    first = parity_ref[0, 0] == 0
    for base in range(0, baselines, LANES):
        lanes = slice(base, base + LANES)
        for time in range(0, times, SUBLANES):
            rows = slice(time, time + SUBLANES)
            total = None
            for k in range(dirs):
                jones_p = read_rows(gathered_ref, dirs, k, base, LANES)
                jones_q = read_rows(gathered_ref, dirs, k, baselines + base, LANES)
                coher = {(i, j): tuple(coher_ref[k, part, i, j, rows, lanes] for part in range(2)) for i, j in INDEX}
                model = mat_mul(jones_p, mat_mul_h(coher, jones_q))
                total = model if total is None else {ij: cadd(total[ij], model[ij]) for ij in INDEX}
            for i, j in INDEX:
                real, imag = total[i, j]
                mine_ref[i, j, rows, lanes] = jnp.where(first, real, imag)
                other_ref[i, j, rows, lanes] = jnp.where(first, imag, real)


def solve_body(parity_ref, gathered_ref, onehot_ref, coher_ref, vis_ref, mine_ref, other_ref, left_ref, numer):
    dirs = coher_ref.shape[0]
    times, baselines = coher_ref.shape[-2:]
    first = parity_ref[0, 0] == 0
    for base in range(0, baselines, LANES):
        lanes = slice(base, base + LANES)
        resid = []
        for time in range(0, times, SUBLANES):
            rows = slice(time, time + SUBLANES)
            piece = {}
            for i, j in INDEX:
                mine = mine_ref[i, j, rows, lanes]
                other = other_ref[i, j, rows, lanes]
                piece[i, j] = (
                    vis_ref[0, i, j, rows, lanes] - jnp.where(first, mine, other),
                    vis_ref[1, i, j, rows, lanes] - jnp.where(first, other, mine),
                )
            resid.append(piece)
        for k in range(dirs):
            jones_p = read_rows(gathered_ref, dirs, k, base, LANES)
            jones_q = read_rows(gathered_ref, dirs, k, baselines + base, LANES)
            sums = None
            for index, time in enumerate(range(0, times, SUBLANES)):
                rows = slice(time, time + SUBLANES)
                coher = {(i, j): tuple(coher_ref[k, part, i, j, rows, lanes] for part in range(2)) for i, j in INDEX}
                along = mat_mul_h(coher, jones_q)
                ahead = mat_mul(jones_p, coher)
                right_p = mat_mul_h(resid[index], along)
                right_q = mat_h_mul(resid[index], ahead)
                cross_p = cadd(cmul_conj(along[0, 0], along[1, 0]), cmul_conj(along[0, 1], along[1, 1]))
                cross_q = cadd(cmul_conj(ahead[0, 1], ahead[0, 0]), cmul_conj(ahead[1, 1], ahead[1, 0]))
                terms_p = [right_p[ij][part] for part in range(2) for ij in INDEX] + [
                    sq(along[0, 0]) + sq(along[0, 1]),
                    sq(along[1, 0]) + sq(along[1, 1]),
                    cross_p[0],
                    cross_p[1],
                ]
                terms_q = [right_q[ij][part] for part in range(2) for ij in INDEX] + [
                    sq(ahead[0, 0]) + sq(ahead[1, 0]),
                    sq(ahead[0, 1]) + sq(ahead[1, 1]),
                    cross_q[0],
                    cross_q[1],
                ]
                terms = terms_p + terms_q
                sums = terms if sums is None else [a + b for a, b in zip(sums, terms)]
            for at, term in enumerate(sums):
                row = (at % 12) * dirs + k
                offset = base + (at // 12) * baselines
                left_ref[row : row + 1, offset : offset + LANES] = jnp.sum(term, axis=0, keepdims=True)

    def group(ref, at):
        return ref[at * dirs : (at + 1) * dirs, :]

    jones = {(i, j): (group(gathered_ref, comp(0, i, j)), group(gathered_ref, comp(1, i, j))) for i, j in INDEX}
    diag0, diag1 = group(left_ref, 8), group(left_ref, 9)
    off = (group(left_ref, 10), group(left_ref, 11))
    off_c = (off[0], -off[1])
    for i in range(2):
        left, right = jones[i, 0], jones[i, 1]
        col0 = cadd((left[0] * diag0, left[1] * diag0), cmul(right, off_c))
        col1 = cadd(cmul(left, off), (right[0] * diag1, right[1] * diag1))
        for j, col in ((0, col0), (1, col1)):
            for part in range(2):
                at = comp(part, i, j) * dirs
                left_ref[at : at + dirs, :] = left_ref[at : at + dirs, :] + col[part]

    sums = split_dot(left_ref[...], onehot_ref[...], ((1,), (1,)))
    m00 = sums[8 * dirs : 9 * dirs] + RHO
    m11 = sums[9 * dirs : 10 * dirs] + RHO
    m01 = (sums[10 * dirs : 11 * dirs], sums[11 * dirs : 12 * dirs])
    m10 = (m01[0], -m01[1])
    scale = 1.0 / (m00 * m11 - sq(m01))
    out = {}
    for i in range(2):
        n = []
        for j in range(2):
            at = [comp(part, i, j) * dirs for part in range(2)]
            n.append(tuple(sums[a : a + dirs] + numer(a) for a in at))
        x0 = cmul(n[1], m10)
        x1 = cmul(n[0], m01)
        out[i, 0] = tuple((n[0][part] * m11 - x0[part]) * scale for part in range(2))
        out[i, 1] = tuple((n[1][part] * m00 - x1[part]) * scale for part in range(2))
    return out


def first_solve_kernel(
    parity_ref, gathered_ref, onehot_ref, coher_ref, vis_ref, mine_ref, other_ref, consensus_ref, dual_ref,
    jones_ref, shared_ref, left_ref,
):
    dirs = coher_ref.shape[0]

    def numer(a):
        return RHO * consensus_ref[a : a + dirs, :] - dual_ref[a : a + dirs, :]

    out = solve_body(
        parity_ref, gathered_ref, onehot_ref, coher_ref, vis_ref, mine_ref, other_ref, left_ref, numer
    )
    write_solved(out, dirs, jones_ref, shared_ref, lambda a: dual_ref[a : a + dirs, :])


def write_solved(out, dirs, jones_ref, shared_ref, dual):
    for (i, j), parts in out.items():
        for part in range(2):
            a = comp(part, i, j) * dirs
            jones_ref[a : a + dirs, :] = parts[part]
            value = parts[part] + dual(a) * (1.0 / RHO)
            if len(shared_ref.shape) == 2:
                shared_ref[a : a + dirs, :] = value
            else:
                width = shared_ref.shape[2]
                for chunk in range(shared_ref.shape[0]):
                    shared_ref[chunk, a : a + dirs, :] = value[:, chunk * width : (chunk + 1) * width]


def next_solve_kernel(
    parity_ref, gathered_ref, onehot_ref, coher_ref, vis_ref, mine_ref, other_ref, consensus_ref, dual_ref, before_ref,
    jones_ref, shared_ref, dual_out_ref, left_ref,
):
    dirs = coher_ref.shape[0]

    def consensus(a):
        if len(consensus_ref.shape) == 2:
            return consensus_ref[a : a + dirs, :]
        pieces = [consensus_ref[chunk, a : a + dirs, :] for chunk in range(consensus_ref.shape[0])]
        return jnp.concatenate(pieces, axis=1)

    for a in range(0, 8 * dirs, dirs):
        dual_out_ref[a : a + dirs, :] = dual_ref[a : a + dirs, :] + RHO * (before_ref[a : a + dirs, :] - consensus(a))

    def numer(a):
        return RHO * consensus(a) - dual_out_ref[a : a + dirs, :]

    out = solve_body(
        parity_ref, gathered_ref, onehot_ref, coher_ref, vis_ref, mine_ref, other_ref, left_ref, numer
    )
    write_solved(out, dirs, jones_ref, shared_ref, lambda a: dual_out_ref[a : a + dirs, :])


def weights_kernel(basis_ref, weights_ref):
    bands, terms = basis_ref.shape
    basis = basis_ref[...]
    hi = lax.Precision.HIGHEST
    gram = lax.dot_general(basis, basis, (((0,), (0,)), ((), ())), precision=hi, preferred_element_type=jnp.float32)
    row = lax.broadcasted_iota(jnp.int32, (terms, terms), 0)
    col = lax.broadcasted_iota(jnp.int32, (terms, terms), 1)
    gram = gram + jnp.where(row == col, RIDGE * bands, 0.0)
    inverse = jnp.where(row == col, 1.0, 0.0)
    for t in range(terms):
        scale = 1.0 / gram[t : t + 1, t : t + 1]
        g_row = gram[t : t + 1, :] * scale
        i_row = inverse[t : t + 1, :] * scale
        factor = gram[:, t : t + 1]
        here = row == t
        gram = jnp.where(here, g_row, gram - factor * g_row)
        inverse = jnp.where(here, i_row, inverse - factor * i_row)
    weights = lax.dot_general(inverse, basis, (((1,), (1,)), ((), ())), precision=hi, preferred_element_type=jnp.float32)
    weights_ref[:terms, :] = weights
    weights_ref[terms:, :] = jnp.dot(basis, weights, precision=hi, preferred_element_type=jnp.float32)


def mix_kernel(weights_ref, shared_ref, out_ref):
    bands = shared_ref.shape[0]
    terms = weights_ref.shape[0] - bands
    values = [shared_ref[f] for f in range(bands)]
    for g in range(bands):
        total = values[0] * weights_ref[terms + g, 0]
        for f in range(1, bands):
            total = total + values[f] * weights_ref[terms + g, f]
        out_ref[g] = total


def final_kernel(weights_ref, own_ref, jones_ref, dual_ref, *refs):
    shared_refs, (coeffs_ref, dual_out_ref) = refs[:-2], refs[-2:]
    terms = weights_ref.shape[0]
    rows = jones_ref.shape[0]
    for r in range(0, rows, SUBLANES):
        span = slice(r, r + SUBLANES)
        values = [ref[span, :] for ref in shared_refs]
        consensus = None
        for m in range(terms):
            total = values[0] * weights_ref[m, 0]
            for f in range(1, len(values)):
                total = total + values[f] * weights_ref[m, f]
            coeffs_ref[m, span, :] = total
            part = total * own_ref[0, m]
            consensus = part if consensus is None else consensus + part
        dual_out_ref[span, :] = dual_ref[span, :] + RHO * (jones_ref[span, :] - consensus)


def struct(*shape, dtype=jnp.float32):
    return jax.ShapeDtypeStruct(shape, dtype)


def call(kernel, out_shape, in_specs, args, scratch=()):
    many = isinstance(out_shape, (tuple, list))
    return pl.pallas_call(
        kernel,
        out_shape=out_shape,
        in_specs=in_specs,
        out_specs=tuple(VMEM for _ in out_shape) if many else VMEM,
        scratch_shapes=list(scratch),
        compiler_params=PARAMS,
    )(*args)


def swap(value, axis, bit):
    size = lax.axis_size(axis)
    return lax.ppermute(value, axis, [(i, i ^ bit) for i in range(size)])


def to_rows(value):
    dirs, stations = value.shape[0], value.shape[-1]
    return value.reshape(dirs, 8, stations).transpose(1, 0, 2).reshape(8 * dirs, stations)


def from_rows(value, dirs):
    stations = value.shape[-1]
    lead = value.shape[:-2]
    value = value.reshape(lead + (8, dirs, stations))
    value = jnp.swapaxes(value, -3, -2)
    return value.reshape(lead + (dirs, 2, 2, 2, stations))


def sum_over_dir(mine, other):
    size = lax.axis_size("dir")
    mine = mine + swap(other, "dir", 1)
    bit = 2
    while bit < size:
        mine = mine + swap(mine, "dir", bit)
        bit *= 2
    return mine, swap(mine, "dir", 1)


def ring_gather(value):
    size = lax.axis_size("band")
    order = list(range(0, size, 2)) + list(range(size - 1, 0, -2))
    ahead = [(order[i], order[(i + 1) % size]) for i in range(size)]
    behind = [(b, a) for a, b in ahead]
    place = [order.index(i) for i in range(size)]
    at = jnp.asarray(place)[lax.axis_index("band")]
    order = jnp.asarray(order)
    values, sources = [value], [at]
    up = down = value
    for step in range(1, (size - 1) // 2 + 1):
        up = lax.ppermute(up, "band", ahead)
        down = lax.ppermute(down, "band", behind)
        values += [up, down]
        sources += [at - step, at + step]
    half = value.shape[0] // 2
    top = lax.ppermute(up[:half], "band", ahead)
    bottom = lax.ppermute(down[half:], "band", behind)
    values.append(jnp.concatenate([top, bottom], axis=0))
    sources.append(at + size // 2)
    return values, order[jnp.stack(sources) % size]


def local(visibilities, coherencies, jones_start, dual_start, consensus_start, freq_basis, pairs):
    row = freq_basis[0]
    terms = row.shape[0]
    bands = lax.axis_size("band")
    vis, coher = visibilities[0], coherencies[0]
    dirs, stations = jones_start.shape[1], jones_start.shape[-1]
    times, baselines = coher.shape[-2:]
    rows = 8 * dirs
    parity = (lax.axis_index("dir") % 2).astype(jnp.int32).reshape(1, 1)
    chunked = stations % (bands * LANES) == 0
    hi = lax.Precision.HIGHEST

    onehot = call(onehot_kernel, struct(stations, 2 * baselines, dtype=jnp.bfloat16), [VMEM], (pairs,))
    jones = to_rows(jones_start[0])
    dual = to_rows(dual_start[0])
    consensus = to_rows(jnp.tensordot(row, consensus_start, axes=(0, 0), precision=hi))
    half = struct(2, 2, times, baselines)
    flat = struct(rows, stations)
    left = pltpu.VMEM((12 * dirs, 2 * baselines), jnp.float32)

    if chunked:
        basis = lax.all_to_all(jnp.broadcast_to(freq_basis, (bands, terms)), "band", 0, 0, tiled=True)
        weights = call(weights_kernel, struct(terms + bands, bands), [VMEM], (basis,))
    else:
        gram = lax.psum(row[:, None] * row[None, :], "band") + RIDGE * bands * jnp.eye(terms, dtype=jnp.float32)
        factor = jnp.linalg.cholesky(gram)

    before = None
    for turn in range(ITERS):
        last = turn == ITERS - 1
        gathered, mine, other = call(
            model_kernel, (struct(rows, 2 * baselines), half, half), [SMEM, VMEM, VMEM, VMEM],
            (parity, jones, onehot, coher),
        )
        mine, other = sum_over_dir(mine, other)
        common = (parity, gathered, onehot, coher, vis, mine, other, consensus, dual)
        shared_shape = struct(bands, rows, stations // bands) if chunked and not last else flat
        if turn == 0:
            jones, shared = call(first_solve_kernel, (flat, shared_shape), [SMEM] + [VMEM] * 8, common, [left])
        else:
            jones, shared, dual = call(
                next_solve_kernel, (flat, shared_shape, flat), [SMEM] + [VMEM] * 9, common + (jones,), [left]
            )
        if last:
            break
        if chunked:
            shared = lax.all_to_all(shared, "band", 0, 0)
            mixed = call(mix_kernel, struct(*shared.shape), [SMEM, VMEM], (weights, shared))
            consensus = lax.all_to_all(mixed, "band", 0, 0)
        else:
            coeffs = reduce_bands(shared, row, factor)
            consensus = jnp.tensordot(row, coeffs, axes=(0, 0), precision=hi)
    if chunked:
        values, sources = ring_gather(shared)
        coeffs, dual = call(
            final_kernel, (struct(terms, rows, stations), flat), [SMEM, SMEM] + [VMEM] * (2 + len(values)),
            (weights[:terms][:, sources], freq_basis, jones, dual) + tuple(values),
        )
    else:
        coeffs = reduce_bands(shared, row, factor)
        dual = dual + RHO * (jones - jnp.tensordot(row, coeffs, axes=(0, 0), precision=hi))
    return from_rows(jones, dirs)[None], from_rows(dual, dirs)[None], from_rows(coeffs, dirs)


def reduce_bands(shared, row, factor):
    sums = lax.psum(row[:, None, None] * shared[None], "band")
    flat = sums.reshape(sums.shape[0], -1)
    return jax.scipy.linalg.cho_solve((factor, True), flat).reshape(sums.shape)


def solution(mesh):
    in_specs = (
        P("band", None, None, None, None, None),
        P("band", "dir", None, None, None, None, None),
        P("band", "dir", None, None, None, None),
        P("band", "dir", None, None, None, None),
        P(None, "dir", None, None, None, None),
        P("band", None),
        P(),
    )
    out_specs = (
        P("band", "dir", None, None, None, None),
        P("band", "dir", None, None, None, None),
        P(None, "dir", None, None, None, None),
    )
    return jax.shard_map(local, mesh=mesh, in_specs=in_specs, out_specs=out_specs, check_vma=False)
```

time: 548 us -> 134 us (0.24); the launches traced: 538 us -> 133 us
  waiting for transfers between devices: 265 us -> 22.7 us
  local copies, waits for them, and re-layouts: 155 us -> 40.2 us
  other arithmetic: 56.7 us -> 4.96 us
  starting transfers between devices: 0.9 us -> 39.2 us
  blocking collectives: 23.1 us -> 0 us
  Pallas kernels: 0 us -> 19.1 us
  matrix products: 20.7 us -> 1.63 us
  between operations: 16.6 us -> 5.52 us
    psum x6 -> x0, waiting for transfers between devices: 265 us -> none  [the longest x3 224 us: local(): coeff_sums = lax.psum(local_terms, 'band')]
    mul x92 -> x0, local copies, waits for them, and re-layouts: 57.9 us -> none  [small_mul(): return left[:, 0:1] * right[0:1] + left[:, 1:2] * right[1:2]]
    gather x6 -> x3, local copies, waits for them, and re-layouts: 42.8 us -> 1.27 us  [the longest x1 0.64 us: ring_gather(): return (values, order[jnp.stack(sources) % size])]
    all_to_all x0 -> x5, starting transfers between devices: none -> 25.4 us  [the longest x2 10.2 us: local(): shared = lax.all_to_all(shared, 'band', 0, 0)]
    psum x1 -> x0, blocking collectives: 23.1 us -> none  [local(): lax.psum(outer, 'band')]
    sub x27 -> x0, other arithmetic: 20.1 us -> none  [the longest x21 15.8 us: complex_mul(): real_part = small_mul(left[0], right[0]) - small_mul(left[1], right[1])]
    pallas_call x0 -> x11, Pallas kernels: none -> 19.1 us  [call(): pl.pallas_call(kernel, out_shape=out_shape, in_specs=in_specs, out_specs=...]
    slice x11 -> x4, local copies, waits for them, and re-layouts: 17.2 us -> 0.08 us  [the longest x2 0.07 us: local(): weights[:terms][:, sources]]
  transfers between devices with their start and end apart: 6 -> 22, of which waited for: 5 -> 13; matrix products, arithmetic and copies ran while one was open for 10% -> 14% of each run, Pallas kernels for 0% -> 7%
where the time goes in v1:
time: 134 us; the launch traced here: 133 us
  local copies, waits for them, and re-layouts  40.2 us (30%)
  starting transfers between devices  39.2 us (29%)
  waiting for transfers between devices  22.7 us (17%)
  Pallas kernels  19.1 us (14%)
  between operations  5.52 us (4%)
  other arithmetic  4.96 us (4%)
  matrix products  1.63 us (1%)
    unnamed x74, local copies, waits for them, and re-layouts  23.8 us
    pallas_call x11, Pallas kernels, call(): pl.pallas_call(kernel, out_shape=out_shape, in_specs=in_specs, out_specs=...  19.1 us
    all_to_all x2, starting transfers between devices, local(): shared = lax.all_to_all(shared, 'band', 0, 0)  10.2 us
    all_to_all x2, starting transfers between devices, local(): consensus = lax.all_to_all(mixed, 'band', 0, 0)  9.4 us
    all_to_all x2, waiting for transfers between devices, local(): consensus = lax.all_to_all(mixed, 'band', 0, 0)  8.76 us
    ppermute x3, waiting for transfers between devices, ring_gather(): down = lax.ppermute(down, 'band', behind)  6.17 us
    all_to_all x1, starting transfers between devices, local(): lax.all_to_all(jnp.broadcast_to(freq_basis, (bands, terms)), 'band', 0, 0...  5.83 us
    ppermute x9, starting transfers between devices, swap(): return lax.ppermute(value, axis, [(i, i ^ bit) for i in range(size)])  5.79 us
  transfers between devices with their start and end apart: 22, of which 13 were waited for; matrix products, arithmetic and copies ran while one was open for 14% of the time, Pallas kernels for 7%

profile of v1, /device:TPU:0, one launch (start us, length us, event | category | flops | bytes accessed | tf_op | source)
XLA Modules:
  0.0 133.2 jit_solution(4986588506230741081)
XLA Ops:
  2.9 1.1 shard_map.113
  6.2 2.9 %collective-permute-start.1 = (f32[2,2,16,512]{3,2,1,0:T(8,128)S(1)}, f32[2,2,16,512]{3,2,1,0:T(8,128)}, u32[]{:S(2)}, u32[]{:S(2)}) collective-permute-start(f32[2,2,16,512]{3,2,1,0:T(8,128)S(1)} %add.81), channel_id=1, source_target_pairs={{0,2},{1,3},{2,0},{3,1},{4,6},{5,7},{6,4},{7,5},{8,10},{9,11},{10,... | collective-permute-start | bytes 393224 | tf_op jit(solution)/shard_map/ppermute | solution.py:311
  9.7 5.8 %all-to-all-start = ((f32[8,1,8]{2,1,0:T(1,128)}), f32[8,1,8]{2,1,0:T(1,128)S(1)}, u32[]{:S(2)}, u32[]{:S(2)}) async-start(f32[8,1,8]{2,1,0:T(1,128)} %broadcast_in_dim.2), calls=%async_computation | async-start | bytes 8192 | tf_op jit(solution)/shard_map/all_to_all | solution.py:381
  16.3 1.9 %copy.37 = f32[4,2,2,2,1024,8]{4,5,3,2,1,0:T(8,128)S(1)} copy(f32[4,2,2,2,1024,8]{4,3,2,1,0,5:T(2,128)} %bitcast.63) | data formatting | bytes 2097152 | tf_op jit(solution)/shard_map/dot_general | solution.py:375
  18.2 1.6 %add.82.mine_ref = f32[2,2,16,512]{3,2,1,0:T(8,128)} add(f32[2,2,16,512]{3,2,1,0:T(8,128)S(1)} %add.81, f32[2,2,16,512]{3,2,1,0:T(8,128)} %collective-permute-done.1) | non-fusion elementwise | flops 32768 | bytes 393216 | tf_op jit(solution)/shard_map/add | solution.py:332
  19.8 1.6 %fusion.3 = f32[1,4,8,1024]{3,0,2,1:T(1,128)} fusion(f32[4,8,1024,8]{2,3,1,0:T(8,128)S(1)} %bitcast.61, f32[1,8]{1,0:T(1,128)S(1)} %copy-done.33), kind=kOutput, calls=%fused_computation.14 | convolution fusion | flops 3145728 | bytes 1179680 | tf_op jit(solution)/shard_map/dot_general | solution.py:375
  22.4 1.6 %copy.43 = f32[1,4,8,1024]{3,1,2,0:T(4,128)} copy(f32[1,4,8,1024]{3,0,2,1:T(1,128)} %fusion.3) | data formatting | bytes 262144 | tf_op jit(solution)/shard_map/dot_general | solution.py:375
  24.0 1.6 %reshape.419.consensus_ref = f32[32,1024]{1,0:T(8,128)} reshape(f32[8,4,1024]{2,1,0:T(4,128)} %bitcast.65) | data formatting | bytes 262144 | tf_op jit(solution)/shard_map/reshape | solution.py:316
  27.4 3.4 %shard_map.114 = (f32[32,1024]{1,0:T(8,128)S(1)}, f32[8,32,128]{2,1,0:T(8,128)S(1)}) custom-call(s32[1,1]{1,0:T(1,128)} %bitcast.parity_ref, f32[32,1024]{1,0:T(8,128)S(1)} %copy-done.26, bf16[1024,1024]{1,0:T(8,128)(2,1)S(1)} %shard_map.112.onehot_ref, f32[4,2,2,2,16,512]{5,4,3,2,1,0:T(8,128)S(1)} %bitcast.50, f32[2,2,2,16,512]{4,3,2,1,0:T(8,128)S(1)} %bitcast.55, ...), custom_call_target="tpu_custom_call" | custom-call | tf_op jit(solution)/shard_map/pallas_call | solution.py:299
  32.1 6.0 %all-to-all-start.1 = ((f32[8,32,128]{2,1,0:T(8,128)}), f32[8,32,128]{2,1,0:T(8,128)}, u32[]{:S(2)}, u32[]{:S(2)}) async-start(f32[8,32,128]{2,1,0:T(8,128)} %copy-done.31), calls=%async_computation.1 | async-start | bytes 262144 | tf_op jit(solution)/shard_map/all_to_all | solution.py:406
  39.0 1.1 shard_map.115
  41.0 1.1 collective-permute-done.3
  44.4 1.4 %all-to-all-done.1.shared_ref = f32[8,32,128]{2,1,0:T(8,128)} async-done(((f32[8,32,128]{2,1,0:T(8,128)}), f32[8,32,128]{2,1,0:T(8,128)}, u32[]{:S(2)}, u32[]{:S(2)}) %all-to-all-start.1) | async-done | bytes 131104 | tf_op jit(solution)/shard_map/all_to_all | solution.py:406
  47.5 4.6 %all-to-all-start.2 = ((f32[8,32,128]{2,1,0:T(8,128)}), f32[8,32,128]{2,1,0:T(8,128)}, u32[]{:S(2)}, u32[]{:S(2)}) async-start(f32[8,32,128]{2,1,0:T(8,128)} %copy-done.15), calls=%async_computation.2 | async-start | bytes 262144 | tf_op jit(solution)/shard_map/all_to_all | solution.py:408
  55.2 4.4 %all-to-all-done.2.consensus_ref = f32[8,32,128]{2,1,0:T(8,128)} async-done(((f32[8,32,128]{2,1,0:T(8,128)}), f32[8,32,128]{2,1,0:T(8,128)}, u32[]{:S(2)}, u32[]{:S(2)}) %all-to-all-start.2) | async-done | bytes 131104 | tf_op jit(solution)/shard_map/all_to_all | solution.py:408
  63.2 3.3 %shard_map.118 = (f32[32,1024]{1,0:T(8,128)S(1)}, f32[8,32,128]{2,1,0:T(8,128)S(1)}, f32[32,1024]{1,0:T(8,128)S(1)}) custom-call(s32[1,1]{1,0:T(1,128)} %bitcast.parity_ref, f32[32,1024]{1,0:T(8,128)S(1)} %copy-done.24, bf16[1024,1024]{1,0:T(8,128)(2,1)S(1)} %shard_map.112.onehot_ref, f32[4,2,2,2,16,512]{5,4,3,2,1,0:T(8,128)S(1)} %bitcast.52, ...), custom_call_target="tpu_custom_call" | custom-call | tf_op jit(solution)/shard_map/pallas_call | solution.py:299
  68.5 4.2 %all-to-all-start.3 = ((f32[8,32,128]{2,1,0:T(8,128)}), f32[8,32,128]{2,1,0:T(8,128)}, u32[]{:S(2)}, u32[]{:S(2)}) async-start(f32[8,32,128]{2,1,0:T(8,128)} %copy-done.32), calls=%async_computation.3 | async-start | bytes 262144 | tf_op jit(solution)/shard_map/all_to_all | solution.py:406
  73.5 1.1 shard_map.119
  75.4 1.3 %collective-permute-done.6 = f32[2,2,16,512]{3,2,1,0:T(8,128)S(1)} collective-permute-done((f32[2,2,16,512]{3,2,1,0:T(8,128)S(1)}, f32[2,2,16,512]{3,2,1,0:T(8,128)S(1)}, u32[]{:S(2)}, u32[]{:S(2)}) %collective-permute-start.6) | collective-permute-done | bytes 131104 | tf_op jit(solution)/shard_map/ppermute | solution.py:311
  77.4 1.5 %collective-permute-start.7 = (f32[2,2,16,512]{3,2,1,0:T(8,128)}, f32[2,2,16,512]{3,2,1,0:T(8,128)}, u32[]{:S(2)}, u32[]{:S(2)}) collective-permute-start(f32[2,2,16,512]{3,2,1,0:T(8,128)} %add.85), channel_id=1, source_target_pairs={{0,2},{1,3},{2,0},{3,1},{4,6},{5,7},{6,4},{7,5},{8,10},{9,11},{10,... | collective-permute-start | bytes 393224 | tf_op jit(solution)/shard_map/ppermute | solution.py:311
  81.5 4.8 %all-to-all-start.4 = ((f32[8,32,128]{2,1,0:T(8,128)}), f32[8,32,128]{2,1,0:T(8,128)}, u32[]{:S(2)}, u32[]{:S(2)}) async-start(f32[8,32,128]{2,1,0:T(8,128)} %copy-done.16), calls=%async_computation.4 | async-start | bytes 262144 | tf_op jit(solution)/shard_map/all_to_all | solution.py:408
  89.3 4.4 %all-to-all-done.4.consensus_ref = f32[8,32,128]{2,1,0:T(8,128)} async-done(((f32[8,32,128]{2,1,0:T(8,128)}), f32[8,32,128]{2,1,0:T(8,128)}, u32[]{:S(2)}, u32[]{:S(2)}) %all-to-all-start.4) | async-done | bytes 131104 | tf_op jit(solution)/shard_map/all_to_all | solution.py:408
  97.3 4.0 %shard_map.121 = (f32[32,1024]{1,0:T(8,128)S(1)}, f32[32,1024]{1,0:T(8,128)}, f32[32,1024]{1,0:T(8,128)S(1)}) custom-call(s32[1,1]{1,0:T(1,128)} %bitcast.parity_ref, f32[32,1024]{1,0:T(8,128)S(1)} %copy-done.22, bf16[1024,1024]{1,0:T(8,128)(2,1)S(1)} %shard_map.112.onehot_ref, f32[4,2,2,2,16,512]{5,4,3,2,1,0:T(8,128)S(1)} %bitcast.54, ...), custom_call_target="tpu_custom_call" | custom-call | tf_op jit(solution)/shard_map/pallas_call | solution.py:299
  102.8 1.8 %collective-permute-start.9 = (f32[32,1024]{1,0:T(8,128)}, f32[32,1024]{1,0:T(8,128)S(1)}, u32[]{:S(2)}, u32[]{:S(2)}) collective-permute-start(f32[32,1024]{1,0:T(8,128)} %get-tuple-element.38.refs_0_), channel_id=1, source_target_pairs={{0,8},{8,16},{16,24},{24,28},{28,20},{20,12},{12,4},{4,0},{1,9},{9... | collective-permute-start | bytes 393224 | tf_op jit(solution)/shard_map/ppermute | solution.py:348
  104.6 1.2 dynamic_slice.3
  111.4 1.8 %collective-permute-start.11 = (f32[32,1024]{1,0:T(8,128)S(1)}, f32[32,1024]{1,0:T(8,128)S(1)}, u32[]{:S(2)}, u32[]{:S(2)}) collective-permute-start(f32[32,1024]{1,0:T(8,128)S(1)} %collective-permute-done.9.refs_1_), channel_id=1, source_target_pairs={{0,8},{8,16},{16,24},{24,28},{28,20},{20,12},{12,4},{4,0},{1,9},{9... | collective-permute-start | bytes 393224 | tf_op jit(solution)/shard_map/ppermute | solution.py:348
  113.9 2.9 %collective-permute-done.12.refs_4_ = f32[32,1024]{1,0:T(8,128)S(1)} collective-permute-done((f32[32,1024]{1,0:T(8,128)S(1)}, f32[32,1024]{1,0:T(8,128)S(1)}, u32[]{:S(2)}, u32[]{:S(2)}) %collective-permute-start.12) | collective-permute-done | bytes 131104 | tf_op jit(solution)/shard_map/ppermute | solution.py:349
  117.2 1.6 %collective-permute-start.13 = (f32[32,1024]{1,0:T(8,128)S(1)}, f32[32,1024]{1,0:T(8,128)S(1)}, u32[]{:S(2)}, u32[]{:S(2)}) collective-permute-start(f32[32,1024]{1,0:T(8,128)S(1)} %collective-permute-done.11.refs_3_), channel_id=1, source_target_pairs={{0,8},{8,16},{16,24},{24,28},{28,20},{20,12},{12,4},{4,0},{1,9},{9... | collective-permute-start | bytes 393224 | tf_op jit(solution)/shard_map/ppermute | solution.py:348
  118.9 3.2 %collective-permute-done.14.refs_6_ = f32[32,1024]{1,0:T(8,128)S(1)} collective-permute-done((f32[32,1024]{1,0:T(8,128)S(1)}, f32[32,1024]{1,0:T(8,128)S(1)}, u32[]{:S(2)}, u32[]{:S(2)}) %collective-permute-start.14) | collective-permute-done | bytes 131104 | tf_op jit(solution)/shard_map/ppermute | solution.py:349
  122.6 1.6 %collective-permute-start.15 = (f32[16,1024]{1,0:T(8,128)S(1)}, f32[16,1024]{1,0:T(8,128)S(1)}, u32[]{:S(2)}, u32[]{:S(2)}) collective-permute-start(f32[16,1024]{1,0:T(8,128)S(1)} %slice.17), channel_id=1, source_target_pairs={{0,8},{8,16},{16,24},{24,28},{28,20},{20,12},{12,4},{4,0},{1,9},{9... | collective-permute-start | bytes 196616 | tf_op jit(solution)/shard_map/ppermute | solution.py:353
  128.8 1.6 %shard_map.122 = (f32[8,32,1024]{2,1,0:T(8,128)S(1)}, f32[32,1024]{1,0:T(8,128)S(1)}) custom-call(f32[8,8]{1,0:T(8,128)S(1)} %bitcast.58, f32[1,8]{1,0:T(1,128)S(1)} %copy-done.33, f32[32,1024]{1,0:T(8,128)S(1)} %copy-done.13, f32[32,1024]{1,0:T(8,128)S(1)} %copy-done.18, f32[32,1024]{1,0:T(8,128)} %get-tuple-element.38.refs_0_, ...), custom_call_target="tpu_custom_call" | custom-call | tf_op jit(solution)/shard_map/pallas_call | solution.py:299
  131.5 1.8 %copy.41 = f32[8,4,2,2,2,1024]{5,4,3,2,1,0:T(2,128)} copy(f32[8,4,2,2,2,1024]{5,1,4,3,2,0:T(4,128)S(1)} %bitcast.62) | data formatting | bytes 2097152 | tf_op jit(solution)/shard_map/reshape | solution.py:324
  (132 shorter events, 45.4 us)
Async XLA Ops:
  0.6 2.3 %copy-start = (f32[1,4,2,2,2,16,512]{6,5,4,3,2,1,0:T(8,128)S(1)}, f32[1,4,2,2,2,16,512]{6,5,4,3,2,1,0:T(8,128)}, u32[]{:S(2)}) copy-start(f32[1,4,2,2,2,16,512]{6,5,4,3,2,1,0:T(8,128)} %param.10) | copy-start | bytes 3145732
  2.9 6.3 %copy-start.33 = (f32[1,8]{1,0:T(1,128)S(1)}, f32[1,8]{1,0:T(1,128)}, u32[]{:S(2)}) copy-start(f32[1,8]{1,0:T(1,128)} %own_ref.1) | copy-start | bytes 100
  2.9 12.7 %copy-start.36 = (f32[1,4,2,2,2,1024]{5,4,3,2,1,0:T(2,128)S(1)}, f32[1,4,2,2,2,1024]{5,4,3,2,1,0:T(2,128)}, u32[]{:S(2)}) copy-start(f32[1,4,2,2,2,1024]{5,4,3,2,1,0:T(2,128)} %param.12) | copy-start | bytes 393220
  4.7 1.5 %collective-permute-start = (f32[2,2,16,512]{3,2,1,0:T(8,128)S(1)}, f32[2,2,16,512]{3,2,1,0:T(8,128)S(1)}, u32[]{:S(2)}, u32[]{:S(2)}) collective-permute-start(f32[2,2,16,512]{3,2,1,0:T(8,128)S(1)} %get-tuple-element.24), channel_id=1, source_target_pairs={{0,1},{1,0},{2,3},{3,2},{4,5},{5,4},{6,7},{7,6},{8,9},{9,8},{10,11... | collective-permute-start | bytes 393224 | tf_op jit(solution)/shard_map/ppermute | solution.py:311
  6.2 12.0 %collective-permute-start.1 = (f32[2,2,16,512]{3,2,1,0:T(8,128)S(1)}, f32[2,2,16,512]{3,2,1,0:T(8,128)}, u32[]{:S(2)}, u32[]{:S(2)}) collective-permute-start(f32[2,2,16,512]{3,2,1,0:T(8,128)S(1)} %add.81), channel_id=1, source_target_pairs={{0,2},{1,3},{2,0},{3,1},{4,6},{5,7},{6,4},{7,5},{8,10},{9,11},{10,... | collective-permute-start | bytes 393224 | tf_op jit(solution)/shard_map/ppermute | solution.py:311
  9.7 22.4 %all-to-all-start = ((f32[8,1,8]{2,1,0:T(1,128)}), f32[8,1,8]{2,1,0:T(1,128)S(1)}, u32[]{:S(2)}, u32[]{:S(2)}) async-start(f32[8,1,8]{2,1,0:T(1,128)} %broadcast_in_dim.2), calls=%async_computation | async-start | bytes 8192 | tf_op jit(solution)/shard_map/all_to_all | solution.py:381
  16.3 9.3 %copy-start.1 = (f32[1,2,2,2,16,512]{5,4,3,2,1,0:T(8,128)S(1)}, f32[1,2,2,2,16,512]{5,4,3,2,1,0:T(8,128)}, u32[]{:S(2)}) copy-start(f32[1,2,2,2,16,512]{5,4,3,2,1,0:T(8,128)} %param.9) | copy-start | bytes 786436
  19.8 5.8 %collective-permute-start.2 = (f32[2,2,16,512]{3,2,1,0:T(8,128)}, f32[2,2,16,512]{3,2,1,0:T(8,128)}, u32[]{:S(2)}, u32[]{:S(2)}) collective-permute-start(f32[2,2,16,512]{3,2,1,0:T(8,128)} %add.82.mine_ref), channel_id=1, source_target_pairs={{0,1},{1,0},{2,3},{3,2},{4,5},{5,4},{6,7},{7,6},{8,9},{9,8},{10,11... | collective-permute-start | bytes 393224 | tf_op jit(solution)/shard_map/ppermute | solution.py:311
  25.6 0.9 copy-start.14
  32.1 13.8 %all-to-all-start.1 = ((f32[8,32,128]{2,1,0:T(8,128)}), f32[8,32,128]{2,1,0:T(8,128)}, u32[]{:S(2)}, u32[]{:S(2)}) async-start(f32[8,32,128]{2,1,0:T(8,128)} %copy-done.31), calls=%async_computation.1 | async-start | bytes 262144 | tf_op jit(solution)/shard_map/all_to_all | solution.py:406
  40.8 1.3 %collective-permute-start.3 = (f32[2,2,16,512]{3,2,1,0:T(8,128)S(1)}, f32[2,2,16,512]{3,2,1,0:T(8,128)S(1)}, u32[]{:S(2)}, u32[]{:S(2)}) collective-permute-start(f32[2,2,16,512]{3,2,1,0:T(8,128)S(1)} %get-tuple-element.28), channel_id=1, source_target_pairs={{0,1},{1,0},{2,3},{3,2},{4,5},{5,4},{6,7},{7,6},{8,9},{9,8},{10,11... | collective-permute-start | bytes 393224 | tf_op jit(solution)/shard_map/ppermute | solution.py:311
  42.8 9.3 %collective-permute-start.4 = (f32[2,2,16,512]{3,2,1,0:T(8,128)}, f32[2,2,16,512]{3,2,1,0:T(8,128)}, u32[]{:S(2)}, u32[]{:S(2)}) collective-permute-start(f32[2,2,16,512]{3,2,1,0:T(8,128)} %add.83), channel_id=1, source_target_pairs={{0,2},{1,3},{2,0},{3,1},{4,6},{5,7},{6,4},{7,5},{8,10},{9,11},{10,... | collective-permute-start | bytes 393224 | tf_op jit(solution)/shard_map/ppermute | solution.py:311
  47.5 12.1 %all-to-all-start.2 = ((f32[8,32,128]{2,1,0:T(8,128)}), f32[8,32,128]{2,1,0:T(8,128)}, u32[]{:S(2)}, u32[]{:S(2)}) async-start(f32[8,32,128]{2,1,0:T(8,128)} %copy-done.15), calls=%async_computation.2 | async-start | bytes 262144 | tf_op jit(solution)/shard_map/all_to_all | solution.py:408
  53.1 1.4 %collective-permute-start.5 = (f32[2,2,16,512]{3,2,1,0:T(8,128)S(1)}, f32[2,2,16,512]{3,2,1,0:T(8,128)S(1)}, u32[]{:S(2)}, u32[]{:S(2)}) collective-permute-start(f32[2,2,16,512]{3,2,1,0:T(8,128)S(1)} %add.84.mine_ref), channel_id=1, source_target_pairs={{0,1},{1,0},{2,3},{3,2},{4,5},{5,4},{6,7},{7,6},{8,9},{9,8},{10,11... | collective-permute-start | bytes 393224 | tf_op jit(solution)/shard_map/ppermute | solution.py:311
  68.5 11.4 %all-to-all-start.3 = ((f32[8,32,128]{2,1,0:T(8,128)}), f32[8,32,128]{2,1,0:T(8,128)}, u32[]{:S(2)}, u32[]{:S(2)}) async-start(f32[8,32,128]{2,1,0:T(8,128)} %copy-done.32), calls=%async_computation.3 | async-start | bytes 262144 | tf_op jit(solution)/shard_map/all_to_all | solution.py:406
  72.6 0.9 copy-start.6
  73.5 20.2 %copy-start.7 = (f32[32,1024]{1,0:T(8,128)S(1)}, f32[32,1024]{1,0:T(8,128)}, u32[]{:S(2)}) copy-start(f32[32,1024]{1,0:T(8,128)} %copy-done.5) | copy-start | bytes 393220
  75.4 1.3 %collective-permute-start.6 = (f32[2,2,16,512]{3,2,1,0:T(8,128)S(1)}, f32[2,2,16,512]{3,2,1,0:T(8,128)S(1)}, u32[]{:S(2)}, u32[]{:S(2)}) collective-permute-start(f32[2,2,16,512]{3,2,1,0:T(8,128)S(1)} %get-tuple-element.33), channel_id=1, source_target_pairs={{0,1},{1,0},{2,3},{3,2},{4,5},{5,4},{6,7},{7,6},{8,9},{9,8},{10,11... | collective-permute-start | bytes 393224 | tf_op jit(solution)/shard_map/ppermute | solution.py:311
  77.4 8.9 %collective-permute-start.7 = (f32[2,2,16,512]{3,2,1,0:T(8,128)}, f32[2,2,16,512]{3,2,1,0:T(8,128)}, u32[]{:S(2)}, u32[]{:S(2)}) collective-permute-start(f32[2,2,16,512]{3,2,1,0:T(8,128)} %add.85), channel_id=1, source_target_pairs={{0,2},{1,3},{2,0},{3,1},{4,6},{5,7},{6,4},{7,5},{8,10},{9,11},{10,... | collective-permute-start | bytes 393224 | tf_op jit(solution)/shard_map/ppermute | solution.py:311
  81.5 12.2 %all-to-all-start.4 = ((f32[8,32,128]{2,1,0:T(8,128)}), f32[8,32,128]{2,1,0:T(8,128)}, u32[]{:S(2)}, u32[]{:S(2)}) async-start(f32[8,32,128]{2,1,0:T(8,128)} %copy-done.16), calls=%async_computation.4 | async-start | bytes 262144 | tf_op jit(solution)/shard_map/all_to_all | solution.py:408
  87.3 1.4 %collective-permute-start.8 = (f32[2,2,16,512]{3,2,1,0:T(8,128)S(1)}, f32[2,2,16,512]{3,2,1,0:T(8,128)S(1)}, u32[]{:S(2)}, u32[]{:S(2)}) collective-permute-start(f32[2,2,16,512]{3,2,1,0:T(8,128)S(1)} %add.86.mine_ref), channel_id=1, source_target_pairs={{0,1},{1,0},{2,3},{3,2},{4,5},{5,4},{6,7},{7,6},{8,9},{9,8},{10,11... | collective-permute-start | bytes 393224 | tf_op jit(solution)/shard_map/ppermute | solution.py:311
  93.7 0.9 copy-start.9
  97.3 15.9 %copy-start.35 = (s32[8]{0:T(128)S(1)}, s32[8]{0:T(128)}, u32[]{:S(2)}) copy-start(s32[8]{0:T(128)} %constant.64.clone) | copy-start | bytes 100
  102.6 8.5 %collective-permute-start.10 = (f32[32,1024]{1,0:T(8,128)}, f32[32,1024]{1,0:T(8,128)S(1)}, u32[]{:S(2)}, u32[]{:S(2)}) collective-permute-start(f32[32,1024]{1,0:T(8,128)} %get-tuple-element.38.refs_0_), channel_id=1, source_target_pairs={{8,0},{16,8},{24,16},{28,24},{20,28},{12,20},{4,12},{0,4},{9,1},{1... | collective-permute-start | bytes 393224 | tf_op jit(solution)/shard_map/ppermute | solution.py:349
  102.8 8.6 %collective-permute-start.9 = (f32[32,1024]{1,0:T(8,128)}, f32[32,1024]{1,0:T(8,128)S(1)}, u32[]{:S(2)}, u32[]{:S(2)}) collective-permute-start(f32[32,1024]{1,0:T(8,128)} %get-tuple-element.38.refs_0_), channel_id=1, source_target_pairs={{0,8},{8,16},{16,24},{24,28},{28,20},{20,12},{12,4},{4,0},{1,9},{9... | collective-permute-start | bytes 393224 | tf_op jit(solution)/shard_map/ppermute | solution.py:348
  111.1 5.7 %collective-permute-start.12 = (f32[32,1024]{1,0:T(8,128)S(1)}, f32[32,1024]{1,0:T(8,128)S(1)}, u32[]{:S(2)}, u32[]{:S(2)}) collective-permute-start(f32[32,1024]{1,0:T(8,128)S(1)} %collective-permute-done.10.refs_2_), channel_id=1, source_target_pairs={{8,0},{16,8},{24,16},{28,24},{20,28},{12,20},{4,12},{0,4},{9,1},{1... | collective-permute-start | bytes 393224 | tf_op jit(solution)/shard_map/ppermute | solution.py:349
  111.4 5.8 %collective-permute-start.11 = (f32[32,1024]{1,0:T(8,128)S(1)}, f32[32,1024]{1,0:T(8,128)S(1)}, u32[]{:S(2)}, u32[]{:S(2)}) collective-permute-start(f32[32,1024]{1,0:T(8,128)S(1)} %collective-permute-done.9.refs_1_), channel_id=1, source_target_pairs={{0,8},{8,16},{16,24},{24,28},{28,20},{20,12},{12,4},{4,0},{1,9},{9... | collective-permute-start | bytes 393224 | tf_op jit(solution)/shard_map/ppermute | solution.py:348
  116.8 5.3 %collective-permute-start.14 = (f32[32,1024]{1,0:T(8,128)S(1)}, f32[32,1024]{1,0:T(8,128)S(1)}, u32[]{:S(2)}, u32[]{:S(2)}) collective-permute-start(f32[32,1024]{1,0:T(8,128)S(1)} %collective-permute-done.12.refs_4_), channel_id=1, source_target_pairs={{8,0},{16,8},{24,16},{28,24},{20,28},{12,20},{4,12},{0,4},{9,1},{1... | collective-permute-start | bytes 393224 | tf_op jit(solution)/shard_map/ppermute | solution.py:349
  117.2 5.4 %collective-permute-start.13 = (f32[32,1024]{1,0:T(8,128)S(1)}, f32[32,1024]{1,0:T(8,128)S(1)}, u32[]{:S(2)}, u32[]{:S(2)}) collective-permute-start(f32[32,1024]{1,0:T(8,128)S(1)} %collective-permute-done.11.refs_3_), channel_id=1, source_target_pairs={{0,8},{8,16},{16,24},{24,28},{28,20},{20,12},{12,4},{4,0},{1,9},{9... | collective-permute-start | bytes 393224 | tf_op jit(solution)/shard_map/ppermute | solution.py:348
  122.1 4.5 %collective-permute-start.16 = (f32[16,1024]{1,0:T(8,128)S(1)}, f32[16,1024]{1,0:T(8,128)S(1)}, u32[]{:S(2)}, u32[]{:S(2)}) collective-permute-start(f32[16,1024]{1,0:T(8,128)S(1)} %slice.18), channel_id=1, source_target_pairs={{8,0},{16,8},{24,16},{28,24},{20,28},{12,20},{4,12},{0,4},{9,1},{1... | collective-permute-start | bytes 196616 | tf_op jit(solution)/shard_map/ppermute | solution.py:354
  122.6 4.3 %collective-permute-start.15 = (f32[16,1024]{1,0:T(8,128)S(1)}, f32[16,1024]{1,0:T(8,128)S(1)}, u32[]{:S(2)}, u32[]{:S(2)}) collective-permute-start(f32[16,1024]{1,0:T(8,128)S(1)} %slice.17), channel_id=1, source_target_pairs={{0,8},{8,16},{16,24},{24,28},{28,20},{20,12},{12,4},{4,0},{1,9},{9... | collective-permute-start | bytes 196616 | tf_op jit(solution)/shard_map/ppermute | solution.py:353
  127.0 0.9 copy-start.13
  (27 other events, 20.2 us)

commit v2 on v1

v2 whole, which is shorter than its diff:
```python
import jax
import jax.numpy as jnp
from jax import lax
from jax.experimental import pallas as pl
from jax.experimental.pallas import tpu as pltpu
from jax.sharding import PartitionSpec as P

ITERS = 3
RHO = 5.0
RIDGE = 0.25
LANES = 128
SUBLANES = 8

VMEM = pl.BlockSpec(memory_space=pltpu.VMEM)
SMEM = pl.BlockSpec(memory_space=pltpu.SMEM)
PARAMS = pltpu.CompilerParams(vmem_limit_bytes=16 * 1024 * 1024)

INDEX = ((0, 0), (0, 1), (1, 0), (1, 1))


def comp(part, i, j):
    return part * 4 + i * 2 + j


def cadd(a, b):
    return (a[0] + b[0], a[1] + b[1])


def cmul(a, b):
    return (a[0] * b[0] - a[1] * b[1], a[0] * b[1] + a[1] * b[0])


def cmul_conj(a, b):
    return (a[0] * b[0] + a[1] * b[1], a[1] * b[0] - a[0] * b[1])


def mat_mul(a, b):
    return {(i, j): cadd(cmul(a[i, 0], b[0, j]), cmul(a[i, 1], b[1, j])) for i, j in INDEX}


def mat_mul_h(a, b):
    return {(i, j): cadd(cmul_conj(a[i, 0], b[j, 0]), cmul_conj(a[i, 1], b[j, 1])) for i, j in INDEX}


def mat_h_mul(a, b):
    return {(i, j): cadd(cmul_conj(b[0, j], a[0, i]), cmul_conj(b[1, j], a[1, i])) for i, j in INDEX}


def sq(a):
    return a[0] * a[0] + a[1] * a[1]


def split_dot(left, right, dims):
    high = left.astype(jnp.bfloat16)
    low = (left - high.astype(jnp.float32)).astype(jnp.bfloat16)
    both = jnp.concatenate([high, low], axis=0)
    out = lax.dot_general(both, right, (dims, ((), ())), preferred_element_type=jnp.float32)
    return out[: left.shape[0]] + out[left.shape[0] :]


def fill_onehot(pairs_ref, onehot_ref):
    stations = onehot_ref.shape[0]
    baselines = pairs_ref.shape[1]
    for half in range(2):
        ids = pairs_ref[half : half + 1, :]
        for base in range(0, stations, LANES):
            station = lax.broadcasted_iota(jnp.int32, (LANES, baselines), 0) + base
            hit = jnp.where(station == ids, 1.0, 0.0).astype(jnp.bfloat16)
            onehot_ref[base : base + LANES, half * baselines : (half + 1) * baselines] = hit


def read_rows(ref, dirs, k, base, width):
    def one(part, i, j):
        row = comp(part, i, j) * dirs + k
        return jnp.broadcast_to(ref[row : row + 1, base : base + width], (SUBLANES, width))

    return {(i, j): (one(0, i, j), one(1, i, j)) for i, j in INDEX}


def native_to_rows(block, dirs, store):
    for k in range(dirs):
        for part in range(2):
            for i in range(2):
                value = block(k, part, i)
                for j in range(2):
                    store(comp(part, i, j) * dirs + k, value[j : j + 1, :])


def prepare_kernel(basis_ref, dual_ref, coeffs_ref, dual_out_ref, known_ref):
    terms, dirs = coeffs_ref.shape[:2]

    def put(ref):
        def store(row, value):
            ref[row : row + 1, :] = value

        return store

    def known(k, part, i):
        total = coeffs_ref[0, k, part, i] * basis_ref[0, 0]
        for m in range(1, terms):
            total = total + coeffs_ref[m, k, part, i] * basis_ref[0, m]
        return RHO * total - dual_ref[k, part, i]

    native_to_rows(lambda k, part, i: dual_ref[k, part, i], dirs, put(dual_out_ref))
    native_to_rows(known, dirs, put(known_ref))


def model_body(parity_ref, jones, onehot_ref, coher_ref, gathered_ref, mine_ref, other_ref):
    dirs = coher_ref.shape[0]
    times, baselines = coher_ref.shape[-2:]
    gathered_ref[...] = split_dot(jones, onehot_ref[...], ((1,), (0,)))
    first = parity_ref[0, 0] == 0
    for base in range(0, baselines, LANES):
        lanes = slice(base, base + LANES)
        for time in range(0, times, SUBLANES):
            rows = slice(time, time + SUBLANES)
            total = None
            for k in range(dirs):
                jones_p = read_rows(gathered_ref, dirs, k, base, LANES)
                jones_q = read_rows(gathered_ref, dirs, k, baselines + base, LANES)
                coher = {(i, j): tuple(coher_ref[k, part, i, j, rows, lanes] for part in range(2)) for i, j in INDEX}
                model = mat_mul(jones_p, mat_mul_h(coher, jones_q))
                total = model if total is None else {ij: cadd(total[ij], model[ij]) for ij in INDEX}
            for i, j in INDEX:
                real, imag = total[i, j]
                mine_ref[i, j, rows, lanes] = jnp.where(first, real, imag)
                other_ref[i, j, rows, lanes] = jnp.where(first, imag, real)


def first_model_kernel(
    parity_ref, jones_ref, pairs_ref, coher_ref, gathered_ref, mine_ref, other_ref, onehot_ref, rows_ref
):
    fill_onehot(pairs_ref, onehot_ref)

    def store(row, value):
        rows_ref[row : row + 1, :] = value

    native_to_rows(lambda k, part, i: jones_ref[k, part, i], coher_ref.shape[0], store)
    model_body(parity_ref, rows_ref[...], onehot_ref, coher_ref, gathered_ref, mine_ref, other_ref)


def model_kernel(parity_ref, jones_ref, pairs_ref, coher_ref, gathered_ref, mine_ref, other_ref, onehot_ref):
    fill_onehot(pairs_ref, onehot_ref)
    model_body(parity_ref, jones_ref[...], onehot_ref, coher_ref, gathered_ref, mine_ref, other_ref)


def sums_kernel(
    parity_ref, gathered_ref, pairs_ref, coher_ref, vis_ref, mine_ref, other_ref, right_ref, inverse_ref,
    onehot_ref, left_ref,
):
    dirs = coher_ref.shape[0]
    times, baselines = coher_ref.shape[-2:]
    fill_onehot(pairs_ref, onehot_ref)
    first = parity_ref[0, 0] == 0
    for base in range(0, baselines, LANES):
        lanes = slice(base, base + LANES)
        resid = []
        for time in range(0, times, SUBLANES):
            rows = slice(time, time + SUBLANES)
            piece = {}
            for i, j in INDEX:
                mine = mine_ref[i, j, rows, lanes]
                other = other_ref[i, j, rows, lanes]
                piece[i, j] = (
                    vis_ref[0, i, j, rows, lanes] - jnp.where(first, mine, other),
                    vis_ref[1, i, j, rows, lanes] - jnp.where(first, other, mine),
                )
            resid.append(piece)
        for k in range(dirs):
            jones_p = read_rows(gathered_ref, dirs, k, base, LANES)
            jones_q = read_rows(gathered_ref, dirs, k, baselines + base, LANES)
            sums = None
            for index, time in enumerate(range(0, times, SUBLANES)):
                rows = slice(time, time + SUBLANES)
                coher = {(i, j): tuple(coher_ref[k, part, i, j, rows, lanes] for part in range(2)) for i, j in INDEX}
                along = mat_mul_h(coher, jones_q)
                ahead = mat_mul(jones_p, coher)
                right_p = mat_mul_h(resid[index], along)
                right_q = mat_h_mul(resid[index], ahead)
                cross_p = cadd(cmul_conj(along[0, 0], along[1, 0]), cmul_conj(along[0, 1], along[1, 1]))
                cross_q = cadd(cmul_conj(ahead[0, 1], ahead[0, 0]), cmul_conj(ahead[1, 1], ahead[1, 0]))
                terms_p = [right_p[ij][part] for part in range(2) for ij in INDEX] + [
                    sq(along[0, 0]) + sq(along[0, 1]),
                    sq(along[1, 0]) + sq(along[1, 1]),
                    cross_p[0],
                    cross_p[1],
                ]
                terms_q = [right_q[ij][part] for part in range(2) for ij in INDEX] + [
                    sq(ahead[0, 0]) + sq(ahead[1, 0]),
                    sq(ahead[0, 1]) + sq(ahead[1, 1]),
                    cross_q[0],
                    cross_q[1],
                ]
                terms = terms_p + terms_q
                sums = terms if sums is None else [a + b for a, b in zip(sums, terms)]
            for at, term in enumerate(sums):
                row = (at % 12) * dirs + k
                offset = base + (at // 12) * baselines
                left_ref[row : row + 1, offset : offset + LANES] = jnp.sum(term, axis=0, keepdims=True)

    def group(ref, at):
        return ref[at * dirs : (at + 1) * dirs, :]

    jones = {(i, j): (group(gathered_ref, comp(0, i, j)), group(gathered_ref, comp(1, i, j))) for i, j in INDEX}
    diag0, diag1 = group(left_ref, 8), group(left_ref, 9)
    off = (group(left_ref, 10), group(left_ref, 11))
    off_c = (off[0], -off[1])
    for i in range(2):
        left, right = jones[i, 0], jones[i, 1]
        col0 = cadd((left[0] * diag0, left[1] * diag0), cmul(right, off_c))
        col1 = cadd(cmul(left, off), (right[0] * diag1, right[1] * diag1))
        for j, col in ((0, col0), (1, col1)):
            for part in range(2):
                at = comp(part, i, j) * dirs
                left_ref[at : at + dirs, :] = left_ref[at : at + dirs, :] + col[part]

    sums = split_dot(left_ref[...], onehot_ref[...], ((1,), (1,)))
    right_ref[...] = sums[: 8 * dirs]
    m00 = sums[8 * dirs : 9 * dirs] + RHO
    m11 = sums[9 * dirs : 10 * dirs] + RHO
    m01 = (sums[10 * dirs : 11 * dirs], sums[11 * dirs : 12 * dirs])
    scale = 1.0 / (m00 * m11 - sq(m01))
    inverse_ref[0:dirs, :] = m11 * scale
    inverse_ref[dirs : 2 * dirs, :] = m00 * scale
    inverse_ref[2 * dirs : 3 * dirs, :] = -m01[0] * scale
    inverse_ref[3 * dirs :, :] = -m01[1] * scale


def solve(right_ref, inverse_ref, known, dirs):
    i00, i11, re01, im01 = (inverse_ref[at * dirs : (at + 1) * dirs, :] for at in range(4))
    i01, i10 = (re01, im01), (re01, -im01)
    out = {}
    for i in range(2):
        n = []
        for j in range(2):
            at = [comp(part, i, j) * dirs for part in range(2)]
            n.append(tuple(right_ref[a : a + dirs, :] + known(a) for a in at))
        out[i, 0] = cadd((n[0][0] * i00, n[0][1] * i00), cmul(n[1], i10))
        out[i, 1] = cadd(cmul(n[0], i01), (n[1][0] * i11, n[1][1] * i11))
    return out


def store_chunks(ref, a, value):
    width = ref.shape[2]
    for chunk in range(ref.shape[0]):
        ref[chunk, a : a + value.shape[0], :] = value[:, chunk * width : (chunk + 1) * width]


def store_shared(ref, a, value):
    if len(ref.shape) == 3:
        store_chunks(ref, a, value)
    else:
        ref[a : a + value.shape[0], :] = value


def first_update_kernel(basis_ref, right_ref, inverse_ref, known_ref, dual_ref, jones_ref, shared_ref):
    dirs = inverse_ref.shape[0] // 4
    out = solve(right_ref, inverse_ref, lambda a: known_ref[a : a + dirs, :], dirs)
    for (i, j), parts in out.items():
        for part in range(2):
            a = comp(part, i, j) * dirs
            jones_ref[a : a + dirs, :] = parts[part]
            store_shared(shared_ref, a, parts[part] + dual_ref[a : a + dirs, :] * (1.0 / RHO))
    if len(shared_ref.shape) == 3:
        rows, width = 8 * dirs, shared_ref.shape[2]
        terms = basis_ref.shape[1]
        for chunk in range(shared_ref.shape[0]):
            shared_ref[chunk, rows:, :] = jnp.zeros((shared_ref.shape[1] - rows, width), jnp.float32)
            shared_ref[chunk, rows : rows + 1, :terms] = basis_ref[...]


def advance_dual(consensus_ref, dual_ref, before_ref, dual_out_ref, dirs):
    def consensus(a):
        if len(consensus_ref.shape) == 2:
            return consensus_ref[a : a + dirs, :]
        pieces = [consensus_ref[chunk, a : a + dirs, :] for chunk in range(consensus_ref.shape[0])]
        return jnp.concatenate(pieces, axis=1)

    known = {}
    for a in range(0, 8 * dirs, dirs):
        value = consensus(a)
        dual = dual_ref[a : a + dirs, :] + RHO * (before_ref[a : a + dirs, :] - value)
        dual_out_ref[a : a + dirs, :] = dual
        known[a] = RHO * value - dual
    return known


def update_kernel(
    right_ref, inverse_ref, consensus_ref, dual_ref, before_ref, jones_ref, shared_ref, dual_out_ref
):
    dirs = inverse_ref.shape[0] // 4
    known = advance_dual(consensus_ref, dual_ref, before_ref, dual_out_ref, dirs)
    out = solve(right_ref, inverse_ref, known.get, dirs)
    for (i, j), parts in out.items():
        for part in range(2):
            a = comp(part, i, j) * dirs
            jones_ref[a : a + dirs, :] = parts[part]
            store_shared(shared_ref, a, parts[part] + dual_out_ref[a : a + dirs, :] * (1.0 / RHO))


def last_update_kernel(
    right_ref, inverse_ref, consensus_ref, dual_ref, before_ref, jones_ref, shared_ref, dual_out_ref, rows_ref
):
    dirs = inverse_ref.shape[0] // 4
    known = advance_dual(consensus_ref, dual_ref, before_ref, rows_ref, dirs)
    out = solve(right_ref, inverse_ref, known.get, dirs)
    for (i, j), parts in out.items():
        for part in range(2):
            a = comp(part, i, j) * dirs
            dual = rows_ref[a : a + dirs, :]
            shared = parts[part] + dual * (1.0 / RHO)
            for k in range(dirs):
                jones_ref[k, part, i, j : j + 1, :] = parts[part][k : k + 1, :]
                shared_ref[k, part, i, j : j + 1, :] = shared[k : k + 1, :]
                dual_out_ref[k, part, i, j : j + 1, :] = dual[k : k + 1, :]


def mix(matrix, values):
    out = []
    for g in range(matrix.shape[0]):
        total = None
        for f, value in enumerate(values):
            weight = jnp.broadcast_to(matrix[g : g + 1, f : f + 1], value.shape[-2:])
            total = weight * value if total is None else total + weight * value
        out.append(total)
    return out


def first_mix_kernel(place_ref, shared_ref, out_ref, spread_ref, weights_ref):
    bands = shared_ref.shape[0]
    rows = out_ref.shape[1]
    terms = weights_ref.shape[0]
    hi = lax.Precision.HIGHEST
    basis = jnp.concatenate([shared_ref[f, rows : rows + 1, :terms] for f in range(bands)], axis=0)
    gram = lax.dot_general(basis, basis, (((0,), (0,)), ((), ())), precision=hi, preferred_element_type=jnp.float32)
    row = lax.broadcasted_iota(jnp.int32, (terms, terms), 0)
    col = lax.broadcasted_iota(jnp.int32, (terms, terms), 1)
    gram = gram + jnp.where(row == col, RIDGE * bands, 0.0)
    inverse = jnp.where(row == col, 1.0, 0.0)
    for t in range(terms):
        scale = 1.0 / gram[t : t + 1, t : t + 1]
        g_row = gram[t : t + 1, :] * scale
        i_row = inverse[t : t + 1, :] * scale
        factor = gram[:, t : t + 1]
        here = row == t
        gram = jnp.where(here, g_row, gram - factor * g_row)
        inverse = jnp.where(here, i_row, inverse - factor * i_row)
    weights = lax.dot_general(inverse, basis, (((1,), (1,)), ((), ())), precision=hi, preferred_element_type=jnp.float32)
    spread = jnp.dot(basis, weights, precision=hi, preferred_element_type=jnp.float32)
    spread_ref[...] = spread
    for g, value in enumerate(mix(spread, [shared_ref[f, :rows, :] for f in range(bands)])):
        out_ref[g] = value
    band = lax.broadcasted_iota(jnp.int32, (bands, bands), 0)
    slot = lax.broadcasted_iota(jnp.int32, (bands, bands), 1)
    step = (slot + 1) // 2
    spot = lax.rem(place_ref[0, 0] + jnp.where(slot % 2 == 1, -step, step) + 2 * bands, bands)
    source = jnp.where(spot < bands // 2, 2 * spot, 2 * (bands - 1 - spot) + 1)
    chosen = jnp.where(source == band, 1.0, 0.0)
    weights_ref[...] = jnp.dot(weights, chosen, precision=hi, preferred_element_type=jnp.float32)


def mix_kernel(spread_ref, shared_ref, out_ref):
    for g, value in enumerate(mix(spread_ref[...], [shared_ref[f] for f in range(shared_ref.shape[0])])):
        out_ref[g] = value


def final_kernel(weights_ref, basis_ref, jones_ref, dual_ref, *refs):
    shared_refs, (coeffs_ref, dual_out_ref) = refs[:-2], refs[-2:]
    dirs = jones_ref.shape[0]
    half = dirs // 2
    weights = weights_ref[...]
    for k in range(dirs):
        for part in range(2):
            for i in range(2):
                values = [ref[k, part, i] for ref in shared_refs[:-2]]
                values.append(shared_refs[-2][k, part, i] if k < half else shared_refs[-1][k - half, part, i])
                consensus = None
                for m, value in enumerate(mix(weights, values)):
                    coeffs_ref[m, k, part, i] = value
                    share = value * basis_ref[0, m]
                    consensus = share if consensus is None else consensus + share
                dual_out_ref[k, part, i] = dual_ref[k, part, i] + RHO * (jones_ref[k, part, i] - consensus)


def struct(*shape, dtype=jnp.float32):
    return jax.ShapeDtypeStruct(shape, dtype)


def call(kernel, out_shape, scalars, args, scratch=()):
    many = isinstance(out_shape, (tuple, list))
    return pl.pallas_call(
        kernel,
        out_shape=out_shape,
        in_specs=[SMEM if at < scalars else VMEM for at in range(len(args))],
        out_specs=tuple(VMEM for _ in out_shape) if many else VMEM,
        scratch_shapes=list(scratch),
        compiler_params=PARAMS,
    )(*args)


def swap(value, axis, bit):
    size = lax.axis_size(axis)
    return lax.ppermute(value, axis, [(i, i ^ bit) for i in range(size)])


def sum_over_dir(mine, other):
    size = lax.axis_size("dir")
    mine = mine + swap(other, "dir", 1)
    bit = 2
    while bit < size:
        mine = mine + swap(mine, "dir", bit)
        bit *= 2
    return mine, swap(mine, "dir", 1)


def ring_place(size):
    at = lax.axis_index("band")
    return jnp.where(at % 2 == 0, at // 2, size - 1 - at // 2).astype(jnp.int32).reshape(1, 1)


def ring_gather(value):
    size = lax.axis_size("band")
    order = list(range(0, size, 2)) + list(range(size - 1, 0, -2))
    ahead = [(order[i], order[(i + 1) % size]) for i in range(size)]
    behind = [(b, a) for a, b in ahead]
    values = [value]
    up = down = value
    for step in range(1, (size - 1) // 2 + 1):
        up = lax.ppermute(up, "band", ahead)
        down = lax.ppermute(down, "band", behind)
        values += [up, down]
    half = value.shape[0] // 2
    return values + [lax.ppermute(up[:half], "band", ahead), lax.ppermute(down[half:], "band", behind)]


def reduce_bands(shared, row, factor):
    sums = lax.psum(row.reshape((-1,) + (1,) * shared.ndim) * shared[None], "band")
    flat = sums.reshape(sums.shape[0], -1)
    return jax.scipy.linalg.cho_solve((factor, True), flat).reshape(sums.shape)


def local(visibilities, coherencies, jones_start, dual_start, consensus_start, freq_basis, pairs):
    row = freq_basis[0]
    terms = row.shape[0]
    bands = lax.axis_size("band")
    vis, coher = visibilities[0], coherencies[0]
    native = jones_start.shape[1:]
    dirs, stations = native[0], native[-1]
    times, baselines = coher.shape[-2:]
    rows = 8 * dirs
    parity = (lax.axis_index("dir") % 2).astype(jnp.int32).reshape(1, 1)
    chunked = stations % (bands * LANES) == 0 and bands % 2 == 0 and dirs % 2 == 0
    hi = lax.Precision.HIGHEST
    half = struct(2, 2, times, baselines)
    flat = struct(rows, stations)
    onehot = pltpu.VMEM((stations, 2 * baselines), jnp.bfloat16)
    left = pltpu.VMEM((12 * dirs, 2 * baselines), jnp.float32)
    in_rows = pltpu.VMEM((rows, stations), jnp.float32)
    model_out = (struct(rows, 2 * baselines), half, half)

    if not chunked:
        gram = lax.psum(row[:, None] * row[None, :], "band") + RIDGE * bands * jnp.eye(terms, dtype=jnp.float32)
        factor = jnp.linalg.cholesky(gram)

    jones = jones_start[0]
    for turn in range(ITERS):
        last = turn == ITERS - 1
        gathered, mine, other = call(
            model_kernel if turn else first_model_kernel, model_out, 1, (parity, jones, pairs, coher),
            [onehot] if turn else [onehot, in_rows],
        )
        if turn == 0:
            dual, known = call(prepare_kernel, (flat, flat), 1, (freq_basis, dual_start[0], consensus_start))
        mine, other = sum_over_dir(mine, other)
        right, inverse = call(
            sums_kernel, (flat, struct(4 * dirs, stations)), 1,
            (parity, gathered, pairs, coher, vis, mine, other), [onehot, left],
        )
        if turn == 0:
            shape = struct(bands, rows + SUBLANES, stations // bands) if chunked else flat
            jones, shared = call(
                first_update_kernel, (flat, shape), 0, (freq_basis, right, inverse, known, dual)
            )
        elif not last:
            shape = struct(bands, rows, stations // bands) if chunked else flat
            jones, shared, dual = call(
                update_kernel, (flat, shape, flat), 0, (right, inverse, consensus, dual, jones)
            )
        else:
            jones, shared, dual = call(
                last_update_kernel, (struct(*native),) * 3, 0, (right, inverse, consensus, dual, jones), [in_rows]
            )
            break
        if chunked:
            shared = lax.all_to_all(shared, "band", 0, 0)
            mixed = struct(bands, rows, stations // bands)
            if turn == 0:
                mixed, spread, weights = call(
                    first_mix_kernel, (mixed, struct(bands, bands), struct(terms, bands)), 1,
                    (ring_place(bands), shared),
                )
            else:
                mixed = call(mix_kernel, mixed, 0, (spread, shared))
            consensus = lax.all_to_all(mixed, "band", 0, 0)
        else:
            coeffs = reduce_bands(shared, row, factor)
            consensus = jnp.tensordot(row, coeffs, axes=(0, 0), precision=hi)
    if chunked:
        values = ring_gather(shared)

        def kernel(weights_ref, basis_ref, *refs):
            final_kernel(weights_ref, basis_ref, *refs)

        coeffs, dual = pl.pallas_call(
            kernel,
            out_shape=(struct(terms, *native), struct(*native)),
            in_specs=[VMEM, SMEM] + [VMEM] * (2 + len(values)),
            out_specs=(VMEM, VMEM),
            compiler_params=PARAMS,
        )(weights, freq_basis, jones, dual, *values)
    else:
        coeffs = reduce_bands(shared, row, factor)
        dual = dual + RHO * (jones - jnp.tensordot(row, coeffs, axes=(0, 0), precision=hi))
    return jones[None], dual[None], coeffs


def solution(mesh):
    in_specs = (
        P("band", None, None, None, None, None),
        P("band", "dir", None, None, None, None, None),
        P("band", "dir", None, None, None, None),
        P("band", "dir", None, None, None, None),
        P(None, "dir", None, None, None, None),
        P("band", None),
        P(),
    )
    out_specs = (
        P("band", "dir", None, None, None, None),
        P("band", "dir", None, None, None, None),
        P(None, "dir", None, None, None, None),
    )
    return jax.shard_map(local, mesh=mesh, in_specs=in_specs, out_specs=out_specs, check_vma=False)
```

time: 134 us -> 92 us (0.69)
  local copies, waits for them, and re-layouts: 40.2 us -> 2.84 us
  waiting for transfers between devices: 22.7 us -> 37.2 us
  starting transfers between devices: 39.2 us -> 31.5 us
  other arithmetic: 4.96 us -> 0.12 us
  between operations: 5.52 us -> 0.88 us
  matrix products: 1.63 us -> 0 us
    unnamed x74 -> x18, local copies, waits for them, and re-layouts: 23.8 us -> 2.83 us
    ppermute x9, waiting for transfers between devices: 4.82 us -> 10.8 us  [swap(): return lax.ppermute(value, axis, [(i, i ^ bit) for i in range(size)])]
    all_to_all x1 -> x0, starting transfers between devices: 5.83 us -> none  [local(): lax.all_to_all(jnp.broadcast_to(freq_basis, (bands, terms)), 'band', 0, 0...]
    reshape x7 -> x0, local copies, waits for them, and re-layouts: 5.67 us -> none  [the longest x3 2.6 us: to_rows(): value.reshape(dirs, 8, stations).transpose(1, 0, 2)]
    all_to_all x2, waiting for transfers between devices: 2.34 us -> 6.73 us  [local(): shared = lax.all_to_all(shared, 'band', 0, 0)]
    ppermute x3, waiting for transfers between devices: 6.17 us -> 10.5 us  [ring_gather(): down = lax.ppermute(down, 'band', behind)]
    another operation x5 -> x0, local copies, waits for them, and re-layouts: 4.08 us -> none  [the longest x2 1.82 us: to_rows(): value.reshape(dirs, 8, stations).transpose(1, 0, 2)]
    dot_general x2 -> x0, local copies, waits for them, and re-layouts: 3.52 us -> none  [local(): jnp.tensordot(row, consensus_start, axes=(0, 0), precision=hi)]
  transfers between devices with their start and end apart: 22 -> 21, of which waited for: 13 -> 16; matrix products, arithmetic and copies ran while one was open for 14% -> 0% of each run, Pallas kernels for 7% -> 12%
where the time goes in v2:
time: 92 us; the launch traced here: 91.4 us
  waiting for transfers between devices  37.2 us (40%)
  starting transfers between devices  31.5 us (34%)
  Pallas kernels  18.9 us (21%)
  local copies, waits for them, and re-layouts  2.84 us (3%)
    pallas_call x12, Pallas kernels, call(): pl.pallas_call(kernel, out_shape=out_shape, in_specs=[SMEM if at < scalar...  16.6 us
    ppermute x9, waiting for transfers between devices, swap(): return lax.ppermute(value, axis, [(i, i ^ bit) for i in range(size)])  10.8 us
    ppermute x3, waiting for transfers between devices, ring_gather(): down = lax.ppermute(down, 'band', behind)  10.5 us
    all_to_all x2, starting transfers between devices, local(): shared = lax.all_to_all(shared, 'band', 0, 0)  9.45 us
    ppermute x9, starting transfers between devices, swap(): return lax.ppermute(value, axis, [(i, i ^ bit) for i in range(size)])  6.93 us
    all_to_all x2, starting transfers between devices, local(): consensus = lax.all_to_all(mixed, 'band', 0, 0)  6.92 us
    all_to_all x2, waiting for transfers between devices, local(): consensus = lax.all_to_all(mixed, 'band', 0, 0)  6.75 us
    all_to_all x2, waiting for transfers between devices, local(): shared = lax.all_to_all(shared, 'band', 0, 0)  6.73 us
  transfers between devices with their start and end apart: 21, of which 16 were waited for; matrix products, arithmetic and copies ran while one was open for 0% of the time, Pallas kernels for 12%

profile of v2, /device:TPU:0, one launch (start us, length us, event | category | flops | bytes accessed | tf_op | source)
XLA Modules:
  0.0 91.4 jit_solution(2776340492747022091)
XLA Ops:
  1.3 1.2 %copy-done = f32[1,4,2,2,2,16,512]{6,5,4,3,2,1,0:T(8,128)S(1)} copy-done((f32[1,4,2,2,2,16,512]{6,5,4,3,2,1,0:T(8,128)S(1)}, f32[1,4,2,2,2,16,512]{6,5,4,3,2,1,0:T(8,128)}, u32[]{:S(2)}) %copy-start) | copy-done | bytes 1048600
  3.5 1.2 %shard_map.94 = (f32[32,1024]{1,0:T(8,128)S(1)}, f32[2,2,16,512]{3,2,1,0:T(8,128)S(1)}, f32[2,2,16,512]{3,2,1,0:T(8,128)S(1)}) custom-call(s32[1,1]{1,0:T(1,128)} %bitcast.parity_ref, f32[4,2,2,2,1024]{4,3,2,1,0:T(2,128)S(1)} %bitcast.17, s32[2,512]{1,0:T(2,128)S(1)} %copy-done.4, f32[4,2,2,2,16,512]{5,4,3,2,1,0:T(8,128)S(1)} %bitcast.8), custom_call_target="tpu_custom_call" | custom-call | tf_op jit(solution)/shard_map/pallas_call | solution.py:391
  6.2 2.9 %collective-permute-start.1 = (f32[2,2,16,512]{3,2,1,0:T(8,128)S(1)}, f32[2,2,16,512]{3,2,1,0:T(8,128)S(1)}, u32[]{:S(2)}, u32[]{:S(2)}) collective-permute-start(f32[2,2,16,512]{3,2,1,0:T(8,128)S(1)} %add.27), channel_id=1, source_target_pairs={{0,2},{1,3},{2,0},{3,1},{4,6},{5,7},{6,4},{7,5},{8,10},{9,11},{10,... | collective-permute-start | bytes 393224 | tf_op jit(solution)/shard_map/ppermute | solution.py:403
  9.2 3.8 %collective-permute-done.1 = f32[2,2,16,512]{3,2,1,0:T(8,128)S(1)} collective-permute-done((f32[2,2,16,512]{3,2,1,0:T(8,128)S(1)}, f32[2,2,16,512]{3,2,1,0:T(8,128)S(1)}, u32[]{:S(2)}, u32[]{:S(2)}) %collective-permute-start.1) | collective-permute-done | bytes 131104 | tf_op jit(solution)/shard_map/ppermute | solution.py:403
  14.4 2.4 %shard_map.95 = (f32[32,1024]{1,0:T(8,128)S(1)}, f32[16,1024]{1,0:T(8,128)S(1)}) custom-call(s32[1,1]{1,0:T(1,128)} %bitcast.parity_ref, f32[32,1024]{1,0:T(8,128)S(1)} %get-tuple-element.33.gathered_ref, s32[2,512]{1,0:T(2,128)S(1)} %copy-done.4, f32[4,2,2,2,16,512]{5,4,3,2,1,0:T(8,128)S(1)} %bitcast.9, f32[2,2,2,16,512]{4,3,2,1,0:T(8,128)S(1)} %bitcast.14, ...), custom_call_target="tpu_custom_call" | custom-call | tf_op jit(solution)/shard_map/pallas_call | solution.py:391
  17.6 6.1 %all-to-all-start = ((f32[8,40,128]{2,1,0:T(8,128)}), f32[8,40,128]{2,1,0:T(8,128)S(1)}, u32[]{:S(2)}, u32[]{:S(2)}) async-start(f32[8,40,128]{2,1,0:T(8,128)} %get-tuple-element.46), calls=%async_computation | async-start | bytes 327680 | tf_op jit(solution)/shard_map/all_to_all | solution.py:495
  23.6 1.2 %shard_map.98 = (f32[32,1024]{1,0:T(8,128)S(1)}, f32[2,2,16,512]{3,2,1,0:T(8,128)S(1)}, f32[2,2,16,512]{3,2,1,0:T(8,128)S(1)}) custom-call(s32[1,1]{1,0:T(1,128)} %bitcast.parity_ref, f32[32,1024]{1,0:T(8,128)S(1)} %get-tuple-element.40.jones_ref.before_ref, s32[2,512]{1,0:T(2,128)S(1)} %copy-done.4, f32[4,2,2,2,16,512]{5,4,3,2,1,0:T(8,128)S(1)} %bitcast.10), custom_call_target="tpu_custom_call" | custom-call | tf_op jit(solution)/shard_map/pallas_call | solution.py:391
  24.9 1.3 %collective-permute-done.3 = f32[2,2,16,512]{3,2,1,0:T(8,128)S(1)} collective-permute-done((f32[2,2,16,512]{3,2,1,0:T(8,128)S(1)}, f32[2,2,16,512]{3,2,1,0:T(8,128)S(1)}, u32[]{:S(2)}, u32[]{:S(2)}) %collective-permute-start.3) | collective-permute-done | bytes 131104 | tf_op jit(solution)/shard_map/ppermute | solution.py:403
  26.2 1.6 %collective-permute-start.4 = (f32[2,2,16,512]{3,2,1,0:T(8,128)S(1)}, f32[2,2,16,512]{3,2,1,0:T(8,128)S(1)}, u32[]{:S(2)}, u32[]{:S(2)}) collective-permute-start(f32[2,2,16,512]{3,2,1,0:T(8,128)S(1)} %add.29), channel_id=1, source_target_pairs={{0,2},{1,3},{2,0},{3,1},{4,6},{5,7},{6,4},{7,5},{8,10},{9,11},{10,... | collective-permute-start | bytes 393224 | tf_op jit(solution)/shard_map/ppermute | solution.py:403
  27.8 3.6 %all-to-all-done.shared_ref = f32[8,40,128]{2,1,0:T(8,128)S(1)} async-done(((f32[8,40,128]{2,1,0:T(8,128)}), f32[8,40,128]{2,1,0:T(8,128)S(1)}, u32[]{:S(2)}, u32[]{:S(2)}) %all-to-all-start) | async-done | bytes 163872 | tf_op jit(solution)/shard_map/all_to_all | solution.py:495
  31.4 2.0 %shard_map.100 = (f32[8,32,128]{2,1,0:T(8,128)}, f32[8,8]{1,0:T(8,128)S(1)}, f32[8,8]{1,0:T(8,128)S(1)}) custom-call(s32[1,1]{1,0:T(1,128)} %bitcast.5.place_ref, f32[8,40,128]{2,1,0:T(8,128)S(1)} %all-to-all-done.shared_ref), custom_call_target="tpu_custom_call" | custom-call | tf_op jit(solution)/shard_map/pallas_call | solution.py:391
  33.4 3.4 %all-to-all-start.1 = ((f32[8,32,128]{2,1,0:T(8,128)}), f32[8,32,128]{2,1,0:T(8,128)S(1)}, u32[]{:S(2)}, u32[]{:S(2)}) async-start(f32[8,32,128]{2,1,0:T(8,128)} %get-tuple-element.47), calls=%async_computation.1 | async-start | bytes 262144 | tf_op jit(solution)/shard_map/all_to_all | solution.py:504
  36.9 1.3 %collective-permute-done.5.other_ref = f32[2,2,16,512]{3,2,1,0:T(8,128)S(1)} collective-permute-done((f32[2,2,16,512]{3,2,1,0:T(8,128)S(1)}, f32[2,2,16,512]{3,2,1,0:T(8,128)S(1)}, u32[]{:S(2)}, u32[]{:S(2)}) %collective-permute-start.5) | collective-permute-done | bytes 131104 | tf_op jit(solution)/shard_map/ppermute | solution.py:403
  38.2 2.4 %shard_map.99 = (f32[32,1024]{1,0:T(8,128)S(1)}, f32[16,1024]{1,0:T(8,128)S(1)}) custom-call(s32[1,1]{1,0:T(1,128)} %bitcast.parity_ref, f32[32,1024]{1,0:T(8,128)S(1)} %get-tuple-element.41.gathered_ref, s32[2,512]{1,0:T(2,128)S(1)} %copy-done.4, f32[4,2,2,2,16,512]{5,4,3,2,1,0:T(8,128)S(1)} %bitcast.11, f32[2,2,2,16,512]{4,3,2,1,0:T(8,128)S(1)} %bitcast.15, ...), custom_call_target="tpu_custom_call" | custom-call | tf_op jit(solution)/shard_map/pallas_call | solution.py:391
  40.6 3.5 %all-to-all-done.1.consensus_ref = f32[8,32,128]{2,1,0:T(8,128)S(1)} async-done(((f32[8,32,128]{2,1,0:T(8,128)}), f32[8,32,128]{2,1,0:T(8,128)S(1)}, u32[]{:S(2)}, u32[]{:S(2)}) %all-to-all-start.1) | async-done | bytes 131104 | tf_op jit(solution)/shard_map/all_to_all | solution.py:504
  44.9 3.4 %all-to-all-start.2 = ((f32[8,32,128]{2,1,0:T(8,128)}), f32[8,32,128]{2,1,0:T(8,128)S(1)}, u32[]{:S(2)}, u32[]{:S(2)}) async-start(f32[8,32,128]{2,1,0:T(8,128)} %get-tuple-element.55), calls=%async_computation.2 | async-start | bytes 262144 | tf_op jit(solution)/shard_map/all_to_all | solution.py:495
  49.5 1.3 %collective-permute-done.6 = f32[2,2,16,512]{3,2,1,0:T(8,128)S(1)} collective-permute-done((f32[2,2,16,512]{3,2,1,0:T(8,128)S(1)}, f32[2,2,16,512]{3,2,1,0:T(8,128)S(1)}, u32[]{:S(2)}, u32[]{:S(2)}) %collective-permute-start.6) | collective-permute-done | bytes 131104 | tf_op jit(solution)/shard_map/ppermute | solution.py:403
  50.9 1.6 %collective-permute-start.7 = (f32[2,2,16,512]{3,2,1,0:T(8,128)S(1)}, f32[2,2,16,512]{3,2,1,0:T(8,128)S(1)}, u32[]{:S(2)}, u32[]{:S(2)}) collective-permute-start(f32[2,2,16,512]{3,2,1,0:T(8,128)S(1)} %add.32), channel_id=1, source_target_pairs={{0,2},{1,3},{2,0},{3,1},{4,6},{5,7},{6,4},{7,5},{8,10},{9,11},{10,... | collective-permute-start | bytes 393224 | tf_op jit(solution)/shard_map/ppermute | solution.py:403
  52.4 3.1 %all-to-all-done.2.shared_ref = f32[8,32,128]{2,1,0:T(8,128)S(1)} async-done(((f32[8,32,128]{2,1,0:T(8,128)}), f32[8,32,128]{2,1,0:T(8,128)S(1)}, u32[]{:S(2)}, u32[]{:S(2)}) %all-to-all-start.2) | async-done | bytes 131104 | tf_op jit(solution)/shard_map/all_to_all | solution.py:495
  56.4 3.6 %all-to-all-start.3 = ((f32[8,32,128]{2,1,0:T(8,128)}), f32[8,32,128]{2,1,0:T(8,128)S(1)}, u32[]{:S(2)}, u32[]{:S(2)}) async-start(f32[8,32,128]{2,1,0:T(8,128)} %shard_map.104), calls=%async_computation.3 | async-start | bytes 262144 | tf_op jit(solution)/shard_map/all_to_all | solution.py:504
  60.1 1.3 %collective-permute-done.8.other_ref = f32[2,2,16,512]{3,2,1,0:T(8,128)S(1)} collective-permute-done((f32[2,2,16,512]{3,2,1,0:T(8,128)S(1)}, f32[2,2,16,512]{3,2,1,0:T(8,128)S(1)}, u32[]{:S(2)}, u32[]{:S(2)}) %collective-permute-start.8) | collective-permute-done | bytes 131104 | tf_op jit(solution)/shard_map/ppermute | solution.py:403
  61.4 2.4 %shard_map.103 = (f32[32,1024]{1,0:T(8,128)S(1)}, f32[16,1024]{1,0:T(8,128)S(1)}) custom-call(s32[1,1]{1,0:T(1,128)} %bitcast.parity_ref, f32[32,1024]{1,0:T(8,128)S(1)} %get-tuple-element.49.gathered_ref, s32[2,512]{1,0:T(2,128)S(1)} %copy-done.4, f32[4,2,2,2,16,512]{5,4,3,2,1,0:T(8,128)S(1)} %bitcast.13, f32[2,2,2,16,512]{4,3,2,1,0:T(8,128)S(1)} %bitcast.16, ...), custom_call_target="tpu_custom_call" | custom-call | tf_op jit(solution)/shard_map/pallas_call | solution.py:391
  63.8 3.3 %all-to-all-done.3.consensus_ref = f32[8,32,128]{2,1,0:T(8,128)S(1)} async-done(((f32[8,32,128]{2,1,0:T(8,128)}), f32[8,32,128]{2,1,0:T(8,128)S(1)}, u32[]{:S(2)}, u32[]{:S(2)}) %all-to-all-start.3) | async-done | bytes 131104 | tf_op jit(solution)/shard_map/all_to_all | solution.py:504
  68.2 1.8 %collective-permute-start.9 = (f32[4,2,2,2,1024]{4,3,2,1,0:T(2,128)S(1)}, f32[4,2,2,2,1024]{4,3,2,1,0:T(2,128)S(1)}, u32[]{:S(2)}, u32[]{:S(2)}) collective-permute-start(f32[4,2,2,2,1024]{4,3,2,1,0:T(2,128)S(1)} %get-tuple-element.60.refs_2_), channel_id=1, source_target_pairs={{0,8},{8,16},{16,24},{24,28},{28,20},{20,12},{12,4},{4,0},{1,9},{9... | collective-permute-start | bytes 393224 | tf_op jit(solution)/shard_map/ppermute | solution.py:429
  70.0 3.6 %collective-permute-done.10.refs_4_ = f32[4,2,2,2,1024]{4,3,2,1,0:T(2,128)S(1)} collective-permute-done((f32[4,2,2,2,1024]{4,3,2,1,0:T(2,128)S(1)}, f32[4,2,2,2,1024]{4,3,2,1,0:T(2,128)S(1)}, u32[]{:S(2)}, u32[]{:S(2)}) %collective-permute-start.10) | collective-permute-done | bytes 131104 | tf_op jit(solution)/shard_map/ppermute | solution.py:430
  73.6 2.0 %collective-permute-start.11 = (f32[4,2,2,2,1024]{4,3,2,1,0:T(2,128)S(1)}, f32[4,2,2,2,1024]{4,3,2,1,0:T(2,128)S(1)}, u32[]{:S(2)}, u32[]{:S(2)}) collective-permute-start(f32[4,2,2,2,1024]{4,3,2,1,0:T(2,128)S(1)} %collective-permute-done.9.refs_3_), channel_id=1, source_target_pairs={{0,8},{8,16},{16,24},{24,28},{28,20},{20,12},{12,4},{4,0},{1,9},{9... | collective-permute-start | bytes 393224 | tf_op jit(solution)/shard_map/ppermute | solution.py:429
  75.6 4.0 %collective-permute-done.12.refs_6_ = f32[4,2,2,2,1024]{4,3,2,1,0:T(2,128)S(1)} collective-permute-done((f32[4,2,2,2,1024]{4,3,2,1,0:T(2,128)S(1)}, f32[4,2,2,2,1024]{4,3,2,1,0:T(2,128)S(1)}, u32[]{:S(2)}, u32[]{:S(2)}) %collective-permute-start.12) | collective-permute-done | bytes 131104 | tf_op jit(solution)/shard_map/ppermute | solution.py:430
  79.9 1.7 %collective-permute-start.13 = (f32[4,2,2,2,1024]{4,3,2,1,0:T(2,128)S(1)}, f32[4,2,2,2,1024]{4,3,2,1,0:T(2,128)S(1)}, u32[]{:S(2)}, u32[]{:S(2)}) collective-permute-start(f32[4,2,2,2,1024]{4,3,2,1,0:T(2,128)S(1)} %collective-permute-done.11.refs_5_), channel_id=1, source_target_pairs={{0,8},{8,16},{16,24},{24,28},{28,20},{20,12},{12,4},{4,0},{1,9},{9... | collective-permute-start | bytes 393224 | tf_op jit(solution)/shard_map/ppermute | solution.py:429
  81.6 2.9 %collective-permute-done.14.refs_8_ = f32[4,2,2,2,1024]{4,3,2,1,0:T(2,128)S(1)} collective-permute-done((f32[4,2,2,2,1024]{4,3,2,1,0:T(2,128)S(1)}, f32[4,2,2,2,1024]{4,3,2,1,0:T(2,128)S(1)}, u32[]{:S(2)}, u32[]{:S(2)}) %collective-permute-start.14) | collective-permute-done | bytes 131104 | tf_op jit(solution)/shard_map/ppermute | solution.py:430
  84.8 1.8 %collective-permute-start.15 = (f32[2,2,2,2,1024]{4,3,2,1,0:T(2,128)S(1)}, f32[2,2,2,2,1024]{4,3,2,1,0:T(2,128)S(1)}, u32[]{:S(2)}, u32[]{:S(2)}) collective-permute-start(f32[2,2,2,2,1024]{4,3,2,1,0:T(2,128)S(1)} %slice.8), channel_id=1, source_target_pairs={{0,8},{8,16},{16,24},{24,28},{28,20},{20,12},{12,4},{4,0},{1,9},{9... | collective-permute-start | bytes 196616 | tf_op jit(solution)/shard_map/ppermute | solution.py:433
  86.6 2.2 %collective-permute-done.16.refs_10_ = f32[2,2,2,2,1024]{4,3,2,1,0:T(2,128)S(1)} collective-permute-done((f32[2,2,2,2,1024]{4,3,2,1,0:T(2,128)S(1)}, f32[2,2,2,2,1024]{4,3,2,1,0:T(2,128)S(1)}, u32[]{:S(2)}, u32[]{:S(2)}) %collective-permute-start.16) | collective-permute-done | bytes 65568 | tf_op jit(solution)/shard_map/ppermute | solution.py:433
  89.2 2.2 %shard_map.106 = (f32[8,4,2,2,2,1024]{5,4,3,2,1,0:T(2,128)}, f32[4,2,2,2,1024]{4,3,2,1,0:T(2,128)}) custom-call(f32[8,8]{1,0:T(8,128)S(1)} %get-tuple-element.58.weights_ref, f32[1,8]{1,0:T(1,128)S(1)} %copy-done.8, f32[4,2,2,2,1024]{4,3,2,1,0:T(2,128)S(1)} %copy-done.7, f32[4,2,2,2,1024]{4,3,2,1,0:T(2,128)S(1)} %get-tuple-element.59.refs_1_, ...), custom_call_target="tpu_custom_call" | custom-call | tf_op jit(solution)/shard_map/pallas_call | solution.py:514
  (49 shorter events, 10.6 us)
Async XLA Ops:
  0.6 0.7 copy-start.4
  1.3 1.2 %copy-start = (f32[1,4,2,2,2,16,512]{6,5,4,3,2,1,0:T(8,128)S(1)}, f32[1,4,2,2,2,16,512]{6,5,4,3,2,1,0:T(8,128)}, u32[]{:S(2)}) copy-start(f32[1,4,2,2,2,16,512]{6,5,4,3,2,1,0:T(8,128)} %param.8) | copy-start | bytes 3145732
  2.6 0.9 copy-start.5
  3.5 9.6 %copy-start.3 = (f32[8,4,2,2,2,1024]{5,4,3,2,1,0:T(2,128)S(1)}, f32[8,4,2,2,2,1024]{5,4,3,2,1,0:T(2,128)}, u32[]{:S(2)}) copy-start(f32[8,4,2,2,2,1024]{5,4,3,2,1,0:T(2,128)} %coeffs_ref.1) | copy-start | bytes 3145732
  3.5 9.6 %copy-start.6 = (f32[1,4,2,2,2,1024]{5,4,3,2,1,0:T(2,128)S(1)}, f32[1,4,2,2,2,1024]{5,4,3,2,1,0:T(2,128)}, u32[]{:S(2)}) copy-start(f32[1,4,2,2,2,1024]{5,4,3,2,1,0:T(2,128)} %param.10) | copy-start | bytes 393220
  3.5 9.6 %copy-start.8 = (f32[1,8]{1,0:T(1,128)S(1)}, f32[1,8]{1,0:T(1,128)}, u32[]{:S(2)}) copy-start(f32[1,8]{1,0:T(1,128)} %basis_ref.5) | copy-start | bytes 100
  4.7 9.7 %copy-start.1 = (f32[1,4,2,2,2,16,512]{6,5,4,3,2,1,0:T(8,128)S(1)}, f32[1,4,2,2,2,16,512]{6,5,4,3,2,1,0:T(8,128)}, u32[]{:S(2)}) copy-start(f32[1,4,2,2,2,16,512]{6,5,4,3,2,1,0:T(8,128)} %param.8) | copy-start | bytes 3145732
  4.7 1.5 %collective-permute-start = (f32[2,2,16,512]{3,2,1,0:T(8,128)S(1)}, f32[2,2,16,512]{3,2,1,0:T(8,128)S(1)}, u32[]{:S(2)}, u32[]{:S(2)}) collective-permute-start(f32[2,2,16,512]{3,2,1,0:T(8,128)S(1)} %get-tuple-element.35), channel_id=1, source_target_pairs={{0,1},{1,0},{2,3},{3,2},{4,5},{5,4},{6,7},{7,6},{8,9},{9,8},{10,11... | collective-permute-start | bytes 393224 | tf_op jit(solution)/shard_map/ppermute | solution.py:403
  6.2 6.7 %collective-permute-start.1 = (f32[2,2,16,512]{3,2,1,0:T(8,128)S(1)}, f32[2,2,16,512]{3,2,1,0:T(8,128)S(1)}, u32[]{:S(2)}, u32[]{:S(2)}) collective-permute-start(f32[2,2,16,512]{3,2,1,0:T(8,128)S(1)} %add.27), channel_id=1, source_target_pairs={{0,2},{1,3},{2,0},{3,1},{4,6},{5,7},{6,4},{7,5},{8,10},{9,11},{10,... | collective-permute-start | bytes 393224 | tf_op jit(solution)/shard_map/ppermute | solution.py:403
  13.0 1.4 %collective-permute-start.2 = (f32[2,2,16,512]{3,2,1,0:T(8,128)S(1)}, f32[2,2,16,512]{3,2,1,0:T(8,128)S(1)}, u32[]{:S(2)}, u32[]{:S(2)}) collective-permute-start(f32[2,2,16,512]{3,2,1,0:T(8,128)S(1)} %add.28.mine_ref), channel_id=1, source_target_pairs={{0,1},{1,0},{2,3},{3,2},{4,5},{5,4},{6,7},{7,6},{8,9},{9,8},{10,11... | collective-permute-start | bytes 393224 | tf_op jit(solution)/shard_map/ppermute | solution.py:403
  13.1 1.3 %copy-start.2 = (f32[1,2,2,2,16,512]{5,4,3,2,1,0:T(8,128)S(1)}, f32[1,2,2,2,16,512]{5,4,3,2,1,0:T(8,128)}, u32[]{:S(2)}) copy-start(f32[1,2,2,2,16,512]{5,4,3,2,1,0:T(8,128)} %param.7) | copy-start | bytes 786436
  17.6 13.9 %all-to-all-start = ((f32[8,40,128]{2,1,0:T(8,128)}), f32[8,40,128]{2,1,0:T(8,128)S(1)}, u32[]{:S(2)}, u32[]{:S(2)}) async-start(f32[8,40,128]{2,1,0:T(8,128)} %get-tuple-element.46), calls=%async_computation | async-start | bytes 327680 | tf_op jit(solution)/shard_map/all_to_all | solution.py:495
  24.8 1.4 %collective-permute-start.3 = (f32[2,2,16,512]{3,2,1,0:T(8,128)S(1)}, f32[2,2,16,512]{3,2,1,0:T(8,128)S(1)}, u32[]{:S(2)}, u32[]{:S(2)}) collective-permute-start(f32[2,2,16,512]{3,2,1,0:T(8,128)S(1)} %get-tuple-element.43), channel_id=1, source_target_pairs={{0,1},{1,0},{2,3},{3,2},{4,5},{5,4},{6,7},{7,6},{8,9},{9,8},{10,11... | collective-permute-start | bytes 393224 | tf_op jit(solution)/shard_map/ppermute | solution.py:403
  26.2 10.5 %collective-permute-start.4 = (f32[2,2,16,512]{3,2,1,0:T(8,128)S(1)}, f32[2,2,16,512]{3,2,1,0:T(8,128)S(1)}, u32[]{:S(2)}, u32[]{:S(2)}) collective-permute-start(f32[2,2,16,512]{3,2,1,0:T(8,128)S(1)} %add.29), channel_id=1, source_target_pairs={{0,2},{1,3},{2,0},{3,1},{4,6},{5,7},{6,4},{7,5},{8,10},{9,11},{10,... | collective-permute-start | bytes 393224 | tf_op jit(solution)/shard_map/ppermute | solution.py:403
  33.4 10.7 %all-to-all-start.1 = ((f32[8,32,128]{2,1,0:T(8,128)}), f32[8,32,128]{2,1,0:T(8,128)S(1)}, u32[]{:S(2)}, u32[]{:S(2)}) async-start(f32[8,32,128]{2,1,0:T(8,128)} %get-tuple-element.47), calls=%async_computation.1 | async-start | bytes 262144 | tf_op jit(solution)/shard_map/all_to_all | solution.py:504
  36.8 1.4 %collective-permute-start.5 = (f32[2,2,16,512]{3,2,1,0:T(8,128)S(1)}, f32[2,2,16,512]{3,2,1,0:T(8,128)S(1)}, u32[]{:S(2)}, u32[]{:S(2)}) collective-permute-start(f32[2,2,16,512]{3,2,1,0:T(8,128)S(1)} %add.30.mine_ref), channel_id=1, source_target_pairs={{0,1},{1,0},{2,3},{3,2},{4,5},{5,4},{6,7},{7,6},{8,9},{9,8},{10,11... | collective-permute-start | bytes 393224 | tf_op jit(solution)/shard_map/ppermute | solution.py:403
  44.9 10.7 %all-to-all-start.2 = ((f32[8,32,128]{2,1,0:T(8,128)}), f32[8,32,128]{2,1,0:T(8,128)S(1)}, u32[]{:S(2)}, u32[]{:S(2)}) async-start(f32[8,32,128]{2,1,0:T(8,128)} %get-tuple-element.55), calls=%async_computation.2 | async-start | bytes 262144 | tf_op jit(solution)/shard_map/all_to_all | solution.py:495
  49.4 1.4 %collective-permute-start.6 = (f32[2,2,16,512]{3,2,1,0:T(8,128)S(1)}, f32[2,2,16,512]{3,2,1,0:T(8,128)S(1)}, u32[]{:S(2)}, u32[]{:S(2)}) collective-permute-start(f32[2,2,16,512]{3,2,1,0:T(8,128)S(1)} %get-tuple-element.51), channel_id=1, source_target_pairs={{0,1},{1,0},{2,3},{3,2},{4,5},{5,4},{6,7},{7,6},{8,9},{9,8},{10,11... | collective-permute-start | bytes 393224 | tf_op jit(solution)/shard_map/ppermute | solution.py:403
  50.9 9.1 %collective-permute-start.7 = (f32[2,2,16,512]{3,2,1,0:T(8,128)S(1)}, f32[2,2,16,512]{3,2,1,0:T(8,128)S(1)}, u32[]{:S(2)}, u32[]{:S(2)}) collective-permute-start(f32[2,2,16,512]{3,2,1,0:T(8,128)S(1)} %add.32), channel_id=1, source_target_pairs={{0,2},{1,3},{2,0},{3,1},{4,6},{5,7},{6,4},{7,5},{8,10},{9,11},{10,... | collective-permute-start | bytes 393224 | tf_op jit(solution)/shard_map/ppermute | solution.py:403
  56.4 10.7 %all-to-all-start.3 = ((f32[8,32,128]{2,1,0:T(8,128)}), f32[8,32,128]{2,1,0:T(8,128)S(1)}, u32[]{:S(2)}, u32[]{:S(2)}) async-start(f32[8,32,128]{2,1,0:T(8,128)} %shard_map.104), calls=%async_computation.3 | async-start | bytes 262144 | tf_op jit(solution)/shard_map/all_to_all | solution.py:504
  60.0 1.4 %collective-permute-start.8 = (f32[2,2,16,512]{3,2,1,0:T(8,128)S(1)}, f32[2,2,16,512]{3,2,1,0:T(8,128)S(1)}, u32[]{:S(2)}, u32[]{:S(2)}) collective-permute-start(f32[2,2,16,512]{3,2,1,0:T(8,128)S(1)} %add.33.mine_ref), channel_id=1, source_target_pairs={{0,1},{1,0},{2,3},{3,2},{4,5},{5,4},{6,7},{7,6},{8,9},{9,8},{10,11... | collective-permute-start | bytes 393224 | tf_op jit(solution)/shard_map/ppermute | solution.py:403
  68.0 21.2 %copy-start.7 = (f32[4,2,2,2,1024]{4,3,2,1,0:T(2,128)S(1)}, f32[4,2,2,2,1024]{4,3,2,1,0:T(2,128)}, u32[]{:S(2)}) copy-start(f32[4,2,2,2,1024]{4,3,2,1,0:T(2,128)} %get-tuple-element.57.refs_0_) | copy-start | bytes 393220
  68.0 5.6 %collective-permute-start.10 = (f32[4,2,2,2,1024]{4,3,2,1,0:T(2,128)S(1)}, f32[4,2,2,2,1024]{4,3,2,1,0:T(2,128)S(1)}, u32[]{:S(2)}, u32[]{:S(2)}) collective-permute-start(f32[4,2,2,2,1024]{4,3,2,1,0:T(2,128)S(1)} %get-tuple-element.60.refs_2_), channel_id=1, source_target_pairs={{8,0},{16,8},{24,16},{28,24},{20,28},{12,20},{4,12},{0,4},{9,1},{1... | collective-permute-start | bytes 393224 | tf_op jit(solution)/shard_map/ppermute | solution.py:430
  68.2 5.4 %collective-permute-start.9 = (f32[4,2,2,2,1024]{4,3,2,1,0:T(2,128)S(1)}, f32[4,2,2,2,1024]{4,3,2,1,0:T(2,128)S(1)}, u32[]{:S(2)}, u32[]{:S(2)}) collective-permute-start(f32[4,2,2,2,1024]{4,3,2,1,0:T(2,128)S(1)} %get-tuple-element.60.refs_2_), channel_id=1, source_target_pairs={{0,8},{8,16},{16,24},{24,28},{28,20},{20,12},{12,4},{4,0},{1,9},{9... | collective-permute-start | bytes 393224 | tf_op jit(solution)/shard_map/ppermute | solution.py:429
  73.6 6.0 %collective-permute-start.12 = (f32[4,2,2,2,1024]{4,3,2,1,0:T(2,128)S(1)}, f32[4,2,2,2,1024]{4,3,2,1,0:T(2,128)S(1)}, u32[]{:S(2)}, u32[]{:S(2)}) collective-permute-start(f32[4,2,2,2,1024]{4,3,2,1,0:T(2,128)S(1)} %collective-permute-done.10.refs_4_), channel_id=1, source_target_pairs={{8,0},{16,8},{24,16},{28,24},{20,28},{12,20},{4,12},{0,4},{9,1},{1... | collective-permute-start | bytes 393224 | tf_op jit(solution)/shard_map/ppermute | solution.py:430
  73.6 6.3 %collective-permute-start.11 = (f32[4,2,2,2,1024]{4,3,2,1,0:T(2,128)S(1)}, f32[4,2,2,2,1024]{4,3,2,1,0:T(2,128)S(1)}, u32[]{:S(2)}, u32[]{:S(2)}) collective-permute-start(f32[4,2,2,2,1024]{4,3,2,1,0:T(2,128)S(1)} %collective-permute-done.9.refs_3_), channel_id=1, source_target_pairs={{0,8},{8,16},{16,24},{24,28},{28,20},{20,12},{12,4},{4,0},{1,9},{9... | collective-permute-start | bytes 393224 | tf_op jit(solution)/shard_map/ppermute | solution.py:429
  79.6 5.0 %collective-permute-start.14 = (f32[4,2,2,2,1024]{4,3,2,1,0:T(2,128)S(1)}, f32[4,2,2,2,1024]{4,3,2,1,0:T(2,128)S(1)}, u32[]{:S(2)}, u32[]{:S(2)}) collective-permute-start(f32[4,2,2,2,1024]{4,3,2,1,0:T(2,128)S(1)} %collective-permute-done.12.refs_6_), channel_id=1, source_target_pairs={{8,0},{16,8},{24,16},{28,24},{20,28},{12,20},{4,12},{0,4},{9,1},{1... | collective-permute-start | bytes 393224 | tf_op jit(solution)/shard_map/ppermute | solution.py:430
  79.9 5.0 %collective-permute-start.13 = (f32[4,2,2,2,1024]{4,3,2,1,0:T(2,128)S(1)}, f32[4,2,2,2,1024]{4,3,2,1,0:T(2,128)S(1)}, u32[]{:S(2)}, u32[]{:S(2)}) collective-permute-start(f32[4,2,2,2,1024]{4,3,2,1,0:T(2,128)S(1)} %collective-permute-done.11.refs_5_), channel_id=1, source_target_pairs={{0,8},{8,16},{16,24},{24,28},{28,20},{20,12},{12,4},{4,0},{1,9},{9... | collective-permute-start | bytes 393224 | tf_op jit(solution)/shard_map/ppermute | solution.py:429
  84.5 4.3 %collective-permute-start.16 = (f32[2,2,2,2,1024]{4,3,2,1,0:T(2,128)S(1)}, f32[2,2,2,2,1024]{4,3,2,1,0:T(2,128)S(1)}, u32[]{:S(2)}, u32[]{:S(2)}) collective-permute-start(f32[2,2,2,2,1024]{4,3,2,1,0:T(2,128)S(1)} %slice.9), channel_id=1, source_target_pairs={{8,0},{16,8},{24,16},{28,24},{20,28},{12,20},{4,12},{0,4},{9,1},{1... | collective-permute-start | bytes 196616 | tf_op jit(solution)/shard_map/ppermute | solution.py:433
  84.8 4.3 %collective-permute-start.15 = (f32[2,2,2,2,1024]{4,3,2,1,0:T(2,128)S(1)}, f32[2,2,2,2,1024]{4,3,2,1,0:T(2,128)S(1)}, u32[]{:S(2)}, u32[]{:S(2)}) collective-permute-start(f32[2,2,2,2,1024]{4,3,2,1,0:T(2,128)S(1)} %slice.8), channel_id=1, source_target_pairs={{0,8},{8,16},{16,24},{24,28},{28,20},{20,12},{12,4},{4,0},{1,9},{9... | collective-permute-start | bytes 196616 | tf_op jit(solution)/shard_map/ppermute | solution.py:433

commit v3 on v2

--- a/solution.py
+++ b/solution.py
@@ -86,14 +86,14 @@
                     store(comp(part, i, j) * dirs + k, value[j : j + 1, :])
 
 
-def prepare_kernel(basis_ref, dual_ref, coeffs_ref, dual_out_ref, known_ref):
+def store_chunks(ref, row, value):
+    width = ref.shape[2]
+    for chunk in range(ref.shape[0]):
+        ref[chunk, row : row + value.shape[0], :] = value[:, chunk * width : (chunk + 1) * width]
+
+
+def prepare_kernel(basis_ref, dual_ref, coeffs_ref, known_ref, lag_ref):
     terms, dirs = coeffs_ref.shape[:2]
-
-    def put(ref):
-        def store(row, value):
-            ref[row : row + 1, :] = value
-
-        return store
 
     def known(k, part, i):
         total = coeffs_ref[0, k, part, i] * basis_ref[0, 0]
@@ -101,8 +101,11 @@
             total = total + coeffs_ref[m, k, part, i] * basis_ref[0, m]
         return RHO * total - dual_ref[k, part, i]
 
-    native_to_rows(lambda k, part, i: dual_ref[k, part, i], dirs, put(dual_out_ref))
-    native_to_rows(known, dirs, put(known_ref))
+    native_to_rows(known, dirs, lambda row, value: store_chunks(known_ref, row, value))
+    native_to_rows(
+        lambda k, part, i: dual_ref[k, part, i] * (1.0 / RHO), dirs,
+        lambda row, value: store_chunks(lag_ref, row, value),
+    )
 
 
 def model_body(parity_ref, jones, onehot_ref, coher_ref, gathered_ref, mine_ref, other_ref):
@@ -145,8 +148,7 @@
 
 
 def sums_kernel(
-    parity_ref, gathered_ref, pairs_ref, coher_ref, vis_ref, mine_ref, other_ref, right_ref, inverse_ref,
-    onehot_ref, left_ref,
+    parity_ref, gathered_ref, pairs_ref, coher_ref, vis_ref, mine_ref, other_ref, sums_ref, onehot_ref, left_ref
 ):
     dirs = coher_ref.shape[0]
     times, baselines = coher_ref.shape[-2:]
@@ -215,123 +217,111 @@
                 left_ref[at : at + dirs, :] = left_ref[at : at + dirs, :] + col[part]
 
     sums = split_dot(left_ref[...], onehot_ref[...], ((1,), (1,)))
-    right_ref[...] = sums[: 8 * dirs]
+    store_chunks(sums_ref, 0, sums[: 8 * dirs])
     m00 = sums[8 * dirs : 9 * dirs] + RHO
     m11 = sums[9 * dirs : 10 * dirs] + RHO
     m01 = (sums[10 * dirs : 11 * dirs], sums[11 * dirs : 12 * dirs])
     scale = 1.0 / (m00 * m11 - sq(m01))
-    inverse_ref[0:dirs, :] = m11 * scale
-    inverse_ref[dirs : 2 * dirs, :] = m00 * scale
-    inverse_ref[2 * dirs : 3 * dirs, :] = -m01[0] * scale
-    inverse_ref[3 * dirs :, :] = -m01[1] * scale
-
-
-def solve(right_ref, inverse_ref, known, dirs):
-    i00, i11, re01, im01 = (inverse_ref[at * dirs : (at + 1) * dirs, :] for at in range(4))
+    store_chunks(sums_ref, 8 * dirs, m11 * scale)
+    store_chunks(sums_ref, 9 * dirs, m00 * scale)
+    store_chunks(sums_ref, 10 * dirs, -m01[0] * scale)
+    store_chunks(sums_ref, 11 * dirs, -m01[1] * scale)
+
+
+def solve(sums, known, dirs):
+    i00, i11, re01, im01 = (sums(at * dirs) for at in range(8, 12))
     i01, i10 = (re01, im01), (re01, -im01)
     out = {}
     for i in range(2):
         n = []
         for j in range(2):
             at = [comp(part, i, j) * dirs for part in range(2)]
-            n.append(tuple(right_ref[a : a + dirs, :] + known(a) for a in at))
-        out[i, 0] = cadd((n[0][0] * i00, n[0][1] * i00), cmul(n[1], i10))
-        out[i, 1] = cadd(cmul(n[0], i01), (n[1][0] * i11, n[1][1] * i11))
+            n.append(tuple(sums(a) + known(a) for a in at))
+        left = cadd((n[0][0] * i00, n[0][1] * i00), cmul(n[1], i10))
+        right = cadd(cmul(n[0], i01), (n[1][0] * i11, n[1][1] * i11))
+        for part in range(2):
+            out[comp(part, i, 0) * dirs] = left[part]
+            out[comp(part, i, 1) * dirs] = right[part]
     return out
 
 
-def store_chunks(ref, a, value):
-    width = ref.shape[2]
-    for chunk in range(ref.shape[0]):
-        ref[chunk, a : a + value.shape[0], :] = value[:, chunk * width : (chunk + 1) * width]
-
-
-def store_shared(ref, a, value):
-    if len(ref.shape) == 3:
-        store_chunks(ref, a, value)
-    else:
-        ref[a : a + value.shape[0], :] = value
-
-
-def first_update_kernel(basis_ref, right_ref, inverse_ref, known_ref, dual_ref, jones_ref, shared_ref):
-    dirs = inverse_ref.shape[0] // 4
-    out = solve(right_ref, inverse_ref, lambda a: known_ref[a : a + dirs, :], dirs)
-    for (i, j), parts in out.items():
-        for part in range(2):
-            a = comp(part, i, j) * dirs
-            jones_ref[a : a + dirs, :] = parts[part]
-            store_shared(shared_ref, a, parts[part] + dual_ref[a : a + dirs, :] * (1.0 / RHO))
-    if len(shared_ref.shape) == 3:
-        rows, width = 8 * dirs, shared_ref.shape[2]
-        terms = basis_ref.shape[1]
-        for chunk in range(shared_ref.shape[0]):
-            shared_ref[chunk, rows:, :] = jnp.zeros((shared_ref.shape[1] - rows, width), jnp.float32)
-            shared_ref[chunk, rows : rows + 1, :terms] = basis_ref[...]
-
-
-def advance_dual(consensus_ref, dual_ref, before_ref, dual_out_ref, dirs):
-    def consensus(a):
-        if len(consensus_ref.shape) == 2:
-            return consensus_ref[a : a + dirs, :]
-        pieces = [consensus_ref[chunk, a : a + dirs, :] for chunk in range(consensus_ref.shape[0])]
-        return jnp.concatenate(pieces, axis=1)
-
-    known = {}
-    for a in range(0, 8 * dirs, dirs):
-        value = consensus(a)
-        dual = dual_ref[a : a + dirs, :] + RHO * (before_ref[a : a + dirs, :] - value)
-        dual_out_ref[a : a + dirs, :] = dual
-        known[a] = RHO * value - dual
-    return known
-
-
-def update_kernel(
-    right_ref, inverse_ref, consensus_ref, dual_ref, before_ref, jones_ref, shared_ref, dual_out_ref
-):
-    dirs = inverse_ref.shape[0] // 4
-    known = advance_dual(consensus_ref, dual_ref, before_ref, dual_out_ref, dirs)
-    out = solve(right_ref, inverse_ref, known.get, dirs)
-    for (i, j), parts in out.items():
-        for part in range(2):
-            a = comp(part, i, j) * dirs
-            jones_ref[a : a + dirs, :] = parts[part]
-            store_shared(shared_ref, a, parts[part] + dual_out_ref[a : a + dirs, :] * (1.0 / RHO))
-
-
-def last_update_kernel(
-    right_ref, inverse_ref, consensus_ref, dual_ref, before_ref, jones_ref, shared_ref, dual_out_ref, rows_ref
-):
-    dirs = inverse_ref.shape[0] // 4
-    known = advance_dual(consensus_ref, dual_ref, before_ref, rows_ref, dirs)
-    out = solve(right_ref, inverse_ref, known.get, dirs)
-    for (i, j), parts in out.items():
-        for part in range(2):
-            a = comp(part, i, j) * dirs
-            dual = rows_ref[a : a + dirs, :]
-            shared = parts[part] + dual * (1.0 / RHO)
+def first_update_kernel(basis_ref, sums_ref, known_ref, lag_ref, jones_ref, unit_ref):
+    dirs = sums_ref.shape[1] // 12
+    chunks, rows, width = known_ref.shape
+    terms = basis_ref.shape[1]
+    for chunk in range(chunks):
+        out = solve(
+            lambda a: sums_ref[chunk, a : a + dirs, :], lambda a: known_ref[chunk, a : a + dirs, :], dirs
+        )
+        for a, value in out.items():
+            jones_ref[a : a + dirs, chunk * width : (chunk + 1) * width] = value
+            at = chunk * rows + a
+            unit_ref[at : at + dirs, :] = value + lag_ref[chunk, a : a + dirs, :]
+    unit_ref[chunks * rows :, :] = jnp.zeros((SUBLANES, width), jnp.float32)
+    unit_ref[chunks * rows : chunks * rows + 1, :terms] = basis_ref[...]
+
+
+def solve_next(sums, consensus, before, dirs):
+    out = solve(sums, lambda a: RHO * (2.0 * consensus(a) - before(a)), dirs)
+    return out, {a: value + (before(a) - consensus(a)) for a, value in out.items()}
+
+
+def solve_chunk(chunk, sums_ref, consensus_ref, before_ref):
+    dirs = sums_ref.shape[1] // 12
+
+    def rows(ref):
+        return lambda a: ref[chunk, a : a + dirs, :]
+
+    return solve_next(rows(sums_ref), rows(consensus_ref), rows(before_ref), dirs)
+
+
+def update_kernel(sums_ref, consensus_ref, before_ref, jones_ref, shared_ref):
+    dirs, width = sums_ref.shape[1] // 12, sums_ref.shape[2]
+    for chunk in range(sums_ref.shape[0]):
+        jones, shared = solve_chunk(chunk, sums_ref, consensus_ref, before_ref)
+        for a in jones:
+            jones_ref[a : a + dirs, chunk * width : (chunk + 1) * width] = jones[a]
+            shared_ref[chunk, a : a + dirs, :] = shared[a]
+
+
+def store_native(chunk, width, dirs, rows, ref):
+    for part in range(2):
+        for i, j in INDEX:
+            value = rows[comp(part, i, j) * dirs]
             for k in range(dirs):
-                jones_ref[k, part, i, j : j + 1, :] = parts[part][k : k + 1, :]
-                shared_ref[k, part, i, j : j + 1, :] = shared[k : k + 1, :]
-                dual_out_ref[k, part, i, j : j + 1, :] = dual[k : k + 1, :]
-
-
-def mix(matrix, values):
-    out = []
-    for g in range(matrix.shape[0]):
-        total = None
-        for f, value in enumerate(values):
-            weight = jnp.broadcast_to(matrix[g : g + 1, f : f + 1], value.shape[-2:])
-            total = weight * value if total is None else total + weight * value
-        out.append(total)
-    return out
-
-
-def first_mix_kernel(place_ref, shared_ref, out_ref, spread_ref, weights_ref):
-    bands = shared_ref.shape[0]
-    rows = out_ref.shape[1]
+                ref[k, part, i, j : j + 1, chunk * width : (chunk + 1) * width] = value[k : k + 1, :]
+
+
+def last_update_kernel(sums_ref, consensus_ref, before_ref, jones_ref, shared_ref):
+    dirs, width = sums_ref.shape[1] // 12, sums_ref.shape[2]
+    for chunk in range(sums_ref.shape[0]):
+        jones, shared = solve_chunk(chunk, sums_ref, consensus_ref, before_ref)
+        store_native(chunk, width, dirs, jones, jones_ref)
+        store_native(chunk, width, dirs, shared, shared_ref)
+
+
+def weighted(matrix, g, values):
+    total = None
+    for f, value in enumerate(values):
+        weight = jnp.broadcast_to(matrix[g : g + 1, f : f + 1], value.shape[-2:])
+        total = weight * value if total is None else total + weight * value
+    return total
+
+
+def gathered_update_kernel(sums_ref, *refs):
+    units, (jones_ref, shared_ref, spread_ref, weights_ref) = refs[:-4], refs[-4:]
+    own, tail = units[0], units[-1]
+    dirs = sums_ref.shape[1] // 12
+    chunks, _, width = sums_ref.shape
+    rows = 8 * dirs
     terms = weights_ref.shape[0]
+    bands = len(units) - 1
     hi = lax.Precision.HIGHEST
-    basis = jnp.concatenate([shared_ref[f, rows : rows + 1, :terms] for f in range(bands)], axis=0)
+    at = chunks * rows
+    start = own.shape[0] - tail.shape[0]
+    basis = jnp.concatenate(
+        [ref[at : at + 1, :terms] for ref in units[:-2]] + [tail[at - start : at - start + 1, :terms]], axis=0
+    )
     gram = lax.dot_general(basis, basis, (((0,), (0,)), ((), ())), precision=hi, preferred_element_type=jnp.float32)
     row = lax.broadcasted_iota(jnp.int32, (terms, terms), 0)
     col = lax.broadcasted_iota(jnp.int32, (terms, terms), 1)
@@ -348,25 +338,42 @@
     weights = lax.dot_general(inverse, basis, (((1,), (1,)), ((), ())), precision=hi, preferred_element_type=jnp.float32)
     spread = jnp.dot(basis, weights, precision=hi, preferred_element_type=jnp.float32)
     spread_ref[...] = spread
-    for g, value in enumerate(mix(spread, [shared_ref[f, :rows, :] for f in range(bands)])):
-        out_ref[g] = value
-    band = lax.broadcasted_iota(jnp.int32, (bands, bands), 0)
-    slot = lax.broadcasted_iota(jnp.int32, (bands, bands), 1)
-    step = (slot + 1) // 2
-    spot = lax.rem(place_ref[0, 0] + jnp.where(slot % 2 == 1, -step, step) + 2 * bands, bands)
-    source = jnp.where(spot < bands // 2, 2 * spot, 2 * (bands - 1 - spot) + 1)
-    chosen = jnp.where(source == band, 1.0, 0.0)
-    weights_ref[...] = jnp.dot(weights, chosen, precision=hi, preferred_element_type=jnp.float32)
-
-
-def mix_kernel(spread_ref, shared_ref, out_ref):
-    for g, value in enumerate(mix(spread_ref[...], [shared_ref[f] for f in range(shared_ref.shape[0])])):
-        out_ref[g] = value
-
-
-def final_kernel(weights_ref, basis_ref, jones_ref, dual_ref, *refs):
-    shared_refs, (coeffs_ref, dual_out_ref) = refs[:-2], refs[-2:]
-    dirs = jones_ref.shape[0]
+    weights_ref[...] = weights
+    for chunk in range(chunks):
+        jones, shared = solve_gathered(chunk, spread, sums_ref, units, rows)
+        for a in jones:
+            jones_ref[a : a + dirs, chunk * width : (chunk + 1) * width] = jones[a]
+            shared_ref[chunk * rows + a : chunk * rows + a + dirs, :] = shared[a]
+
+
+def solve_gathered(chunk, spread, sums_ref, units, rows):
+    dirs = sums_ref.shape[1] // 12
+    head, tail = units[-2:]
+    base, start = chunk * rows, head.shape[0]
+    values = [ref[base : base + rows, :] for ref in units[:-2]]
+    values.append(head[base : base + rows, :] if base < start else tail[base - start : base - start + rows, :])
+    consensus = weighted(spread, 0, values)
+    return solve_next(
+        lambda a: sums_ref[chunk, a : a + dirs, :],
+        lambda a: consensus[a : a + dirs],
+        lambda a: values[0][a : a + dirs],
+        dirs,
+    )
+
+
+def gathered_last_kernel(spread_ref, sums_ref, *refs):
+    units, (jones_ref, shared_ref) = refs[:-2], refs[-2:]
+    dirs, width = sums_ref.shape[1] // 12, sums_ref.shape[2]
+    spread = spread_ref[...]
+    for chunk in range(sums_ref.shape[0]):
+        jones, shared = solve_gathered(chunk, spread, sums_ref, units, 8 * dirs)
+        store_native(chunk, width, dirs, jones, jones_ref)
+        store_native(chunk, width, dirs, shared, shared_ref)
+
+
+def final_kernel(weights_ref, basis_ref, *refs):
+    shared_refs, (coeffs_ref, dual_ref) = refs[:-2], refs[-2:]
+    dirs = dual_ref.shape[0]
     half = dirs // 2
     weights = weights_ref[...]
     for k in range(dirs):
@@ -375,11 +382,12 @@
                 values = [ref[k, part, i] for ref in shared_refs[:-2]]
                 values.append(shared_refs[-2][k, part, i] if k < half else shared_refs[-1][k - half, part, i])
                 consensus = None
-                for m, value in enumerate(mix(weights, values)):
+                for m in range(weights.shape[0]):
+                    value = weighted(weights, m, values)
                     coeffs_ref[m, k, part, i] = value
                     share = value * basis_ref[0, m]
                     consensus = share if consensus is None else consensus + share
-                dual_out_ref[k, part, i] = dual_ref[k, part, i] + RHO * (jones_ref[k, part, i] - consensus)
+                dual_ref[k, part, i] = RHO * (values[0] - consensus)
 
 
 def struct(*shape, dtype=jnp.float32):
@@ -413,12 +421,7 @@
     return mine, swap(mine, "dir", 1)
 
 
-def ring_place(size):
-    at = lax.axis_index("band")
-    return jnp.where(at % 2 == 0, at // 2, size - 1 - at // 2).astype(jnp.int32).reshape(1, 1)
-
-
-def ring_gather(value):
+def ring_gather(value, half):
     size = lax.axis_size("band")
     order = list(range(0, size, 2)) + list(range(size - 1, 0, -2))
     ahead = [(order[i], order[(i + 1) % size]) for i in range(size)]
@@ -429,7 +432,6 @@
         up = lax.ppermute(up, "band", ahead)
         down = lax.ppermute(down, "band", behind)
         values += [up, down]
-    half = value.shape[0] // 2
     return values + [lax.ppermute(up[:half], "band", ahead), lax.ppermute(down[half:], "band", behind)]
 
 
@@ -451,8 +453,11 @@
     parity = (lax.axis_index("dir") % 2).astype(jnp.int32).reshape(1, 1)
     chunked = stations % (bands * LANES) == 0 and bands % 2 == 0 and dirs % 2 == 0
     hi = lax.Precision.HIGHEST
+    width = stations // bands if chunked else LANES
+    chunks = stations // width
     half = struct(2, 2, times, baselines)
     flat = struct(rows, stations)
+    spread_rows = struct(chunks, rows, width)
     onehot = pltpu.VMEM((stations, 2 * baselines), jnp.bfloat16)
     left = pltpu.VMEM((12 * dirs, 2 * baselines), jnp.float32)
     in_rows = pltpu.VMEM((rows, stations), jnp.float32)
@@ -462,65 +467,59 @@
         gram = lax.psum(row[:, None] * row[None, :], "band") + RIDGE * bands * jnp.eye(terms, dtype=jnp.float32)
         factor = jnp.linalg.cholesky(gram)
 
-    jones = jones_start[0]
-    for turn in range(ITERS):
-        last = turn == ITERS - 1
-        gathered, mine, other = call(
-            model_kernel if turn else first_model_kernel, model_out, 1, (parity, jones, pairs, coher),
-            [onehot] if turn else [onehot, in_rows],
+    def model(jones, first=False):
+        return call(
+            first_model_kernel if first else model_kernel, model_out, 1, (parity, jones, pairs, coher),
+            [onehot, in_rows] if first else [onehot],
         )
-        if turn == 0:
-            dual, known = call(prepare_kernel, (flat, flat), 1, (freq_basis, dual_start[0], consensus_start))
+
+    def station_sums(gathered, mine, other):
         mine, other = sum_over_dir(mine, other)
-        right, inverse = call(
-            sums_kernel, (flat, struct(4 * dirs, stations)), 1,
+        return call(
+            sums_kernel, struct(chunks, 12 * dirs, width), 1,
             (parity, gathered, pairs, coher, vis, mine, other), [onehot, left],
         )
-        if turn == 0:
-            shape = struct(bands, rows + SUBLANES, stations // bands) if chunked else flat
-            jones, shared = call(
-                first_update_kernel, (flat, shape), 0, (freq_basis, right, inverse, known, dual)
-            )
-        elif not last:
-            shape = struct(bands, rows, stations // bands) if chunked else flat
-            jones, shared, dual = call(
-                update_kernel, (flat, shape, flat), 0, (right, inverse, consensus, dual, jones)
-            )
-        else:
-            jones, shared, dual = call(
-                last_update_kernel, (struct(*native),) * 3, 0, (right, inverse, consensus, dual, jones), [in_rows]
-            )
-            break
-        if chunked:
-            shared = lax.all_to_all(shared, "band", 0, 0)
-            mixed = struct(bands, rows, stations // bands)
-            if turn == 0:
-                mixed, spread, weights = call(
-                    first_mix_kernel, (mixed, struct(bands, bands), struct(terms, bands)), 1,
-                    (ring_place(bands), shared),
-                )
-            else:
-                mixed = call(mix_kernel, mixed, 0, (spread, shared))
-            consensus = lax.all_to_all(mixed, "band", 0, 0)
-        else:
-            coeffs = reduce_bands(shared, row, factor)
-            consensus = jnp.tensordot(row, coeffs, axes=(0, 0), precision=hi)
+
+    def share(shared):
+        coeffs = reduce_bands(shared, row, factor)
+        return coeffs, jnp.tensordot(row, coeffs, axes=(0, 0), precision=hi)
+
+    started = model(jones_start[0], True)
+    known, lag = call(prepare_kernel, (spread_rows,) * 2, 1, (freq_basis, dual_start[0], consensus_start))
+    jones, unit = call(
+        first_update_kernel, (flat, struct(stations * rows // width + SUBLANES, width)), 0,
+        (freq_basis, station_sums(*started), known, lag),
+    )
     if chunked:
-        values = ring_gather(shared)
-
-        def kernel(weights_ref, basis_ref, *refs):
-            final_kernel(weights_ref, basis_ref, *refs)
-
+        half_rows = chunks // 2 * rows
+        units = ring_gather(unit, half_rows)
+        sums = station_sums(*model(jones))
+        jones, unit, spread, weights = call(
+            gathered_update_kernel,
+            (flat, struct(chunks * rows, width), struct(bands, bands), struct(terms, bands)), 0, (sums, *units),
+        )
+        units = ring_gather(unit, half_rows)
+        sums = station_sums(*model(jones))
+        jones, shared = call(gathered_last_kernel, (struct(*native),) * 2, 0, (spread, sums, *units))
+        values = ring_gather(shared, dirs // 2)
         coeffs, dual = pl.pallas_call(
-            kernel,
+            final_kernel,
             out_shape=(struct(terms, *native), struct(*native)),
-            in_specs=[VMEM, SMEM] + [VMEM] * (2 + len(values)),
+            in_specs=[VMEM, SMEM] + [VMEM] * len(values),
             out_specs=(VMEM, VMEM),
             compiler_params=PARAMS,
-        )(weights, freq_basis, jones, dual, *values)
+        )(weights, freq_basis, *values)
     else:
-        coeffs = reduce_bands(shared, row, factor)
-        dual = dual + RHO * (jones - jnp.tensordot(row, coeffs, axes=(0, 0), precision=hi))
+        shared = unit[: chunks * rows].reshape(spread_rows.shape)
+        for _ in range(ITERS - 2):
+            consensus = share(shared)[1]
+            sums = station_sums(*model(jones))
+            jones, shared = call(update_kernel, (flat, spread_rows), 0, (sums, consensus, shared))
+        consensus = share(shared)[1]
+        sums = station_sums(*model(jones))
+        jones, shared = call(last_update_kernel, (struct(*native),) * 2, 0, (sums, consensus, shared))
+        coeffs, consensus = share(shared)
+        dual = RHO * (shared - consensus)
     return jones[None], dual[None], coeffs
 
 

time: 92 us -> 86 us (0.935)
  waiting for transfers between devices: 37.2 us -> 34 us
  Pallas kernels: 18.9 us -> 16.1 us
    all_to_all x4 -> x0, starting transfers between devices: 16.4 us -> none  [the longest x2 9.45 us: local(): shared = lax.all_to_all(shared, 'band', 0, 0)]
    ppermute x3 -> x9, starting transfers between devices: 0.5 us -> 14.7 us  [ring_gather(): down = lax.ppermute(down, 'band', behind)]
    all_to_all x4 -> x0, waiting for transfers between devices: 13.5 us -> none  [the longest x2 6.75 us: local(): consensus = lax.all_to_all(mixed, 'band', 0, 0)]
    ppermute x3 -> x9, waiting for transfers between devices: 10.5 us -> 21.6 us  [ring_gather(): down = lax.ppermute(down, 'band', behind)]
    ppermute x9, waiting for transfers between devices: 10.8 us -> 5.52 us  [swap(): return lax.ppermute(value, axis, [(i, i ^ bit) for i in range(size)])]
    ppermute x1 -> x3, starting transfers between devices: 0.28 us -> 4.84 us  [ring_gather(): lax.ppermute(down[half:], 'band', behind)]
    ppermute x1 -> x3, waiting for transfers between devices: 0.35 us -> 4.61 us  [ring_gather(): lax.ppermute(up[:half], 'band', ahead)]
    pallas_call x12 -> x10, Pallas kernels: 16.6 us -> 13.9 us  [call(): pl.pallas_call(kernel, out_shape=out_shape, in_specs=[SMEM if at < scalar...]
  transfers between devices with their start and end apart: 21 -> 33, of which waited for: 16 -> 17; matrix products, arithmetic and copies ran while one was open for 0% -> 0% of each run, Pallas kernels for 12% -> 9%
where the time goes in v3:
time: 86 us; the launch traced here: 85.8 us
  waiting for transfers between devices  34 us (40%)
  starting transfers between devices  31.8 us (37%)
  Pallas kernels  16.1 us (19%)
  local copies, waits for them, and re-layouts  2.86 us (3%)
  between operations  0.87 us (1%)
    ppermute x9, waiting for transfers between devices, ring_gather(): down = lax.ppermute(down, 'band', behind)  21.6 us
    ppermute x9, starting transfers between devices, ring_gather(): down = lax.ppermute(down, 'band', behind)  14.7 us
    pallas_call x10, Pallas kernels, call(): pl.pallas_call(kernel, out_shape=out_shape, in_specs=[SMEM if at < scalar...  13.9 us
    ppermute x9, starting transfers between devices, swap(): return lax.ppermute(value, axis, [(i, i ^ bit) for i in range(size)])  7.09 us
    ppermute x9, waiting for transfers between devices, swap(): return lax.ppermute(value, axis, [(i, i ^ bit) for i in range(size)])  5.52 us
    ppermute x3, starting transfers between devices, ring_gather(): lax.ppermute(down[half:], 'band', behind)  4.84 us
    ppermute x3, waiting for transfers between devices, ring_gather(): lax.ppermute(up[:half], 'band', ahead)  4.61 us
    ppermute x9, starting transfers between devices, ring_gather(): up = lax.ppermute(up, 'band', ahead)  3.64 us
  transfers between devices with their start and end apart: 33, of which 17 were waited for; matrix products, arithmetic and copies ran while one was open for 0% of the time, Pallas kernels for 9%

profile of v3, /device:TPU:0, one launch (start us, length us, event | category | flops | bytes accessed | tf_op | source)
XLA Modules:
  0.0 85.8 jit_solution(11964897434027860189)
XLA Ops:
  6.3 2.9 %collective-permute-start.1 = (f32[2,2,16,512]{3,2,1,0:T(8,128)S(1)}, f32[2,2,16,512]{3,2,1,0:T(8,128)S(1)}, u32[]{:S(2)}, u32[]{:S(2)}) collective-permute-start(f32[2,2,16,512]{3,2,1,0:T(8,128)S(1)} %add.23), channel_id=1, source_target_pairs={{0,2},{1,3},{2,0},{3,1},{4,6},{5,7},{6,4},{7,5},{8,10},{9,11},{10,... | collective-permute-start | bytes 393224 | tf_op jit(solution)/shard_map/ppermute | solution.py:411
  9.2 3.8 %collective-permute-done.1 = f32[2,2,16,512]{3,2,1,0:T(8,128)S(1)} collective-permute-done((f32[2,2,16,512]{3,2,1,0:T(8,128)S(1)}, f32[2,2,16,512]{3,2,1,0:T(8,128)S(1)}, u32[]{:S(2)}, u32[]{:S(2)}) %collective-permute-start.1) | collective-permute-done | bytes 131104 | tf_op jit(solution)/shard_map/ppermute | solution.py:411
  14.4 2.4 %shard_map.95.sums_ref = f32[8,48,128]{2,1,0:T(8,128)S(1)} custom-call(s32[1,1]{1,0:T(1,128)} %bitcast.parity_ref, f32[32,1024]{1,0:T(8,128)S(1)} %get-tuple-element.24.gathered_ref, s32[2,512]{1,0:T(2,128)S(1)} %copy-done.4, f32[4,2,2,2,16,512]{5,4,3,2,1,0:T(8,128)S(1)} %bitcast.8, f32[2,2,2,16,512]{4,3,2,1,0:T(8,128)S(1)} %bitcast.13, ...), custom_call_target="tpu_custom_call" | custom-call | tf_op jit(solution)/shard_map/pallas_call | solution.py:399
  16.9 1.8 %collective-permute-start.7 = (f32[264,128]{1,0:T(8,128)S(1)}, f32[264,128]{1,0:T(8,128)S(1)}, u32[]{:S(2)}, u32[]{:S(2)}) collective-permute-start(f32[264,128]{1,0:T(8,128)S(1)} %get-tuple-element.33.refs_0_), channel_id=1, source_target_pairs={{8,0},{16,8},{24,16},{28,24},{20,28},{12,20},{4,12},{0,4},{9,1},{1... | collective-permute-start | bytes 405512 | tf_op jit(solution)/shard_map/ppermute | solution.py:433
  20.3 2.4 %collective-permute-done.7.refs_2_ = f32[264,128]{1,0:T(8,128)S(1)} collective-permute-done((f32[264,128]{1,0:T(8,128)S(1)}, f32[264,128]{1,0:T(8,128)S(1)}, u32[]{:S(2)}, u32[]{:S(2)}) %collective-permute-start.7) | collective-permute-done | bytes 135200 | tf_op jit(solution)/shard_map/ppermute | solution.py:433
  22.6 1.7 %collective-permute-start.9 = (f32[264,128]{1,0:T(8,128)S(1)}, f32[264,128]{1,0:T(8,128)S(1)}, u32[]{:S(2)}, u32[]{:S(2)}) collective-permute-start(f32[264,128]{1,0:T(8,128)S(1)} %collective-permute-done.7.refs_2_), channel_id=1, source_target_pairs={{8,0},{16,8},{24,16},{28,24},{20,28},{12,20},{4,12},{0,4},{9,1},{1... | collective-permute-start | bytes 405512 | tf_op jit(solution)/shard_map/ppermute | solution.py:433
  24.7 1.7 %collective-permute-start.4 = (f32[2,2,16,512]{3,2,1,0:T(8,128)S(1)}, f32[2,2,16,512]{3,2,1,0:T(8,128)S(1)}, u32[]{:S(2)}, u32[]{:S(2)}) collective-permute-start(f32[2,2,16,512]{3,2,1,0:T(8,128)S(1)} %add.25), channel_id=1, source_target_pairs={{0,2},{1,3},{2,0},{3,1},{4,6},{5,7},{6,4},{7,5},{8,10},{9,11},{10,... | collective-permute-start | bytes 393224 | tf_op jit(solution)/shard_map/ppermute | solution.py:411
  27.7 1.7 %collective-permute-start.11 = (f32[264,128]{1,0:T(8,128)S(1)}, f32[264,128]{1,0:T(8,128)S(1)}, u32[]{:S(2)}, u32[]{:S(2)}) collective-permute-start(f32[264,128]{1,0:T(8,128)S(1)} %collective-permute-done.9.refs_4_), channel_id=1, source_target_pairs={{8,0},{16,8},{24,16},{28,24},{20,28},{12,20},{4,12},{0,4},{9,1},{1... | collective-permute-start | bytes 405512 | tf_op jit(solution)/shard_map/ppermute | solution.py:433
  29.8 2.8 %collective-permute-done.11.refs_6_ = f32[264,128]{1,0:T(8,128)S(1)} collective-permute-done((f32[264,128]{1,0:T(8,128)S(1)}, f32[264,128]{1,0:T(8,128)S(1)}, u32[]{:S(2)}, u32[]{:S(2)}) %collective-permute-start.11) | collective-permute-done | bytes 135200 | tf_op jit(solution)/shard_map/ppermute | solution.py:433
  32.7 1.7 %collective-permute-start.13 = (f32[136,128]{1,0:T(8,128)S(1)}, f32[136,128]{1,0:T(8,128)S(1)}, u32[]{:S(2)}, u32[]{:S(2)}) collective-permute-start(f32[136,128]{1,0:T(8,128)S(1)} %slice.25), channel_id=1, source_target_pairs={{8,0},{16,8},{24,16},{28,24},{20,28},{12,20},{4,12},{0,4},{9,1},{1... | collective-permute-start | bytes 208904 | tf_op jit(solution)/shard_map/ppermute | solution.py:435
  34.8 2.4 %shard_map.99.sums_ref = f32[8,48,128]{2,1,0:T(8,128)S(1)} custom-call(s32[1,1]{1,0:T(1,128)} %bitcast.parity_ref, f32[32,1024]{1,0:T(8,128)S(1)} %get-tuple-element.30.gathered_ref, s32[2,512]{1,0:T(2,128)S(1)} %copy-done.4, f32[4,2,2,2,16,512]{5,4,3,2,1,0:T(8,128)S(1)} %bitcast.10, f32[2,2,2,16,512]{4,3,2,1,0:T(8,128)S(1)} %bitcast.14, ...), custom_call_target="tpu_custom_call" | custom-call | tf_op jit(solution)/shard_map/pallas_call | solution.py:399
  37.1 1.5 %collective-permute-done.12.refs_7_ = f32[128,128]{1,0:T(8,128)S(1)} collective-permute-done((f32[128,128]{1,0:T(8,128)S(1)}, f32[128,128]{1,0:T(8,128)S(1)}, u32[]{:S(2)}, u32[]{:S(2)}) %collective-permute-start.12) | collective-permute-done | bytes 65568 | tf_op jit(solution)/shard_map/ppermute | solution.py:435
  38.7 1.4 %shard_map.100 = (f32[32,1024]{1,0:T(8,128)S(1)}, f32[256,128]{1,0:T(8,128)S(1)}, f32[8,8]{1,0:T(8,128)S(1)}, f32[8,8]{1,0:T(8,128)S(1)}) custom-call(f32[8,48,128]{2,1,0:T(8,128)S(1)} %shard_map.99.sums_ref, f32[264,128]{1,0:T(8,128)S(1)} %get-tuple-element.33.refs_0_, f32[264,128]{1,0:T(8,128)S(1)} %collective-permute-done.6.refs_1_, ...), custom_call_target="tpu_custom_call" | custom-call | tf_op jit(solution)/shard_map/pallas_call | solution.py:399
  40.1 1.6 %collective-permute-start.18 = (f32[256,128]{1,0:T(8,128)S(1)}, f32[256,128]{1,0:T(8,128)S(1)}, u32[]{:S(2)}, u32[]{:S(2)}) collective-permute-start(f32[256,128]{1,0:T(8,128)S(1)} %get-tuple-element.39.refs_0_), channel_id=1, source_target_pairs={{8,0},{16,8},{24,16},{28,24},{20,28},{12,20},{4,12},{0,4},{9,1},{1... | collective-permute-start | bytes 393224 | tf_op jit(solution)/shard_map/ppermute | solution.py:433
  43.4 1.6 %collective-permute-done.18.refs_2_ = f32[256,128]{1,0:T(8,128)S(1)} collective-permute-done((f32[256,128]{1,0:T(8,128)S(1)}, f32[256,128]{1,0:T(8,128)S(1)}, u32[]{:S(2)}, u32[]{:S(2)}) %collective-permute-start.18) | collective-permute-done | bytes 131104 | tf_op jit(solution)/shard_map/ppermute | solution.py:433
  45.1 1.6 %collective-permute-start.20 = (f32[256,128]{1,0:T(8,128)S(1)}, f32[256,128]{1,0:T(8,128)S(1)}, u32[]{:S(2)}, u32[]{:S(2)}) collective-permute-start(f32[256,128]{1,0:T(8,128)S(1)} %collective-permute-done.18.refs_2_), channel_id=1, source_target_pairs={{8,0},{16,8},{24,16},{28,24},{20,28},{12,20},{4,12},{0,4},{9,1},{1... | collective-permute-start | bytes 393224 | tf_op jit(solution)/shard_map/ppermute | solution.py:433
  47.1 1.6 %collective-permute-start.15 = (f32[2,2,16,512]{3,2,1,0:T(8,128)S(1)}, f32[2,2,16,512]{3,2,1,0:T(8,128)S(1)}, u32[]{:S(2)}, u32[]{:S(2)}) collective-permute-start(f32[2,2,16,512]{3,2,1,0:T(8,128)S(1)} %add.27), channel_id=1, source_target_pairs={{0,2},{1,3},{2,0},{3,1},{4,6},{5,7},{6,4},{7,5},{8,10},{9,11},{10,... | collective-permute-start | bytes 393224 | tf_op jit(solution)/shard_map/ppermute | solution.py:411
  50.1 1.6 %collective-permute-start.22 = (f32[256,128]{1,0:T(8,128)S(1)}, f32[256,128]{1,0:T(8,128)S(1)}, u32[]{:S(2)}, u32[]{:S(2)}) collective-permute-start(f32[256,128]{1,0:T(8,128)S(1)} %collective-permute-done.20.refs_4_), channel_id=1, source_target_pairs={{8,0},{16,8},{24,16},{28,24},{20,28},{12,20},{4,12},{0,4},{9,1},{1... | collective-permute-start | bytes 393224 | tf_op jit(solution)/shard_map/ppermute | solution.py:433
  52.3 2.7 %collective-permute-done.22.refs_6_ = f32[256,128]{1,0:T(8,128)S(1)} collective-permute-done((f32[256,128]{1,0:T(8,128)S(1)}, f32[256,128]{1,0:T(8,128)S(1)}, u32[]{:S(2)}, u32[]{:S(2)}) %collective-permute-start.22) | collective-permute-done | bytes 131104 | tf_op jit(solution)/shard_map/ppermute | solution.py:433
  55.0 1.6 %collective-permute-start.24 = (f32[128,128]{1,0:T(8,128)S(1)}, f32[128,128]{1,0:T(8,128)S(1)}, u32[]{:S(2)}, u32[]{:S(2)}) collective-permute-start(f32[128,128]{1,0:T(8,128)S(1)} %slice.27), channel_id=1, source_target_pairs={{8,0},{16,8},{24,16},{28,24},{20,28},{12,20},{4,12},{0,4},{9,1},{1... | collective-permute-start | bytes 196616 | tf_op jit(solution)/shard_map/ppermute | solution.py:435
  57.3 2.4 %shard_map.102.sums_ref = f32[8,48,128]{2,1,0:T(8,128)S(1)} custom-call(s32[1,1]{1,0:T(1,128)} %bitcast.parity_ref, f32[32,1024]{1,0:T(8,128)S(1)} %get-tuple-element.36.gathered_ref, s32[2,512]{1,0:T(2,128)S(1)} %copy-done.4, f32[4,2,2,2,16,512]{5,4,3,2,1,0:T(8,128)S(1)} %bitcast.12, f32[2,2,2,16,512]{4,3,2,1,0:T(8,128)S(1)} %bitcast.15, ...), custom_call_target="tpu_custom_call" | custom-call | tf_op jit(solution)/shard_map/pallas_call | solution.py:399
  59.7 1.4 %collective-permute-done.23.refs_7_ = f32[128,128]{1,0:T(8,128)S(1)} collective-permute-done((f32[128,128]{1,0:T(8,128)S(1)}, f32[128,128]{1,0:T(8,128)S(1)}, u32[]{:S(2)}, u32[]{:S(2)}) %collective-permute-start.23) | collective-permute-done | bytes 65568 | tf_op jit(solution)/shard_map/ppermute | solution.py:435
  62.1 1.6 %collective-permute-start.26 = (f32[4,2,2,2,1024]{4,3,2,1,0:T(2,128)S(1)}, f32[4,2,2,2,1024]{4,3,2,1,0:T(2,128)S(1)}, u32[]{:S(2)}, u32[]{:S(2)}) collective-permute-start(f32[4,2,2,2,1024]{4,3,2,1,0:T(2,128)S(1)} %get-tuple-element.42.refs_0_), channel_id=1, source_target_pairs={{8,0},{16,8},{24,16},{28,24},{20,28},{12,20},{4,12},{0,4},{9,1},{1... | collective-permute-start | bytes 393224 | tf_op jit(solution)/shard_map/ppermute | solution.py:433
  64.1 3.6 %collective-permute-done.26.refs_2_ = f32[4,2,2,2,1024]{4,3,2,1,0:T(2,128)S(1)} collective-permute-done((f32[4,2,2,2,1024]{4,3,2,1,0:T(2,128)S(1)}, f32[4,2,2,2,1024]{4,3,2,1,0:T(2,128)S(1)}, u32[]{:S(2)}, u32[]{:S(2)}) %collective-permute-start.26) | collective-permute-done | bytes 131104 | tf_op jit(solution)/shard_map/ppermute | solution.py:433
  67.7 1.6 %collective-permute-start.28 = (f32[4,2,2,2,1024]{4,3,2,1,0:T(2,128)S(1)}, f32[4,2,2,2,1024]{4,3,2,1,0:T(2,128)S(1)}, u32[]{:S(2)}, u32[]{:S(2)}) collective-permute-start(f32[4,2,2,2,1024]{4,3,2,1,0:T(2,128)S(1)} %collective-permute-done.26.refs_2_), channel_id=1, source_target_pairs={{8,0},{16,8},{24,16},{28,24},{20,28},{12,20},{4,12},{0,4},{9,1},{1... | collective-permute-start | bytes 393224 | tf_op jit(solution)/shard_map/ppermute | solution.py:433
  69.7 2.9 %collective-permute-done.28.refs_4_ = f32[4,2,2,2,1024]{4,3,2,1,0:T(2,128)S(1)} collective-permute-done((f32[4,2,2,2,1024]{4,3,2,1,0:T(2,128)S(1)}, f32[4,2,2,2,1024]{4,3,2,1,0:T(2,128)S(1)}, u32[]{:S(2)}, u32[]{:S(2)}) %collective-permute-start.28) | collective-permute-done | bytes 131104 | tf_op jit(solution)/shard_map/ppermute | solution.py:433
  72.7 1.6 %collective-permute-start.30 = (f32[4,2,2,2,1024]{4,3,2,1,0:T(2,128)S(1)}, f32[4,2,2,2,1024]{4,3,2,1,0:T(2,128)S(1)}, u32[]{:S(2)}, u32[]{:S(2)}) collective-permute-start(f32[4,2,2,2,1024]{4,3,2,1,0:T(2,128)S(1)} %collective-permute-done.28.refs_4_), channel_id=1, source_target_pairs={{8,0},{16,8},{24,16},{28,24},{20,28},{12,20},{4,12},{0,4},{9,1},{1... | collective-permute-start | bytes 393224 | tf_op jit(solution)/shard_map/ppermute | solution.py:433
  74.7 2.9 %collective-permute-done.30.refs_6_ = f32[4,2,2,2,1024]{4,3,2,1,0:T(2,128)S(1)} collective-permute-done((f32[4,2,2,2,1024]{4,3,2,1,0:T(2,128)S(1)}, f32[4,2,2,2,1024]{4,3,2,1,0:T(2,128)S(1)}, u32[]{:S(2)}, u32[]{:S(2)}) %collective-permute-start.30) | collective-permute-done | bytes 131104 | tf_op jit(solution)/shard_map/ppermute | solution.py:433
  77.7 1.6 %collective-permute-start.32 = (f32[2,2,2,2,1024]{4,3,2,1,0:T(2,128)S(1)}, f32[2,2,2,2,1024]{4,3,2,1,0:T(2,128)S(1)}, u32[]{:S(2)}, u32[]{:S(2)}) collective-permute-start(f32[2,2,2,2,1024]{4,3,2,1,0:T(2,128)S(1)} %slice.29), channel_id=1, source_target_pairs={{8,0},{16,8},{24,16},{28,24},{20,28},{12,20},{4,12},{0,4},{9,1},{1... | collective-permute-start | bytes 196616 | tf_op jit(solution)/shard_map/ppermute | solution.py:435
  79.7 2.2 %collective-permute-done.32.refs_8_ = f32[2,2,2,2,1024]{4,3,2,1,0:T(2,128)S(1)} collective-permute-done((f32[2,2,2,2,1024]{4,3,2,1,0:T(2,128)S(1)}, f32[2,2,2,2,1024]{4,3,2,1,0:T(2,128)S(1)}, u32[]{:S(2)}, u32[]{:S(2)}) %collective-permute-start.32) | collective-permute-done | bytes 65568 | tf_op jit(solution)/shard_map/ppermute | solution.py:435
  81.9 1.6 %collective-permute-done.31.refs_7_ = f32[2,2,2,2,1024]{4,3,2,1,0:T(2,128)S(1)} collective-permute-done((f32[2,2,2,2,1024]{4,3,2,1,0:T(2,128)S(1)}, f32[2,2,2,2,1024]{4,3,2,1,0:T(2,128)S(1)}, u32[]{:S(2)}, u32[]{:S(2)}) %collective-permute-start.31) | collective-permute-done | bytes 65568 | tf_op jit(solution)/shard_map/ppermute | solution.py:435
  83.6 2.2 %shard_map.104 = (f32[8,4,2,2,2,1024]{5,4,3,2,1,0:T(2,128)}, f32[4,2,2,2,1024]{4,3,2,1,0:T(2,128)}) custom-call(f32[8,8]{1,0:T(8,128)S(1)} %get-tuple-element.41.weights_ref, f32[1,8]{1,0:T(1,128)S(1)} %copy-done.7, f32[4,2,2,2,1024]{4,3,2,1,0:T(2,128)S(1)} %get-tuple-element.42.refs_0_, f32[4,2,2,2,1024]{4,3,2,1,0:T(2,128)S(1)} %collective-permute-done.25.refs_1_, ...), custom_call_target="tpu_custom_call" | custom-call | tf_op jit(solution)/shard_map/pallas_call | solution.py:505
  (73 shorter events, 18.9 us)
Async XLA Ops:
  4.7 1.5 %collective-permute-start = (f32[2,2,16,512]{3,2,1,0:T(8,128)S(1)}, f32[2,2,16,512]{3,2,1,0:T(8,128)S(1)}, u32[]{:S(2)}, u32[]{:S(2)}) collective-permute-start(f32[2,2,16,512]{3,2,1,0:T(8,128)S(1)} %get-tuple-element.26), channel_id=1, source_target_pairs={{0,1},{1,0},{2,3},{3,2},{4,5},{5,4},{6,7},{7,6},{8,9},{9,8},{10,11... | collective-permute-start | bytes 393224 | tf_op jit(solution)/shard_map/ppermute | solution.py:411
  6.3 6.7 %collective-permute-start.1 = (f32[2,2,16,512]{3,2,1,0:T(8,128)S(1)}, f32[2,2,16,512]{3,2,1,0:T(8,128)S(1)}, u32[]{:S(2)}, u32[]{:S(2)}) collective-permute-start(f32[2,2,16,512]{3,2,1,0:T(8,128)S(1)} %add.23), channel_id=1, source_target_pairs={{0,2},{1,3},{2,0},{3,1},{4,6},{5,7},{6,4},{7,5},{8,10},{9,11},{10,... | collective-permute-start | bytes 393224 | tf_op jit(solution)/shard_map/ppermute | solution.py:411
  16.9 5.8 %collective-permute-start.7 = (f32[264,128]{1,0:T(8,128)S(1)}, f32[264,128]{1,0:T(8,128)S(1)}, u32[]{:S(2)}, u32[]{:S(2)}) collective-permute-start(f32[264,128]{1,0:T(8,128)S(1)} %get-tuple-element.33.refs_0_), channel_id=1, source_target_pairs={{8,0},{16,8},{24,16},{28,24},{20,28},{12,20},{4,12},{0,4},{9,1},{1... | collective-permute-start | bytes 405512 | tf_op jit(solution)/shard_map/ppermute | solution.py:433
  18.7 5.6 %collective-permute-start.6 = (f32[264,128]{1,0:T(8,128)S(1)}, f32[264,128]{1,0:T(8,128)S(1)}, u32[]{:S(2)}, u32[]{:S(2)}) collective-permute-start(f32[264,128]{1,0:T(8,128)S(1)} %get-tuple-element.33.refs_0_), channel_id=1, source_target_pairs={{0,8},{8,16},{16,24},{24,28},{28,20},{20,12},{12,4},{4,0},{1,9},{9... | collective-permute-start | bytes 405512 | tf_op jit(solution)/shard_map/ppermute | solution.py:432
  20.2 4.5 %collective-permute-start.3 = (f32[2,2,16,512]{3,2,1,0:T(8,128)S(1)}, f32[2,2,16,512]{3,2,1,0:T(8,128)S(1)}, u32[]{:S(2)}, u32[]{:S(2)}) collective-permute-start(f32[2,2,16,512]{3,2,1,0:T(8,128)S(1)} %get-tuple-element.32), channel_id=1, source_target_pairs={{0,1},{1,0},{2,3},{3,2},{4,5},{5,4},{6,7},{7,6},{8,9},{9,8},{10,11... | collective-permute-start | bytes 393224 | tf_op jit(solution)/shard_map/ppermute | solution.py:411
  22.6 5.0 %collective-permute-start.9 = (f32[264,128]{1,0:T(8,128)S(1)}, f32[264,128]{1,0:T(8,128)S(1)}, u32[]{:S(2)}, u32[]{:S(2)}) collective-permute-start(f32[264,128]{1,0:T(8,128)S(1)} %collective-permute-done.7.refs_2_), channel_id=1, source_target_pairs={{8,0},{16,8},{24,16},{28,24},{20,28},{12,20},{4,12},{0,4},{9,1},{1... | collective-permute-start | bytes 405512 | tf_op jit(solution)/shard_map/ppermute | solution.py:433
  24.3 5.0 %collective-permute-start.8 = (f32[264,128]{1,0:T(8,128)S(1)}, f32[264,128]{1,0:T(8,128)S(1)}, u32[]{:S(2)}, u32[]{:S(2)}) collective-permute-start(f32[264,128]{1,0:T(8,128)S(1)} %collective-permute-done.6.refs_1_), channel_id=1, source_target_pairs={{0,8},{8,16},{16,24},{24,28},{28,20},{20,12},{12,4},{4,0},{1,9},{9... | collective-permute-start | bytes 405512 | tf_op jit(solution)/shard_map/ppermute | solution.py:432
  24.7 5.0 %collective-permute-start.4 = (f32[2,2,16,512]{3,2,1,0:T(8,128)S(1)}, f32[2,2,16,512]{3,2,1,0:T(8,128)S(1)}, u32[]{:S(2)}, u32[]{:S(2)}) collective-permute-start(f32[2,2,16,512]{3,2,1,0:T(8,128)S(1)} %add.25), channel_id=1, source_target_pairs={{0,2},{1,3},{2,0},{3,1},{4,6},{5,7},{6,4},{7,5},{8,10},{9,11},{10,... | collective-permute-start | bytes 393224 | tf_op jit(solution)/shard_map/ppermute | solution.py:411
  27.7 5.0 %collective-permute-start.11 = (f32[264,128]{1,0:T(8,128)S(1)}, f32[264,128]{1,0:T(8,128)S(1)}, u32[]{:S(2)}, u32[]{:S(2)}) collective-permute-start(f32[264,128]{1,0:T(8,128)S(1)} %collective-permute-done.9.refs_4_), channel_id=1, source_target_pairs={{8,0},{16,8},{24,16},{28,24},{20,28},{12,20},{4,12},{0,4},{9,1},{1... | collective-permute-start | bytes 405512 | tf_op jit(solution)/shard_map/ppermute | solution.py:433
  29.3 5.0 %collective-permute-start.10 = (f32[264,128]{1,0:T(8,128)S(1)}, f32[264,128]{1,0:T(8,128)S(1)}, u32[]{:S(2)}, u32[]{:S(2)}) collective-permute-start(f32[264,128]{1,0:T(8,128)S(1)} %collective-permute-done.8.refs_3_), channel_id=1, source_target_pairs={{0,8},{8,16},{16,24},{24,28},{28,20},{20,12},{12,4},{4,0},{1,9},{9... | collective-permute-start | bytes 405512 | tf_op jit(solution)/shard_map/ppermute | solution.py:432
  29.8 5.0 %collective-permute-start.5 = (f32[2,2,16,512]{3,2,1,0:T(8,128)S(1)}, f32[2,2,16,512]{3,2,1,0:T(8,128)S(1)}, u32[]{:S(2)}, u32[]{:S(2)}) collective-permute-start(f32[2,2,16,512]{3,2,1,0:T(8,128)S(1)} %add.26.mine_ref), channel_id=1, source_target_pairs={{0,1},{1,0},{2,3},{3,2},{4,5},{5,4},{6,7},{7,6},{8,9},{9,8},{10,11... | collective-permute-start | bytes 393224 | tf_op jit(solution)/shard_map/ppermute | solution.py:411
  32.7 6.0 %collective-permute-start.13 = (f32[136,128]{1,0:T(8,128)S(1)}, f32[136,128]{1,0:T(8,128)S(1)}, u32[]{:S(2)}, u32[]{:S(2)}) collective-permute-start(f32[136,128]{1,0:T(8,128)S(1)} %slice.25), channel_id=1, source_target_pairs={{8,0},{16,8},{24,16},{28,24},{20,28},{12,20},{4,12},{0,4},{9,1},{1... | collective-permute-start | bytes 208904 | tf_op jit(solution)/shard_map/ppermute | solution.py:435
  34.4 4.3 %collective-permute-start.12 = (f32[128,128]{1,0:T(8,128)S(1)}, f32[128,128]{1,0:T(8,128)S(1)}, u32[]{:S(2)}, u32[]{:S(2)}) collective-permute-start(f32[128,128]{1,0:T(8,128)S(1)} %slice.24), channel_id=1, source_target_pairs={{0,8},{8,16},{16,24},{24,28},{28,20},{20,12},{12,4},{4,0},{1,9},{9... | collective-permute-start | bytes 196616 | tf_op jit(solution)/shard_map/ppermute | solution.py:435
  40.1 5.0 %collective-permute-start.18 = (f32[256,128]{1,0:T(8,128)S(1)}, f32[256,128]{1,0:T(8,128)S(1)}, u32[]{:S(2)}, u32[]{:S(2)}) collective-permute-start(f32[256,128]{1,0:T(8,128)S(1)} %get-tuple-element.39.refs_0_), channel_id=1, source_target_pairs={{8,0},{16,8},{24,16},{28,24},{20,28},{12,20},{4,12},{0,4},{9,1},{1... | collective-permute-start | bytes 393224 | tf_op jit(solution)/shard_map/ppermute | solution.py:433
  41.7 5.0 %collective-permute-start.17 = (f32[256,128]{1,0:T(8,128)S(1)}, f32[256,128]{1,0:T(8,128)S(1)}, u32[]{:S(2)}, u32[]{:S(2)}) collective-permute-start(f32[256,128]{1,0:T(8,128)S(1)} %get-tuple-element.39.refs_0_), channel_id=1, source_target_pairs={{0,8},{8,16},{16,24},{24,28},{28,20},{20,12},{12,4},{4,0},{1,9},{9... | collective-permute-start | bytes 393224 | tf_op jit(solution)/shard_map/ppermute | solution.py:432
  43.4 3.8 %collective-permute-start.14 = (f32[2,2,16,512]{3,2,1,0:T(8,128)S(1)}, f32[2,2,16,512]{3,2,1,0:T(8,128)S(1)}, u32[]{:S(2)}, u32[]{:S(2)}) collective-permute-start(f32[2,2,16,512]{3,2,1,0:T(8,128)S(1)} %get-tuple-element.38), channel_id=1, source_target_pairs={{0,1},{1,0},{2,3},{3,2},{4,5},{5,4},{6,7},{7,6},{8,9},{9,8},{10,11... | collective-permute-start | bytes 393224 | tf_op jit(solution)/shard_map/ppermute | solution.py:411
  45.1 5.0 %collective-permute-start.20 = (f32[256,128]{1,0:T(8,128)S(1)}, f32[256,128]{1,0:T(8,128)S(1)}, u32[]{:S(2)}, u32[]{:S(2)}) collective-permute-start(f32[256,128]{1,0:T(8,128)S(1)} %collective-permute-done.18.refs_2_), channel_id=1, source_target_pairs={{8,0},{16,8},{24,16},{28,24},{20,28},{12,20},{4,12},{0,4},{9,1},{1... | collective-permute-start | bytes 393224 | tf_op jit(solution)/shard_map/ppermute | solution.py:433
  46.7 5.0 %collective-permute-start.19 = (f32[256,128]{1,0:T(8,128)S(1)}, f32[256,128]{1,0:T(8,128)S(1)}, u32[]{:S(2)}, u32[]{:S(2)}) collective-permute-start(f32[256,128]{1,0:T(8,128)S(1)} %collective-permute-done.17.refs_1_), channel_id=1, source_target_pairs={{0,8},{8,16},{16,24},{24,28},{28,20},{20,12},{12,4},{4,0},{1,9},{9... | collective-permute-start | bytes 393224 | tf_op jit(solution)/shard_map/ppermute | solution.py:432
  47.1 5.0 %collective-permute-start.15 = (f32[2,2,16,512]{3,2,1,0:T(8,128)S(1)}, f32[2,2,16,512]{3,2,1,0:T(8,128)S(1)}, u32[]{:S(2)}, u32[]{:S(2)}) collective-permute-start(f32[2,2,16,512]{3,2,1,0:T(8,128)S(1)} %add.27), channel_id=1, source_target_pairs={{0,2},{1,3},{2,0},{3,1},{4,6},{5,7},{6,4},{7,5},{8,10},{9,11},{10,... | collective-permute-start | bytes 393224 | tf_op jit(solution)/shard_map/ppermute | solution.py:411
  50.1 5.0 %collective-permute-start.22 = (f32[256,128]{1,0:T(8,128)S(1)}, f32[256,128]{1,0:T(8,128)S(1)}, u32[]{:S(2)}, u32[]{:S(2)}) collective-permute-start(f32[256,128]{1,0:T(8,128)S(1)} %collective-permute-done.20.refs_4_), channel_id=1, source_target_pairs={{8,0},{16,8},{24,16},{28,24},{20,28},{12,20},{4,12},{0,4},{9,1},{1... | collective-permute-start | bytes 393224 | tf_op jit(solution)/shard_map/ppermute | solution.py:433
  51.6 5.0 %collective-permute-start.21 = (f32[256,128]{1,0:T(8,128)S(1)}, f32[256,128]{1,0:T(8,128)S(1)}, u32[]{:S(2)}, u32[]{:S(2)}) collective-permute-start(f32[256,128]{1,0:T(8,128)S(1)} %collective-permute-done.19.refs_3_), channel_id=1, source_target_pairs={{0,8},{8,16},{16,24},{24,28},{28,20},{20,12},{12,4},{4,0},{1,9},{9... | collective-permute-start | bytes 393224 | tf_op jit(solution)/shard_map/ppermute | solution.py:432
  52.2 5.1 %collective-permute-start.16 = (f32[2,2,16,512]{3,2,1,0:T(8,128)S(1)}, f32[2,2,16,512]{3,2,1,0:T(8,128)S(1)}, u32[]{:S(2)}, u32[]{:S(2)}) collective-permute-start(f32[2,2,16,512]{3,2,1,0:T(8,128)S(1)} %add.28.mine_ref), channel_id=1, source_target_pairs={{0,1},{1,0},{2,3},{3,2},{4,5},{5,4},{6,7},{7,6},{8,9},{9,8},{10,11... | collective-permute-start | bytes 393224 | tf_op jit(solution)/shard_map/ppermute | solution.py:411
  55.0 4.7 %collective-permute-start.24 = (f32[128,128]{1,0:T(8,128)S(1)}, f32[128,128]{1,0:T(8,128)S(1)}, u32[]{:S(2)}, u32[]{:S(2)}) collective-permute-start(f32[128,128]{1,0:T(8,128)S(1)} %slice.27), channel_id=1, source_target_pairs={{8,0},{16,8},{24,16},{28,24},{20,28},{12,20},{4,12},{0,4},{9,1},{1... | collective-permute-start | bytes 196616 | tf_op jit(solution)/shard_map/ppermute | solution.py:435
  56.6 4.5 %collective-permute-start.23 = (f32[128,128]{1,0:T(8,128)S(1)}, f32[128,128]{1,0:T(8,128)S(1)}, u32[]{:S(2)}, u32[]{:S(2)}) collective-permute-start(f32[128,128]{1,0:T(8,128)S(1)} %slice.26), channel_id=1, source_target_pairs={{0,8},{8,16},{16,24},{24,28},{28,20},{20,12},{12,4},{4,0},{1,9},{9... | collective-permute-start | bytes 196616 | tf_op jit(solution)/shard_map/ppermute | solution.py:435
  62.1 5.6 %collective-permute-start.26 = (f32[4,2,2,2,1024]{4,3,2,1,0:T(2,128)S(1)}, f32[4,2,2,2,1024]{4,3,2,1,0:T(2,128)S(1)}, u32[]{:S(2)}, u32[]{:S(2)}) collective-permute-start(f32[4,2,2,2,1024]{4,3,2,1,0:T(2,128)S(1)} %get-tuple-element.42.refs_0_), channel_id=1, source_target_pairs={{8,0},{16,8},{24,16},{28,24},{20,28},{12,20},{4,12},{0,4},{9,1},{1... | collective-permute-start | bytes 393224 | tf_op jit(solution)/shard_map/ppermute | solution.py:433
  63.7 5.6 %collective-permute-start.25 = (f32[4,2,2,2,1024]{4,3,2,1,0:T(2,128)S(1)}, f32[4,2,2,2,1024]{4,3,2,1,0:T(2,128)S(1)}, u32[]{:S(2)}, u32[]{:S(2)}) collective-permute-start(f32[4,2,2,2,1024]{4,3,2,1,0:T(2,128)S(1)} %get-tuple-element.42.refs_0_), channel_id=1, source_target_pairs={{0,8},{8,16},{16,24},{24,28},{28,20},{20,12},{12,4},{4,0},{1,9},{9... | collective-permute-start | bytes 393224 | tf_op jit(solution)/shard_map/ppermute | solution.py:432
  67.7 5.0 %collective-permute-start.28 = (f32[4,2,2,2,1024]{4,3,2,1,0:T(2,128)S(1)}, f32[4,2,2,2,1024]{4,3,2,1,0:T(2,128)S(1)}, u32[]{:S(2)}, u32[]{:S(2)}) collective-permute-start(f32[4,2,2,2,1024]{4,3,2,1,0:T(2,128)S(1)} %collective-permute-done.26.refs_2_), channel_id=1, source_target_pairs={{8,0},{16,8},{24,16},{28,24},{20,28},{12,20},{4,12},{0,4},{9,1},{1... | collective-permute-start | bytes 393224 | tf_op jit(solution)/shard_map/ppermute | solution.py:433
  69.3 5.0 %collective-permute-start.27 = (f32[4,2,2,2,1024]{4,3,2,1,0:T(2,128)S(1)}, f32[4,2,2,2,1024]{4,3,2,1,0:T(2,128)S(1)}, u32[]{:S(2)}, u32[]{:S(2)}) collective-permute-start(f32[4,2,2,2,1024]{4,3,2,1,0:T(2,128)S(1)} %collective-permute-done.25.refs_1_), channel_id=1, source_target_pairs={{0,8},{8,16},{16,24},{24,28},{28,20},{20,12},{12,4},{4,0},{1,9},{9... | collective-permute-start | bytes 393224 | tf_op jit(solution)/shard_map/ppermute | solution.py:432
  72.7 5.0 %collective-permute-start.30 = (f32[4,2,2,2,1024]{4,3,2,1,0:T(2,128)S(1)}, f32[4,2,2,2,1024]{4,3,2,1,0:T(2,128)S(1)}, u32[]{:S(2)}, u32[]{:S(2)}) collective-permute-start(f32[4,2,2,2,1024]{4,3,2,1,0:T(2,128)S(1)} %collective-permute-done.28.refs_4_), channel_id=1, source_target_pairs={{8,0},{16,8},{24,16},{28,24},{20,28},{12,20},{4,12},{0,4},{9,1},{1... | collective-permute-start | bytes 393224 | tf_op jit(solution)/shard_map/ppermute | solution.py:433
  74.3 5.0 %collective-permute-start.29 = (f32[4,2,2,2,1024]{4,3,2,1,0:T(2,128)S(1)}, f32[4,2,2,2,1024]{4,3,2,1,0:T(2,128)S(1)}, u32[]{:S(2)}, u32[]{:S(2)}) collective-permute-start(f32[4,2,2,2,1024]{4,3,2,1,0:T(2,128)S(1)} %collective-permute-done.27.refs_3_), channel_id=1, source_target_pairs={{0,8},{8,16},{16,24},{24,28},{28,20},{20,12},{12,4},{4,0},{1,9},{9... | collective-permute-start | bytes 393224 | tf_op jit(solution)/shard_map/ppermute | solution.py:432
  77.7 4.3 %collective-permute-start.32 = (f32[2,2,2,2,1024]{4,3,2,1,0:T(2,128)S(1)}, f32[2,2,2,2,1024]{4,3,2,1,0:T(2,128)S(1)}, u32[]{:S(2)}, u32[]{:S(2)}) collective-permute-start(f32[2,2,2,2,1024]{4,3,2,1,0:T(2,128)S(1)} %slice.29), channel_id=1, source_target_pairs={{8,0},{16,8},{24,16},{28,24},{20,28},{12,20},{4,12},{0,4},{9,1},{1... | collective-permute-start | bytes 196616 | tf_op jit(solution)/shard_map/ppermute | solution.py:435
  79.2 4.3 %collective-permute-start.31 = (f32[2,2,2,2,1024]{4,3,2,1,0:T(2,128)S(1)}, f32[2,2,2,2,1024]{4,3,2,1,0:T(2,128)S(1)}, u32[]{:S(2)}, u32[]{:S(2)}) collective-permute-start(f32[2,2,2,2,1024]{4,3,2,1,0:T(2,128)S(1)} %slice.28), channel_id=1, source_target_pairs={{0,8},{8,16},{16,24},{24,28},{28,20},{20,12},{12,4},{4,0},{1,9},{9... | collective-permute-start | bytes 196616 | tf_op jit(solution)/shard_map/ppermute | solution.py:435
  (9 other events, 44.2 us)

commit v4 on v3

--- a/solution.py
+++ b/solution.py
@@ -13,6 +13,7 @@
 
 VMEM = pl.BlockSpec(memory_space=pltpu.VMEM)
 SMEM = pl.BlockSpec(memory_space=pltpu.SMEM)
+HBM = pl.BlockSpec(memory_space=pltpu.HBM)
 PARAMS = pltpu.CompilerParams(vmem_limit_bytes=16 * 1024 * 1024)
 
 INDEX = ((0, 0), (0, 1), (1, 0), (1, 1))
@@ -131,14 +132,26 @@
 
 
 def first_model_kernel(
-    parity_ref, jones_ref, pairs_ref, coher_ref, gathered_ref, mine_ref, other_ref, onehot_ref, rows_ref
+    parity_ref, jones_hbm, pairs_hbm, coher_hbm, gathered_ref, mine_ref, other_ref,
+    onehot_ref, rows_ref, jones_ref, pairs_ref, coher_ref, sems,
 ):
+    copies = [
+        pltpu.make_async_copy(source, target, sems.at[at])
+        for at, (source, target) in enumerate(
+            ((pairs_hbm, pairs_ref), (jones_hbm, jones_ref), (coher_hbm, coher_ref))
+        )
+    ]
+    for copy in copies:
+        copy.start()
+    copies[0].wait()
     fill_onehot(pairs_ref, onehot_ref)
+    copies[1].wait()
 
     def store(row, value):
         rows_ref[row : row + 1, :] = value
 
     native_to_rows(lambda k, part, i: jones_ref[k, part, i], coher_ref.shape[0], store)
+    copies[2].wait()
     model_body(parity_ref, rows_ref[...], onehot_ref, coher_ref, gathered_ref, mine_ref, other_ref)
 
 
@@ -361,46 +374,92 @@
     )
 
 
-def gathered_last_kernel(spread_ref, sums_ref, *refs):
-    units, (jones_ref, shared_ref) = refs[:-2], refs[-2:]
+def partial_consensus_kernel(spread_ref, *refs):
+    units, out_ref = refs[:-1], refs[-1]
+    rows = out_ref.shape[0]
+    spread = spread_ref[...]
+    step = 4 * SUBLANES
+    for base in range(0, rows, step):
+        out_ref[base : base + step, :] = weighted(spread, 0, [ref[base : base + step, :] for ref in units])
+
+
+def gathered_last_kernel(spread_ref, sums_ref, own_ref, partial_ref, head_ref, tail_ref, jones_ref, shared_ref):
     dirs, width = sums_ref.shape[1] // 12, sums_ref.shape[2]
-    spread = spread_ref[...]
+    rows = 8 * dirs
+    bands = spread_ref.shape[0]
+    start = head_ref.shape[0]
+    last = spread_ref[0:1, bands - 1 : bands]
     for chunk in range(sums_ref.shape[0]):
-        jones, shared = solve_gathered(chunk, spread, sums_ref, units, 8 * dirs)
-        store_native(chunk, width, dirs, jones, jones_ref)
+        base = chunk * rows
+        far = head_ref[base : base + rows, :] if base < start else tail_ref[base - start : base - start + rows, :]
+        consensus = partial_ref[base : base + rows, :] + jnp.broadcast_to(last, far.shape) * far
+        jones, shared = solve_next(
+            lambda a: sums_ref[chunk, a : a + dirs, :],
+            lambda a: consensus[a : a + dirs],
+            lambda a: own_ref[base + a : base + a + dirs, :],
+            dirs,
+        )
+        for a in jones:
+            jones_ref[a : a + dirs, chunk * width : (chunk + 1) * width] = jones[a]
         store_native(chunk, width, dirs, shared, shared_ref)
 
 
-def final_kernel(weights_ref, basis_ref, *refs):
-    shared_refs, (coeffs_ref, dual_ref) = refs[:-2], refs[-2:]
-    dirs = dual_ref.shape[0]
-    half = dirs // 2
+def native_kernel(rows_ref, out_ref):
+    dirs = out_ref.shape[0]
+    rows = {a: rows_ref[a : a + dirs, :] for a in range(0, 8 * dirs, dirs)}
+    store_native(0, rows_ref.shape[1], dirs, rows, out_ref)
+
+
+def partial_coeffs_kernel(weights_ref, *refs):
+    units, out_ref = refs[:-1], refs[-1]
     weights = weights_ref[...]
+    for k in range(out_ref.shape[1]):
+        for part in range(2):
+            for i in range(2):
+                values = [ref[k, part, i] for ref in units]
+                for m in range(weights.shape[0]):
+                    out_ref[m, k, part, i] = weighted(weights, m, values)
+
+
+def final_kernel(
+    basis_ref, weights_ref, own_ref, partial_ref, head_ref, tail_ref, coeffs_hbm, dual_hbm, coeffs_ref, dual_ref, sems
+):
+    terms, dirs = coeffs_ref.shape[:2]
+    half = head_ref.shape[0]
+    weights = weights_ref[...]
+    far = weights.shape[1] - 1
+    copies = []
     for k in range(dirs):
         for part in range(2):
             for i in range(2):
-                values = [ref[k, part, i] for ref in shared_refs[:-2]]
-                values.append(shared_refs[-2][k, part, i] if k < half else shared_refs[-1][k - half, part, i])
+                value = head_ref[k, part, i] if k < half else tail_ref[k - half, part, i]
                 consensus = None
-                for m in range(weights.shape[0]):
-                    value = weighted(weights, m, values)
-                    coeffs_ref[m, k, part, i] = value
-                    share = value * basis_ref[0, m]
+                for m in range(terms):
+                    weight = jnp.broadcast_to(weights[m : m + 1, far:], value.shape)
+                    total = partial_ref[m, k, part, i] + weight * value
+                    coeffs_ref[m, k, part, i] = total
+                    share = total * basis_ref[0, m]
                     consensus = share if consensus is None else consensus + share
-                dual_ref[k, part, i] = RHO * (values[0] - consensus)
+                dual_ref[k, part, i] = RHO * (own_ref[k, part, i] - consensus)
+        copies.append(pltpu.make_async_copy(coeffs_ref.at[:, k], coeffs_hbm.at[:, k], sems.at[k]))
+        copies[-1].start()
+    copies.append(pltpu.make_async_copy(dual_ref, dual_hbm, sems.at[dirs]))
+    copies[-1].start()
+    for copy in copies:
+        copy.wait()
 
 
 def struct(*shape, dtype=jnp.float32):
     return jax.ShapeDtypeStruct(shape, dtype)
 
 
-def call(kernel, out_shape, scalars, args, scratch=()):
+def call(kernel, out_shape, scalars, args, scratch=(), space=VMEM, out_space=VMEM):
     many = isinstance(out_shape, (tuple, list))
     return pl.pallas_call(
         kernel,
         out_shape=out_shape,
-        in_specs=[SMEM if at < scalars else VMEM for at in range(len(args))],
-        out_specs=tuple(VMEM for _ in out_shape) if many else VMEM,
+        in_specs=[SMEM if at < scalars else space for at in range(len(args))],
+        out_specs=tuple(out_space for _ in out_shape) if many else out_space,
         scratch_shapes=list(scratch),
         compiler_params=PARAMS,
     )(*args)
@@ -460,18 +519,14 @@
     spread_rows = struct(chunks, rows, width)
     onehot = pltpu.VMEM((stations, 2 * baselines), jnp.bfloat16)
     left = pltpu.VMEM((12 * dirs, 2 * baselines), jnp.float32)
-    in_rows = pltpu.VMEM((rows, stations), jnp.float32)
     model_out = (struct(rows, 2 * baselines), half, half)
 
     if not chunked:
         gram = lax.psum(row[:, None] * row[None, :], "band") + RIDGE * bands * jnp.eye(terms, dtype=jnp.float32)
         factor = jnp.linalg.cholesky(gram)
 
-    def model(jones, first=False):
-        return call(
-            first_model_kernel if first else model_kernel, model_out, 1, (parity, jones, pairs, coher),
-            [onehot, in_rows] if first else [onehot],
-        )
+    def model(jones):
+        return call(model_kernel, model_out, 1, (parity, jones, pairs, coher), [onehot])
 
     def station_sums(gathered, mine, other):
         mine, other = sum_over_dir(mine, other)
@@ -484,7 +539,19 @@
         coeffs = reduce_bands(shared, row, factor)
         return coeffs, jnp.tensordot(row, coeffs, axes=(0, 0), precision=hi)
 
-    started = model(jones_start[0], True)
+    started = call(
+        first_model_kernel, model_out, 1,
+        (parity, *(pltpu.with_memory_space_constraint(x, pltpu.HBM) for x in (jones_start[0], pairs, coher))),
+        [
+            onehot,
+            pltpu.VMEM((rows, stations), jnp.float32),
+            pltpu.VMEM(native, jnp.float32),
+            pltpu.VMEM(pairs.shape, pairs.dtype),
+            pltpu.VMEM(coher.shape, jnp.float32),
+            pltpu.SemaphoreType.DMA((3,)),
+        ],
+        HBM,
+    )
     known, lag = call(prepare_kernel, (spread_rows,) * 2, 1, (freq_basis, dual_start[0], consensus_start))
     jones, unit = call(
         first_update_kernel, (flat, struct(stations * rows // width + SUBLANES, width)), 0,
@@ -500,15 +567,23 @@
         )
         units = ring_gather(unit, half_rows)
         sums = station_sums(*model(jones))
-        jones, shared = call(gathered_last_kernel, (struct(*native),) * 2, 0, (spread, sums, *units))
-        values = ring_gather(shared, dirs // 2)
-        coeffs, dual = pl.pallas_call(
-            final_kernel,
-            out_shape=(struct(terms, *native), struct(*native)),
-            in_specs=[VMEM, SMEM] + [VMEM] * len(values),
-            out_specs=(VMEM, VMEM),
-            compiler_params=PARAMS,
-        )(weights, freq_basis, *values)
+        partial = call(partial_consensus_kernel, struct(chunks * rows, width), 0, (spread, *units[:-2]))
+        jones, shared = call(
+            gathered_last_kernel, (flat, struct(*native)), 0, (spread, sums, unit, partial, *units[-2:])
+        )
+        jones = call(native_kernel, struct(*native), 0, (jones,))
+        units = ring_gather(shared, dirs // 2)
+        partial = call(partial_coeffs_kernel, struct(terms, *native), 0, (weights, *units[:-2]))
+        coeffs, dual = call(
+            final_kernel, (struct(terms, *native), struct(*native)), 1,
+            (freq_basis, weights, shared, partial, *units[-2:]),
+            [
+                pltpu.VMEM((terms, *native), jnp.float32),
+                pltpu.VMEM(native, jnp.float32),
+                pltpu.SemaphoreType.DMA((dirs + 1,)),
+            ],
+            out_space=HBM,
+        )
     else:
         shared = unit[: chunks * rows].reshape(spread_rows.shape)
         for _ in range(ITERS - 2):

time: 86 us -> 83.6 us (0.972)
  local copies, waits for them, and re-layouts: 2.86 us -> 0.06 us
  Pallas kernels: 16.1 us -> 17.8 us
  waiting for transfers between devices: 34 us -> 32.5 us
    pallas_call x10 -> x14, Pallas kernels: 13.9 us -> 17.8 us  [call(): pl.pallas_call(kernel, out_shape=out_shape, in_specs=[SMEM if at < scalar...]
    unnamed x16 -> x12, local copies, waits for them, and re-layouts: 2.83 us -> 0.03 us
    pallas_call x1 -> x0, Pallas kernels: 2.23 us -> none  [local(): pl.pallas_call(final_kernel, out_shape=(struct(terms, *native), struct(*n...]
    ppermute x3, waiting for transfers between devices: 2.18 us -> 0.88 us  [ring_gather(): lax.ppermute(down[half:], 'band', behind)]
  transfers between devices with their start and end apart: 33 -> 33, of which waited for: 17 -> 17; matrix products, arithmetic and copies ran while one was open for 0% -> 0% of each run, Pallas kernels for 9% -> 11%
where the time goes in v4:
time: 83.6 us; the launch traced here: 83.4 us
  waiting for transfers between devices  32.5 us (39%)
  starting transfers between devices  31.9 us (38%)
  Pallas kernels  17.8 us (21%)
  between operations  1.08 us (1%)
    ppermute x9, waiting for transfers between devices, ring_gather(): down = lax.ppermute(down, 'band', behind)  21.6 us
    pallas_call x14, Pallas kernels, call(): pl.pallas_call(kernel, out_shape=out_shape, in_specs=[SMEM if at < scalar...  17.8 us
    ppermute x9, starting transfers between devices, ring_gather(): down = lax.ppermute(down, 'band', behind)  14.8 us
    ppermute x9, starting transfers between devices, swap(): return lax.ppermute(value, axis, [(i, i ^ bit) for i in range(size)])  7.09 us
    ppermute x9, waiting for transfers between devices, swap(): return lax.ppermute(value, axis, [(i, i ^ bit) for i in range(size)])  5.5 us
    ppermute x3, starting transfers between devices, ring_gather(): lax.ppermute(down[half:], 'band', behind)  4.84 us
    ppermute x3, waiting for transfers between devices, ring_gather(): lax.ppermute(up[:half], 'band', ahead)  4.44 us
    ppermute x9, starting transfers between devices, ring_gather(): up = lax.ppermute(up, 'band', ahead)  3.64 us
  transfers between devices with their start and end apart: 33, of which 17 were waited for; matrix products, arithmetic and copies ran while one was open for 0% of the time, Pallas kernels for 11%

profile of v4, /device:TPU:0, one launch (start us, length us, event | category | flops | bytes accessed | tf_op | source)
XLA Modules:
  0.0 83.4 jit_solution(1291241162853940613)
XLA Ops:
  0.7 2.6 %shard_map.94 = (f32[32,1024]{1,0:T(8,128)S(1)}, f32[2,2,16,512]{3,2,1,0:T(8,128)S(1)}, f32[2,2,16,512]{3,2,1,0:T(8,128)S(1)}) custom-call(s32[1,1]{1,0:T(1,128)} %bitcast.parity_ref, f32[4,2,2,2,1024]{4,3,2,1,0:T(2,128)} %bitcast.17, s32[2,512]{1,0:T(2,128)} %pairs_ref.9, f32[4,2,2,2,16,512]{5,4,3,2,1,0:T(8,128)} %bitcast.7), custom_call_target="tpu_custom_call" | custom-call | tf_op jit(solution)/shard_map/pallas_call | solution.py:458
  4.9 2.9 %collective-permute-start.1 = (f32[2,2,16,512]{3,2,1,0:T(8,128)S(1)}, f32[2,2,16,512]{3,2,1,0:T(8,128)S(1)}, u32[]{:S(2)}, u32[]{:S(2)}) collective-permute-start(f32[2,2,16,512]{3,2,1,0:T(8,128)S(1)} %add.23), channel_id=1, source_target_pairs={{0,2},{1,3},{2,0},{3,1},{4,6},{5,7},{6,4},{7,5},{8,10},{9,11},{10,... | collective-permute-start | bytes 393224 | tf_op jit(solution)/shard_map/ppermute | solution.py:470
  7.8 3.8 %collective-permute-done.1 = f32[2,2,16,512]{3,2,1,0:T(8,128)S(1)} collective-permute-done((f32[2,2,16,512]{3,2,1,0:T(8,128)S(1)}, f32[2,2,16,512]{3,2,1,0:T(8,128)S(1)}, u32[]{:S(2)}, u32[]{:S(2)}) %collective-permute-start.1) | collective-permute-done | bytes 131104 | tf_op jit(solution)/shard_map/ppermute | solution.py:470
  13.0 2.4 %shard_map.95.sums_ref = f32[8,48,128]{2,1,0:T(8,128)S(1)} custom-call(s32[1,1]{1,0:T(1,128)} %bitcast.parity_ref, f32[32,1024]{1,0:T(8,128)S(1)} %get-tuple-element.24.gathered_ref, s32[2,512]{1,0:T(2,128)S(1)} %copy-done.3, f32[4,2,2,2,16,512]{5,4,3,2,1,0:T(8,128)S(1)} %bitcast.8, f32[2,2,2,16,512]{4,3,2,1,0:T(8,128)S(1)} %bitcast.13, ...), custom_call_target="tpu_custom_call" | custom-call | tf_op jit(solution)/shard_map/pallas_call | solution.py:458
  15.5 1.8 %collective-permute-start.7 = (f32[264,128]{1,0:T(8,128)S(1)}, f32[264,128]{1,0:T(8,128)S(1)}, u32[]{:S(2)}, u32[]{:S(2)}) collective-permute-start(f32[264,128]{1,0:T(8,128)S(1)} %get-tuple-element.33.refs_0_), channel_id=1, source_target_pairs={{8,0},{16,8},{24,16},{28,24},{20,28},{12,20},{4,12},{0,4},{9,1},{1... | collective-permute-start | bytes 405512 | tf_op jit(solution)/shard_map/ppermute | solution.py:492
  18.9 2.4 %collective-permute-done.7.refs_2_ = f32[264,128]{1,0:T(8,128)S(1)} collective-permute-done((f32[264,128]{1,0:T(8,128)S(1)}, f32[264,128]{1,0:T(8,128)S(1)}, u32[]{:S(2)}, u32[]{:S(2)}) %collective-permute-start.7) | collective-permute-done | bytes 135200 | tf_op jit(solution)/shard_map/ppermute | solution.py:492
  21.3 1.7 %collective-permute-start.9 = (f32[264,128]{1,0:T(8,128)S(1)}, f32[264,128]{1,0:T(8,128)S(1)}, u32[]{:S(2)}, u32[]{:S(2)}) collective-permute-start(f32[264,128]{1,0:T(8,128)S(1)} %collective-permute-done.7.refs_2_), channel_id=1, source_target_pairs={{8,0},{16,8},{24,16},{28,24},{20,28},{12,20},{4,12},{0,4},{9,1},{1... | collective-permute-start | bytes 405512 | tf_op jit(solution)/shard_map/ppermute | solution.py:492
  23.3 1.7 %collective-permute-start.4 = (f32[2,2,16,512]{3,2,1,0:T(8,128)S(1)}, f32[2,2,16,512]{3,2,1,0:T(8,128)S(1)}, u32[]{:S(2)}, u32[]{:S(2)}) collective-permute-start(f32[2,2,16,512]{3,2,1,0:T(8,128)S(1)} %add.25), channel_id=1, source_target_pairs={{0,2},{1,3},{2,0},{3,1},{4,6},{5,7},{6,4},{7,5},{8,10},{9,11},{10,... | collective-permute-start | bytes 393224 | tf_op jit(solution)/shard_map/ppermute | solution.py:470
  26.3 1.7 %collective-permute-start.11 = (f32[264,128]{1,0:T(8,128)S(1)}, f32[264,128]{1,0:T(8,128)S(1)}, u32[]{:S(2)}, u32[]{:S(2)}) collective-permute-start(f32[264,128]{1,0:T(8,128)S(1)} %collective-permute-done.9.refs_4_), channel_id=1, source_target_pairs={{8,0},{16,8},{24,16},{28,24},{20,28},{12,20},{4,12},{0,4},{9,1},{1... | collective-permute-start | bytes 405512 | tf_op jit(solution)/shard_map/ppermute | solution.py:492
  28.5 2.8 %collective-permute-done.11.refs_6_ = f32[264,128]{1,0:T(8,128)S(1)} collective-permute-done((f32[264,128]{1,0:T(8,128)S(1)}, f32[264,128]{1,0:T(8,128)S(1)}, u32[]{:S(2)}, u32[]{:S(2)}) %collective-permute-start.11) | collective-permute-done | bytes 135200 | tf_op jit(solution)/shard_map/ppermute | solution.py:492
  31.3 1.7 %collective-permute-start.13 = (f32[136,128]{1,0:T(8,128)S(1)}, f32[136,128]{1,0:T(8,128)S(1)}, u32[]{:S(2)}, u32[]{:S(2)}) collective-permute-start(f32[136,128]{1,0:T(8,128)S(1)} %slice.25), channel_id=1, source_target_pairs={{8,0},{16,8},{24,16},{28,24},{20,28},{12,20},{4,12},{0,4},{9,1},{1... | collective-permute-start | bytes 208904 | tf_op jit(solution)/shard_map/ppermute | solution.py:494
  33.4 2.4 %shard_map.99.sums_ref = f32[8,48,128]{2,1,0:T(8,128)S(1)} custom-call(s32[1,1]{1,0:T(1,128)} %bitcast.parity_ref, f32[32,1024]{1,0:T(8,128)S(1)} %get-tuple-element.30.gathered_ref, s32[2,512]{1,0:T(2,128)S(1)} %copy-done.3, f32[4,2,2,2,16,512]{5,4,3,2,1,0:T(8,128)S(1)} %bitcast.10, f32[2,2,2,16,512]{4,3,2,1,0:T(8,128)S(1)} %bitcast.14, ...), custom_call_target="tpu_custom_call" | custom-call | tf_op jit(solution)/shard_map/pallas_call | solution.py:458
  35.8 1.5 %collective-permute-done.12.refs_7_ = f32[128,128]{1,0:T(8,128)S(1)} collective-permute-done((f32[128,128]{1,0:T(8,128)S(1)}, f32[128,128]{1,0:T(8,128)S(1)}, u32[]{:S(2)}, u32[]{:S(2)}) %collective-permute-start.12) | collective-permute-done | bytes 65568 | tf_op jit(solution)/shard_map/ppermute | solution.py:494
  37.3 1.4 %shard_map.100 = (f32[32,1024]{1,0:T(8,128)S(1)}, f32[256,128]{1,0:T(8,128)S(1)}, f32[8,8]{1,0:T(8,128)S(1)}, f32[8,8]{1,0:T(8,128)S(1)}) custom-call(f32[8,48,128]{2,1,0:T(8,128)S(1)} %shard_map.99.sums_ref, f32[264,128]{1,0:T(8,128)S(1)} %get-tuple-element.33.refs_0_, f32[264,128]{1,0:T(8,128)S(1)} %collective-permute-done.6.refs_1_, ...), custom_call_target="tpu_custom_call" | custom-call | tf_op jit(solution)/shard_map/pallas_call | solution.py:458
  38.7 1.6 %collective-permute-start.18 = (f32[256,128]{1,0:T(8,128)S(1)}, f32[256,128]{1,0:T(8,128)S(1)}, u32[]{:S(2)}, u32[]{:S(2)}) collective-permute-start(f32[256,128]{1,0:T(8,128)S(1)} %get-tuple-element.39.refs_0_.own_ref), channel_id=1, source_target_pairs={{8,0},{16,8},{24,16},{28,24},{20,28},{12,20},{4,12},{0,4},{9,1},{1... | collective-permute-start | bytes 393224 | tf_op jit(solution)/shard_map/ppermute | solution.py:492
  42.1 1.6 %collective-permute-done.18.refs_2_ = f32[256,128]{1,0:T(8,128)S(1)} collective-permute-done((f32[256,128]{1,0:T(8,128)S(1)}, f32[256,128]{1,0:T(8,128)S(1)}, u32[]{:S(2)}, u32[]{:S(2)}) %collective-permute-start.18) | collective-permute-done | bytes 131104 | tf_op jit(solution)/shard_map/ppermute | solution.py:492
  43.7 1.6 %collective-permute-start.20 = (f32[256,128]{1,0:T(8,128)S(1)}, f32[256,128]{1,0:T(8,128)S(1)}, u32[]{:S(2)}, u32[]{:S(2)}) collective-permute-start(f32[256,128]{1,0:T(8,128)S(1)} %collective-permute-done.18.refs_2_), channel_id=1, source_target_pairs={{8,0},{16,8},{24,16},{28,24},{20,28},{12,20},{4,12},{0,4},{9,1},{1... | collective-permute-start | bytes 393224 | tf_op jit(solution)/shard_map/ppermute | solution.py:492
  45.8 1.6 %collective-permute-start.15 = (f32[2,2,16,512]{3,2,1,0:T(8,128)S(1)}, f32[2,2,16,512]{3,2,1,0:T(8,128)S(1)}, u32[]{:S(2)}, u32[]{:S(2)}) collective-permute-start(f32[2,2,16,512]{3,2,1,0:T(8,128)S(1)} %add.27), channel_id=1, source_target_pairs={{0,2},{1,3},{2,0},{3,1},{4,6},{5,7},{6,4},{7,5},{8,10},{9,11},{10,... | collective-permute-start | bytes 393224 | tf_op jit(solution)/shard_map/ppermute | solution.py:470
  47.3 1.4 %collective-permute-done.20.refs_4_ = f32[256,128]{1,0:T(8,128)S(1)} collective-permute-done((f32[256,128]{1,0:T(8,128)S(1)}, f32[256,128]{1,0:T(8,128)S(1)}, u32[]{:S(2)}, u32[]{:S(2)}) %collective-permute-start.20) | collective-permute-done | bytes 131104 | tf_op jit(solution)/shard_map/ppermute | solution.py:492
  48.7 1.6 %collective-permute-start.22 = (f32[256,128]{1,0:T(8,128)S(1)}, f32[256,128]{1,0:T(8,128)S(1)}, u32[]{:S(2)}, u32[]{:S(2)}) collective-permute-start(f32[256,128]{1,0:T(8,128)S(1)} %collective-permute-done.20.refs_4_), channel_id=1, source_target_pairs={{8,0},{16,8},{24,16},{28,24},{20,28},{12,20},{4,12},{0,4},{9,1},{1... | collective-permute-start | bytes 393224 | tf_op jit(solution)/shard_map/ppermute | solution.py:492
  50.9 2.7 %collective-permute-done.22.refs_6_ = f32[256,128]{1,0:T(8,128)S(1)} collective-permute-done((f32[256,128]{1,0:T(8,128)S(1)}, f32[256,128]{1,0:T(8,128)S(1)}, u32[]{:S(2)}, u32[]{:S(2)}) %collective-permute-start.22) | collective-permute-done | bytes 131104 | tf_op jit(solution)/shard_map/ppermute | solution.py:492
  53.7 1.6 %collective-permute-start.24 = (f32[128,128]{1,0:T(8,128)S(1)}, f32[128,128]{1,0:T(8,128)S(1)}, u32[]{:S(2)}, u32[]{:S(2)}) collective-permute-start(f32[128,128]{1,0:T(8,128)S(1)} %slice.27), channel_id=1, source_target_pairs={{8,0},{16,8},{24,16},{28,24},{20,28},{12,20},{4,12},{0,4},{9,1},{1... | collective-permute-start | bytes 196616 | tf_op jit(solution)/shard_map/ppermute | solution.py:494
  56.1 2.4 %shard_map.102.sums_ref = f32[8,48,128]{2,1,0:T(8,128)S(1)} custom-call(s32[1,1]{1,0:T(1,128)} %bitcast.parity_ref, f32[32,1024]{1,0:T(8,128)S(1)} %get-tuple-element.36.gathered_ref, s32[2,512]{1,0:T(2,128)S(1)} %copy-done.3, f32[4,2,2,2,16,512]{5,4,3,2,1,0:T(8,128)S(1)} %bitcast.12, f32[2,2,2,16,512]{4,3,2,1,0:T(8,128)S(1)} %bitcast.15, ...), custom_call_target="tpu_custom_call" | custom-call | tf_op jit(solution)/shard_map/pallas_call | solution.py:458
  60.0 1.6 %collective-permute-start.26 = (f32[4,2,2,2,1024]{4,3,2,1,0:T(2,128)S(1)}, f32[4,2,2,2,1024]{4,3,2,1,0:T(2,128)S(1)}, u32[]{:S(2)}, u32[]{:S(2)}) collective-permute-start(f32[4,2,2,2,1024]{4,3,2,1,0:T(2,128)S(1)} %get-tuple-element.42.refs_0_.own_ref), channel_id=1, source_target_pairs={{8,0},{16,8},{24,16},{28,24},{20,28},{12,20},{4,12},{0,4},{9,1},{1... | collective-permute-start | bytes 393224 | tf_op jit(solution)/shard_map/ppermute | solution.py:492
  62.1 3.6 %collective-permute-done.26.refs_2_ = f32[4,2,2,2,1024]{4,3,2,1,0:T(2,128)S(1)} collective-permute-done((f32[4,2,2,2,1024]{4,3,2,1,0:T(2,128)S(1)}, f32[4,2,2,2,1024]{4,3,2,1,0:T(2,128)S(1)}, u32[]{:S(2)}, u32[]{:S(2)}) %collective-permute-start.26) | collective-permute-done | bytes 131104 | tf_op jit(solution)/shard_map/ppermute | solution.py:492
  65.7 1.6 %collective-permute-start.28 = (f32[4,2,2,2,1024]{4,3,2,1,0:T(2,128)S(1)}, f32[4,2,2,2,1024]{4,3,2,1,0:T(2,128)S(1)}, u32[]{:S(2)}, u32[]{:S(2)}) collective-permute-start(f32[4,2,2,2,1024]{4,3,2,1,0:T(2,128)S(1)} %collective-permute-done.26.refs_2_), channel_id=1, source_target_pairs={{8,0},{16,8},{24,16},{28,24},{20,28},{12,20},{4,12},{0,4},{9,1},{1... | collective-permute-start | bytes 393224 | tf_op jit(solution)/shard_map/ppermute | solution.py:492
  67.7 2.9 %collective-permute-done.28.refs_4_ = f32[4,2,2,2,1024]{4,3,2,1,0:T(2,128)S(1)} collective-permute-done((f32[4,2,2,2,1024]{4,3,2,1,0:T(2,128)S(1)}, f32[4,2,2,2,1024]{4,3,2,1,0:T(2,128)S(1)}, u32[]{:S(2)}, u32[]{:S(2)}) %collective-permute-start.28) | collective-permute-done | bytes 131104 | tf_op jit(solution)/shard_map/ppermute | solution.py:492
  70.6 1.6 %collective-permute-start.30 = (f32[4,2,2,2,1024]{4,3,2,1,0:T(2,128)S(1)}, f32[4,2,2,2,1024]{4,3,2,1,0:T(2,128)S(1)}, u32[]{:S(2)}, u32[]{:S(2)}) collective-permute-start(f32[4,2,2,2,1024]{4,3,2,1,0:T(2,128)S(1)} %collective-permute-done.28.refs_4_), channel_id=1, source_target_pairs={{8,0},{16,8},{24,16},{28,24},{20,28},{12,20},{4,12},{0,4},{9,1},{1... | collective-permute-start | bytes 393224 | tf_op jit(solution)/shard_map/ppermute | solution.py:492
  72.7 2.9 %collective-permute-done.30.refs_6_ = f32[4,2,2,2,1024]{4,3,2,1,0:T(2,128)S(1)} collective-permute-done((f32[4,2,2,2,1024]{4,3,2,1,0:T(2,128)S(1)}, f32[4,2,2,2,1024]{4,3,2,1,0:T(2,128)S(1)}, u32[]{:S(2)}, u32[]{:S(2)}) %collective-permute-start.30) | collective-permute-done | bytes 131104 | tf_op jit(solution)/shard_map/ppermute | solution.py:492
  75.6 1.6 %collective-permute-start.32 = (f32[2,2,2,2,1024]{4,3,2,1,0:T(2,128)S(1)}, f32[2,2,2,2,1024]{4,3,2,1,0:T(2,128)S(1)}, u32[]{:S(2)}, u32[]{:S(2)}) collective-permute-start(f32[2,2,2,2,1024]{4,3,2,1,0:T(2,128)S(1)} %slice.29), channel_id=1, source_target_pairs={{8,0},{16,8},{24,16},{28,24},{20,28},{12,20},{4,12},{0,4},{9,1},{1... | collective-permute-start | bytes 196616 | tf_op jit(solution)/shard_map/ppermute | solution.py:494
  79.9 1.6 %collective-permute-done.31.head_ref = f32[2,2,2,2,1024]{4,3,2,1,0:T(2,128)S(1)} collective-permute-done((f32[2,2,2,2,1024]{4,3,2,1,0:T(2,128)S(1)}, f32[2,2,2,2,1024]{4,3,2,1,0:T(2,128)S(1)}, u32[]{:S(2)}, u32[]{:S(2)}) %collective-permute-start.31) | collective-permute-done | bytes 65568 | tf_op jit(solution)/shard_map/ppermute | solution.py:494
  81.5 1.7 %shard_map.107 = (f32[8,4,2,2,2,1024]{5,4,3,2,1,0:T(2,128)}, f32[4,2,2,2,1024]{4,3,2,1,0:T(2,128)}) custom-call(f32[1,8]{1,0:T(1,128)S(1)} %copy-done.5, f32[8,8]{1,0:T(8,128)S(1)} %get-tuple-element.41.weights_ref, f32[4,2,2,2,1024]{4,3,2,1,0:T(2,128)S(1)} %get-tuple-element.42.refs_0_.own_ref, f32[8,4,2,2,2,1024]{5,4,3,2,1,0:T(2,128)S(1)} %shard_map.106.partial_ref, ...), custom_call_target="tpu_custom_call" | custom-call | tf_op jit(solution)/shard_map/pallas_call | solution.py:458
  (72 shorter events, 16.4 us)
Async XLA Ops:
  3.3 1.5 %collective-permute-start = (f32[2,2,16,512]{3,2,1,0:T(8,128)S(1)}, f32[2,2,16,512]{3,2,1,0:T(8,128)S(1)}, u32[]{:S(2)}, u32[]{:S(2)}) collective-permute-start(f32[2,2,16,512]{3,2,1,0:T(8,128)S(1)} %get-tuple-element.26), channel_id=1, source_target_pairs={{0,1},{1,0},{2,3},{3,2},{4,5},{5,4},{6,7},{7,6},{8,9},{9,8},{10,11... | collective-permute-start | bytes 393224 | tf_op jit(solution)/shard_map/ppermute | solution.py:470
  4.9 6.7 %collective-permute-start.1 = (f32[2,2,16,512]{3,2,1,0:T(8,128)S(1)}, f32[2,2,16,512]{3,2,1,0:T(8,128)S(1)}, u32[]{:S(2)}, u32[]{:S(2)}) collective-permute-start(f32[2,2,16,512]{3,2,1,0:T(8,128)S(1)} %add.23), channel_id=1, source_target_pairs={{0,2},{1,3},{2,0},{3,1},{4,6},{5,7},{6,4},{7,5},{8,10},{9,11},{10,... | collective-permute-start | bytes 393224 | tf_op jit(solution)/shard_map/ppermute | solution.py:470
  15.5 5.8 %collective-permute-start.7 = (f32[264,128]{1,0:T(8,128)S(1)}, f32[264,128]{1,0:T(8,128)S(1)}, u32[]{:S(2)}, u32[]{:S(2)}) collective-permute-start(f32[264,128]{1,0:T(8,128)S(1)} %get-tuple-element.33.refs_0_), channel_id=1, source_target_pairs={{8,0},{16,8},{24,16},{28,24},{20,28},{12,20},{4,12},{0,4},{9,1},{1... | collective-permute-start | bytes 405512 | tf_op jit(solution)/shard_map/ppermute | solution.py:492
  17.3 5.6 %collective-permute-start.6 = (f32[264,128]{1,0:T(8,128)S(1)}, f32[264,128]{1,0:T(8,128)S(1)}, u32[]{:S(2)}, u32[]{:S(2)}) collective-permute-start(f32[264,128]{1,0:T(8,128)S(1)} %get-tuple-element.33.refs_0_), channel_id=1, source_target_pairs={{0,8},{8,16},{16,24},{24,28},{28,20},{20,12},{12,4},{4,0},{1,9},{9... | collective-permute-start | bytes 405512 | tf_op jit(solution)/shard_map/ppermute | solution.py:491
  18.8 4.5 %collective-permute-start.3 = (f32[2,2,16,512]{3,2,1,0:T(8,128)S(1)}, f32[2,2,16,512]{3,2,1,0:T(8,128)S(1)}, u32[]{:S(2)}, u32[]{:S(2)}) collective-permute-start(f32[2,2,16,512]{3,2,1,0:T(8,128)S(1)} %get-tuple-element.32), channel_id=1, source_target_pairs={{0,1},{1,0},{2,3},{3,2},{4,5},{5,4},{6,7},{7,6},{8,9},{9,8},{10,11... | collective-permute-start | bytes 393224 | tf_op jit(solution)/shard_map/ppermute | solution.py:470
  21.3 5.0 %collective-permute-start.9 = (f32[264,128]{1,0:T(8,128)S(1)}, f32[264,128]{1,0:T(8,128)S(1)}, u32[]{:S(2)}, u32[]{:S(2)}) collective-permute-start(f32[264,128]{1,0:T(8,128)S(1)} %collective-permute-done.7.refs_2_), channel_id=1, source_target_pairs={{8,0},{16,8},{24,16},{28,24},{20,28},{12,20},{4,12},{0,4},{9,1},{1... | collective-permute-start | bytes 405512 | tf_op jit(solution)/shard_map/ppermute | solution.py:492
  23.0 5.0 %collective-permute-start.8 = (f32[264,128]{1,0:T(8,128)S(1)}, f32[264,128]{1,0:T(8,128)S(1)}, u32[]{:S(2)}, u32[]{:S(2)}) collective-permute-start(f32[264,128]{1,0:T(8,128)S(1)} %collective-permute-done.6.refs_1_), channel_id=1, source_target_pairs={{0,8},{8,16},{16,24},{24,28},{28,20},{20,12},{12,4},{4,0},{1,9},{9... | collective-permute-start | bytes 405512 | tf_op jit(solution)/shard_map/ppermute | solution.py:491
  23.3 5.0 %collective-permute-start.4 = (f32[2,2,16,512]{3,2,1,0:T(8,128)S(1)}, f32[2,2,16,512]{3,2,1,0:T(8,128)S(1)}, u32[]{:S(2)}, u32[]{:S(2)}) collective-permute-start(f32[2,2,16,512]{3,2,1,0:T(8,128)S(1)} %add.25), channel_id=1, source_target_pairs={{0,2},{1,3},{2,0},{3,1},{4,6},{5,7},{6,4},{7,5},{8,10},{9,11},{10,... | collective-permute-start | bytes 393224 | tf_op jit(solution)/shard_map/ppermute | solution.py:470
  26.3 5.0 %collective-permute-start.11 = (f32[264,128]{1,0:T(8,128)S(1)}, f32[264,128]{1,0:T(8,128)S(1)}, u32[]{:S(2)}, u32[]{:S(2)}) collective-permute-start(f32[264,128]{1,0:T(8,128)S(1)} %collective-permute-done.9.refs_4_), channel_id=1, source_target_pairs={{8,0},{16,8},{24,16},{28,24},{20,28},{12,20},{4,12},{0,4},{9,1},{1... | collective-permute-start | bytes 405512 | tf_op jit(solution)/shard_map/ppermute | solution.py:492
  28.0 5.0 %collective-permute-start.10 = (f32[264,128]{1,0:T(8,128)S(1)}, f32[264,128]{1,0:T(8,128)S(1)}, u32[]{:S(2)}, u32[]{:S(2)}) collective-permute-start(f32[264,128]{1,0:T(8,128)S(1)} %collective-permute-done.8.refs_3_), channel_id=1, source_target_pairs={{0,8},{8,16},{16,24},{24,28},{28,20},{20,12},{12,4},{4,0},{1,9},{9... | collective-permute-start | bytes 405512 | tf_op jit(solution)/shard_map/ppermute | solution.py:491
  28.4 5.0 %collective-permute-start.5 = (f32[2,2,16,512]{3,2,1,0:T(8,128)S(1)}, f32[2,2,16,512]{3,2,1,0:T(8,128)S(1)}, u32[]{:S(2)}, u32[]{:S(2)}) collective-permute-start(f32[2,2,16,512]{3,2,1,0:T(8,128)S(1)} %add.26.mine_ref), channel_id=1, source_target_pairs={{0,1},{1,0},{2,3},{3,2},{4,5},{5,4},{6,7},{7,6},{8,9},{9,8},{10,11... | collective-permute-start | bytes 393224 | tf_op jit(solution)/shard_map/ppermute | solution.py:470
  31.3 6.0 %collective-permute-start.13 = (f32[136,128]{1,0:T(8,128)S(1)}, f32[136,128]{1,0:T(8,128)S(1)}, u32[]{:S(2)}, u32[]{:S(2)}) collective-permute-start(f32[136,128]{1,0:T(8,128)S(1)} %slice.25), channel_id=1, source_target_pairs={{8,0},{16,8},{24,16},{28,24},{20,28},{12,20},{4,12},{0,4},{9,1},{1... | collective-permute-start | bytes 208904 | tf_op jit(solution)/shard_map/ppermute | solution.py:494
  33.0 4.3 %collective-permute-start.12 = (f32[128,128]{1,0:T(8,128)S(1)}, f32[128,128]{1,0:T(8,128)S(1)}, u32[]{:S(2)}, u32[]{:S(2)}) collective-permute-start(f32[128,128]{1,0:T(8,128)S(1)} %slice.24), channel_id=1, source_target_pairs={{0,8},{8,16},{16,24},{24,28},{28,20},{20,12},{12,4},{4,0},{1,9},{9... | collective-permute-start | bytes 196616 | tf_op jit(solution)/shard_map/ppermute | solution.py:494
  38.7 5.0 %collective-permute-start.18 = (f32[256,128]{1,0:T(8,128)S(1)}, f32[256,128]{1,0:T(8,128)S(1)}, u32[]{:S(2)}, u32[]{:S(2)}) collective-permute-start(f32[256,128]{1,0:T(8,128)S(1)} %get-tuple-element.39.refs_0_.own_ref), channel_id=1, source_target_pairs={{8,0},{16,8},{24,16},{28,24},{20,28},{12,20},{4,12},{0,4},{9,1},{1... | collective-permute-start | bytes 393224 | tf_op jit(solution)/shard_map/ppermute | solution.py:492
  40.3 5.0 %collective-permute-start.17 = (f32[256,128]{1,0:T(8,128)S(1)}, f32[256,128]{1,0:T(8,128)S(1)}, u32[]{:S(2)}, u32[]{:S(2)}) collective-permute-start(f32[256,128]{1,0:T(8,128)S(1)} %get-tuple-element.39.refs_0_.own_ref), channel_id=1, source_target_pairs={{0,8},{8,16},{16,24},{24,28},{28,20},{20,12},{12,4},{4,0},{1,9},{9... | collective-permute-start | bytes 393224 | tf_op jit(solution)/shard_map/ppermute | solution.py:491
  42.0 3.7 %collective-permute-start.14 = (f32[2,2,16,512]{3,2,1,0:T(8,128)S(1)}, f32[2,2,16,512]{3,2,1,0:T(8,128)S(1)}, u32[]{:S(2)}, u32[]{:S(2)}) collective-permute-start(f32[2,2,16,512]{3,2,1,0:T(8,128)S(1)} %get-tuple-element.38), channel_id=1, source_target_pairs={{0,1},{1,0},{2,3},{3,2},{4,5},{5,4},{6,7},{7,6},{8,9},{9,8},{10,11... | collective-permute-start | bytes 393224 | tf_op jit(solution)/shard_map/ppermute | solution.py:470
  43.7 5.0 %collective-permute-start.20 = (f32[256,128]{1,0:T(8,128)S(1)}, f32[256,128]{1,0:T(8,128)S(1)}, u32[]{:S(2)}, u32[]{:S(2)}) collective-permute-start(f32[256,128]{1,0:T(8,128)S(1)} %collective-permute-done.18.refs_2_), channel_id=1, source_target_pairs={{8,0},{16,8},{24,16},{28,24},{20,28},{12,20},{4,12},{0,4},{9,1},{1... | collective-permute-start | bytes 393224 | tf_op jit(solution)/shard_map/ppermute | solution.py:492
  45.3 5.0 %collective-permute-start.19 = (f32[256,128]{1,0:T(8,128)S(1)}, f32[256,128]{1,0:T(8,128)S(1)}, u32[]{:S(2)}, u32[]{:S(2)}) collective-permute-start(f32[256,128]{1,0:T(8,128)S(1)} %collective-permute-done.17.refs_1_), channel_id=1, source_target_pairs={{0,8},{8,16},{16,24},{24,28},{28,20},{20,12},{12,4},{4,0},{1,9},{9... | collective-permute-start | bytes 393224 | tf_op jit(solution)/shard_map/ppermute | solution.py:491
  45.8 5.0 %collective-permute-start.15 = (f32[2,2,16,512]{3,2,1,0:T(8,128)S(1)}, f32[2,2,16,512]{3,2,1,0:T(8,128)S(1)}, u32[]{:S(2)}, u32[]{:S(2)}) collective-permute-start(f32[2,2,16,512]{3,2,1,0:T(8,128)S(1)} %add.27), channel_id=1, source_target_pairs={{0,2},{1,3},{2,0},{3,1},{4,6},{5,7},{6,4},{7,5},{8,10},{9,11},{10,... | collective-permute-start | bytes 393224 | tf_op jit(solution)/shard_map/ppermute | solution.py:470
  48.7 5.0 %collective-permute-start.22 = (f32[256,128]{1,0:T(8,128)S(1)}, f32[256,128]{1,0:T(8,128)S(1)}, u32[]{:S(2)}, u32[]{:S(2)}) collective-permute-start(f32[256,128]{1,0:T(8,128)S(1)} %collective-permute-done.20.refs_4_), channel_id=1, source_target_pairs={{8,0},{16,8},{24,16},{28,24},{20,28},{12,20},{4,12},{0,4},{9,1},{1... | collective-permute-start | bytes 393224 | tf_op jit(solution)/shard_map/ppermute | solution.py:492
  50.3 5.0 %collective-permute-start.21 = (f32[256,128]{1,0:T(8,128)S(1)}, f32[256,128]{1,0:T(8,128)S(1)}, u32[]{:S(2)}, u32[]{:S(2)}) collective-permute-start(f32[256,128]{1,0:T(8,128)S(1)} %collective-permute-done.19.refs_3_), channel_id=1, source_target_pairs={{0,8},{8,16},{16,24},{24,28},{28,20},{20,12},{12,4},{4,0},{1,9},{9... | collective-permute-start | bytes 393224 | tf_op jit(solution)/shard_map/ppermute | solution.py:491
  50.8 5.3 %collective-permute-start.16 = (f32[2,2,16,512]{3,2,1,0:T(8,128)S(1)}, f32[2,2,16,512]{3,2,1,0:T(8,128)S(1)}, u32[]{:S(2)}, u32[]{:S(2)}) collective-permute-start(f32[2,2,16,512]{3,2,1,0:T(8,128)S(1)} %add.28.mine_ref), channel_id=1, source_target_pairs={{0,1},{1,0},{2,3},{3,2},{4,5},{5,4},{6,7},{7,6},{8,9},{9,8},{10,11... | collective-permute-start | bytes 393224 | tf_op jit(solution)/shard_map/ppermute | solution.py:470
  53.7 4.8 %collective-permute-start.24 = (f32[128,128]{1,0:T(8,128)S(1)}, f32[128,128]{1,0:T(8,128)S(1)}, u32[]{:S(2)}, u32[]{:S(2)}) collective-permute-start(f32[128,128]{1,0:T(8,128)S(1)} %slice.27), channel_id=1, source_target_pairs={{8,0},{16,8},{24,16},{28,24},{20,28},{12,20},{4,12},{0,4},{9,1},{1... | collective-permute-start | bytes 196616 | tf_op jit(solution)/shard_map/ppermute | solution.py:494
  55.2 4.5 %collective-permute-start.23 = (f32[128,128]{1,0:T(8,128)S(1)}, f32[128,128]{1,0:T(8,128)S(1)}, u32[]{:S(2)}, u32[]{:S(2)}) collective-permute-start(f32[128,128]{1,0:T(8,128)S(1)} %slice.26), channel_id=1, source_target_pairs={{0,8},{8,16},{16,24},{24,28},{28,20},{20,12},{12,4},{4,0},{1,9},{9... | collective-permute-start | bytes 196616 | tf_op jit(solution)/shard_map/ppermute | solution.py:494
  60.0 5.7 %collective-permute-start.26 = (f32[4,2,2,2,1024]{4,3,2,1,0:T(2,128)S(1)}, f32[4,2,2,2,1024]{4,3,2,1,0:T(2,128)S(1)}, u32[]{:S(2)}, u32[]{:S(2)}) collective-permute-start(f32[4,2,2,2,1024]{4,3,2,1,0:T(2,128)S(1)} %get-tuple-element.42.refs_0_.own_ref), channel_id=1, source_target_pairs={{8,0},{16,8},{24,16},{28,24},{20,28},{12,20},{4,12},{0,4},{9,1},{1... | collective-permute-start | bytes 393224 | tf_op jit(solution)/shard_map/ppermute | solution.py:492
  61.7 5.6 %collective-permute-start.25 = (f32[4,2,2,2,1024]{4,3,2,1,0:T(2,128)S(1)}, f32[4,2,2,2,1024]{4,3,2,1,0:T(2,128)S(1)}, u32[]{:S(2)}, u32[]{:S(2)}) collective-permute-start(f32[4,2,2,2,1024]{4,3,2,1,0:T(2,128)S(1)} %get-tuple-element.42.refs_0_.own_ref), channel_id=1, source_target_pairs={{0,8},{8,16},{16,24},{24,28},{28,20},{20,12},{12,4},{4,0},{1,9},{9... | collective-permute-start | bytes 393224 | tf_op jit(solution)/shard_map/ppermute | solution.py:491
  65.7 5.0 %collective-permute-start.28 = (f32[4,2,2,2,1024]{4,3,2,1,0:T(2,128)S(1)}, f32[4,2,2,2,1024]{4,3,2,1,0:T(2,128)S(1)}, u32[]{:S(2)}, u32[]{:S(2)}) collective-permute-start(f32[4,2,2,2,1024]{4,3,2,1,0:T(2,128)S(1)} %collective-permute-done.26.refs_2_), channel_id=1, source_target_pairs={{8,0},{16,8},{24,16},{28,24},{20,28},{12,20},{4,12},{0,4},{9,1},{1... | collective-permute-start | bytes 393224 | tf_op jit(solution)/shard_map/ppermute | solution.py:492
  67.3 5.0 %collective-permute-start.27 = (f32[4,2,2,2,1024]{4,3,2,1,0:T(2,128)S(1)}, f32[4,2,2,2,1024]{4,3,2,1,0:T(2,128)S(1)}, u32[]{:S(2)}, u32[]{:S(2)}) collective-permute-start(f32[4,2,2,2,1024]{4,3,2,1,0:T(2,128)S(1)} %collective-permute-done.25.refs_1_), channel_id=1, source_target_pairs={{0,8},{8,16},{16,24},{24,28},{28,20},{20,12},{12,4},{4,0},{1,9},{9... | collective-permute-start | bytes 393224 | tf_op jit(solution)/shard_map/ppermute | solution.py:491
  70.6 5.0 %collective-permute-start.30 = (f32[4,2,2,2,1024]{4,3,2,1,0:T(2,128)S(1)}, f32[4,2,2,2,1024]{4,3,2,1,0:T(2,128)S(1)}, u32[]{:S(2)}, u32[]{:S(2)}) collective-permute-start(f32[4,2,2,2,1024]{4,3,2,1,0:T(2,128)S(1)} %collective-permute-done.28.refs_4_), channel_id=1, source_target_pairs={{8,0},{16,8},{24,16},{28,24},{20,28},{12,20},{4,12},{0,4},{9,1},{1... | collective-permute-start | bytes 393224 | tf_op jit(solution)/shard_map/ppermute | solution.py:492
  72.2 5.0 %collective-permute-start.29 = (f32[4,2,2,2,1024]{4,3,2,1,0:T(2,128)S(1)}, f32[4,2,2,2,1024]{4,3,2,1,0:T(2,128)S(1)}, u32[]{:S(2)}, u32[]{:S(2)}) collective-permute-start(f32[4,2,2,2,1024]{4,3,2,1,0:T(2,128)S(1)} %collective-permute-done.27.refs_3_), channel_id=1, source_target_pairs={{0,8},{8,16},{16,24},{24,28},{28,20},{20,12},{12,4},{4,0},{1,9},{9... | collective-permute-start | bytes 393224 | tf_op jit(solution)/shard_map/ppermute | solution.py:491
  75.6 4.3 %collective-permute-start.32 = (f32[2,2,2,2,1024]{4,3,2,1,0:T(2,128)S(1)}, f32[2,2,2,2,1024]{4,3,2,1,0:T(2,128)S(1)}, u32[]{:S(2)}, u32[]{:S(2)}) collective-permute-start(f32[2,2,2,2,1024]{4,3,2,1,0:T(2,128)S(1)} %slice.29), channel_id=1, source_target_pairs={{8,0},{16,8},{24,16},{28,24},{20,28},{12,20},{4,12},{0,4},{9,1},{1... | collective-permute-start | bytes 196616 | tf_op jit(solution)/shard_map/ppermute | solution.py:494
  77.2 4.3 %collective-permute-start.31 = (f32[2,2,2,2,1024]{4,3,2,1,0:T(2,128)S(1)}, f32[2,2,2,2,1024]{4,3,2,1,0:T(2,128)S(1)}, u32[]{:S(2)}, u32[]{:S(2)}) collective-permute-start(f32[2,2,2,2,1024]{4,3,2,1,0:T(2,128)S(1)} %slice.28), channel_id=1, source_target_pairs={{0,8},{8,16},{16,24},{24,28},{28,20},{20,12},{12,4},{4,0},{1,9},{9... | collective-permute-start | bytes 196616 | tf_op jit(solution)/shard_map/ppermute | solution.py:494
  (7 other events, 46.9 us)

commit v5 on v4

--- a/solution.py
+++ b/solution.py
@@ -323,18 +323,14 @@
 
 def gathered_update_kernel(sums_ref, *refs):
     units, (jones_ref, shared_ref, spread_ref, weights_ref) = refs[:-4], refs[-4:]
-    own, tail = units[0], units[-1]
     dirs = sums_ref.shape[1] // 12
     chunks, _, width = sums_ref.shape
     rows = 8 * dirs
     terms = weights_ref.shape[0]
-    bands = len(units) - 1
+    bands = len(units)
     hi = lax.Precision.HIGHEST
     at = chunks * rows
-    start = own.shape[0] - tail.shape[0]
-    basis = jnp.concatenate(
-        [ref[at : at + 1, :terms] for ref in units[:-2]] + [tail[at - start : at - start + 1, :terms]], axis=0
-    )
+    basis = jnp.concatenate([ref[at : at + 1, :terms] for ref in units], axis=0)
     gram = lax.dot_general(basis, basis, (((0,), (0,)), ((), ())), precision=hi, preferred_element_type=jnp.float32)
     row = lax.broadcasted_iota(jnp.int32, (terms, terms), 0)
     col = lax.broadcasted_iota(jnp.int32, (terms, terms), 1)
@@ -361,10 +357,8 @@
 
 def solve_gathered(chunk, spread, sums_ref, units, rows):
     dirs = sums_ref.shape[1] // 12
-    head, tail = units[-2:]
-    base, start = chunk * rows, head.shape[0]
-    values = [ref[base : base + rows, :] for ref in units[:-2]]
-    values.append(head[base : base + rows, :] if base < start else tail[base - start : base - start + rows, :])
+    base = chunk * rows
+    values = [ref[base : base + rows, :] for ref in units]
     consensus = weighted(spread, 0, values)
     return solve_next(
         lambda a: sums_ref[chunk, a : a + dirs, :],
@@ -383,16 +377,15 @@
         out_ref[base : base + step, :] = weighted(spread, 0, [ref[base : base + step, :] for ref in units])
 
 
-def gathered_last_kernel(spread_ref, sums_ref, own_ref, partial_ref, head_ref, tail_ref, jones_ref, shared_ref):
+def gathered_last_kernel(spread_ref, sums_ref, own_ref, partial_ref, *refs):
+    units, (jones_ref, shared_ref) = refs[:-2], refs[-2:]
     dirs, width = sums_ref.shape[1] // 12, sums_ref.shape[2]
     rows = 8 * dirs
-    bands = spread_ref.shape[0]
-    start = head_ref.shape[0]
-    last = spread_ref[0:1, bands - 1 : bands]
+    spread = spread_ref[0:1, spread_ref.shape[0] - len(units) :]
     for chunk in range(sums_ref.shape[0]):
         base = chunk * rows
-        far = head_ref[base : base + rows, :] if base < start else tail_ref[base - start : base - start + rows, :]
-        consensus = partial_ref[base : base + rows, :] + jnp.broadcast_to(last, far.shape) * far
+        rest = weighted(spread, 0, [ref[base : base + rows, :] for ref in units])
+        consensus = partial_ref[base : base + rows, :] + rest
         jones, shared = solve_next(
             lambda a: sums_ref[chunk, a : a + dirs, :],
             lambda a: consensus[a : a + dirs],
@@ -421,22 +414,18 @@
                     out_ref[m, k, part, i] = weighted(weights, m, values)
 
 
-def final_kernel(
-    basis_ref, weights_ref, own_ref, partial_ref, head_ref, tail_ref, coeffs_hbm, dual_hbm, coeffs_ref, dual_ref, sems
-):
+def final_kernel(basis_ref, weights_ref, own_ref, partial_ref, *refs):
+    units, (coeffs_hbm, dual_hbm, coeffs_ref, dual_ref, sems) = refs[:-5], refs[-5:]
     terms, dirs = coeffs_ref.shape[:2]
-    half = head_ref.shape[0]
-    weights = weights_ref[...]
-    far = weights.shape[1] - 1
+    weights = weights_ref[:, weights_ref.shape[1] - len(units) :]
     copies = []
     for k in range(dirs):
         for part in range(2):
             for i in range(2):
-                value = head_ref[k, part, i] if k < half else tail_ref[k - half, part, i]
+                values = [ref[k, part, i] for ref in units]
                 consensus = None
                 for m in range(terms):
-                    weight = jnp.broadcast_to(weights[m : m + 1, far:], value.shape)
-                    total = partial_ref[m, k, part, i] + weight * value
+                    total = partial_ref[m, k, part, i] + weighted(weights, m, values)
                     coeffs_ref[m, k, part, i] = total
                     share = total * basis_ref[0, m]
                     consensus = share if consensus is None else consensus + share
@@ -480,18 +469,16 @@
     return mine, swap(mine, "dir", 1)
 
 
-def ring_gather(value, half):
-    size = lax.axis_size("band")
-    order = list(range(0, size, 2)) + list(range(size - 1, 0, -2))
-    ahead = [(order[i], order[(i + 1) % size]) for i in range(size)]
-    behind = [(b, a) for a, b in ahead]
-    values = [value]
-    up = down = value
-    for step in range(1, (size - 1) // 2 + 1):
-        up = lax.ppermute(up, "band", ahead)
-        down = lax.ppermute(down, "band", behind)
-        values += [up, down]
-    return values + [lax.ppermute(up[:half], "band", ahead), lax.ppermute(down[half:], "band", behind)]
+def gather_bands(value):
+    half = lax.axis_size("band") // 2
+    far = swap(value, "band", half)
+    near = [value]
+    for bit in range(1, half):
+        near.append(swap(value, "band", bit))
+    passed = [far]
+    for bit in range(1, half):
+        passed.append(swap(far, "band", bit))
+    return near + passed
 
 
 def reduce_bands(shared, row, factor):
@@ -510,7 +497,7 @@
     times, baselines = coher.shape[-2:]
     rows = 8 * dirs
     parity = (lax.axis_index("dir") % 2).astype(jnp.int32).reshape(1, 1)
-    chunked = stations % (bands * LANES) == 0 and bands % 2 == 0 and dirs % 2 == 0
+    chunked = stations % (bands * LANES) == 0 and bands > 2 and bands & (bands - 1) == 0
     hi = lax.Precision.HIGHEST
     width = stations // bands if chunked else LANES
     chunks = stations // width
@@ -558,25 +545,27 @@
         (freq_basis, station_sums(*started), known, lag),
     )
     if chunked:
-        half_rows = chunks // 2 * rows
-        units = ring_gather(unit, half_rows)
-        sums = station_sums(*model(jones))
+        early = bands // 2 + 1
+        units = gather_bands(unit)
+        started = model(jones)
+        sums = station_sums(*started)
         jones, unit, spread, weights = call(
             gathered_update_kernel,
             (flat, struct(chunks * rows, width), struct(bands, bands), struct(terms, bands)), 0, (sums, *units),
         )
-        units = ring_gather(unit, half_rows)
-        sums = station_sums(*model(jones))
-        partial = call(partial_consensus_kernel, struct(chunks * rows, width), 0, (spread, *units[:-2]))
+        units = gather_bands(unit)
+        started = model(jones)
+        sums = station_sums(*started)
+        partial = call(partial_consensus_kernel, struct(chunks * rows, width), 0, (spread, *units[:early]))
         jones, shared = call(
-            gathered_last_kernel, (flat, struct(*native)), 0, (spread, sums, unit, partial, *units[-2:])
+            gathered_last_kernel, (flat, struct(*native)), 0, (spread, sums, unit, partial, *units[early:])
         )
         jones = call(native_kernel, struct(*native), 0, (jones,))
-        units = ring_gather(shared, dirs // 2)
-        partial = call(partial_coeffs_kernel, struct(terms, *native), 0, (weights, *units[:-2]))
+        units = gather_bands(shared)
+        partial = call(partial_coeffs_kernel, struct(terms, *native), 0, (weights, *units[:early]))
         coeffs, dual = call(
             final_kernel, (struct(terms, *native), struct(*native)), 1,
-            (freq_basis, weights, shared, partial, *units[-2:]),
+            (freq_basis, weights, shared, partial, *units[early:]),
             [
                 pltpu.VMEM((terms, *native), jnp.float32),
                 pltpu.VMEM(native, jnp.float32),
@@ -613,4 +602,5 @@
         P("band", "dir", None, None, None, None),
         P(None, "dir", None, None, None, None),
     )
+
     return jax.shard_map(local, mesh=mesh, in_specs=in_specs, out_specs=out_specs, check_vma=False)

time: 83.6 us -> 81.8 us (0.978)
  waiting for transfers between devices: 32.5 us -> 28.6 us
  starting transfers between devices: 31.9 us -> 34.4 us
    ppermute x9 -> x30, starting transfers between devices: 7.09 us -> 34.4 us  [swap(): return lax.ppermute(value, axis, [(i, i ^ bit) for i in range(size)])]
    ppermute x24 -> x0, waiting for transfers between devices: 27 us -> none  [the longest x9 21.6 us: ring_gather(): down = lax.ppermute(down, 'band', behind)]
    ppermute x24 -> x0, starting transfers between devices: 24.8 us -> none  [the longest x9 14.8 us: ring_gather(): down = lax.ppermute(down, 'band', behind)]
    ppermute x9 -> x30, waiting for transfers between devices: 5.5 us -> 28.6 us  [swap(): return lax.ppermute(value, axis, [(i, i ^ bit) for i in range(size)])]
  transfers between devices with their start and end apart: 33 -> 30, of which waited for: 17 -> 18; matrix products, arithmetic and copies ran while one was open for 0% -> 0% of each run, Pallas kernels for 11% -> 8%
where the time goes in v5:
time: 81.8 us; the launch traced here: 81.7 us
  starting transfers between devices  34.4 us (42%)
  waiting for transfers between devices  28.6 us (35%)
  Pallas kernels  17.6 us (22%)
  between operations  0.9 us (1%)
    ppermute x30, starting transfers between devices, swap(): return lax.ppermute(value, axis, [(i, i ^ bit) for i in range(size)])  34.4 us
    ppermute x30, waiting for transfers between devices, swap(): return lax.ppermute(value, axis, [(i, i ^ bit) for i in range(size)])  28.6 us
    pallas_call x14, Pallas kernels, call(): pl.pallas_call(kernel, out_shape=out_shape, in_specs=[SMEM if at < scalar...  17.6 us
  transfers between devices with their start and end apart: 30, of which 18 were waited for; matrix products, arithmetic and copies ran while one was open for 0% of the time, Pallas kernels for 8%

profile of v5, /device:TPU:0, one launch (start us, length us, event | category | flops | bytes accessed | tf_op | source)
XLA Modules:
  0.0 81.7 jit_solution(2847619611038577725)
XLA Ops:
  0.7 2.6 %shard_map.94 = (f32[32,1024]{1,0:T(8,128)S(1)}, f32[2,2,16,512]{3,2,1,0:T(8,128)S(1)}, f32[2,2,16,512]{3,2,1,0:T(8,128)S(1)}) custom-call(s32[1,1]{1,0:T(1,128)} %bitcast.parity_ref, f32[4,2,2,2,1024]{4,3,2,1,0:T(2,128)} %bitcast.17, s32[2,512]{1,0:T(2,128)} %pairs_ref.9, f32[4,2,2,2,16,512]{5,4,3,2,1,0:T(8,128)} %bitcast.7), custom_call_target="tpu_custom_call" | custom-call | tf_op jit(solution)/shard_map/pallas_call | solution.py:447
  4.9 2.9 %collective-permute-start.1 = (f32[2,2,16,512]{3,2,1,0:T(8,128)S(1)}, f32[2,2,16,512]{3,2,1,0:T(8,128)S(1)}, u32[]{:S(2)}, u32[]{:S(2)}) collective-permute-start(f32[2,2,16,512]{3,2,1,0:T(8,128)S(1)} %add.23), channel_id=1, source_target_pairs={{0,2},{1,3},{2,0},{3,1},{4,6},{5,7},{6,4},{7,5},{8,10},{9,11},{10,... | collective-permute-start | bytes 393224 | tf_op jit(solution)/shard_map/ppermute | solution.py:459
  7.8 3.8 %collective-permute-done.1 = f32[2,2,16,512]{3,2,1,0:T(8,128)S(1)} collective-permute-done((f32[2,2,16,512]{3,2,1,0:T(8,128)S(1)}, f32[2,2,16,512]{3,2,1,0:T(8,128)S(1)}, u32[]{:S(2)}, u32[]{:S(2)}) %collective-permute-start.1) | collective-permute-done | bytes 131104 | tf_op jit(solution)/shard_map/ppermute | solution.py:459
  13.0 2.4 %shard_map.95.sums_ref = f32[8,48,128]{2,1,0:T(8,128)S(1)} custom-call(s32[1,1]{1,0:T(1,128)} %bitcast.parity_ref, f32[32,1024]{1,0:T(8,128)S(1)} %get-tuple-element.24.gathered_ref, s32[2,512]{1,0:T(2,128)S(1)} %copy-done.3, f32[4,2,2,2,16,512]{5,4,3,2,1,0:T(8,128)S(1)} %bitcast.8, f32[2,2,2,16,512]{4,3,2,1,0:T(8,128)S(1)} %bitcast.13, ...), custom_call_target="tpu_custom_call" | custom-call | tf_op jit(solution)/shard_map/pallas_call | solution.py:447
  15.5 1.2 %shard_map.98 = (f32[32,1024]{1,0:T(8,128)S(1)}, f32[2,2,16,512]{3,2,1,0:T(8,128)S(1)}, f32[2,2,16,512]{3,2,1,0:T(8,128)S(1)}) custom-call(s32[1,1]{1,0:T(1,128)} %bitcast.parity_ref, f32[32,1024]{1,0:T(8,128)S(1)} %get-tuple-element.29.jones_ref, s32[2,512]{1,0:T(2,128)S(1)} %copy-done.3, f32[4,2,2,2,16,512]{5,4,3,2,1,0:T(8,128)S(1)} %bitcast.9), custom_call_target="tpu_custom_call" | custom-call | tf_op jit(solution)/shard_map/pallas_call | solution.py:447
  16.9 1.2 %collective-permute-done.3 = f32[2,2,16,512]{3,2,1,0:T(8,128)S(1)} collective-permute-done((f32[2,2,16,512]{3,2,1,0:T(8,128)S(1)}, f32[2,2,16,512]{3,2,1,0:T(8,128)S(1)}, u32[]{:S(2)}, u32[]{:S(2)}) %collective-permute-start.3) | collective-permute-done | bytes 131104 | tf_op jit(solution)/shard_map/ppermute | solution.py:459
  18.2 1.8 %collective-permute-start.4 = (f32[2,2,16,512]{3,2,1,0:T(8,128)S(1)}, f32[2,2,16,512]{3,2,1,0:T(8,128)S(1)}, u32[]{:S(2)}, u32[]{:S(2)}) collective-permute-start(f32[2,2,16,512]{3,2,1,0:T(8,128)S(1)} %add.25), channel_id=1, source_target_pairs={{0,2},{1,3},{2,0},{3,1},{4,6},{5,7},{6,4},{7,5},{8,10},{9,11},{10,... | collective-permute-start | bytes 393224 | tf_op jit(solution)/shard_map/ppermute | solution.py:459
  20.0 2.6 %collective-permute-start.9 = (f32[264,128]{1,0:T(8,128)S(1)}, f32[264,128]{1,0:T(8,128)S(1)}, u32[]{:S(2)}, u32[]{:S(2)}) collective-permute-start(f32[264,128]{1,0:T(8,128)S(1)} %get-tuple-element.33.refs_0_), channel_id=1, source_target_pairs={{0,16},{4,20},{8,24},{12,28},{16,0},{20,4},{24,8},{28,12},{1,17},{... | collective-permute-start | bytes 405512 | tf_op jit(solution)/shard_map/ppermute | solution.py:459
  22.6 2.5 %collective-permute-start.8 = (f32[264,128]{1,0:T(8,128)S(1)}, f32[264,128]{1,0:T(8,128)S(1)}, u32[]{:S(2)}, u32[]{:S(2)}) collective-permute-start(f32[264,128]{1,0:T(8,128)S(1)} %get-tuple-element.33.refs_0_), channel_id=1, source_target_pairs={{0,12},{4,8},{8,4},{12,0},{16,28},{20,24},{24,20},{28,16},{1,13},{... | collective-permute-start | bytes 405512 | tf_op jit(solution)/shard_map/ppermute | solution.py:459
  25.8 1.5 %collective-permute-start.6 = (f32[264,128]{1,0:T(8,128)S(1)}, f32[264,128]{1,0:T(8,128)S(1)}, u32[]{:S(2)}, u32[]{:S(2)}) collective-permute-start(f32[264,128]{1,0:T(8,128)S(1)} %get-tuple-element.33.refs_0_), channel_id=1, source_target_pairs={{0,4},{4,0},{8,12},{12,8},{16,20},{20,16},{24,28},{28,24},{1,5},{5... | collective-permute-start | bytes 405512 | tf_op jit(solution)/shard_map/ppermute | solution.py:459
  27.3 1.9 %collective-permute-done.9.refs_4_ = f32[264,128]{1,0:T(8,128)S(1)} collective-permute-done((f32[264,128]{1,0:T(8,128)S(1)}, f32[264,128]{1,0:T(8,128)S(1)}, u32[]{:S(2)}, u32[]{:S(2)}) %collective-permute-start.9) | collective-permute-done | bytes 135200 | tf_op jit(solution)/shard_map/ppermute | solution.py:459
  29.2 1.6 %collective-permute-start.12 = (f32[264,128]{1,0:T(8,128)S(1)}, f32[264,128]{1,0:T(8,128)S(1)}, u32[]{:S(2)}, u32[]{:S(2)}) collective-permute-start(f32[264,128]{1,0:T(8,128)S(1)} %collective-permute-done.9.refs_4_), channel_id=1, source_target_pairs={{0,12},{4,8},{8,4},{12,0},{16,28},{20,24},{24,20},{28,16},{1,13},{... | collective-permute-start | bytes 405512 | tf_op jit(solution)/shard_map/ppermute | solution.py:459
  31.1 1.8 %collective-permute-start.11 = (f32[264,128]{1,0:T(8,128)S(1)}, f32[264,128]{1,0:T(8,128)S(1)}, u32[]{:S(2)}, u32[]{:S(2)}) collective-permute-start(f32[264,128]{1,0:T(8,128)S(1)} %collective-permute-done.9.refs_4_), channel_id=1, source_target_pairs={{0,8},{4,12},{8,0},{12,4},{16,24},{20,28},{24,16},{28,20},{1,9},{5... | collective-permute-start | bytes 405512 | tf_op jit(solution)/shard_map/ppermute | solution.py:459
  33.0 2.4 %shard_map.99.sums_ref = f32[8,48,128]{2,1,0:T(8,128)S(1)} custom-call(s32[1,1]{1,0:T(1,128)} %bitcast.parity_ref, f32[32,1024]{1,0:T(8,128)S(1)} %get-tuple-element.30.gathered_ref, s32[2,512]{1,0:T(2,128)S(1)} %copy-done.3, f32[4,2,2,2,16,512]{5,4,3,2,1,0:T(8,128)S(1)} %bitcast.10, f32[2,2,2,16,512]{4,3,2,1,0:T(8,128)S(1)} %bitcast.14, ...), custom_call_target="tpu_custom_call" | custom-call | tf_op jit(solution)/shard_map/pallas_call | solution.py:447
  35.4 1.5 %collective-permute-done.12.refs_7_ = f32[264,128]{1,0:T(8,128)S(1)} collective-permute-done((f32[264,128]{1,0:T(8,128)S(1)}, f32[264,128]{1,0:T(8,128)S(1)}, u32[]{:S(2)}, u32[]{:S(2)}) %collective-permute-start.12) | collective-permute-done | bytes 135200 | tf_op jit(solution)/shard_map/ppermute | solution.py:459
  36.9 2.1 %collective-permute-done.11.refs_6_ = f32[264,128]{1,0:T(8,128)S(1)} collective-permute-done((f32[264,128]{1,0:T(8,128)S(1)}, f32[264,128]{1,0:T(8,128)S(1)}, u32[]{:S(2)}, u32[]{:S(2)}) %collective-permute-start.11) | collective-permute-done | bytes 135200 | tf_op jit(solution)/shard_map/ppermute | solution.py:459
  39.1 1.4 %shard_map.100 = (f32[32,1024]{1,0:T(8,128)S(1)}, f32[256,128]{1,0:T(8,128)S(1)}, f32[8,8]{1,0:T(8,128)S(1)}, f32[8,8]{1,0:T(8,128)S(1)}) custom-call(f32[8,48,128]{2,1,0:T(8,128)S(1)} %shard_map.99.sums_ref, f32[264,128]{1,0:T(8,128)S(1)} %get-tuple-element.33.refs_0_, f32[264,128]{1,0:T(8,128)S(1)} %collective-permute-done.6.refs_1_, ...), custom_call_target="tpu_custom_call" | custom-call | tf_op jit(solution)/shard_map/pallas_call | solution.py:447
  40.4 1.2 %shard_map.101 = (f32[32,1024]{1,0:T(8,128)S(1)}, f32[2,2,16,512]{3,2,1,0:T(8,128)S(1)}, f32[2,2,16,512]{3,2,1,0:T(8,128)S(1)}) custom-call(s32[1,1]{1,0:T(1,128)} %bitcast.parity_ref, f32[32,1024]{1,0:T(8,128)S(1)} %get-tuple-element.35.jones_ref, s32[2,512]{1,0:T(2,128)S(1)} %copy-done.3, f32[4,2,2,2,16,512]{5,4,3,2,1,0:T(8,128)S(1)} %bitcast.11), custom_call_target="tpu_custom_call" | custom-call | tf_op jit(solution)/shard_map/pallas_call | solution.py:447
  41.8 1.3 %collective-permute-done.13 = f32[2,2,16,512]{3,2,1,0:T(8,128)S(1)} collective-permute-done((f32[2,2,16,512]{3,2,1,0:T(8,128)S(1)}, f32[2,2,16,512]{3,2,1,0:T(8,128)S(1)}, u32[]{:S(2)}, u32[]{:S(2)}) %collective-permute-start.13) | collective-permute-done | bytes 131104 | tf_op jit(solution)/shard_map/ppermute | solution.py:459
  43.7 1.8 %collective-permute-start.19 = (f32[256,128]{1,0:T(8,128)S(1)}, f32[256,128]{1,0:T(8,128)S(1)}, u32[]{:S(2)}, u32[]{:S(2)}) collective-permute-start(f32[256,128]{1,0:T(8,128)S(1)} %get-tuple-element.39.refs_0_.own_ref), channel_id=1, source_target_pairs={{0,16},{4,20},{8,24},{12,28},{16,0},{20,4},{24,8},{28,12},{1,17},{... | collective-permute-start | bytes 393224 | tf_op jit(solution)/shard_map/ppermute | solution.py:459
  45.4 2.6 %collective-permute-start.18 = (f32[256,128]{1,0:T(8,128)S(1)}, f32[256,128]{1,0:T(8,128)S(1)}, u32[]{:S(2)}, u32[]{:S(2)}) collective-permute-start(f32[256,128]{1,0:T(8,128)S(1)} %get-tuple-element.39.refs_0_.own_ref), channel_id=1, source_target_pairs={{0,12},{4,8},{8,4},{12,0},{16,28},{20,24},{24,20},{28,16},{1,13},{... | collective-permute-start | bytes 393224 | tf_op jit(solution)/shard_map/ppermute | solution.py:459
  49.0 3.7 %collective-permute-done.19.refs_4_ = f32[256,128]{1,0:T(8,128)S(1)} collective-permute-done((f32[256,128]{1,0:T(8,128)S(1)}, f32[256,128]{1,0:T(8,128)S(1)}, u32[]{:S(2)}, u32[]{:S(2)}) %collective-permute-start.19) | collective-permute-done | bytes 131104 | tf_op jit(solution)/shard_map/ppermute | solution.py:459
  53.5 1.4 %collective-permute-done.18.refs_3_ = f32[256,128]{1,0:T(8,128)S(1)} collective-permute-done((f32[256,128]{1,0:T(8,128)S(1)}, f32[256,128]{1,0:T(8,128)S(1)}, u32[]{:S(2)}, u32[]{:S(2)}) %collective-permute-start.18) | collective-permute-done | bytes 131104 | tf_op jit(solution)/shard_map/ppermute | solution.py:459
  56.0 2.3 %collective-permute-start.20 = (f32[256,128]{1,0:T(8,128)S(1)}, f32[256,128]{1,0:T(8,128)S(1)}, u32[]{:S(2)}, u32[]{:S(2)}) collective-permute-start(f32[256,128]{1,0:T(8,128)S(1)} %collective-permute-done.19.refs_4_), channel_id=1, source_target_pairs={{0,4},{4,0},{8,12},{12,8},{16,20},{20,16},{24,28},{28,24},{1,5},{5... | collective-permute-start | bytes 393224 | tf_op jit(solution)/shard_map/ppermute | solution.py:459
  58.4 2.4 %shard_map.102.sums_ref = f32[8,48,128]{2,1,0:T(8,128)S(1)} custom-call(s32[1,1]{1,0:T(1,128)} %bitcast.parity_ref, f32[32,1024]{1,0:T(8,128)S(1)} %get-tuple-element.36.gathered_ref, s32[2,512]{1,0:T(2,128)S(1)} %copy-done.3, f32[4,2,2,2,16,512]{5,4,3,2,1,0:T(8,128)S(1)} %bitcast.12, f32[2,2,2,16,512]{4,3,2,1,0:T(8,128)S(1)} %bitcast.15, ...), custom_call_target="tpu_custom_call" | custom-call | tf_op jit(solution)/shard_map/pallas_call | solution.py:447
  62.5 1.2 %collective-permute-start.26 = (f32[4,2,2,2,1024]{4,3,2,1,0:T(2,128)S(1)}, f32[4,2,2,2,1024]{4,3,2,1,0:T(2,128)S(1)}, u32[]{:S(2)}, u32[]{:S(2)}) collective-permute-start(f32[4,2,2,2,1024]{4,3,2,1,0:T(2,128)S(1)} %get-tuple-element.42.refs_0_.own_ref), channel_id=1, source_target_pairs={{0,16},{4,20},{8,24},{12,28},{16,0},{20,4},{24,8},{28,12},{1,17},{... | collective-permute-start | bytes 393224 | tf_op jit(solution)/shard_map/ppermute | solution.py:459
  63.7 2.6 %collective-permute-start.25 = (f32[4,2,2,2,1024]{4,3,2,1,0:T(2,128)S(1)}, f32[4,2,2,2,1024]{4,3,2,1,0:T(2,128)S(1)}, u32[]{:S(2)}, u32[]{:S(2)}) collective-permute-start(f32[4,2,2,2,1024]{4,3,2,1,0:T(2,128)S(1)} %get-tuple-element.42.refs_0_.own_ref), channel_id=1, source_target_pairs={{0,12},{4,8},{8,4},{12,0},{16,28},{20,24},{24,20},{28,16},{1,13},{... | collective-permute-start | bytes 393224 | tf_op jit(solution)/shard_map/ppermute | solution.py:459
  67.2 3.9 %collective-permute-done.26.refs_4_ = f32[4,2,2,2,1024]{4,3,2,1,0:T(2,128)S(1)} collective-permute-done((f32[4,2,2,2,1024]{4,3,2,1,0:T(2,128)S(1)}, f32[4,2,2,2,1024]{4,3,2,1,0:T(2,128)S(1)}, u32[]{:S(2)}, u32[]{:S(2)}) %collective-permute-start.26) | collective-permute-done | bytes 131104 | tf_op jit(solution)/shard_map/ppermute | solution.py:459
  71.1 1.8 %collective-permute-start.28 = (f32[4,2,2,2,1024]{4,3,2,1,0:T(2,128)S(1)}, f32[4,2,2,2,1024]{4,3,2,1,0:T(2,128)S(1)}, u32[]{:S(2)}, u32[]{:S(2)}) collective-permute-start(f32[4,2,2,2,1024]{4,3,2,1,0:T(2,128)S(1)} %collective-permute-done.26.refs_4_), channel_id=1, source_target_pairs={{0,8},{4,12},{8,0},{12,4},{16,24},{20,28},{24,16},{28,20},{1,9},{5... | collective-permute-start | bytes 393224 | tf_op jit(solution)/shard_map/ppermute | solution.py:459
  72.9 1.7 %collective-permute-start.27 = (f32[4,2,2,2,1024]{4,3,2,1,0:T(2,128)S(1)}, f32[4,2,2,2,1024]{4,3,2,1,0:T(2,128)S(1)}, u32[]{:S(2)}, u32[]{:S(2)}) collective-permute-start(f32[4,2,2,2,1024]{4,3,2,1,0:T(2,128)S(1)} %collective-permute-done.26.refs_4_), channel_id=1, source_target_pairs={{0,4},{4,0},{8,12},{12,8},{16,20},{20,16},{24,28},{28,24},{1,5},{5... | collective-permute-start | bytes 393224 | tf_op jit(solution)/shard_map/ppermute | solution.py:459
  75.8 2.6 %collective-permute-done.29.refs_2_ = f32[4,2,2,2,1024]{4,3,2,1,0:T(2,128)S(1)} collective-permute-done((f32[4,2,2,2,1024]{4,3,2,1,0:T(2,128)S(1)}, f32[4,2,2,2,1024]{4,3,2,1,0:T(2,128)S(1)}, u32[]{:S(2)}, u32[]{:S(2)}) %collective-permute-start.29) | collective-permute-done | bytes 131104 | tf_op jit(solution)/shard_map/ppermute | solution.py:459
  79.9 1.7 %shard_map.107 = (f32[8,4,2,2,2,1024]{5,4,3,2,1,0:T(2,128)}, f32[4,2,2,2,1024]{4,3,2,1,0:T(2,128)}) custom-call(f32[1,8]{1,0:T(1,128)S(1)} %copy-done.5, f32[8,8]{1,0:T(8,128)S(1)} %get-tuple-element.41.weights_ref, f32[4,2,2,2,1024]{4,3,2,1,0:T(2,128)S(1)} %get-tuple-element.42.refs_0_.own_ref, f32[8,4,2,2,2,1024]{5,4,3,2,1,0:T(2,128)S(1)} %shard_map.106.partial_ref, ...), custom_call_target="tpu_custom_call" | custom-call | tf_op jit(solution)/shard_map/pallas_call | solution.py:447
  (60 shorter events, 13.1 us)
Async XLA Ops:
  0.6 11.1 %copy-start.2 = (f32[8,4,2,2,2,1024]{5,4,3,2,1,0:T(2,128)S(1)}, f32[8,4,2,2,2,1024]{5,4,3,2,1,0:T(2,128)}, u32[]{:S(2)}) copy-start(f32[8,4,2,2,2,1024]{5,4,3,2,1,0:T(2,128)} %coeffs_ref.1) | copy-start | bytes 3145732
  0.7 11.1 %copy-start.4 = (f32[1,4,2,2,2,1024]{5,4,3,2,1,0:T(2,128)S(1)}, f32[1,4,2,2,2,1024]{5,4,3,2,1,0:T(2,128)}, u32[]{:S(2)}) copy-start(f32[1,4,2,2,2,1024]{5,4,3,2,1,0:T(2,128)} %param.10) | copy-start | bytes 393220
  3.3 1.5 %collective-permute-start = (f32[2,2,16,512]{3,2,1,0:T(8,128)S(1)}, f32[2,2,16,512]{3,2,1,0:T(8,128)S(1)}, u32[]{:S(2)}, u32[]{:S(2)}) collective-permute-start(f32[2,2,16,512]{3,2,1,0:T(8,128)S(1)} %get-tuple-element.26), channel_id=1, source_target_pairs={{0,1},{1,0},{2,3},{3,2},{4,5},{5,4},{6,7},{7,6},{8,9},{9,8},{10,11... | collective-permute-start | bytes 393224 | tf_op jit(solution)/shard_map/ppermute | solution.py:459
  4.9 6.7 %collective-permute-start.1 = (f32[2,2,16,512]{3,2,1,0:T(8,128)S(1)}, f32[2,2,16,512]{3,2,1,0:T(8,128)S(1)}, u32[]{:S(2)}, u32[]{:S(2)}) collective-permute-start(f32[2,2,16,512]{3,2,1,0:T(8,128)S(1)} %add.23), channel_id=1, source_target_pairs={{0,2},{1,3},{2,0},{3,1},{4,6},{5,7},{6,4},{7,5},{8,10},{9,11},{10,... | collective-permute-start | bytes 393224 | tf_op jit(solution)/shard_map/ppermute | solution.py:459
  11.6 1.4 %collective-permute-start.2 = (f32[2,2,16,512]{3,2,1,0:T(8,128)S(1)}, f32[2,2,16,512]{3,2,1,0:T(8,128)S(1)}, u32[]{:S(2)}, u32[]{:S(2)}) collective-permute-start(f32[2,2,16,512]{3,2,1,0:T(8,128)S(1)} %add.24.mine_ref), channel_id=1, source_target_pairs={{0,1},{1,0},{2,3},{3,2},{4,5},{5,4},{6,7},{7,6},{8,9},{9,8},{10,11... | collective-permute-start | bytes 393224 | tf_op jit(solution)/shard_map/ppermute | solution.py:459
  16.7 1.4 %collective-permute-start.3 = (f32[2,2,16,512]{3,2,1,0:T(8,128)S(1)}, f32[2,2,16,512]{3,2,1,0:T(8,128)S(1)}, u32[]{:S(2)}, u32[]{:S(2)}) collective-permute-start(f32[2,2,16,512]{3,2,1,0:T(8,128)S(1)} %get-tuple-element.32), channel_id=1, source_target_pairs={{0,1},{1,0},{2,3},{3,2},{4,5},{5,4},{6,7},{7,6},{8,9},{9,8},{10,11... | collective-permute-start | bytes 393224 | tf_op jit(solution)/shard_map/ppermute | solution.py:459
  18.2 6.9 %collective-permute-start.4 = (f32[2,2,16,512]{3,2,1,0:T(8,128)S(1)}, f32[2,2,16,512]{3,2,1,0:T(8,128)S(1)}, u32[]{:S(2)}, u32[]{:S(2)}) collective-permute-start(f32[2,2,16,512]{3,2,1,0:T(8,128)S(1)} %add.25), channel_id=1, source_target_pairs={{0,2},{1,3},{2,0},{3,1},{4,6},{5,7},{6,4},{7,5},{8,10},{9,11},{10,... | collective-permute-start | bytes 393224 | tf_op jit(solution)/shard_map/ppermute | solution.py:459
  20.0 9.3 %collective-permute-start.9 = (f32[264,128]{1,0:T(8,128)S(1)}, f32[264,128]{1,0:T(8,128)S(1)}, u32[]{:S(2)}, u32[]{:S(2)}) collective-permute-start(f32[264,128]{1,0:T(8,128)S(1)} %get-tuple-element.33.refs_0_), channel_id=1, source_target_pairs={{0,16},{4,20},{8,24},{12,28},{16,0},{20,4},{24,8},{28,12},{1,17},{... | collective-permute-start | bytes 405512 | tf_op jit(solution)/shard_map/ppermute | solution.py:459
  22.6 8.5 %collective-permute-start.8 = (f32[264,128]{1,0:T(8,128)S(1)}, f32[264,128]{1,0:T(8,128)S(1)}, u32[]{:S(2)}, u32[]{:S(2)}) collective-permute-start(f32[264,128]{1,0:T(8,128)S(1)} %get-tuple-element.33.refs_0_), channel_id=1, source_target_pairs={{0,12},{4,8},{8,4},{12,0},{16,28},{20,24},{24,20},{28,16},{1,13},{... | collective-permute-start | bytes 405512 | tf_op jit(solution)/shard_map/ppermute | solution.py:459
  25.1 7.8 %collective-permute-start.5 = (f32[2,2,16,512]{3,2,1,0:T(8,128)S(1)}, f32[2,2,16,512]{3,2,1,0:T(8,128)S(1)}, u32[]{:S(2)}, u32[]{:S(2)}) collective-permute-start(f32[2,2,16,512]{3,2,1,0:T(8,128)S(1)} %add.26.mine_ref), channel_id=1, source_target_pairs={{0,1},{1,0},{2,3},{3,2},{4,5},{5,4},{6,7},{7,6},{8,9},{9,8},{10,11... | collective-permute-start | bytes 393224 | tf_op jit(solution)/shard_map/ppermute | solution.py:459
  25.2 10.2 %collective-permute-start.7 = (f32[264,128]{1,0:T(8,128)S(1)}, f32[264,128]{1,0:T(8,128)S(1)}, u32[]{:S(2)}, u32[]{:S(2)}) collective-permute-start(f32[264,128]{1,0:T(8,128)S(1)} %get-tuple-element.33.refs_0_), channel_id=1, source_target_pairs={{0,8},{4,12},{8,0},{12,4},{16,24},{20,28},{24,16},{28,20},{1,9},{5... | collective-permute-start | bytes 405512 | tf_op jit(solution)/shard_map/ppermute | solution.py:459
  25.8 9.6 %collective-permute-start.6 = (f32[264,128]{1,0:T(8,128)S(1)}, f32[264,128]{1,0:T(8,128)S(1)}, u32[]{:S(2)}, u32[]{:S(2)}) collective-permute-start(f32[264,128]{1,0:T(8,128)S(1)} %get-tuple-element.33.refs_0_), channel_id=1, source_target_pairs={{0,4},{4,0},{8,12},{12,8},{16,20},{20,16},{24,28},{28,24},{1,5},{5... | collective-permute-start | bytes 405512 | tf_op jit(solution)/shard_map/ppermute | solution.py:459
  29.2 7.7 %collective-permute-start.12 = (f32[264,128]{1,0:T(8,128)S(1)}, f32[264,128]{1,0:T(8,128)S(1)}, u32[]{:S(2)}, u32[]{:S(2)}) collective-permute-start(f32[264,128]{1,0:T(8,128)S(1)} %collective-permute-done.9.refs_4_), channel_id=1, source_target_pairs={{0,12},{4,8},{8,4},{12,0},{16,28},{20,24},{24,20},{28,16},{1,13},{... | collective-permute-start | bytes 405512 | tf_op jit(solution)/shard_map/ppermute | solution.py:459
  31.1 8.0 %collective-permute-start.11 = (f32[264,128]{1,0:T(8,128)S(1)}, f32[264,128]{1,0:T(8,128)S(1)}, u32[]{:S(2)}, u32[]{:S(2)}) collective-permute-start(f32[264,128]{1,0:T(8,128)S(1)} %collective-permute-done.9.refs_4_), channel_id=1, source_target_pairs={{0,8},{4,12},{8,0},{12,4},{16,24},{20,28},{24,16},{28,20},{1,9},{5... | collective-permute-start | bytes 405512 | tf_op jit(solution)/shard_map/ppermute | solution.py:459
  32.9 6.2 %collective-permute-start.10 = (f32[264,128]{1,0:T(8,128)S(1)}, f32[264,128]{1,0:T(8,128)S(1)}, u32[]{:S(2)}, u32[]{:S(2)}) collective-permute-start(f32[264,128]{1,0:T(8,128)S(1)} %collective-permute-done.9.refs_4_), channel_id=1, source_target_pairs={{0,4},{4,0},{8,12},{12,8},{16,20},{20,16},{24,28},{28,24},{1,5},{5... | collective-permute-start | bytes 405512 | tf_op jit(solution)/shard_map/ppermute | solution.py:459
  41.7 1.4 %collective-permute-start.13 = (f32[2,2,16,512]{3,2,1,0:T(8,128)S(1)}, f32[2,2,16,512]{3,2,1,0:T(8,128)S(1)}, u32[]{:S(2)}, u32[]{:S(2)}) collective-permute-start(f32[2,2,16,512]{3,2,1,0:T(8,128)S(1)} %get-tuple-element.38), channel_id=1, source_target_pairs={{0,1},{1,0},{2,3},{3,2},{4,5},{5,4},{6,7},{7,6},{8,9},{9,8},{10,11... | collective-permute-start | bytes 393224 | tf_op jit(solution)/shard_map/ppermute | solution.py:459
  43.1 5.8 %collective-permute-start.14 = (f32[2,2,16,512]{3,2,1,0:T(8,128)S(1)}, f32[2,2,16,512]{3,2,1,0:T(8,128)S(1)}, u32[]{:S(2)}, u32[]{:S(2)}) collective-permute-start(f32[2,2,16,512]{3,2,1,0:T(8,128)S(1)} %add.27), channel_id=1, source_target_pairs={{0,2},{1,3},{2,0},{3,1},{4,6},{5,7},{6,4},{7,5},{8,10},{9,11},{10,... | collective-permute-start | bytes 393224 | tf_op jit(solution)/shard_map/ppermute | solution.py:459
  43.7 9.1 %collective-permute-start.19 = (f32[256,128]{1,0:T(8,128)S(1)}, f32[256,128]{1,0:T(8,128)S(1)}, u32[]{:S(2)}, u32[]{:S(2)}) collective-permute-start(f32[256,128]{1,0:T(8,128)S(1)} %get-tuple-element.39.refs_0_.own_ref), channel_id=1, source_target_pairs={{0,16},{4,20},{8,24},{12,28},{16,0},{20,4},{24,8},{28,12},{1,17},{... | collective-permute-start | bytes 393224 | tf_op jit(solution)/shard_map/ppermute | solution.py:459
  45.4 9.4 %collective-permute-start.18 = (f32[256,128]{1,0:T(8,128)S(1)}, f32[256,128]{1,0:T(8,128)S(1)}, u32[]{:S(2)}, u32[]{:S(2)}) collective-permute-start(f32[256,128]{1,0:T(8,128)S(1)} %get-tuple-element.39.refs_0_.own_ref), channel_id=1, source_target_pairs={{0,12},{4,8},{8,4},{12,0},{16,28},{20,24},{24,20},{28,16},{1,13},{... | collective-permute-start | bytes 393224 | tf_op jit(solution)/shard_map/ppermute | solution.py:459
  48.1 7.9 %collective-permute-start.17 = (f32[256,128]{1,0:T(8,128)S(1)}, f32[256,128]{1,0:T(8,128)S(1)}, u32[]{:S(2)}, u32[]{:S(2)}) collective-permute-start(f32[256,128]{1,0:T(8,128)S(1)} %get-tuple-element.39.refs_0_.own_ref), channel_id=1, source_target_pairs={{0,8},{4,12},{8,0},{12,4},{16,24},{20,28},{24,16},{28,20},{1,9},{5... | collective-permute-start | bytes 393224 | tf_op jit(solution)/shard_map/ppermute | solution.py:459
  48.4 9.9 %collective-permute-start.16 = (f32[256,128]{1,0:T(8,128)S(1)}, f32[256,128]{1,0:T(8,128)S(1)}, u32[]{:S(2)}, u32[]{:S(2)}) collective-permute-start(f32[256,128]{1,0:T(8,128)S(1)} %get-tuple-element.39.refs_0_.own_ref), channel_id=1, source_target_pairs={{0,4},{4,0},{8,12},{12,8},{16,20},{20,16},{24,28},{28,24},{1,5},{5... | collective-permute-start | bytes 393224 | tf_op jit(solution)/shard_map/ppermute | solution.py:459
  49.0 9.4 %collective-permute-start.15 = (f32[2,2,16,512]{3,2,1,0:T(8,128)S(1)}, f32[2,2,16,512]{3,2,1,0:T(8,128)S(1)}, u32[]{:S(2)}, u32[]{:S(2)}) collective-permute-start(f32[2,2,16,512]{3,2,1,0:T(8,128)S(1)} %add.28.mine_ref), channel_id=1, source_target_pairs={{0,1},{1,0},{2,3},{3,2},{4,5},{5,4},{6,7},{7,6},{8,9},{9,8},{10,11... | collective-permute-start | bytes 393224 | tf_op jit(solution)/shard_map/ppermute | solution.py:459
  52.7 8.1 %collective-permute-start.22 = (f32[256,128]{1,0:T(8,128)S(1)}, f32[256,128]{1,0:T(8,128)S(1)}, u32[]{:S(2)}, u32[]{:S(2)}) collective-permute-start(f32[256,128]{1,0:T(8,128)S(1)} %collective-permute-done.19.refs_4_), channel_id=1, source_target_pairs={{0,12},{4,8},{8,4},{12,0},{16,28},{20,24},{24,20},{28,16},{1,13},{... | collective-permute-start | bytes 393224 | tf_op jit(solution)/shard_map/ppermute | solution.py:459
  54.9 6.8 %collective-permute-start.21 = (f32[256,128]{1,0:T(8,128)S(1)}, f32[256,128]{1,0:T(8,128)S(1)}, u32[]{:S(2)}, u32[]{:S(2)}) collective-permute-start(f32[256,128]{1,0:T(8,128)S(1)} %collective-permute-done.19.refs_4_), channel_id=1, source_target_pairs={{0,8},{4,12},{8,0},{12,4},{16,24},{20,28},{24,16},{28,20},{1,9},{5... | collective-permute-start | bytes 393224 | tf_op jit(solution)/shard_map/ppermute | solution.py:459
  56.0 6.2 %collective-permute-start.20 = (f32[256,128]{1,0:T(8,128)S(1)}, f32[256,128]{1,0:T(8,128)S(1)}, u32[]{:S(2)}, u32[]{:S(2)}) collective-permute-start(f32[256,128]{1,0:T(8,128)S(1)} %collective-permute-done.19.refs_4_), channel_id=1, source_target_pairs={{0,4},{4,0},{8,12},{12,8},{16,20},{20,16},{24,28},{28,24},{1,5},{5... | collective-permute-start | bytes 393224 | tf_op jit(solution)/shard_map/ppermute | solution.py:459
  62.5 8.6 %collective-permute-start.26 = (f32[4,2,2,2,1024]{4,3,2,1,0:T(2,128)S(1)}, f32[4,2,2,2,1024]{4,3,2,1,0:T(2,128)S(1)}, u32[]{:S(2)}, u32[]{:S(2)}) collective-permute-start(f32[4,2,2,2,1024]{4,3,2,1,0:T(2,128)S(1)} %get-tuple-element.42.refs_0_.own_ref), channel_id=1, source_target_pairs={{0,16},{4,20},{8,24},{12,28},{16,0},{20,4},{24,8},{28,12},{1,17},{... | collective-permute-start | bytes 393224 | tf_op jit(solution)/shard_map/ppermute | solution.py:459
  63.7 9.2 %collective-permute-start.25 = (f32[4,2,2,2,1024]{4,3,2,1,0:T(2,128)S(1)}, f32[4,2,2,2,1024]{4,3,2,1,0:T(2,128)S(1)}, u32[]{:S(2)}, u32[]{:S(2)}) collective-permute-start(f32[4,2,2,2,1024]{4,3,2,1,0:T(2,128)S(1)} %get-tuple-element.42.refs_0_.own_ref), channel_id=1, source_target_pairs={{0,12},{4,8},{8,4},{12,0},{16,28},{20,24},{24,20},{28,16},{1,13},{... | collective-permute-start | bytes 393224 | tf_op jit(solution)/shard_map/ppermute | solution.py:459
  66.3 9.0 %collective-permute-start.24 = (f32[4,2,2,2,1024]{4,3,2,1,0:T(2,128)S(1)}, f32[4,2,2,2,1024]{4,3,2,1,0:T(2,128)S(1)}, u32[]{:S(2)}, u32[]{:S(2)}) collective-permute-start(f32[4,2,2,2,1024]{4,3,2,1,0:T(2,128)S(1)} %get-tuple-element.42.refs_0_.own_ref), channel_id=1, source_target_pairs={{0,8},{4,12},{8,0},{12,4},{16,24},{20,28},{24,16},{28,20},{1,9},{5... | collective-permute-start | bytes 393224 | tf_op jit(solution)/shard_map/ppermute | solution.py:459
  66.3 9.0 %collective-permute-start.23 = (f32[4,2,2,2,1024]{4,3,2,1,0:T(2,128)S(1)}, f32[4,2,2,2,1024]{4,3,2,1,0:T(2,128)S(1)}, u32[]{:S(2)}, u32[]{:S(2)}) collective-permute-start(f32[4,2,2,2,1024]{4,3,2,1,0:T(2,128)S(1)} %get-tuple-element.42.refs_0_.own_ref), channel_id=1, source_target_pairs={{0,4},{4,0},{8,12},{12,8},{16,20},{20,16},{24,28},{28,24},{1,5},{5... | collective-permute-start | bytes 393224 | tf_op jit(solution)/shard_map/ppermute | solution.py:459
  71.1 7.3 %collective-permute-start.29 = (f32[4,2,2,2,1024]{4,3,2,1,0:T(2,128)S(1)}, f32[4,2,2,2,1024]{4,3,2,1,0:T(2,128)S(1)}, u32[]{:S(2)}, u32[]{:S(2)}) collective-permute-start(f32[4,2,2,2,1024]{4,3,2,1,0:T(2,128)S(1)} %collective-permute-done.26.refs_4_), channel_id=1, source_target_pairs={{0,12},{4,8},{8,4},{12,0},{16,28},{20,24},{24,20},{28,16},{1,13},{... | collective-permute-start | bytes 393224 | tf_op jit(solution)/shard_map/ppermute | solution.py:459
  71.1 8.5 %collective-permute-start.28 = (f32[4,2,2,2,1024]{4,3,2,1,0:T(2,128)S(1)}, f32[4,2,2,2,1024]{4,3,2,1,0:T(2,128)S(1)}, u32[]{:S(2)}, u32[]{:S(2)}) collective-permute-start(f32[4,2,2,2,1024]{4,3,2,1,0:T(2,128)S(1)} %collective-permute-done.26.refs_4_), channel_id=1, source_target_pairs={{0,8},{4,12},{8,0},{12,4},{16,24},{20,28},{24,16},{28,20},{1,9},{5... | collective-permute-start | bytes 393224 | tf_op jit(solution)/shard_map/ppermute | solution.py:459
  72.9 7.0 %collective-permute-start.27 = (f32[4,2,2,2,1024]{4,3,2,1,0:T(2,128)S(1)}, f32[4,2,2,2,1024]{4,3,2,1,0:T(2,128)S(1)}, u32[]{:S(2)}, u32[]{:S(2)}) collective-permute-start(f32[4,2,2,2,1024]{4,3,2,1,0:T(2,128)S(1)} %collective-permute-done.26.refs_4_), channel_id=1, source_target_pairs={{0,4},{4,0},{8,12},{12,8},{16,20},{20,16},{24,28},{28,24},{1,5},{5... | collective-permute-start | bytes 393224 | tf_op jit(solution)/shard_map/ppermute | solution.py:459
  (4 other events, 23.4 us)

commit v6 on v5

--- a/solution.py
+++ b/solution.py
@@ -113,7 +113,7 @@
     dirs = coher_ref.shape[0]
     times, baselines = coher_ref.shape[-2:]
     gathered_ref[...] = split_dot(jones, onehot_ref[...], ((1,), (0,)))
-    first = parity_ref[0, 0] == 0
+    first = parity_ref[...] == 0
     for base in range(0, baselines, LANES):
         lanes = slice(base, base + LANES)
         for time in range(0, times, SUBLANES):
@@ -160,27 +160,11 @@
     model_body(parity_ref, jones_ref[...], onehot_ref, coher_ref, gathered_ref, mine_ref, other_ref)
 
 
-def sums_kernel(
-    parity_ref, gathered_ref, pairs_ref, coher_ref, vis_ref, mine_ref, other_ref, sums_ref, onehot_ref, left_ref
-):
+def reduced_terms(gathered_ref, coher_ref, left_ref, terms_of):
     dirs = coher_ref.shape[0]
     times, baselines = coher_ref.shape[-2:]
-    fill_onehot(pairs_ref, onehot_ref)
-    first = parity_ref[0, 0] == 0
     for base in range(0, baselines, LANES):
         lanes = slice(base, base + LANES)
-        resid = []
-        for time in range(0, times, SUBLANES):
-            rows = slice(time, time + SUBLANES)
-            piece = {}
-            for i, j in INDEX:
-                mine = mine_ref[i, j, rows, lanes]
-                other = other_ref[i, j, rows, lanes]
-                piece[i, j] = (
-                    vis_ref[0, i, j, rows, lanes] - jnp.where(first, mine, other),
-                    vis_ref[1, i, j, rows, lanes] - jnp.where(first, other, mine),
-                )
-            resid.append(piece)
         for k in range(dirs):
             jones_p = read_rows(gathered_ref, dirs, k, base, LANES)
             jones_q = read_rows(gathered_ref, dirs, k, baselines + base, LANES)
@@ -188,37 +172,41 @@
             for index, time in enumerate(range(0, times, SUBLANES)):
                 rows = slice(time, time + SUBLANES)
                 coher = {(i, j): tuple(coher_ref[k, part, i, j, rows, lanes] for part in range(2)) for i, j in INDEX}
-                along = mat_mul_h(coher, jones_q)
-                ahead = mat_mul(jones_p, coher)
-                right_p = mat_mul_h(resid[index], along)
-                right_q = mat_h_mul(resid[index], ahead)
-                cross_p = cadd(cmul_conj(along[0, 0], along[1, 0]), cmul_conj(along[0, 1], along[1, 1]))
-                cross_q = cadd(cmul_conj(ahead[0, 1], ahead[0, 0]), cmul_conj(ahead[1, 1], ahead[1, 0]))
-                terms_p = [right_p[ij][part] for part in range(2) for ij in INDEX] + [
-                    sq(along[0, 0]) + sq(along[0, 1]),
-                    sq(along[1, 0]) + sq(along[1, 1]),
-                    cross_p[0],
-                    cross_p[1],
-                ]
-                terms_q = [right_q[ij][part] for part in range(2) for ij in INDEX] + [
-                    sq(ahead[0, 0]) + sq(ahead[1, 0]),
-                    sq(ahead[0, 1]) + sq(ahead[1, 1]),
-                    cross_q[0],
-                    cross_q[1],
-                ]
-                terms = terms_p + terms_q
+                terms = terms_of(mat_mul_h(coher, jones_q), mat_mul(jones_p, coher), base, index)
                 sums = terms if sums is None else [a + b for a, b in zip(sums, terms)]
+            count = len(sums) // 2
             for at, term in enumerate(sums):
-                row = (at % 12) * dirs + k
-                offset = base + (at // 12) * baselines
+                row = (at % count) * dirs + k
+                offset = base + (at // count) * baselines
                 left_ref[row : row + 1, offset : offset + LANES] = jnp.sum(term, axis=0, keepdims=True)
+
+
+def normal_kernel(gathered_ref, pairs_ref, coher_ref, base_ref, onehot_ref, normal_ref, left_ref):
+    dirs = coher_ref.shape[0]
+    fill_onehot(pairs_ref, onehot_ref)
+
+    def terms_of(along, ahead, base, index):
+        cross_p = cadd(cmul_conj(along[0, 0], along[1, 0]), cmul_conj(along[0, 1], along[1, 1]))
+        cross_q = cadd(cmul_conj(ahead[0, 1], ahead[0, 0]), cmul_conj(ahead[1, 1], ahead[1, 0]))
+        return [
+            sq(along[0, 0]) + sq(along[0, 1]),
+            sq(along[1, 0]) + sq(along[1, 1]),
+            cross_p[0],
+            cross_p[1],
+            sq(ahead[0, 0]) + sq(ahead[1, 0]),
+            sq(ahead[0, 1]) + sq(ahead[1, 1]),
+            cross_q[0],
+            cross_q[1],
+        ]
+
+    reduced_terms(gathered_ref, coher_ref, normal_ref, terms_of)
 
     def group(ref, at):
         return ref[at * dirs : (at + 1) * dirs, :]
 
     jones = {(i, j): (group(gathered_ref, comp(0, i, j)), group(gathered_ref, comp(1, i, j))) for i, j in INDEX}
-    diag0, diag1 = group(left_ref, 8), group(left_ref, 9)
-    off = (group(left_ref, 10), group(left_ref, 11))
+    diag0, diag1 = group(normal_ref, 0), group(normal_ref, 1)
+    off = (group(normal_ref, 2), group(normal_ref, 3))
     off_c = (off[0], -off[1])
     for i in range(2):
         left, right = jones[i, 0], jones[i, 1]
@@ -227,18 +215,58 @@
         for j, col in ((0, col0), (1, col1)):
             for part in range(2):
                 at = comp(part, i, j) * dirs
-                left_ref[at : at + dirs, :] = left_ref[at : at + dirs, :] + col[part]
-
+                left_ref[at : at + dirs, :] = col[part]
+    left_ref[8 * dirs :, :] = normal_ref[...]
     sums = split_dot(left_ref[...], onehot_ref[...], ((1,), (1,)))
-    store_chunks(sums_ref, 0, sums[: 8 * dirs])
+    store_chunks(base_ref, 0, sums[: 8 * dirs])
     m00 = sums[8 * dirs : 9 * dirs] + RHO
     m11 = sums[9 * dirs : 10 * dirs] + RHO
     m01 = (sums[10 * dirs : 11 * dirs], sums[11 * dirs : 12 * dirs])
     scale = 1.0 / (m00 * m11 - sq(m01))
-    store_chunks(sums_ref, 8 * dirs, m11 * scale)
-    store_chunks(sums_ref, 9 * dirs, m00 * scale)
-    store_chunks(sums_ref, 10 * dirs, -m01[0] * scale)
-    store_chunks(sums_ref, 11 * dirs, -m01[1] * scale)
+    store_chunks(base_ref, 8 * dirs, m11 * scale)
+    store_chunks(base_ref, 9 * dirs, m00 * scale)
+    store_chunks(base_ref, 10 * dirs, -m01[0] * scale)
+    store_chunks(base_ref, 11 * dirs, -m01[1] * scale)
+
+
+def right_kernel(
+    parity_ref, gathered_ref, pairs_ref, coher_ref, vis_ref, mine_ref, other_ref, base_ref, sums_ref,
+    onehot_ref, left_ref,
+):
+    dirs = coher_ref.shape[0]
+    fill_onehot(pairs_ref, onehot_ref)
+    first = parity_ref[...] == 0
+
+    def residual(base, index):
+        lanes = slice(base, base + LANES)
+        rows = slice(index * SUBLANES, (index + 1) * SUBLANES)
+        piece = {}
+        for i, j in INDEX:
+            mine = mine_ref[i, j, rows, lanes]
+            other = other_ref[i, j, rows, lanes]
+            piece[i, j] = (
+                vis_ref[0, i, j, rows, lanes] - jnp.where(first, mine, other),
+                vis_ref[1, i, j, rows, lanes] - jnp.where(first, other, mine),
+            )
+        return piece
+
+    kept = {}
+
+    def terms_of(along, ahead, base, index):
+        if (base, index) not in kept:
+            kept[base, index] = residual(base, index)
+        piece = kept[base, index]
+        right_p = mat_mul_h(piece, along)
+        right_q = mat_h_mul(piece, ahead)
+        return [side[ij][part] for side in (right_p, right_q) for part in range(2) for ij in INDEX]
+
+    reduced_terms(gathered_ref, coher_ref, left_ref, terms_of)
+    sums = split_dot(left_ref[...], onehot_ref[...], ((1,), (1,)))
+    rows, width = 8 * dirs, sums_ref.shape[2]
+    for chunk in range(sums_ref.shape[0]):
+        part = sums[:, chunk * width : (chunk + 1) * width]
+        sums_ref[chunk, :rows, :] = base_ref[chunk, :rows, :] + part
+        sums_ref[chunk, rows:, :] = base_ref[chunk, rows:, :]
 
 
 def solve(sums, known, dirs):
@@ -427,7 +455,7 @@
                 for m in range(terms):
                     total = partial_ref[m, k, part, i] + weighted(weights, m, values)
                     coeffs_ref[m, k, part, i] = total
-                    share = total * basis_ref[0, m]
+                    share = total * jnp.broadcast_to(basis_ref[0:1, m : m + 1], total.shape)
                     consensus = share if consensus is None else consensus + share
                 dual_ref[k, part, i] = RHO * (own_ref[k, part, i] - consensus)
         copies.append(pltpu.make_async_copy(coeffs_ref.at[:, k], coeffs_hbm.at[:, k], sems.at[k]))
@@ -442,12 +470,12 @@
     return jax.ShapeDtypeStruct(shape, dtype)
 
 
-def call(kernel, out_shape, scalars, args, scratch=(), space=VMEM, out_space=VMEM):
+def call(kernel, out_shape, first, args, scratch=(), space=VMEM, out_space=VMEM):
     many = isinstance(out_shape, (tuple, list))
     return pl.pallas_call(
         kernel,
         out_shape=out_shape,
-        in_specs=[SMEM if at < scalars else space for at in range(len(args))],
+        in_specs=[space if at else first for at in range(len(args))],
         out_specs=tuple(out_space for _ in out_shape) if many else out_space,
         scratch_shapes=list(scratch),
         compiler_params=PARAMS,
@@ -464,7 +492,8 @@
     mine = mine + swap(other, "dir", 1)
     bit = 2
     while bit < size:
-        mine = mine + swap(mine, "dir", bit)
+        far = swap(mine, "dir", bit)
+        mine = mine + far
         bit *= 2
     return mine, swap(mine, "dir", 1)
 
@@ -496,7 +525,7 @@
     dirs, stations = native[0], native[-1]
     times, baselines = coher.shape[-2:]
     rows = 8 * dirs
-    parity = (lax.axis_index("dir") % 2).astype(jnp.int32).reshape(1, 1)
+    parity = jnp.broadcast_to((lax.axis_index("dir") % 2).astype(jnp.int32), (SUBLANES, LANES))
     chunked = stations % (bands * LANES) == 0 and bands > 2 and bands & (bands - 1) == 0
     hi = lax.Precision.HIGHEST
     width = stations // bands if chunked else LANES
@@ -513,13 +542,18 @@
         factor = jnp.linalg.cholesky(gram)
 
     def model(jones):
-        return call(model_kernel, model_out, 1, (parity, jones, pairs, coher), [onehot])
+        return call(model_kernel, model_out, VMEM, (parity, jones, pairs, coher), [onehot])
 
     def station_sums(gathered, mine, other):
+        base = call(
+            normal_kernel, struct(chunks, 12 * dirs, width), VMEM, (gathered, pairs, coher),
+            [onehot, pltpu.VMEM((4 * dirs, 2 * baselines), jnp.float32), left],
+        )
         mine, other = sum_over_dir(mine, other)
         return call(
-            sums_kernel, struct(chunks, 12 * dirs, width), 1,
-            (parity, gathered, pairs, coher, vis, mine, other), [onehot, left],
+            right_kernel, struct(chunks, 12 * dirs, width), VMEM,
+            (parity, gathered, pairs, coher, vis, mine, other, base),
+            [onehot, pltpu.VMEM((rows, 2 * baselines), jnp.float32)],
         )
 
     def share(shared):
@@ -527,7 +561,7 @@
         return coeffs, jnp.tensordot(row, coeffs, axes=(0, 0), precision=hi)
 
     started = call(
-        first_model_kernel, model_out, 1,
+        first_model_kernel, model_out, VMEM,
         (parity, *(pltpu.with_memory_space_constraint(x, pltpu.HBM) for x in (jones_start[0], pairs, coher))),
         [
             onehot,
@@ -539,9 +573,9 @@
         ],
         HBM,
     )
-    known, lag = call(prepare_kernel, (spread_rows,) * 2, 1, (freq_basis, dual_start[0], consensus_start))
+    known, lag = call(prepare_kernel, (spread_rows,) * 2, SMEM, (freq_basis, dual_start[0], consensus_start))
     jones, unit = call(
-        first_update_kernel, (flat, struct(stations * rows // width + SUBLANES, width)), 0,
+        first_update_kernel, (flat, struct(stations * rows // width + SUBLANES, width)), VMEM,
         (freq_basis, station_sums(*started), known, lag),
     )
     if chunked:
@@ -551,20 +585,20 @@
         sums = station_sums(*started)
         jones, unit, spread, weights = call(
             gathered_update_kernel,
-            (flat, struct(chunks * rows, width), struct(bands, bands), struct(terms, bands)), 0, (sums, *units),
+            (flat, struct(chunks * rows, width), struct(bands, bands), struct(terms, bands)), VMEM, (sums, *units),
         )
         units = gather_bands(unit)
         started = model(jones)
         sums = station_sums(*started)
-        partial = call(partial_consensus_kernel, struct(chunks * rows, width), 0, (spread, *units[:early]))
+        partial = call(partial_consensus_kernel, struct(chunks * rows, width), VMEM, (spread, *units[:early]))
         jones, shared = call(
-            gathered_last_kernel, (flat, struct(*native)), 0, (spread, sums, unit, partial, *units[early:])
-        )
-        jones = call(native_kernel, struct(*native), 0, (jones,))
+            gathered_last_kernel, (flat, struct(*native)), VMEM, (spread, sums, unit, partial, *units[early:])
+        )
+        jones = call(native_kernel, struct(*native), VMEM, (jones,))
         units = gather_bands(shared)
-        partial = call(partial_coeffs_kernel, struct(terms, *native), 0, (weights, *units[:early]))
+        partial = call(partial_coeffs_kernel, struct(terms, *native), VMEM, (weights, *units[:early]))
         coeffs, dual = call(
-            final_kernel, (struct(terms, *native), struct(*native)), 1,
+            final_kernel, (struct(terms, *native), struct(*native)), VMEM,
             (freq_basis, weights, shared, partial, *units[early:]),
             [
                 pltpu.VMEM((terms, *native), jnp.float32),
@@ -578,10 +612,10 @@
         for _ in range(ITERS - 2):
             consensus = share(shared)[1]
             sums = station_sums(*model(jones))
-            jones, shared = call(update_kernel, (flat, spread_rows), 0, (sums, consensus, shared))
+            jones, shared = call(update_kernel, (flat, spread_rows), VMEM, (sums, consensus, shared))
         consensus = share(shared)[1]
         sums = station_sums(*model(jones))
-        jones, shared = call(last_update_kernel, (struct(*native),) * 2, 0, (sums, consensus, shared))
+        jones, shared = call(last_update_kernel, (struct(*native),) * 2, VMEM, (sums, consensus, shared))
         coeffs, consensus = share(shared)
         dual = RHO * (shared - consensus)
     return jones[None], dual[None], coeffs

time: 81.8 us -> 81.9 us (level)
  Pallas kernels: 17.6 us -> 20.3 us
  waiting for transfers between devices: 28.6 us -> 26.8 us
  starting transfers between devices: 34.4 us -> 32.6 us
  local copies, waits for them, and re-layouts: 0.03 us -> 0.87 us
    pallas_call x14 -> x17, Pallas kernels: 17.6 us -> 20.3 us  [call(): pl.pallas_call(kernel, out_shape=out_shape, in_specs=[space if at else fi...]
    ppermute x30, starting transfers between devices: 34.4 us -> 32.6 us  [swap(): return lax.ppermute(value, axis, [(i, i ^ bit) for i in range(size)])]
    ppermute x30, waiting for transfers between devices: 28.6 us -> 26.8 us  [swap(): return lax.ppermute(value, axis, [(i, i ^ bit) for i in range(size)])]
    unnamed x12, local copies, waits for them, and re-layouts: 0.03 us -> 0.87 us
  transfers between devices with their start and end apart: 30 -> 30, of which waited for: 18 -> 16; matrix products, arithmetic and copies ran while one was open for 0% -> 0% of each run, Pallas kernels for 8% -> 13%
where the time goes in v6:
time: 81.9 us; the launch traced here: 81.7 us
  starting transfers between devices  32.6 us (40%)
  waiting for transfers between devices  26.8 us (33%)
  Pallas kernels  20.3 us (25%)
  between operations  1.12 us (1%)
  local copies, waits for them, and re-layouts  0.87 us (1%)
    ppermute x30, starting transfers between devices, swap(): return lax.ppermute(value, axis, [(i, i ^ bit) for i in range(size)])  32.6 us
    ppermute x30, waiting for transfers between devices, swap(): return lax.ppermute(value, axis, [(i, i ^ bit) for i in range(size)])  26.8 us
    pallas_call x17, Pallas kernels, call(): pl.pallas_call(kernel, out_shape=out_shape, in_specs=[space if at else fi...  20.3 us
  transfers between devices with their start and end apart: 30, of which 16 were waited for; matrix products, arithmetic and copies ran while one was open for 0% of the time, Pallas kernels for 13%

profile of v6, /device:TPU:0, one launch (start us, length us, event | category | flops | bytes accessed | tf_op | source)
XLA Modules:
  0.0 81.7 jit_solution(7232455988755518667)
XLA Ops:
  0.7 2.6 %shard_map.94 = (f32[32,1024]{1,0:T(8,128)S(1)}, f32[2,2,16,512]{3,2,1,0:T(8,128)S(1)}, f32[2,2,16,512]{3,2,1,0:T(8,128)S(1)}) custom-call(s32[8,128]{1,0:T(8,128)S(1)} %broadcast_in_dim.9.parity_ref, f32[4,2,2,2,1024]{4,3,2,1,0:T(2,128)} %bitcast.19, s32[2,512]{1,0:T(2,128)} %pairs_ref.15, f32[4,2,2,2,16,512]{5,4,3,2,1,0:T(8,128)} %bitcast.6), custom_call_target="tpu_custom_call" | custom-call | tf_op jit(solution)/shard_map/pallas_call | solution.py:475
  4.9 2.9 %collective-permute-start.1 = (f32[2,2,16,512]{3,2,1,0:T(8,128)S(1)}, f32[2,2,16,512]{3,2,1,0:T(8,128)S(1)}, u32[]{:S(2)}, u32[]{:S(2)}) collective-permute-start(f32[2,2,16,512]{3,2,1,0:T(8,128)S(1)} %add.23), channel_id=1, source_target_pairs={{0,2},{1,3},{2,0},{3,1},{4,6},{5,7},{6,4},{7,5},{8,10},{9,11},{10,... | collective-permute-start | bytes 393224 | tf_op jit(solution)/shard_map/ppermute | solution.py:487
  7.8 3.8 %collective-permute-done.1 = f32[2,2,16,512]{3,2,1,0:T(8,128)S(1)} collective-permute-done((f32[2,2,16,512]{3,2,1,0:T(8,128)S(1)}, f32[2,2,16,512]{3,2,1,0:T(8,128)S(1)}, u32[]{:S(2)}, u32[]{:S(2)}) %collective-permute-start.1) | collective-permute-done | bytes 131104 | tf_op jit(solution)/shard_map/ppermute | solution.py:487
  11.7 1.6 %shard_map.95.base_ref = f32[8,48,128]{2,1,0:T(8,128)S(1)} custom-call(f32[32,1024]{1,0:T(8,128)S(1)} %get-tuple-element.24.gathered_ref, s32[2,512]{1,0:T(2,128)S(1)} %copy-done.3, f32[4,2,2,2,16,512]{5,4,3,2,1,0:T(8,128)S(1)} %bitcast.7), custom_call_target="tpu_custom_call" | custom-call | tf_op jit(solution)/shard_map/pallas_call | solution.py:475
  14.9 1.8 %shard_map.96.sums_ref = f32[8,48,128]{2,1,0:T(8,128)S(1)} custom-call(s32[8,128]{1,0:T(8,128)S(1)} %broadcast_in_dim.9.parity_ref, f32[32,1024]{1,0:T(8,128)S(1)} %get-tuple-element.24.gathered_ref, s32[2,512]{1,0:T(2,128)S(1)} %copy-done.3, f32[4,2,2,2,16,512]{5,4,3,2,1,0:T(8,128)S(1)} %bitcast.8, f32[2,2,2,16,512]{4,3,2,1,0:T(8,128)S(1)} %bitcast.15, ...), custom_call_target="tpu_custom_call" | custom-call | tf_op jit(solution)/shard_map/pallas_call | solution.py:475
  16.8 1.2 %shard_map.99 = (f32[32,1024]{1,0:T(8,128)S(1)}, f32[2,2,16,512]{3,2,1,0:T(8,128)S(1)}, f32[2,2,16,512]{3,2,1,0:T(8,128)S(1)}) custom-call(s32[8,128]{1,0:T(8,128)S(1)} %broadcast_in_dim.9.parity_ref, f32[32,1024]{1,0:T(8,128)S(1)} %get-tuple-element.29.jones_ref, s32[2,512]{1,0:T(2,128)S(1)} %copy-done.3, f32[4,2,2,2,16,512]{5,4,3,2,1,0:T(8,128)S(1)} %bitcast.9), custom_call_target="tpu_custom_call" | custom-call | tf_op jit(solution)/shard_map/pallas_call | solution.py:475
  19.6 1.8 %collective-permute-start.4 = (f32[2,2,16,512]{3,2,1,0:T(8,128)S(1)}, f32[2,2,16,512]{3,2,1,0:T(8,128)S(1)}, u32[]{:S(2)}, u32[]{:S(2)}) collective-permute-start(f32[2,2,16,512]{3,2,1,0:T(8,128)S(1)} %add.25), channel_id=1, source_target_pairs={{0,2},{1,3},{2,0},{3,1},{4,6},{5,7},{6,4},{7,5},{8,10},{9,11},{10,... | collective-permute-start | bytes 393224 | tf_op jit(solution)/shard_map/ppermute | solution.py:487
  21.4 2.6 %collective-permute-start.9 = (f32[264,128]{1,0:T(8,128)S(1)}, f32[264,128]{1,0:T(8,128)S(1)}, u32[]{:S(2)}, u32[]{:S(2)}) collective-permute-start(f32[264,128]{1,0:T(8,128)S(1)} %get-tuple-element.33.refs_0_), channel_id=1, source_target_pairs={{0,16},{4,20},{8,24},{12,28},{16,0},{20,4},{24,8},{28,12},{1,17},{... | collective-permute-start | bytes 405512 | tf_op jit(solution)/shard_map/ppermute | solution.py:487
  24.0 2.5 %collective-permute-start.8 = (f32[264,128]{1,0:T(8,128)S(1)}, f32[264,128]{1,0:T(8,128)S(1)}, u32[]{:S(2)}, u32[]{:S(2)}) collective-permute-start(f32[264,128]{1,0:T(8,128)S(1)} %get-tuple-element.33.refs_0_), channel_id=1, source_target_pairs={{0,12},{4,8},{8,4},{12,0},{16,28},{20,24},{24,20},{28,16},{1,13},{... | collective-permute-start | bytes 405512 | tf_op jit(solution)/shard_map/ppermute | solution.py:487
  27.4 1.5 %collective-permute-start.6 = (f32[264,128]{1,0:T(8,128)S(1)}, f32[264,128]{1,0:T(8,128)S(1)}, u32[]{:S(2)}, u32[]{:S(2)}) collective-permute-start(f32[264,128]{1,0:T(8,128)S(1)} %get-tuple-element.33.refs_0_), channel_id=1, source_target_pairs={{0,4},{4,0},{8,12},{12,8},{16,20},{20,16},{24,28},{28,24},{1,5},{5... | collective-permute-start | bytes 405512 | tf_op jit(solution)/shard_map/ppermute | solution.py:487
  28.9 1.9 %collective-permute-done.9.refs_4_ = f32[264,128]{1,0:T(8,128)S(1)} collective-permute-done((f32[264,128]{1,0:T(8,128)S(1)}, f32[264,128]{1,0:T(8,128)S(1)}, u32[]{:S(2)}, u32[]{:S(2)}) %collective-permute-start.9) | collective-permute-done | bytes 135200 | tf_op jit(solution)/shard_map/ppermute | solution.py:487
  30.9 1.6 %collective-permute-start.12 = (f32[264,128]{1,0:T(8,128)S(1)}, f32[264,128]{1,0:T(8,128)S(1)}, u32[]{:S(2)}, u32[]{:S(2)}) collective-permute-start(f32[264,128]{1,0:T(8,128)S(1)} %collective-permute-done.9.refs_4_), channel_id=1, source_target_pairs={{0,12},{4,8},{8,4},{12,0},{16,28},{20,24},{24,20},{28,16},{1,13},{... | collective-permute-start | bytes 405512 | tf_op jit(solution)/shard_map/ppermute | solution.py:487
  32.7 1.7 %collective-permute-start.11 = (f32[264,128]{1,0:T(8,128)S(1)}, f32[264,128]{1,0:T(8,128)S(1)}, u32[]{:S(2)}, u32[]{:S(2)}) collective-permute-start(f32[264,128]{1,0:T(8,128)S(1)} %collective-permute-done.9.refs_4_), channel_id=1, source_target_pairs={{0,8},{4,12},{8,0},{12,4},{16,24},{20,28},{24,16},{28,20},{1,9},{5... | collective-permute-start | bytes 405512 | tf_op jit(solution)/shard_map/ppermute | solution.py:487
  34.6 1.6 %shard_map.100.base_ref = f32[8,48,128]{2,1,0:T(8,128)S(1)} custom-call(f32[32,1024]{1,0:T(8,128)S(1)} %get-tuple-element.30.gathered_ref, s32[2,512]{1,0:T(2,128)S(1)} %copy-done.3, f32[4,2,2,2,16,512]{5,4,3,2,1,0:T(8,128)S(1)} %bitcast.10), custom_call_target="tpu_custom_call" | custom-call | tf_op jit(solution)/shard_map/pallas_call | solution.py:475
  36.2 1.8 %shard_map.101.sums_ref = f32[8,48,128]{2,1,0:T(8,128)S(1)} custom-call(s32[8,128]{1,0:T(8,128)S(1)} %broadcast_in_dim.9.parity_ref, f32[32,1024]{1,0:T(8,128)S(1)} %get-tuple-element.30.gathered_ref, s32[2,512]{1,0:T(2,128)S(1)} %copy-done.3, f32[4,2,2,2,16,512]{5,4,3,2,1,0:T(8,128)S(1)} %bitcast.11, f32[2,2,2,16,512]{4,3,2,1,0:T(8,128)S(1)} %bitcast.16, ...), custom_call_target="tpu_custom_call" | custom-call | tf_op jit(solution)/shard_map/pallas_call | solution.py:475
  38.5 2.2 %collective-permute-done.11.refs_6_ = f32[264,128]{1,0:T(8,128)S(1)} collective-permute-done((f32[264,128]{1,0:T(8,128)S(1)}, f32[264,128]{1,0:T(8,128)S(1)}, u32[]{:S(2)}, u32[]{:S(2)}) %collective-permute-start.11) | collective-permute-done | bytes 135200 | tf_op jit(solution)/shard_map/ppermute | solution.py:487
  40.7 1.4 %shard_map.102 = (f32[32,1024]{1,0:T(8,128)S(1)}, f32[256,128]{1,0:T(8,128)S(1)}, f32[8,8]{1,0:T(8,128)S(1)}, f32[8,8]{1,0:T(8,128)S(1)}) custom-call(f32[8,48,128]{2,1,0:T(8,128)S(1)} %shard_map.101.sums_ref, f32[264,128]{1,0:T(8,128)S(1)} %get-tuple-element.33.refs_0_, f32[264,128]{1,0:T(8,128)S(1)} %collective-permute-done.6.refs_1_, ...), custom_call_target="tpu_custom_call" | custom-call | tf_op jit(solution)/shard_map/pallas_call | solution.py:475
  42.1 1.2 %shard_map.103 = (f32[32,1024]{1,0:T(8,128)S(1)}, f32[2,2,16,512]{3,2,1,0:T(8,128)S(1)}, f32[2,2,16,512]{3,2,1,0:T(8,128)S(1)}) custom-call(s32[8,128]{1,0:T(8,128)S(1)} %broadcast_in_dim.9.parity_ref, f32[32,1024]{1,0:T(8,128)S(1)} %get-tuple-element.35.jones_ref, s32[2,512]{1,0:T(2,128)S(1)} %copy-done.3, f32[4,2,2,2,16,512]{5,4,3,2,1,0:T(8,128)S(1)} %bitcast.12), custom_call_target="tpu_custom_call" | custom-call | tf_op jit(solution)/shard_map/pallas_call | solution.py:475
  43.3 1.8 %collective-permute-start.19 = (f32[256,128]{1,0:T(8,128)S(1)}, f32[256,128]{1,0:T(8,128)S(1)}, u32[]{:S(2)}, u32[]{:S(2)}) collective-permute-start(f32[256,128]{1,0:T(8,128)S(1)} %get-tuple-element.39.refs_0_.own_ref), channel_id=1, source_target_pairs={{0,16},{4,20},{8,24},{12,28},{16,0},{20,4},{24,8},{28,12},{1,17},{... | collective-permute-start | bytes 393224 | tf_op jit(solution)/shard_map/ppermute | solution.py:487
  45.8 2.6 %collective-permute-start.18 = (f32[256,128]{1,0:T(8,128)S(1)}, f32[256,128]{1,0:T(8,128)S(1)}, u32[]{:S(2)}, u32[]{:S(2)}) collective-permute-start(f32[256,128]{1,0:T(8,128)S(1)} %get-tuple-element.39.refs_0_.own_ref), channel_id=1, source_target_pairs={{0,12},{4,8},{8,4},{12,0},{16,28},{20,24},{24,20},{28,16},{1,13},{... | collective-permute-start | bytes 393224 | tf_op jit(solution)/shard_map/ppermute | solution.py:487
  49.2 3.8 %collective-permute-done.19.refs_4_ = f32[256,128]{1,0:T(8,128)S(1)} collective-permute-done((f32[256,128]{1,0:T(8,128)S(1)}, f32[256,128]{1,0:T(8,128)S(1)}, u32[]{:S(2)}, u32[]{:S(2)}) %collective-permute-start.19) | collective-permute-done | bytes 131104 | tf_op jit(solution)/shard_map/ppermute | solution.py:487
  53.2 1.6 %collective-permute-done.18.refs_3_ = f32[256,128]{1,0:T(8,128)S(1)} collective-permute-done((f32[256,128]{1,0:T(8,128)S(1)}, f32[256,128]{1,0:T(8,128)S(1)}, u32[]{:S(2)}, u32[]{:S(2)}) %collective-permute-start.18) | collective-permute-done | bytes 131104 | tf_op jit(solution)/shard_map/ppermute | solution.py:487
  55.5 2.2 %collective-permute-done.17.refs_2_ = f32[256,128]{1,0:T(8,128)S(1)} collective-permute-done((f32[256,128]{1,0:T(8,128)S(1)}, f32[256,128]{1,0:T(8,128)S(1)}, u32[]{:S(2)}, u32[]{:S(2)}) %collective-permute-start.17) | collective-permute-done | bytes 131104 | tf_op jit(solution)/shard_map/ppermute | solution.py:487
  57.7 1.6 %shard_map.104.base_ref = f32[8,48,128]{2,1,0:T(8,128)S(1)} custom-call(f32[32,1024]{1,0:T(8,128)S(1)} %get-tuple-element.36.gathered_ref, s32[2,512]{1,0:T(2,128)S(1)} %copy-done.3, f32[4,2,2,2,16,512]{5,4,3,2,1,0:T(8,128)S(1)} %bitcast.13), custom_call_target="tpu_custom_call" | custom-call | tf_op jit(solution)/shard_map/pallas_call | solution.py:475
  59.4 1.8 %shard_map.105.sums_ref = f32[8,48,128]{2,1,0:T(8,128)S(1)} custom-call(s32[8,128]{1,0:T(8,128)S(1)} %broadcast_in_dim.9.parity_ref, f32[32,1024]{1,0:T(8,128)S(1)} %get-tuple-element.36.gathered_ref, s32[2,512]{1,0:T(2,128)S(1)} %copy-done.3, f32[4,2,2,2,16,512]{5,4,3,2,1,0:T(8,128)S(1)} %bitcast.14, f32[2,2,2,16,512]{4,3,2,1,0:T(8,128)S(1)} %bitcast.17, ...), custom_call_target="tpu_custom_call" | custom-call | tf_op jit(solution)/shard_map/pallas_call | solution.py:475
  62.9 1.5 %collective-permute-start.26 = (f32[4,2,2,2,1024]{4,3,2,1,0:T(2,128)S(1)}, f32[4,2,2,2,1024]{4,3,2,1,0:T(2,128)S(1)}, u32[]{:S(2)}, u32[]{:S(2)}) collective-permute-start(f32[4,2,2,2,1024]{4,3,2,1,0:T(2,128)S(1)} %get-tuple-element.42.refs_0_.own_ref), channel_id=1, source_target_pairs={{0,16},{4,20},{8,24},{12,28},{16,0},{20,4},{24,8},{28,12},{1,17},{... | collective-permute-start | bytes 393224 | tf_op jit(solution)/shard_map/ppermute | solution.py:487
  64.4 2.9 %collective-permute-start.25 = (f32[4,2,2,2,1024]{4,3,2,1,0:T(2,128)S(1)}, f32[4,2,2,2,1024]{4,3,2,1,0:T(2,128)S(1)}, u32[]{:S(2)}, u32[]{:S(2)}) collective-permute-start(f32[4,2,2,2,1024]{4,3,2,1,0:T(2,128)S(1)} %get-tuple-element.42.refs_0_.own_ref), channel_id=1, source_target_pairs={{0,12},{4,8},{8,4},{12,0},{16,28},{20,24},{24,20},{28,16},{1,13},{... | collective-permute-start | bytes 393224 | tf_op jit(solution)/shard_map/ppermute | solution.py:487
  67.3 1.0 %collective-permute-start.23 = (f32[4,2,2,2,1024]{4,3,2,1,0:T(2,128)S(1)}, f32[4,2,2,2,1024]{4,3,2,1,0:T(2,128)S(1)}, u32[]{:S(2)}, u32[]{:S(2)}) collective-permute-start(f32[4,2,2,2,1024]{4,3,2,1,0:T(2,128)S(1)} %get-tuple-element.42.refs_0_.own_ref), channel_id=1, source_target_pairs={{0,4},{4,0},{8,12},{12,8},{16,20},{20,16},{24,28},{28,24},{1,5},{5... | collective-permute-start | bytes 393224 | tf_op jit(solution)/shard_map/ppermute | solution.py:487
  68.3 2.3 %collective-permute-done.26.refs_4_ = f32[4,2,2,2,1024]{4,3,2,1,0:T(2,128)S(1)} collective-permute-done((f32[4,2,2,2,1024]{4,3,2,1,0:T(2,128)S(1)}, f32[4,2,2,2,1024]{4,3,2,1,0:T(2,128)S(1)}, u32[]{:S(2)}, u32[]{:S(2)}) %collective-permute-start.26) | collective-permute-done | bytes 131104 | tf_op jit(solution)/shard_map/ppermute | solution.py:487
  71.7 2.3 %collective-permute-start.28 = (f32[4,2,2,2,1024]{4,3,2,1,0:T(2,128)S(1)}, f32[4,2,2,2,1024]{4,3,2,1,0:T(2,128)S(1)}, u32[]{:S(2)}, u32[]{:S(2)}) collective-permute-start(f32[4,2,2,2,1024]{4,3,2,1,0:T(2,128)S(1)} %collective-permute-done.26.refs_4_), channel_id=1, source_target_pairs={{0,8},{4,12},{8,0},{12,4},{16,24},{20,28},{24,16},{28,20},{1,9},{5... | collective-permute-start | bytes 393224 | tf_op jit(solution)/shard_map/ppermute | solution.py:487
  75.3 3.9 %collective-permute-done.29.refs_2_ = f32[4,2,2,2,1024]{4,3,2,1,0:T(2,128)S(1)} collective-permute-done((f32[4,2,2,2,1024]{4,3,2,1,0:T(2,128)S(1)}, f32[4,2,2,2,1024]{4,3,2,1,0:T(2,128)S(1)}, u32[]{:S(2)}, u32[]{:S(2)}) %collective-permute-start.29) | collective-permute-done | bytes 131104 | tf_op jit(solution)/shard_map/ppermute | solution.py:487
  80.2 1.4 %shard_map.110 = (f32[8,4,2,2,2,1024]{5,4,3,2,1,0:T(2,128)}, f32[4,2,2,2,1024]{4,3,2,1,0:T(2,128)}) custom-call(f32[1,8]{1,0:T(1,128)S(1)} %copy-done.5, f32[8,8]{1,0:T(8,128)S(1)} %get-tuple-element.41.weights_ref, f32[4,2,2,2,1024]{4,3,2,1,0:T(2,128)S(1)} %get-tuple-element.42.refs_0_.own_ref, f32[8,4,2,2,2,1024]{5,4,3,2,1,0:T(2,128)S(1)} %shard_map.109.partial_ref, ...), custom_call_target="tpu_custom_call" | custom-call | tf_op jit(solution)/shard_map/pallas_call | solution.py:475
  (64 shorter events, 14.2 us)
Async XLA Ops:
  0.6 11.0 %copy-start = (f32[1,4,2,2,2,16,512]{6,5,4,3,2,1,0:T(8,128)S(1)}, f32[1,4,2,2,2,16,512]{6,5,4,3,2,1,0:T(8,128)}, u32[]{:S(2)}) copy-start(f32[1,4,2,2,2,16,512]{6,5,4,3,2,1,0:T(8,128)} %param.8) | copy-start | bytes 3145732
  0.7 11.0 %copy-start.3 = (s32[2,512]{1,0:T(2,128)S(1)}, s32[2,512]{1,0:T(2,128)}, u32[]{:S(2)}) copy-start(s32[2,512]{1,0:T(2,128)} %pairs_ref.15) | copy-start | bytes 12292
  3.3 1.5 %collective-permute-start = (f32[2,2,16,512]{3,2,1,0:T(8,128)S(1)}, f32[2,2,16,512]{3,2,1,0:T(8,128)S(1)}, u32[]{:S(2)}, u32[]{:S(2)}) collective-permute-start(f32[2,2,16,512]{3,2,1,0:T(8,128)S(1)} %get-tuple-element.26), channel_id=1, source_target_pairs={{0,1},{1,0},{2,3},{3,2},{4,5},{5,4},{6,7},{7,6},{8,9},{9,8},{10,11... | collective-permute-start | bytes 393224 | tf_op jit(solution)/shard_map/ppermute | solution.py:487
  4.9 6.7 %collective-permute-start.1 = (f32[2,2,16,512]{3,2,1,0:T(8,128)S(1)}, f32[2,2,16,512]{3,2,1,0:T(8,128)S(1)}, u32[]{:S(2)}, u32[]{:S(2)}) collective-permute-start(f32[2,2,16,512]{3,2,1,0:T(8,128)S(1)} %add.23), channel_id=1, source_target_pairs={{0,2},{1,3},{2,0},{3,1},{4,6},{5,7},{6,4},{7,5},{8,10},{9,11},{10,... | collective-permute-start | bytes 393224 | tf_op jit(solution)/shard_map/ppermute | solution.py:487
  11.6 3.1 %collective-permute-start.2 = (f32[2,2,16,512]{3,2,1,0:T(8,128)S(1)}, f32[2,2,16,512]{3,2,1,0:T(8,128)S(1)}, u32[]{:S(2)}, u32[]{:S(2)}) collective-permute-start(f32[2,2,16,512]{3,2,1,0:T(8,128)S(1)} %add.24.mine_ref), channel_id=1, source_target_pairs={{0,1},{1,0},{2,3},{3,2},{4,5},{5,4},{6,7},{7,6},{8,9},{9,8},{10,11... | collective-permute-start | bytes 393224 | tf_op jit(solution)/shard_map/ppermute | solution.py:487
  18.0 1.5 %collective-permute-start.3 = (f32[2,2,16,512]{3,2,1,0:T(8,128)S(1)}, f32[2,2,16,512]{3,2,1,0:T(8,128)S(1)}, u32[]{:S(2)}, u32[]{:S(2)}) collective-permute-start(f32[2,2,16,512]{3,2,1,0:T(8,128)S(1)} %get-tuple-element.32), channel_id=1, source_target_pairs={{0,1},{1,0},{2,3},{3,2},{4,5},{5,4},{6,7},{7,6},{8,9},{9,8},{10,11... | collective-permute-start | bytes 393224 | tf_op jit(solution)/shard_map/ppermute | solution.py:487
  19.6 6.9 %collective-permute-start.4 = (f32[2,2,16,512]{3,2,1,0:T(8,128)S(1)}, f32[2,2,16,512]{3,2,1,0:T(8,128)S(1)}, u32[]{:S(2)}, u32[]{:S(2)}) collective-permute-start(f32[2,2,16,512]{3,2,1,0:T(8,128)S(1)} %add.25), channel_id=1, source_target_pairs={{0,2},{1,3},{2,0},{3,1},{4,6},{5,7},{6,4},{7,5},{8,10},{9,11},{10,... | collective-permute-start | bytes 393224 | tf_op jit(solution)/shard_map/ppermute | solution.py:487
  21.4 9.5 %collective-permute-start.9 = (f32[264,128]{1,0:T(8,128)S(1)}, f32[264,128]{1,0:T(8,128)S(1)}, u32[]{:S(2)}, u32[]{:S(2)}) collective-permute-start(f32[264,128]{1,0:T(8,128)S(1)} %get-tuple-element.33.refs_0_), channel_id=1, source_target_pairs={{0,16},{4,20},{8,24},{12,28},{16,0},{20,4},{24,8},{28,12},{1,17},{... | collective-permute-start | bytes 405512 | tf_op jit(solution)/shard_map/ppermute | solution.py:487
  24.0 8.7 %collective-permute-start.8 = (f32[264,128]{1,0:T(8,128)S(1)}, f32[264,128]{1,0:T(8,128)S(1)}, u32[]{:S(2)}, u32[]{:S(2)}) collective-permute-start(f32[264,128]{1,0:T(8,128)S(1)} %get-tuple-element.33.refs_0_), channel_id=1, source_target_pairs={{0,12},{4,8},{8,4},{12,0},{16,28},{20,24},{24,20},{28,16},{1,13},{... | collective-permute-start | bytes 405512 | tf_op jit(solution)/shard_map/ppermute | solution.py:487
  26.5 7.8 %collective-permute-start.5 = (f32[2,2,16,512]{3,2,1,0:T(8,128)S(1)}, f32[2,2,16,512]{3,2,1,0:T(8,128)S(1)}, u32[]{:S(2)}, u32[]{:S(2)}) collective-permute-start(f32[2,2,16,512]{3,2,1,0:T(8,128)S(1)} %add.26.mine_ref), channel_id=1, source_target_pairs={{0,1},{1,0},{2,3},{3,2},{4,5},{5,4},{6,7},{7,6},{8,9},{9,8},{10,11... | collective-permute-start | bytes 393224 | tf_op jit(solution)/shard_map/ppermute | solution.py:487
  26.6 11.5 %collective-permute-start.7 = (f32[264,128]{1,0:T(8,128)S(1)}, f32[264,128]{1,0:T(8,128)S(1)}, u32[]{:S(2)}, u32[]{:S(2)}) collective-permute-start(f32[264,128]{1,0:T(8,128)S(1)} %get-tuple-element.33.refs_0_), channel_id=1, source_target_pairs={{0,8},{4,12},{8,0},{12,4},{16,24},{20,28},{24,16},{28,20},{1,9},{5... | collective-permute-start | bytes 405512 | tf_op jit(solution)/shard_map/ppermute | solution.py:487
  27.4 10.7 %collective-permute-start.6 = (f32[264,128]{1,0:T(8,128)S(1)}, f32[264,128]{1,0:T(8,128)S(1)}, u32[]{:S(2)}, u32[]{:S(2)}) collective-permute-start(f32[264,128]{1,0:T(8,128)S(1)} %get-tuple-element.33.refs_0_), channel_id=1, source_target_pairs={{0,4},{4,0},{8,12},{12,8},{16,20},{20,16},{24,28},{28,24},{1,5},{5... | collective-permute-start | bytes 405512 | tf_op jit(solution)/shard_map/ppermute | solution.py:487
  30.9 7.6 %collective-permute-start.12 = (f32[264,128]{1,0:T(8,128)S(1)}, f32[264,128]{1,0:T(8,128)S(1)}, u32[]{:S(2)}, u32[]{:S(2)}) collective-permute-start(f32[264,128]{1,0:T(8,128)S(1)} %collective-permute-done.9.refs_4_), channel_id=1, source_target_pairs={{0,12},{4,8},{8,4},{12,0},{16,28},{20,24},{24,20},{28,16},{1,13},{... | collective-permute-start | bytes 405512 | tf_op jit(solution)/shard_map/ppermute | solution.py:487
  32.7 8.0 %collective-permute-start.11 = (f32[264,128]{1,0:T(8,128)S(1)}, f32[264,128]{1,0:T(8,128)S(1)}, u32[]{:S(2)}, u32[]{:S(2)}) collective-permute-start(f32[264,128]{1,0:T(8,128)S(1)} %collective-permute-done.9.refs_4_), channel_id=1, source_target_pairs={{0,8},{4,12},{8,0},{12,4},{16,24},{20,28},{24,16},{28,20},{1,9},{5... | collective-permute-start | bytes 405512 | tf_op jit(solution)/shard_map/ppermute | solution.py:487
  34.3 6.4 %collective-permute-start.10 = (f32[264,128]{1,0:T(8,128)S(1)}, f32[264,128]{1,0:T(8,128)S(1)}, u32[]{:S(2)}, u32[]{:S(2)}) collective-permute-start(f32[264,128]{1,0:T(8,128)S(1)} %collective-permute-done.9.refs_4_), channel_id=1, source_target_pairs={{0,4},{4,0},{8,12},{12,8},{16,20},{20,16},{24,28},{28,24},{1,5},{5... | collective-permute-start | bytes 405512 | tf_op jit(solution)/shard_map/ppermute | solution.py:487
  43.3 1.9 %collective-permute-start.13 = (f32[2,2,16,512]{3,2,1,0:T(8,128)S(1)}, f32[2,2,16,512]{3,2,1,0:T(8,128)S(1)}, u32[]{:S(2)}, u32[]{:S(2)}) collective-permute-start(f32[2,2,16,512]{3,2,1,0:T(8,128)S(1)} %get-tuple-element.38), channel_id=1, source_target_pairs={{0,1},{1,0},{2,3},{3,2},{4,5},{5,4},{6,7},{7,6},{8,9},{9,8},{10,11... | collective-permute-start | bytes 393224 | tf_op jit(solution)/shard_map/ppermute | solution.py:487
  43.3 9.7 %collective-permute-start.19 = (f32[256,128]{1,0:T(8,128)S(1)}, f32[256,128]{1,0:T(8,128)S(1)}, u32[]{:S(2)}, u32[]{:S(2)}) collective-permute-start(f32[256,128]{1,0:T(8,128)S(1)} %get-tuple-element.39.refs_0_.own_ref), channel_id=1, source_target_pairs={{0,16},{4,20},{8,24},{12,28},{16,0},{20,4},{24,8},{28,12},{1,17},{... | collective-permute-start | bytes 393224 | tf_op jit(solution)/shard_map/ppermute | solution.py:487
  45.2 7.9 %collective-permute-start.14 = (f32[2,2,16,512]{3,2,1,0:T(8,128)S(1)}, f32[2,2,16,512]{3,2,1,0:T(8,128)S(1)}, u32[]{:S(2)}, u32[]{:S(2)}) collective-permute-start(f32[2,2,16,512]{3,2,1,0:T(8,128)S(1)} %add.27), channel_id=1, source_target_pairs={{0,2},{1,3},{2,0},{3,1},{4,6},{5,7},{6,4},{7,5},{8,10},{9,11},{10,... | collective-permute-start | bytes 393224 | tf_op jit(solution)/shard_map/ppermute | solution.py:487
  45.8 9.0 %collective-permute-start.18 = (f32[256,128]{1,0:T(8,128)S(1)}, f32[256,128]{1,0:T(8,128)S(1)}, u32[]{:S(2)}, u32[]{:S(2)}) collective-permute-start(f32[256,128]{1,0:T(8,128)S(1)} %get-tuple-element.39.refs_0_.own_ref), channel_id=1, source_target_pairs={{0,12},{4,8},{8,4},{12,0},{16,28},{20,24},{24,20},{28,16},{1,13},{... | collective-permute-start | bytes 393224 | tf_op jit(solution)/shard_map/ppermute | solution.py:487
  48.4 9.3 %collective-permute-start.17 = (f32[256,128]{1,0:T(8,128)S(1)}, f32[256,128]{1,0:T(8,128)S(1)}, u32[]{:S(2)}, u32[]{:S(2)}) collective-permute-start(f32[256,128]{1,0:T(8,128)S(1)} %get-tuple-element.39.refs_0_.own_ref), channel_id=1, source_target_pairs={{0,8},{4,12},{8,0},{12,4},{16,24},{20,28},{24,16},{28,20},{1,9},{5... | collective-permute-start | bytes 393224 | tf_op jit(solution)/shard_map/ppermute | solution.py:487
  48.7 10.6 %collective-permute-start.16 = (f32[256,128]{1,0:T(8,128)S(1)}, f32[256,128]{1,0:T(8,128)S(1)}, u32[]{:S(2)}, u32[]{:S(2)}) collective-permute-start(f32[256,128]{1,0:T(8,128)S(1)} %get-tuple-element.39.refs_0_.own_ref), channel_id=1, source_target_pairs={{0,4},{4,0},{8,12},{12,8},{16,20},{20,16},{24,28},{28,24},{1,5},{5... | collective-permute-start | bytes 393224 | tf_op jit(solution)/shard_map/ppermute | solution.py:487
  53.0 8.2 %collective-permute-start.22 = (f32[256,128]{1,0:T(8,128)S(1)}, f32[256,128]{1,0:T(8,128)S(1)}, u32[]{:S(2)}, u32[]{:S(2)}) collective-permute-start(f32[256,128]{1,0:T(8,128)S(1)} %collective-permute-done.19.refs_4_), channel_id=1, source_target_pairs={{0,12},{4,8},{8,4},{12,0},{16,28},{20,24},{24,20},{28,16},{1,13},{... | collective-permute-start | bytes 393224 | tf_op jit(solution)/shard_map/ppermute | solution.py:487
  53.1 6.4 %collective-permute-start.15 = (f32[2,2,16,512]{3,2,1,0:T(8,128)S(1)}, f32[2,2,16,512]{3,2,1,0:T(8,128)S(1)}, u32[]{:S(2)}, u32[]{:S(2)}) collective-permute-start(f32[2,2,16,512]{3,2,1,0:T(8,128)S(1)} %add.28.mine_ref), channel_id=1, source_target_pairs={{0,1},{1,0},{2,3},{3,2},{4,5},{5,4},{6,7},{7,6},{8,9},{9,8},{10,11... | collective-permute-start | bytes 393224 | tf_op jit(solution)/shard_map/ppermute | solution.py:487
  54.8 7.4 %collective-permute-start.21 = (f32[256,128]{1,0:T(8,128)S(1)}, f32[256,128]{1,0:T(8,128)S(1)}, u32[]{:S(2)}, u32[]{:S(2)}) collective-permute-start(f32[256,128]{1,0:T(8,128)S(1)} %collective-permute-done.19.refs_4_), channel_id=1, source_target_pairs={{0,8},{4,12},{8,0},{12,4},{16,24},{20,28},{24,16},{28,20},{1,9},{5... | collective-permute-start | bytes 393224 | tf_op jit(solution)/shard_map/ppermute | solution.py:487
  57.7 5.0 %collective-permute-start.20 = (f32[256,128]{1,0:T(8,128)S(1)}, f32[256,128]{1,0:T(8,128)S(1)}, u32[]{:S(2)}, u32[]{:S(2)}) collective-permute-start(f32[256,128]{1,0:T(8,128)S(1)} %collective-permute-done.19.refs_4_), channel_id=1, source_target_pairs={{0,4},{4,0},{8,12},{12,8},{16,20},{20,16},{24,28},{28,24},{1,5},{5... | collective-permute-start | bytes 393224 | tf_op jit(solution)/shard_map/ppermute | solution.py:487
  62.9 7.7 %collective-permute-start.26 = (f32[4,2,2,2,1024]{4,3,2,1,0:T(2,128)S(1)}, f32[4,2,2,2,1024]{4,3,2,1,0:T(2,128)S(1)}, u32[]{:S(2)}, u32[]{:S(2)}) collective-permute-start(f32[4,2,2,2,1024]{4,3,2,1,0:T(2,128)S(1)} %get-tuple-element.42.refs_0_.own_ref), channel_id=1, source_target_pairs={{0,16},{4,20},{8,24},{12,28},{16,0},{20,4},{24,8},{28,12},{1,17},{... | collective-permute-start | bytes 393224 | tf_op jit(solution)/shard_map/ppermute | solution.py:487
  64.4 9.6 %collective-permute-start.25 = (f32[4,2,2,2,1024]{4,3,2,1,0:T(2,128)S(1)}, f32[4,2,2,2,1024]{4,3,2,1,0:T(2,128)S(1)}, u32[]{:S(2)}, u32[]{:S(2)}) collective-permute-start(f32[4,2,2,2,1024]{4,3,2,1,0:T(2,128)S(1)} %get-tuple-element.42.refs_0_.own_ref), channel_id=1, source_target_pairs={{0,12},{4,8},{8,4},{12,0},{16,28},{20,24},{24,20},{28,16},{1,13},{... | collective-permute-start | bytes 393224 | tf_op jit(solution)/shard_map/ppermute | solution.py:487
  67.3 7.6 %collective-permute-start.24 = (f32[4,2,2,2,1024]{4,3,2,1,0:T(2,128)S(1)}, f32[4,2,2,2,1024]{4,3,2,1,0:T(2,128)S(1)}, u32[]{:S(2)}, u32[]{:S(2)}) collective-permute-start(f32[4,2,2,2,1024]{4,3,2,1,0:T(2,128)S(1)} %get-tuple-element.42.refs_0_.own_ref), channel_id=1, source_target_pairs={{0,8},{4,12},{8,0},{12,4},{16,24},{20,28},{24,16},{28,20},{1,9},{5... | collective-permute-start | bytes 393224 | tf_op jit(solution)/shard_map/ppermute | solution.py:487
  67.3 7.6 %collective-permute-start.23 = (f32[4,2,2,2,1024]{4,3,2,1,0:T(2,128)S(1)}, f32[4,2,2,2,1024]{4,3,2,1,0:T(2,128)S(1)}, u32[]{:S(2)}, u32[]{:S(2)}) collective-permute-start(f32[4,2,2,2,1024]{4,3,2,1,0:T(2,128)S(1)} %get-tuple-element.42.refs_0_.own_ref), channel_id=1, source_target_pairs={{0,4},{4,0},{8,12},{12,8},{16,20},{20,16},{24,28},{28,24},{1,5},{5... | collective-permute-start | bytes 393224 | tf_op jit(solution)/shard_map/ppermute | solution.py:487
  70.7 8.5 %collective-permute-start.29 = (f32[4,2,2,2,1024]{4,3,2,1,0:T(2,128)S(1)}, f32[4,2,2,2,1024]{4,3,2,1,0:T(2,128)S(1)}, u32[]{:S(2)}, u32[]{:S(2)}) collective-permute-start(f32[4,2,2,2,1024]{4,3,2,1,0:T(2,128)S(1)} %collective-permute-done.26.refs_4_), channel_id=1, source_target_pairs={{0,12},{4,8},{8,4},{12,0},{16,28},{20,24},{24,20},{28,16},{1,13},{... | collective-permute-start | bytes 393224 | tf_op jit(solution)/shard_map/ppermute | solution.py:487
  71.7 8.3 %collective-permute-start.28 = (f32[4,2,2,2,1024]{4,3,2,1,0:T(2,128)S(1)}, f32[4,2,2,2,1024]{4,3,2,1,0:T(2,128)S(1)}, u32[]{:S(2)}, u32[]{:S(2)}) collective-permute-start(f32[4,2,2,2,1024]{4,3,2,1,0:T(2,128)S(1)} %collective-permute-done.26.refs_4_), channel_id=1, source_target_pairs={{0,8},{4,12},{8,0},{12,4},{16,24},{20,28},{24,16},{28,20},{1,9},{5... | collective-permute-start | bytes 393224 | tf_op jit(solution)/shard_map/ppermute | solution.py:487
  74.0 6.3 %collective-permute-start.27 = (f32[4,2,2,2,1024]{4,3,2,1,0:T(2,128)S(1)}, f32[4,2,2,2,1024]{4,3,2,1,0:T(2,128)S(1)}, u32[]{:S(2)}, u32[]{:S(2)}) collective-permute-start(f32[4,2,2,2,1024]{4,3,2,1,0:T(2,128)S(1)} %collective-permute-done.26.refs_4_), channel_id=1, source_target_pairs={{0,4},{4,0},{8,12},{12,8},{16,20},{20,16},{24,28},{28,24},{1,5},{5... | collective-permute-start | bytes 393224 | tf_op jit(solution)/shard_map/ppermute | solution.py:487
  (4 other events, 11.7 us)

commit v7 on v6

--- a/solution.py
+++ b/solution.py
@@ -349,16 +349,14 @@
     return total
 
 
-def gathered_update_kernel(sums_ref, *refs):
-    units, (jones_ref, shared_ref, spread_ref, weights_ref) = refs[:-4], refs[-4:]
-    dirs = sums_ref.shape[1] // 12
-    chunks, _, width = sums_ref.shape
-    rows = 8 * dirs
-    terms = weights_ref.shape[0]
-    bands = len(units)
+def basis_of(units, at, terms):
+    return jnp.concatenate([ref[at : at + 1, :terms] for ref in units], axis=0)
+
+
+def weights_kernel(basis_ref, weights_ref):
+    terms, bands = weights_ref.shape
     hi = lax.Precision.HIGHEST
-    at = chunks * rows
-    basis = jnp.concatenate([ref[at : at + 1, :terms] for ref in units], axis=0)
+    basis = basis_ref[...]
     gram = lax.dot_general(basis, basis, (((0,), (0,)), ((), ())), precision=hi, preferred_element_type=jnp.float32)
     row = lax.broadcasted_iota(jnp.int32, (terms, terms), 0)
     col = lax.broadcasted_iota(jnp.int32, (terms, terms), 1)
@@ -372,10 +370,58 @@
         here = row == t
         gram = jnp.where(here, g_row, gram - factor * g_row)
         inverse = jnp.where(here, i_row, inverse - factor * i_row)
-    weights = lax.dot_general(inverse, basis, (((1,), (1,)), ((), ())), precision=hi, preferred_element_type=jnp.float32)
-    spread = jnp.dot(basis, weights, precision=hi, preferred_element_type=jnp.float32)
+    weights_ref[...] = lax.dot_general(
+        inverse, basis, (((1,), (1,)), ((), ())), precision=hi, preferred_element_type=jnp.float32
+    )
+
+
+def own_spread(basis):
+    bands, terms = basis.shape
+    entry = [
+        [jnp.broadcast_to(basis[f : f + 1, m : m + 1], (SUBLANES, LANES)) for m in range(terms)] for f in range(bands)
+    ]
+    gram = {}
+    for m in range(terms):
+        for n in range(m, terms):
+            total = None
+            for f in range(bands):
+                product = entry[f][m] * entry[f][n]
+                total = product if total is None else total + product
+            gram[m, n] = total + RIDGE * bands if m == n else total
+    right = list(entry[0])
+    scale = []
+    for t in range(terms):
+        scale.append(1.0 / gram[t, t])
+        for m in range(t + 1, terms):
+            factor = gram[t, m] * scale[t]
+            right[m] = right[m] - factor * right[t]
+            for n in range(m, terms):
+                gram[m, n] = gram[m, n] - factor * gram[t, n]
+    solved = [None] * terms
+    for t in reversed(range(terms)):
+        value = right[t]
+        for n in range(t + 1, terms):
+            value = value - gram[t, n] * solved[n]
+        solved[t] = value * scale[t]
+    out = []
+    for f in range(bands):
+        total = None
+        for m in range(terms):
+            product = solved[m] * entry[f][m]
+            total = product if total is None else total + product
+        out.append(total[0:1, 0:1])
+    return jnp.concatenate(out, axis=1)
+
+
+def gathered_update_kernel(sums_ref, *refs):
+    units, (jones_ref, shared_ref, spread_ref, basis_ref) = refs[:-4], refs[-4:]
+    dirs = sums_ref.shape[1] // 12
+    chunks, _, width = sums_ref.shape
+    rows = 8 * dirs
+    basis = basis_of(units, chunks * rows, basis_ref.shape[1])
+    basis_ref[...] = basis
+    spread = own_spread(basis)
     spread_ref[...] = spread
-    weights_ref[...] = weights
     for chunk in range(chunks):
         jones, shared = solve_gathered(chunk, spread, sums_ref, units, rows)
         for a in jones:
@@ -409,7 +455,7 @@
     units, (jones_ref, shared_ref) = refs[:-2], refs[-2:]
     dirs, width = sums_ref.shape[1] // 12, sums_ref.shape[2]
     rows = 8 * dirs
-    spread = spread_ref[0:1, spread_ref.shape[0] - len(units) :]
+    spread = spread_ref[:, spread_ref.shape[1] - len(units) :]
     for chunk in range(sums_ref.shape[0]):
         base = chunk * rows
         rest = weighted(spread, 0, [ref[base : base + rows, :] for ref in units])
@@ -583,9 +629,9 @@
         units = gather_bands(unit)
         started = model(jones)
         sums = station_sums(*started)
-        jones, unit, spread, weights = call(
+        jones, unit, spread, basis = call(
             gathered_update_kernel,
-            (flat, struct(chunks * rows, width), struct(bands, bands), struct(terms, bands)), VMEM, (sums, *units),
+            (flat, struct(chunks * rows, width), struct(1, bands), struct(bands, terms)), VMEM, (sums, *units),
         )
         units = gather_bands(unit)
         started = model(jones)
@@ -596,6 +642,7 @@
         )
         jones = call(native_kernel, struct(*native), VMEM, (jones,))
         units = gather_bands(shared)
+        weights = call(weights_kernel, struct(terms, bands), VMEM, (basis,))
         partial = call(partial_coeffs_kernel, struct(terms, *native), VMEM, (weights, *units[:early]))
         coeffs, dual = call(
             final_kernel, (struct(terms, *native), struct(*native)), VMEM,

time: 81.9 us -> 81.1 us (level)
  waiting for transfers between devices: 26.8 us -> 25.5 us
    ppermute x30, waiting for transfers between devices: 26.8 us -> 25.5 us  [swap(): return lax.ppermute(value, axis, [(i, i ^ bit) for i in range(size)])]
    pallas_call x17 -> x18, Pallas kernels: 20.3 us -> 20.4 us  [call(): pl.pallas_call(kernel, out_shape=out_shape, in_specs=[space if at else fi...]
  transfers between devices with their start and end apart: 30 -> 30, of which waited for: 16 -> 16; matrix products, arithmetic and copies ran while one was open for 0% -> 0% of each run, Pallas kernels for 13% -> 14%
where the time goes in v7:
time: 81.1 us; the launch traced here: 80.9 us
  starting transfers between devices  32.9 us (41%)
  waiting for transfers between devices  25.5 us (31%)
  Pallas kernels  20.4 us (25%)
  between operations  1.11 us (1%)
  local copies, waits for them, and re-layouts  0.87 us (1%)
    ppermute x30, starting transfers between devices, swap(): return lax.ppermute(value, axis, [(i, i ^ bit) for i in range(size)])  32.9 us
    ppermute x30, waiting for transfers between devices, swap(): return lax.ppermute(value, axis, [(i, i ^ bit) for i in range(size)])  25.5 us
    pallas_call x18, Pallas kernels, call(): pl.pallas_call(kernel, out_shape=out_shape, in_specs=[space if at else fi...  20.4 us
  transfers between devices with their start and end apart: 30, of which 16 were waited for; matrix products, arithmetic and copies ran while one was open for 0% of the time, Pallas kernels for 14%

profile of v7, /device:TPU:0, one launch (start us, length us, event | category | flops | bytes accessed | tf_op | source)
XLA Modules:
  0.0 80.9 jit_solution(898075995693895277)
XLA Ops:
  0.7 2.6 %shard_map.94 = (f32[32,1024]{1,0:T(8,128)S(1)}, f32[2,2,16,512]{3,2,1,0:T(8,128)S(1)}, f32[2,2,16,512]{3,2,1,0:T(8,128)S(1)}) custom-call(s32[8,128]{1,0:T(8,128)S(1)} %broadcast_in_dim.9.parity_ref, f32[4,2,2,2,1024]{4,3,2,1,0:T(2,128)} %bitcast.19, s32[2,512]{1,0:T(2,128)} %pairs_ref.15, f32[4,2,2,2,16,512]{5,4,3,2,1,0:T(8,128)} %bitcast.6), custom_call_target="tpu_custom_call" | custom-call | tf_op jit(solution)/shard_map/pallas_call | solution.py:521
  3.9 1.0 %collective-permute-done = f32[2,2,16,512]{3,2,1,0:T(8,128)S(1)} collective-permute-done((f32[2,2,16,512]{3,2,1,0:T(8,128)S(1)}, f32[2,2,16,512]{3,2,1,0:T(8,128)S(1)}, u32[]{:S(2)}, u32[]{:S(2)}) %collective-permute-start) | collective-permute-done | bytes 131104 | tf_op jit(solution)/shard_map/ppermute | solution.py:533
  4.9 2.9 %collective-permute-start.1 = (f32[2,2,16,512]{3,2,1,0:T(8,128)S(1)}, f32[2,2,16,512]{3,2,1,0:T(8,128)S(1)}, u32[]{:S(2)}, u32[]{:S(2)}) collective-permute-start(f32[2,2,16,512]{3,2,1,0:T(8,128)S(1)} %add.23), channel_id=1, source_target_pairs={{0,2},{1,3},{2,0},{3,1},{4,6},{5,7},{6,4},{7,5},{8,10},{9,11},{10,... | collective-permute-start | bytes 393224 | tf_op jit(solution)/shard_map/ppermute | solution.py:533
  7.8 3.8 %collective-permute-done.1 = f32[2,2,16,512]{3,2,1,0:T(8,128)S(1)} collective-permute-done((f32[2,2,16,512]{3,2,1,0:T(8,128)S(1)}, f32[2,2,16,512]{3,2,1,0:T(8,128)S(1)}, u32[]{:S(2)}, u32[]{:S(2)}) %collective-permute-start.1) | collective-permute-done | bytes 131104 | tf_op jit(solution)/shard_map/ppermute | solution.py:533
  11.7 1.6 %shard_map.95.base_ref = f32[8,48,128]{2,1,0:T(8,128)S(1)} custom-call(f32[32,1024]{1,0:T(8,128)S(1)} %get-tuple-element.24.gathered_ref, s32[2,512]{1,0:T(2,128)S(1)} %copy-done.3, f32[4,2,2,2,16,512]{5,4,3,2,1,0:T(8,128)S(1)} %bitcast.7), custom_call_target="tpu_custom_call" | custom-call | tf_op jit(solution)/shard_map/pallas_call | solution.py:521
  14.9 1.8 %shard_map.96.sums_ref = f32[8,48,128]{2,1,0:T(8,128)S(1)} custom-call(s32[8,128]{1,0:T(8,128)S(1)} %broadcast_in_dim.9.parity_ref, f32[32,1024]{1,0:T(8,128)S(1)} %get-tuple-element.24.gathered_ref, s32[2,512]{1,0:T(2,128)S(1)} %copy-done.3, f32[4,2,2,2,16,512]{5,4,3,2,1,0:T(8,128)S(1)} %bitcast.8, f32[2,2,2,16,512]{4,3,2,1,0:T(8,128)S(1)} %bitcast.15, ...), custom_call_target="tpu_custom_call" | custom-call | tf_op jit(solution)/shard_map/pallas_call | solution.py:521
  16.8 1.2 %shard_map.99 = (f32[32,1024]{1,0:T(8,128)S(1)}, f32[2,2,16,512]{3,2,1,0:T(8,128)S(1)}, f32[2,2,16,512]{3,2,1,0:T(8,128)S(1)}) custom-call(s32[8,128]{1,0:T(8,128)S(1)} %broadcast_in_dim.9.parity_ref, f32[32,1024]{1,0:T(8,128)S(1)} %get-tuple-element.29.jones_ref, s32[2,512]{1,0:T(2,128)S(1)} %copy-done.3, f32[4,2,2,2,16,512]{5,4,3,2,1,0:T(8,128)S(1)} %bitcast.9), custom_call_target="tpu_custom_call" | custom-call | tf_op jit(solution)/shard_map/pallas_call | solution.py:521
  19.6 1.8 %collective-permute-start.4 = (f32[2,2,16,512]{3,2,1,0:T(8,128)S(1)}, f32[2,2,16,512]{3,2,1,0:T(8,128)S(1)}, u32[]{:S(2)}, u32[]{:S(2)}) collective-permute-start(f32[2,2,16,512]{3,2,1,0:T(8,128)S(1)} %add.25), channel_id=1, source_target_pairs={{0,2},{1,3},{2,0},{3,1},{4,6},{5,7},{6,4},{7,5},{8,10},{9,11},{10,... | collective-permute-start | bytes 393224 | tf_op jit(solution)/shard_map/ppermute | solution.py:533
  21.4 2.6 %collective-permute-start.9 = (f32[264,128]{1,0:T(8,128)S(1)}, f32[264,128]{1,0:T(8,128)S(1)}, u32[]{:S(2)}, u32[]{:S(2)}) collective-permute-start(f32[264,128]{1,0:T(8,128)S(1)} %get-tuple-element.33.refs_0_), channel_id=1, source_target_pairs={{0,16},{4,20},{8,24},{12,28},{16,0},{20,4},{24,8},{28,12},{1,17},{... | collective-permute-start | bytes 405512 | tf_op jit(solution)/shard_map/ppermute | solution.py:533
  24.0 2.5 %collective-permute-start.8 = (f32[264,128]{1,0:T(8,128)S(1)}, f32[264,128]{1,0:T(8,128)S(1)}, u32[]{:S(2)}, u32[]{:S(2)}) collective-permute-start(f32[264,128]{1,0:T(8,128)S(1)} %get-tuple-element.33.refs_0_), channel_id=1, source_target_pairs={{0,12},{4,8},{8,4},{12,0},{16,28},{20,24},{24,20},{28,16},{1,13},{... | collective-permute-start | bytes 405512 | tf_op jit(solution)/shard_map/ppermute | solution.py:533
  27.4 1.5 %collective-permute-start.6 = (f32[264,128]{1,0:T(8,128)S(1)}, f32[264,128]{1,0:T(8,128)S(1)}, u32[]{:S(2)}, u32[]{:S(2)}) collective-permute-start(f32[264,128]{1,0:T(8,128)S(1)} %get-tuple-element.33.refs_0_), channel_id=1, source_target_pairs={{0,4},{4,0},{8,12},{12,8},{16,20},{20,16},{24,28},{28,24},{1,5},{5... | collective-permute-start | bytes 405512 | tf_op jit(solution)/shard_map/ppermute | solution.py:533
  28.9 1.9 %collective-permute-done.9.refs_4_ = f32[264,128]{1,0:T(8,128)S(1)} collective-permute-done((f32[264,128]{1,0:T(8,128)S(1)}, f32[264,128]{1,0:T(8,128)S(1)}, u32[]{:S(2)}, u32[]{:S(2)}) %collective-permute-start.9) | collective-permute-done | bytes 135200 | tf_op jit(solution)/shard_map/ppermute | solution.py:533
  30.9 1.6 %collective-permute-start.12 = (f32[264,128]{1,0:T(8,128)S(1)}, f32[264,128]{1,0:T(8,128)S(1)}, u32[]{:S(2)}, u32[]{:S(2)}) collective-permute-start(f32[264,128]{1,0:T(8,128)S(1)} %collective-permute-done.9.refs_4_), channel_id=1, source_target_pairs={{0,12},{4,8},{8,4},{12,0},{16,28},{20,24},{24,20},{28,16},{1,13},{... | collective-permute-start | bytes 405512 | tf_op jit(solution)/shard_map/ppermute | solution.py:533
  32.7 1.7 %collective-permute-start.11 = (f32[264,128]{1,0:T(8,128)S(1)}, f32[264,128]{1,0:T(8,128)S(1)}, u32[]{:S(2)}, u32[]{:S(2)}) collective-permute-start(f32[264,128]{1,0:T(8,128)S(1)} %collective-permute-done.9.refs_4_), channel_id=1, source_target_pairs={{0,8},{4,12},{8,0},{12,4},{16,24},{20,28},{24,16},{28,20},{1,9},{5... | collective-permute-start | bytes 405512 | tf_op jit(solution)/shard_map/ppermute | solution.py:533
  34.6 1.6 %shard_map.100.base_ref = f32[8,48,128]{2,1,0:T(8,128)S(1)} custom-call(f32[32,1024]{1,0:T(8,128)S(1)} %get-tuple-element.30.gathered_ref, s32[2,512]{1,0:T(2,128)S(1)} %copy-done.3, f32[4,2,2,2,16,512]{5,4,3,2,1,0:T(8,128)S(1)} %bitcast.10), custom_call_target="tpu_custom_call" | custom-call | tf_op jit(solution)/shard_map/pallas_call | solution.py:521
  36.2 1.8 %shard_map.101.sums_ref = f32[8,48,128]{2,1,0:T(8,128)S(1)} custom-call(s32[8,128]{1,0:T(8,128)S(1)} %broadcast_in_dim.9.parity_ref, f32[32,1024]{1,0:T(8,128)S(1)} %get-tuple-element.30.gathered_ref, s32[2,512]{1,0:T(2,128)S(1)} %copy-done.3, f32[4,2,2,2,16,512]{5,4,3,2,1,0:T(8,128)S(1)} %bitcast.11, f32[2,2,2,16,512]{4,3,2,1,0:T(8,128)S(1)} %bitcast.16, ...), custom_call_target="tpu_custom_call" | custom-call | tf_op jit(solution)/shard_map/pallas_call | solution.py:521
  38.5 2.2 %collective-permute-done.11.refs_6_ = f32[264,128]{1,0:T(8,128)S(1)} collective-permute-done((f32[264,128]{1,0:T(8,128)S(1)}, f32[264,128]{1,0:T(8,128)S(1)}, u32[]{:S(2)}, u32[]{:S(2)}) %collective-permute-start.11) | collective-permute-done | bytes 135200 | tf_op jit(solution)/shard_map/ppermute | solution.py:533
  41.3 1.2 %shard_map.103 = (f32[32,1024]{1,0:T(8,128)S(1)}, f32[2,2,16,512]{3,2,1,0:T(8,128)S(1)}, f32[2,2,16,512]{3,2,1,0:T(8,128)S(1)}) custom-call(s32[8,128]{1,0:T(8,128)S(1)} %broadcast_in_dim.9.parity_ref, f32[32,1024]{1,0:T(8,128)S(1)} %get-tuple-element.35.jones_ref, s32[2,512]{1,0:T(2,128)S(1)} %copy-done.3, f32[4,2,2,2,16,512]{5,4,3,2,1,0:T(8,128)S(1)} %bitcast.12), custom_call_target="tpu_custom_call" | custom-call | tf_op jit(solution)/shard_map/pallas_call | solution.py:521
  42.5 1.8 %collective-permute-start.19 = (f32[256,128]{1,0:T(8,128)S(1)}, f32[256,128]{1,0:T(8,128)S(1)}, u32[]{:S(2)}, u32[]{:S(2)}) collective-permute-start(f32[256,128]{1,0:T(8,128)S(1)} %get-tuple-element.39.refs_0_.own_ref), channel_id=1, source_target_pairs={{0,16},{4,20},{8,24},{12,28},{16,0},{20,4},{24,8},{28,12},{1,17},{... | collective-permute-start | bytes 393224 | tf_op jit(solution)/shard_map/ppermute | solution.py:533
  45.0 2.6 %collective-permute-start.18 = (f32[256,128]{1,0:T(8,128)S(1)}, f32[256,128]{1,0:T(8,128)S(1)}, u32[]{:S(2)}, u32[]{:S(2)}) collective-permute-start(f32[256,128]{1,0:T(8,128)S(1)} %get-tuple-element.39.refs_0_.own_ref), channel_id=1, source_target_pairs={{0,12},{4,8},{8,4},{12,0},{16,28},{20,24},{24,20},{28,16},{1,13},{... | collective-permute-start | bytes 393224 | tf_op jit(solution)/shard_map/ppermute | solution.py:533
  48.5 3.8 %collective-permute-done.19.refs_4_ = f32[256,128]{1,0:T(8,128)S(1)} collective-permute-done((f32[256,128]{1,0:T(8,128)S(1)}, f32[256,128]{1,0:T(8,128)S(1)}, u32[]{:S(2)}, u32[]{:S(2)}) %collective-permute-start.19) | collective-permute-done | bytes 131104 | tf_op jit(solution)/shard_map/ppermute | solution.py:533
  52.5 1.4 %collective-permute-done.18.refs_3_ = f32[256,128]{1,0:T(8,128)S(1)} collective-permute-done((f32[256,128]{1,0:T(8,128)S(1)}, f32[256,128]{1,0:T(8,128)S(1)}, u32[]{:S(2)}, u32[]{:S(2)}) %collective-permute-start.18) | collective-permute-done | bytes 131104 | tf_op jit(solution)/shard_map/ppermute | solution.py:533
  54.9 2.0 %collective-permute-done.17.refs_2_ = f32[256,128]{1,0:T(8,128)S(1)} collective-permute-done((f32[256,128]{1,0:T(8,128)S(1)}, f32[256,128]{1,0:T(8,128)S(1)}, u32[]{:S(2)}, u32[]{:S(2)}) %collective-permute-start.17) | collective-permute-done | bytes 131104 | tf_op jit(solution)/shard_map/ppermute | solution.py:533
  56.9 1.6 %shard_map.104.base_ref = f32[8,48,128]{2,1,0:T(8,128)S(1)} custom-call(f32[32,1024]{1,0:T(8,128)S(1)} %get-tuple-element.36.gathered_ref, s32[2,512]{1,0:T(2,128)S(1)} %copy-done.3, f32[4,2,2,2,16,512]{5,4,3,2,1,0:T(8,128)S(1)} %bitcast.13), custom_call_target="tpu_custom_call" | custom-call | tf_op jit(solution)/shard_map/pallas_call | solution.py:521
  58.6 1.8 %shard_map.105.sums_ref = f32[8,48,128]{2,1,0:T(8,128)S(1)} custom-call(s32[8,128]{1,0:T(8,128)S(1)} %broadcast_in_dim.9.parity_ref, f32[32,1024]{1,0:T(8,128)S(1)} %get-tuple-element.36.gathered_ref, s32[2,512]{1,0:T(2,128)S(1)} %copy-done.3, f32[4,2,2,2,16,512]{5,4,3,2,1,0:T(8,128)S(1)} %bitcast.14, f32[2,2,2,16,512]{4,3,2,1,0:T(8,128)S(1)} %bitcast.17, ...), custom_call_target="tpu_custom_call" | custom-call | tf_op jit(solution)/shard_map/pallas_call | solution.py:521
  62.1 1.5 %collective-permute-start.26 = (f32[4,2,2,2,1024]{4,3,2,1,0:T(2,128)S(1)}, f32[4,2,2,2,1024]{4,3,2,1,0:T(2,128)S(1)}, u32[]{:S(2)}, u32[]{:S(2)}) collective-permute-start(f32[4,2,2,2,1024]{4,3,2,1,0:T(2,128)S(1)} %get-tuple-element.42.refs_0_.own_ref), channel_id=1, source_target_pairs={{0,16},{4,20},{8,24},{12,28},{16,0},{20,4},{24,8},{28,12},{1,17},{... | collective-permute-start | bytes 393224 | tf_op jit(solution)/shard_map/ppermute | solution.py:533
  63.6 2.9 %collective-permute-start.25 = (f32[4,2,2,2,1024]{4,3,2,1,0:T(2,128)S(1)}, f32[4,2,2,2,1024]{4,3,2,1,0:T(2,128)S(1)}, u32[]{:S(2)}, u32[]{:S(2)}) collective-permute-start(f32[4,2,2,2,1024]{4,3,2,1,0:T(2,128)S(1)} %get-tuple-element.42.refs_0_.own_ref), channel_id=1, source_target_pairs={{0,12},{4,8},{8,4},{12,0},{16,28},{20,24},{24,20},{28,16},{1,13},{... | collective-permute-start | bytes 393224 | tf_op jit(solution)/shard_map/ppermute | solution.py:533
  66.5 1.0 %collective-permute-start.23 = (f32[4,2,2,2,1024]{4,3,2,1,0:T(2,128)S(1)}, f32[4,2,2,2,1024]{4,3,2,1,0:T(2,128)S(1)}, u32[]{:S(2)}, u32[]{:S(2)}) collective-permute-start(f32[4,2,2,2,1024]{4,3,2,1,0:T(2,128)S(1)} %get-tuple-element.42.refs_0_.own_ref), channel_id=1, source_target_pairs={{0,4},{4,0},{8,12},{12,8},{16,20},{20,16},{24,28},{28,24},{1,5},{5... | collective-permute-start | bytes 393224 | tf_op jit(solution)/shard_map/ppermute | solution.py:533
  67.5 2.3 %collective-permute-done.26.refs_4_ = f32[4,2,2,2,1024]{4,3,2,1,0:T(2,128)S(1)} collective-permute-done((f32[4,2,2,2,1024]{4,3,2,1,0:T(2,128)S(1)}, f32[4,2,2,2,1024]{4,3,2,1,0:T(2,128)S(1)}, u32[]{:S(2)}, u32[]{:S(2)}) %collective-permute-start.26) | collective-permute-done | bytes 131104 | tf_op jit(solution)/shard_map/ppermute | solution.py:533
  70.8 2.3 %collective-permute-start.28 = (f32[4,2,2,2,1024]{4,3,2,1,0:T(2,128)S(1)}, f32[4,2,2,2,1024]{4,3,2,1,0:T(2,128)S(1)}, u32[]{:S(2)}, u32[]{:S(2)}) collective-permute-start(f32[4,2,2,2,1024]{4,3,2,1,0:T(2,128)S(1)} %collective-permute-done.26.refs_4_), channel_id=1, source_target_pairs={{0,8},{4,12},{8,0},{12,4},{16,24},{20,28},{24,16},{28,20},{1,9},{5... | collective-permute-start | bytes 393224 | tf_op jit(solution)/shard_map/ppermute | solution.py:533
  75.5 2.9 %collective-permute-done.29.refs_2_ = f32[4,2,2,2,1024]{4,3,2,1,0:T(2,128)S(1)} collective-permute-done((f32[4,2,2,2,1024]{4,3,2,1,0:T(2,128)S(1)}, f32[4,2,2,2,1024]{4,3,2,1,0:T(2,128)S(1)}, u32[]{:S(2)}, u32[]{:S(2)}) %collective-permute-start.29) | collective-permute-done | bytes 131104 | tf_op jit(solution)/shard_map/ppermute | solution.py:533
  79.4 1.4 %shard_map.111 = (f32[8,4,2,2,2,1024]{5,4,3,2,1,0:T(2,128)}, f32[4,2,2,2,1024]{4,3,2,1,0:T(2,128)}) custom-call(f32[1,8]{1,0:T(1,128)S(1)} %copy-done.5, f32[8,8]{1,0:T(8,128)S(1)} %shard_map.109.weights_ref, f32[4,2,2,2,1024]{4,3,2,1,0:T(2,128)S(1)} %get-tuple-element.42.refs_0_.own_ref, f32[8,4,2,2,2,1024]{5,4,3,2,1,0:T(2,128)S(1)} %shard_map.110.partial_ref, ...), custom_call_target="tpu_custom_call" | custom-call | tf_op jit(solution)/shard_map/pallas_call | solution.py:521
  (65 shorter events, 15.1 us)
Async XLA Ops:
  0.6 11.0 %copy-start = (f32[1,4,2,2,2,16,512]{6,5,4,3,2,1,0:T(8,128)S(1)}, f32[1,4,2,2,2,16,512]{6,5,4,3,2,1,0:T(8,128)}, u32[]{:S(2)}) copy-start(f32[1,4,2,2,2,16,512]{6,5,4,3,2,1,0:T(8,128)} %param.8) | copy-start | bytes 3145732
  0.7 11.0 %copy-start.3 = (s32[2,512]{1,0:T(2,128)S(1)}, s32[2,512]{1,0:T(2,128)}, u32[]{:S(2)}) copy-start(s32[2,512]{1,0:T(2,128)} %pairs_ref.15) | copy-start | bytes 12292
  3.3 1.5 %collective-permute-start = (f32[2,2,16,512]{3,2,1,0:T(8,128)S(1)}, f32[2,2,16,512]{3,2,1,0:T(8,128)S(1)}, u32[]{:S(2)}, u32[]{:S(2)}) collective-permute-start(f32[2,2,16,512]{3,2,1,0:T(8,128)S(1)} %get-tuple-element.26), channel_id=1, source_target_pairs={{0,1},{1,0},{2,3},{3,2},{4,5},{5,4},{6,7},{7,6},{8,9},{9,8},{10,11... | collective-permute-start | bytes 393224 | tf_op jit(solution)/shard_map/ppermute | solution.py:533
  4.9 6.7 %collective-permute-start.1 = (f32[2,2,16,512]{3,2,1,0:T(8,128)S(1)}, f32[2,2,16,512]{3,2,1,0:T(8,128)S(1)}, u32[]{:S(2)}, u32[]{:S(2)}) collective-permute-start(f32[2,2,16,512]{3,2,1,0:T(8,128)S(1)} %add.23), channel_id=1, source_target_pairs={{0,2},{1,3},{2,0},{3,1},{4,6},{5,7},{6,4},{7,5},{8,10},{9,11},{10,... | collective-permute-start | bytes 393224 | tf_op jit(solution)/shard_map/ppermute | solution.py:533
  11.6 3.1 %collective-permute-start.2 = (f32[2,2,16,512]{3,2,1,0:T(8,128)S(1)}, f32[2,2,16,512]{3,2,1,0:T(8,128)S(1)}, u32[]{:S(2)}, u32[]{:S(2)}) collective-permute-start(f32[2,2,16,512]{3,2,1,0:T(8,128)S(1)} %add.24.mine_ref), channel_id=1, source_target_pairs={{0,1},{1,0},{2,3},{3,2},{4,5},{5,4},{6,7},{7,6},{8,9},{9,8},{10,11... | collective-permute-start | bytes 393224 | tf_op jit(solution)/shard_map/ppermute | solution.py:533
  18.0 1.5 %collective-permute-start.3 = (f32[2,2,16,512]{3,2,1,0:T(8,128)S(1)}, f32[2,2,16,512]{3,2,1,0:T(8,128)S(1)}, u32[]{:S(2)}, u32[]{:S(2)}) collective-permute-start(f32[2,2,16,512]{3,2,1,0:T(8,128)S(1)} %get-tuple-element.32), channel_id=1, source_target_pairs={{0,1},{1,0},{2,3},{3,2},{4,5},{5,4},{6,7},{7,6},{8,9},{9,8},{10,11... | collective-permute-start | bytes 393224 | tf_op jit(solution)/shard_map/ppermute | solution.py:533
  19.6 6.9 %collective-permute-start.4 = (f32[2,2,16,512]{3,2,1,0:T(8,128)S(1)}, f32[2,2,16,512]{3,2,1,0:T(8,128)S(1)}, u32[]{:S(2)}, u32[]{:S(2)}) collective-permute-start(f32[2,2,16,512]{3,2,1,0:T(8,128)S(1)} %add.25), channel_id=1, source_target_pairs={{0,2},{1,3},{2,0},{3,1},{4,6},{5,7},{6,4},{7,5},{8,10},{9,11},{10,... | collective-permute-start | bytes 393224 | tf_op jit(solution)/shard_map/ppermute | solution.py:533
  21.4 9.5 %collective-permute-start.9 = (f32[264,128]{1,0:T(8,128)S(1)}, f32[264,128]{1,0:T(8,128)S(1)}, u32[]{:S(2)}, u32[]{:S(2)}) collective-permute-start(f32[264,128]{1,0:T(8,128)S(1)} %get-tuple-element.33.refs_0_), channel_id=1, source_target_pairs={{0,16},{4,20},{8,24},{12,28},{16,0},{20,4},{24,8},{28,12},{1,17},{... | collective-permute-start | bytes 405512 | tf_op jit(solution)/shard_map/ppermute | solution.py:533
  24.0 8.7 %collective-permute-start.8 = (f32[264,128]{1,0:T(8,128)S(1)}, f32[264,128]{1,0:T(8,128)S(1)}, u32[]{:S(2)}, u32[]{:S(2)}) collective-permute-start(f32[264,128]{1,0:T(8,128)S(1)} %get-tuple-element.33.refs_0_), channel_id=1, source_target_pairs={{0,12},{4,8},{8,4},{12,0},{16,28},{20,24},{24,20},{28,16},{1,13},{... | collective-permute-start | bytes 405512 | tf_op jit(solution)/shard_map/ppermute | solution.py:533
  26.5 7.8 %collective-permute-start.5 = (f32[2,2,16,512]{3,2,1,0:T(8,128)S(1)}, f32[2,2,16,512]{3,2,1,0:T(8,128)S(1)}, u32[]{:S(2)}, u32[]{:S(2)}) collective-permute-start(f32[2,2,16,512]{3,2,1,0:T(8,128)S(1)} %add.26.mine_ref), channel_id=1, source_target_pairs={{0,1},{1,0},{2,3},{3,2},{4,5},{5,4},{6,7},{7,6},{8,9},{9,8},{10,11... | collective-permute-start | bytes 393224 | tf_op jit(solution)/shard_map/ppermute | solution.py:533
  26.6 11.5 %collective-permute-start.7 = (f32[264,128]{1,0:T(8,128)S(1)}, f32[264,128]{1,0:T(8,128)S(1)}, u32[]{:S(2)}, u32[]{:S(2)}) collective-permute-start(f32[264,128]{1,0:T(8,128)S(1)} %get-tuple-element.33.refs_0_), channel_id=1, source_target_pairs={{0,8},{4,12},{8,0},{12,4},{16,24},{20,28},{24,16},{28,20},{1,9},{5... | collective-permute-start | bytes 405512 | tf_op jit(solution)/shard_map/ppermute | solution.py:533
  27.4 10.7 %collective-permute-start.6 = (f32[264,128]{1,0:T(8,128)S(1)}, f32[264,128]{1,0:T(8,128)S(1)}, u32[]{:S(2)}, u32[]{:S(2)}) collective-permute-start(f32[264,128]{1,0:T(8,128)S(1)} %get-tuple-element.33.refs_0_), channel_id=1, source_target_pairs={{0,4},{4,0},{8,12},{12,8},{16,20},{20,16},{24,28},{28,24},{1,5},{5... | collective-permute-start | bytes 405512 | tf_op jit(solution)/shard_map/ppermute | solution.py:533
  30.9 7.6 %collective-permute-start.12 = (f32[264,128]{1,0:T(8,128)S(1)}, f32[264,128]{1,0:T(8,128)S(1)}, u32[]{:S(2)}, u32[]{:S(2)}) collective-permute-start(f32[264,128]{1,0:T(8,128)S(1)} %collective-permute-done.9.refs_4_), channel_id=1, source_target_pairs={{0,12},{4,8},{8,4},{12,0},{16,28},{20,24},{24,20},{28,16},{1,13},{... | collective-permute-start | bytes 405512 | tf_op jit(solution)/shard_map/ppermute | solution.py:533
  32.7 8.0 %collective-permute-start.11 = (f32[264,128]{1,0:T(8,128)S(1)}, f32[264,128]{1,0:T(8,128)S(1)}, u32[]{:S(2)}, u32[]{:S(2)}) collective-permute-start(f32[264,128]{1,0:T(8,128)S(1)} %collective-permute-done.9.refs_4_), channel_id=1, source_target_pairs={{0,8},{4,12},{8,0},{12,4},{16,24},{20,28},{24,16},{28,20},{1,9},{5... | collective-permute-start | bytes 405512 | tf_op jit(solution)/shard_map/ppermute | solution.py:533
  34.3 6.4 %collective-permute-start.10 = (f32[264,128]{1,0:T(8,128)S(1)}, f32[264,128]{1,0:T(8,128)S(1)}, u32[]{:S(2)}, u32[]{:S(2)}) collective-permute-start(f32[264,128]{1,0:T(8,128)S(1)} %collective-permute-done.9.refs_4_), channel_id=1, source_target_pairs={{0,4},{4,0},{8,12},{12,8},{16,20},{20,16},{24,28},{28,24},{1,5},{5... | collective-permute-start | bytes 405512 | tf_op jit(solution)/shard_map/ppermute | solution.py:533
  42.5 1.9 %collective-permute-start.13 = (f32[2,2,16,512]{3,2,1,0:T(8,128)S(1)}, f32[2,2,16,512]{3,2,1,0:T(8,128)S(1)}, u32[]{:S(2)}, u32[]{:S(2)}) collective-permute-start(f32[2,2,16,512]{3,2,1,0:T(8,128)S(1)} %get-tuple-element.38), channel_id=1, source_target_pairs={{0,1},{1,0},{2,3},{3,2},{4,5},{5,4},{6,7},{7,6},{8,9},{9,8},{10,11... | collective-permute-start | bytes 393224 | tf_op jit(solution)/shard_map/ppermute | solution.py:533
  42.5 9.7 %collective-permute-start.19 = (f32[256,128]{1,0:T(8,128)S(1)}, f32[256,128]{1,0:T(8,128)S(1)}, u32[]{:S(2)}, u32[]{:S(2)}) collective-permute-start(f32[256,128]{1,0:T(8,128)S(1)} %get-tuple-element.39.refs_0_.own_ref), channel_id=1, source_target_pairs={{0,16},{4,20},{8,24},{12,28},{16,0},{20,4},{24,8},{28,12},{1,17},{... | collective-permute-start | bytes 393224 | tf_op jit(solution)/shard_map/ppermute | solution.py:533
  44.4 7.9 %collective-permute-start.14 = (f32[2,2,16,512]{3,2,1,0:T(8,128)S(1)}, f32[2,2,16,512]{3,2,1,0:T(8,128)S(1)}, u32[]{:S(2)}, u32[]{:S(2)}) collective-permute-start(f32[2,2,16,512]{3,2,1,0:T(8,128)S(1)} %add.27), channel_id=1, source_target_pairs={{0,2},{1,3},{2,0},{3,1},{4,6},{5,7},{6,4},{7,5},{8,10},{9,11},{10,... | collective-permute-start | bytes 393224 | tf_op jit(solution)/shard_map/ppermute | solution.py:533
  45.0 9.0 %collective-permute-start.18 = (f32[256,128]{1,0:T(8,128)S(1)}, f32[256,128]{1,0:T(8,128)S(1)}, u32[]{:S(2)}, u32[]{:S(2)}) collective-permute-start(f32[256,128]{1,0:T(8,128)S(1)} %get-tuple-element.39.refs_0_.own_ref), channel_id=1, source_target_pairs={{0,12},{4,8},{8,4},{12,0},{16,28},{20,24},{24,20},{28,16},{1,13},{... | collective-permute-start | bytes 393224 | tf_op jit(solution)/shard_map/ppermute | solution.py:533
  47.6 9.3 %collective-permute-start.17 = (f32[256,128]{1,0:T(8,128)S(1)}, f32[256,128]{1,0:T(8,128)S(1)}, u32[]{:S(2)}, u32[]{:S(2)}) collective-permute-start(f32[256,128]{1,0:T(8,128)S(1)} %get-tuple-element.39.refs_0_.own_ref), channel_id=1, source_target_pairs={{0,8},{4,12},{8,0},{12,4},{16,24},{20,28},{24,16},{28,20},{1,9},{5... | collective-permute-start | bytes 393224 | tf_op jit(solution)/shard_map/ppermute | solution.py:533
  47.9 10.6 %collective-permute-start.16 = (f32[256,128]{1,0:T(8,128)S(1)}, f32[256,128]{1,0:T(8,128)S(1)}, u32[]{:S(2)}, u32[]{:S(2)}) collective-permute-start(f32[256,128]{1,0:T(8,128)S(1)} %get-tuple-element.39.refs_0_.own_ref), channel_id=1, source_target_pairs={{0,4},{4,0},{8,12},{12,8},{16,20},{20,16},{24,28},{28,24},{1,5},{5... | collective-permute-start | bytes 393224 | tf_op jit(solution)/shard_map/ppermute | solution.py:533
  52.2 8.2 %collective-permute-start.22 = (f32[256,128]{1,0:T(8,128)S(1)}, f32[256,128]{1,0:T(8,128)S(1)}, u32[]{:S(2)}, u32[]{:S(2)}) collective-permute-start(f32[256,128]{1,0:T(8,128)S(1)} %collective-permute-done.19.refs_4_), channel_id=1, source_target_pairs={{0,12},{4,8},{8,4},{12,0},{16,28},{20,24},{24,20},{28,16},{1,13},{... | collective-permute-start | bytes 393224 | tf_op jit(solution)/shard_map/ppermute | solution.py:533
  52.3 6.3 %collective-permute-start.15 = (f32[2,2,16,512]{3,2,1,0:T(8,128)S(1)}, f32[2,2,16,512]{3,2,1,0:T(8,128)S(1)}, u32[]{:S(2)}, u32[]{:S(2)}) collective-permute-start(f32[2,2,16,512]{3,2,1,0:T(8,128)S(1)} %add.28.mine_ref), channel_id=1, source_target_pairs={{0,1},{1,0},{2,3},{3,2},{4,5},{5,4},{6,7},{7,6},{8,9},{9,8},{10,11... | collective-permute-start | bytes 393224 | tf_op jit(solution)/shard_map/ppermute | solution.py:533
  54.0 7.4 %collective-permute-start.21 = (f32[256,128]{1,0:T(8,128)S(1)}, f32[256,128]{1,0:T(8,128)S(1)}, u32[]{:S(2)}, u32[]{:S(2)}) collective-permute-start(f32[256,128]{1,0:T(8,128)S(1)} %collective-permute-done.19.refs_4_), channel_id=1, source_target_pairs={{0,8},{4,12},{8,0},{12,4},{16,24},{20,28},{24,16},{28,20},{1,9},{5... | collective-permute-start | bytes 393224 | tf_op jit(solution)/shard_map/ppermute | solution.py:533
  56.9 5.0 %collective-permute-start.20 = (f32[256,128]{1,0:T(8,128)S(1)}, f32[256,128]{1,0:T(8,128)S(1)}, u32[]{:S(2)}, u32[]{:S(2)}) collective-permute-start(f32[256,128]{1,0:T(8,128)S(1)} %collective-permute-done.19.refs_4_), channel_id=1, source_target_pairs={{0,4},{4,0},{8,12},{12,8},{16,20},{20,16},{24,28},{28,24},{1,5},{5... | collective-permute-start | bytes 393224 | tf_op jit(solution)/shard_map/ppermute | solution.py:533
  62.1 7.7 %collective-permute-start.26 = (f32[4,2,2,2,1024]{4,3,2,1,0:T(2,128)S(1)}, f32[4,2,2,2,1024]{4,3,2,1,0:T(2,128)S(1)}, u32[]{:S(2)}, u32[]{:S(2)}) collective-permute-start(f32[4,2,2,2,1024]{4,3,2,1,0:T(2,128)S(1)} %get-tuple-element.42.refs_0_.own_ref), channel_id=1, source_target_pairs={{0,16},{4,20},{8,24},{12,28},{16,0},{20,4},{24,8},{28,12},{1,17},{... | collective-permute-start | bytes 393224 | tf_op jit(solution)/shard_map/ppermute | solution.py:533
  63.6 9.6 %collective-permute-start.25 = (f32[4,2,2,2,1024]{4,3,2,1,0:T(2,128)S(1)}, f32[4,2,2,2,1024]{4,3,2,1,0:T(2,128)S(1)}, u32[]{:S(2)}, u32[]{:S(2)}) collective-permute-start(f32[4,2,2,2,1024]{4,3,2,1,0:T(2,128)S(1)} %get-tuple-element.42.refs_0_.own_ref), channel_id=1, source_target_pairs={{0,12},{4,8},{8,4},{12,0},{16,28},{20,24},{24,20},{28,16},{1,13},{... | collective-permute-start | bytes 393224 | tf_op jit(solution)/shard_map/ppermute | solution.py:533
  66.5 8.5 %collective-permute-start.24 = (f32[4,2,2,2,1024]{4,3,2,1,0:T(2,128)S(1)}, f32[4,2,2,2,1024]{4,3,2,1,0:T(2,128)S(1)}, u32[]{:S(2)}, u32[]{:S(2)}) collective-permute-start(f32[4,2,2,2,1024]{4,3,2,1,0:T(2,128)S(1)} %get-tuple-element.42.refs_0_.own_ref), channel_id=1, source_target_pairs={{0,8},{4,12},{8,0},{12,4},{16,24},{20,28},{24,16},{28,20},{1,9},{5... | collective-permute-start | bytes 393224 | tf_op jit(solution)/shard_map/ppermute | solution.py:533
  66.5 8.5 %collective-permute-start.23 = (f32[4,2,2,2,1024]{4,3,2,1,0:T(2,128)S(1)}, f32[4,2,2,2,1024]{4,3,2,1,0:T(2,128)S(1)}, u32[]{:S(2)}, u32[]{:S(2)}) collective-permute-start(f32[4,2,2,2,1024]{4,3,2,1,0:T(2,128)S(1)} %get-tuple-element.42.refs_0_.own_ref), channel_id=1, source_target_pairs={{0,4},{4,0},{8,12},{12,8},{16,20},{20,16},{24,28},{28,24},{1,5},{5... | collective-permute-start | bytes 393224 | tf_op jit(solution)/shard_map/ppermute | solution.py:533
  69.9 8.6 %collective-permute-start.29 = (f32[4,2,2,2,1024]{4,3,2,1,0:T(2,128)S(1)}, f32[4,2,2,2,1024]{4,3,2,1,0:T(2,128)S(1)}, u32[]{:S(2)}, u32[]{:S(2)}) collective-permute-start(f32[4,2,2,2,1024]{4,3,2,1,0:T(2,128)S(1)} %collective-permute-done.26.refs_4_), channel_id=1, source_target_pairs={{0,12},{4,8},{8,4},{12,0},{16,28},{20,24},{24,20},{28,16},{1,13},{... | collective-permute-start | bytes 393224 | tf_op jit(solution)/shard_map/ppermute | solution.py:533
  70.8 8.3 %collective-permute-start.28 = (f32[4,2,2,2,1024]{4,3,2,1,0:T(2,128)S(1)}, f32[4,2,2,2,1024]{4,3,2,1,0:T(2,128)S(1)}, u32[]{:S(2)}, u32[]{:S(2)}) collective-permute-start(f32[4,2,2,2,1024]{4,3,2,1,0:T(2,128)S(1)} %collective-permute-done.26.refs_4_), channel_id=1, source_target_pairs={{0,8},{4,12},{8,0},{12,4},{16,24},{20,28},{24,16},{28,20},{1,9},{5... | collective-permute-start | bytes 393224 | tf_op jit(solution)/shard_map/ppermute | solution.py:533
  73.1 6.3 %collective-permute-start.27 = (f32[4,2,2,2,1024]{4,3,2,1,0:T(2,128)S(1)}, f32[4,2,2,2,1024]{4,3,2,1,0:T(2,128)S(1)}, u32[]{:S(2)}, u32[]{:S(2)}) collective-permute-start(f32[4,2,2,2,1024]{4,3,2,1,0:T(2,128)S(1)} %collective-permute-done.26.refs_4_), channel_id=1, source_target_pairs={{0,4},{4,0},{8,12},{12,8},{16,20},{20,16},{24,28},{28,24},{1,5},{5... | collective-permute-start | bytes 393224 | tf_op jit(solution)/shard_map/ppermute | solution.py:533
  (4 other events, 11.7 us)
